TPU v7x, 8 devices: a whole 2x2x1 slice. The times are simulated.
8 devices in a mesh: sp: 8 (over z, y, x, core).
Axes of the slice: x: 2, y: 2, z: 1, core: 2. Of those that a mesh axis runs over, the one named last changes fastest.
Arguments:
- x_in: bfloat16 [16, 1024, 2048], P(None, 'sp')
- grad_y: bfloat16 [16, 1024, 2048], P(None, 'sp')
- ln_gain: float32 [2048], replicated
- ln_bias: float32 [2048], replicated
- w_qkv: bfloat16 [2048, 3, 24, 128], replicated
- b_qkv: float32 [3, 24, 128], replicated
- w_out: bfloat16 [24, 128, 2048], replicated
- b_out: float32 [2048], replicated
Outputs:
- output 1: bfloat16 [16, 1024, 2048], P(None, 'sp')
- output 2: bfloat16 [16, 1024, 2048], P(None, 'sp')
- output 3: float32 [2048], replicated
- output 4: float32 [2048], replicated
- output 5: float32 [2048, 3, 24, 128], replicated
- output 6: float32 [3, 24, 128], replicated
- output 7: float32 [24, 128, 2048], replicated
- output 8: float32 [2048], replicated
All inputs are finite; a program needn't handle non-finite values.
Results may differ from a plain program's by a relative error of at most 0.013469.
Values are sent between devices in bfloat16 or wider.
A program may use at most 1 GiB of HBM per device.

v0:
```python
import jax
import jax.numpy as jnp
from jax import lax
from jax.sharding import PartitionSpec as P

LN_EPS = 1e-5


def layer_norm_fwd(x_in, ln_gain, ln_bias):
    x_float = x_in.astype(jnp.float32)
    centered = x_float - jnp.mean(x_float, axis=-1, keepdims=True)
    inv_std = lax.rsqrt(jnp.mean(centered * centered, axis=-1, keepdims=True) + LN_EPS)
    x_hat = centered * inv_std
    normed = (x_hat * ln_gain + ln_bias).astype(jnp.bfloat16)
    return normed, x_hat, inv_std


def layer_norm_bwd(grad_normed, x_hat, inv_std, ln_gain):
    grad_hat = grad_normed * ln_gain
    mean_grad = jnp.mean(grad_hat, axis=-1, keepdims=True)
    mean_proj = jnp.mean(grad_hat * x_hat, axis=-1, keepdims=True)
    return inv_std * (grad_hat - mean_grad - x_hat * mean_proj)


def head_probs(qkv_head):
    attn_scale = qkv_head.shape[-1] ** -0.5
    positions = jnp.arange(qkv_head.shape[2])
    scores = jnp.einsum("crf,clf->crl", qkv_head[0], qkv_head[1], preferred_element_type=jnp.float32) * attn_scale
    scores = jnp.where(positions[:, None] >= positions[None, :], scores, -1e30)
    return jax.nn.softmax(scores, axis=-1)


def head_attention(qkv_head):
    prob_low = head_probs(qkv_head).astype(jnp.bfloat16)
    return jnp.einsum("crl,clf->crf", prob_low, qkv_head[2], preferred_element_type=jnp.float32).astype(jnp.bfloat16)


def head_attention_bwd(operands):
    qkv_head, grad_o = operands
    attn_scale = qkv_head.shape[-1] ** -0.5
    prob_f32 = head_probs(qkv_head)
    grad_v = jnp.einsum("crl,crf->clf", prob_f32.astype(jnp.bfloat16), grad_o, preferred_element_type=jnp.float32)
    grad_p = jnp.einsum("crf,clf->crl", grad_o, qkv_head[2], preferred_element_type=jnp.float32).astype(jnp.bfloat16).astype(jnp.float32)
    grad_s = (prob_f32 * (grad_p - jnp.sum(prob_f32 * grad_p, axis=-1, keepdims=True)) * attn_scale).astype(jnp.bfloat16)
    grad_q = jnp.einsum("crl,clf->crf", grad_s, qkv_head[1], preferred_element_type=jnp.float32)
    grad_k = jnp.einsum("crl,crf->clf", grad_s, qkv_head[0], preferred_element_type=jnp.float32)
    return jnp.stack([grad_q, grad_k, grad_v]).astype(jnp.bfloat16)


def solution(mesh):
    seq_spec = P(None, "sp", None)
    replicated = P()

    def local_block(x_in, grad_y, ln_gain, ln_bias, w_qkv, b_qkv, w_out, b_out):
        normed, x_hat, inv_std = layer_norm_fwd(x_in, ln_gain, ln_bias)
        bias_heads = jnp.transpose(b_qkv, (1, 0, 2))[:, :, None, None, :]
        qkv_local = (jnp.einsum("bsd,dthe->htbse", normed, w_qkv, preferred_element_type=jnp.float32) + bias_heads).astype(jnp.bfloat16)
        qkv_heads = lax.all_to_all(qkv_local, "sp", 0, 3, tiled=True)
        attn_heads = lax.map(head_attention, qkv_heads)
        attn_local = lax.all_to_all(attn_heads, "sp", 2, 0, tiled=True)
        proj_out = jnp.einsum("hbse,hed->bsd", attn_local, w_out, preferred_element_type=jnp.float32) + b_out
        y_out = (x_in.astype(jnp.float32) + proj_out).astype(jnp.bfloat16)
        grad_b_out = jnp.sum(grad_y, axis=(0, 1), dtype=jnp.float32)
        grad_w_out = jnp.einsum("hbse,bsd->hed", attn_local, grad_y, preferred_element_type=jnp.float32)
        grad_attn_local = jnp.einsum("bsd,hed->hbse", grad_y, w_out, preferred_element_type=jnp.float32).astype(jnp.bfloat16)
        grad_attn_heads = lax.all_to_all(grad_attn_local, "sp", 0, 2, tiled=True)
        grad_qkv_heads = lax.map(head_attention_bwd, (qkv_heads, grad_attn_heads))
        grad_qkv_local = lax.all_to_all(grad_qkv_heads, "sp", 3, 0, tiled=True)
        grad_b_qkv = jnp.transpose(jnp.sum(grad_qkv_local, axis=(2, 3), dtype=jnp.float32), (1, 0, 2))
        grad_w_qkv = jnp.einsum("bsd,htbse->dthe", normed, grad_qkv_local, preferred_element_type=jnp.float32)
        grad_normed = jnp.einsum("htbse,dthe->bsd", grad_qkv_local, w_qkv, preferred_element_type=jnp.float32).astype(jnp.bfloat16).astype(jnp.float32)
        grad_ln_gain = jnp.sum(grad_normed * x_hat, axis=(0, 1))
        grad_ln_bias = jnp.sum(grad_normed, axis=(0, 1))
        grad_x = (grad_y.astype(jnp.float32) + layer_norm_bwd(grad_normed, x_hat, inv_std, ln_gain)).astype(jnp.bfloat16)
        param_grads = lax.psum((grad_ln_gain, grad_ln_bias, grad_w_qkv, grad_b_qkv, grad_w_out, grad_b_out), "sp")
        return (y_out, grad_x) + tuple(param_grads)

    return jax.shard_map(local_block, mesh=mesh, in_specs=(seq_spec, seq_spec, replicated, replicated, replicated, replicated, replicated, replicated), out_specs=(seq_spec, seq_spec, replicated, replicated, replicated, replicated, replicated, replicated), check_vma=False)
```

profile of v0, /device:TPU:1, one launch (start us, length us, event | category | flops | bytes accessed | tf_op | source)
XLA Modules:
  0.0 3446.3 jit_solution(1475107049069164772)
XLA Ops:
  54.3 92.3 %fusion.68 = bf16[24,3,16,128,128]{4,3,0,1,2:T(8,128)(2,1)} fusion(f32[24,3,128]{2,0,1:T(8,128)S(1)} %bitcast.284, bf16[2048,3,24,128]{3,2,1,0:T(8,128)(2,1)} %param.16, bf16[16,128,2048]{2,1,0:T(8,128)(2,1)} %param.12, f32[2048]{0:T(1024)S(1)} %copy-done.10, f32[2048]{0:T(1024)S(1)} %copy-done.7, f32[16,128]{1,0:T(8,128)S(1)} %add_rsqrt_fusion, ...), kind=kOutput, calls=%fused_computation.73 | convolution fusion | flops 77372325888 | bytes 83955712 | tf_op jit(solution)/shard_map/bsd,dthe->htbse/dot_general | solution.py:57
  205.8 388.9 %all-to-all-done = bf16[24,3,16,128,128]{4,3,1,2,0:T(8,128)(2,1)} async-done(((bf16[24,3,16,128,128]{4,3,1,2,0:T(8,128)(2,1)}), bf16[24,3,16,128,128]{4,3,1,2,0:T(8,128)(2,1)}, u32[]{:S(2)}, u32[]{:S(2)}) %all-to-all-start) | async-done | bytes 37748768 | tf_op jit(solution)/shard_map/all_to_all | solution.py:58
  620.2 218.6 %while.20 = (s32[]{:T(128)}, bf16[3,16,1024,128]{3,1,0,2:T(8,128)(2,1)}, bf16[3,3,16,1024,128]{4,3,2,1,0:T(8,128)(2,1)}, s32[]{:T(128)}, s32[]{:T(128)}, /*index=5*/s32[]{}, s32[]{}) while((s32[]{:T(128)}, bf16[3,16,1024,128]{3,1,0,2:T(8,128)(2,1)}, bf16[3,3,16,1024,128]{4,3,2,1,0:T(8,128)(2,1)}, s32[]{:T(128)}, s32[]{:T(128)}, /*index=5*/s32[]{}, ...), condition=%wide.region_5.6_spmd, body=%wide.region_2.5_spmd.sunk | while | flops 13039060992 | bytes 36834416 | solution.py:59
  657.2 37.2 %convert_bitcast_fusion.9 = bf16[1,16,1024,128]{3,2,1,0:T(8,128)(2,1)} fusion(bf16[3,3,16,1024,128]{4,3,2,1,0:T(8,128)(2,1)} %get-tuple-element.168, s32[]{:T(128)} %get-tuple-element.159, s32[]{:T(128)S(6)} %add.122, f32[16,1024]{1,0:T(8,128)S(1)} %fusion.146, pred[1024,1024]{0,1:T(8,128)(4,1)S(1)} %iota_compare_fusion.4, s32[]{:T(128)S(6)} %add.123), kind=kOutput, calls=%fused_computation.14.clone.3 | convolution fusion | flops 8675935232 | bytes 17892872 | tf_op jit(solution)/shard_map/while/body/eval_jaxpr/crl,clf->crf/dot_general | solution.py:35
  726.0 37.2 %convert_bitcast_fusion.9 = bf16[1,16,1024,128]{3,2,1,0:T(8,128)(2,1)} fusion(bf16[3,3,16,1024,128]{4,3,2,1,0:T(8,128)(2,1)} %get-tuple-element.168, s32[]{:T(128)} %get-tuple-element.159, s32[]{:T(128)S(6)} %add.122, f32[16,1024]{1,0:T(8,128)S(1)} %fusion.146, pred[1024,1024]{0,1:T(8,128)(4,1)S(1)} %iota_compare_fusion.4, s32[]{:T(128)S(6)} %add.123), kind=kOutput, calls=%fused_computation.14.clone.3 | convolution fusion | flops 8675935232 | bytes 17892872 | tf_op jit(solution)/shard_map/while/body/eval_jaxpr/crl,clf->crf/dot_general | solution.py:35
  794.8 37.2 %convert_bitcast_fusion.9 = bf16[1,16,1024,128]{3,2,1,0:T(8,128)(2,1)} fusion(bf16[3,3,16,1024,128]{4,3,2,1,0:T(8,128)(2,1)} %get-tuple-element.168, s32[]{:T(128)} %get-tuple-element.159, s32[]{:T(128)S(6)} %add.122, f32[16,1024]{1,0:T(8,128)S(1)} %fusion.146, pred[1024,1024]{0,1:T(8,128)(4,1)S(1)} %iota_compare_fusion.4, s32[]{:T(128)S(6)} %add.123), kind=kOutput, calls=%fused_computation.14.clone.3 | convolution fusion | flops 8675935232 | bytes 17892872 | tf_op jit(solution)/shard_map/while/body/eval_jaxpr/crl,clf->crf/dot_general | solution.py:35
  846.3 854.9 %while.21 = (s32[]{:T(128)}, bf16[3,3,16,1024,128]{4,2,1,0,3:T(8,128)(2,1)}, bf16[3,3,16,1024,128]{4,3,2,1,0:T(8,128)(2,1)}, bf16[3,16,1024,128]{3,2,1,0:T(8,128)(2,1)}, s32[]{:T(128)}, /*index=5*/s32[]{:T(128)}, s32[]{}, s32[]{}) while((s32[]{:T(128)}, bf16[3,3,16,1024,128]{4,2,1,0,3:T(8,128)(2,1)}, ...), condition=%wide.region_10.11_spmd, body=%wide.region_6.0_spmd.sunk | while | flops 26259542016 | bytes 620106368 | solution.py:67
  916.3 79.8 %convert_bitcast_fusion.12 = bf16[1,1,16,1024,128]{4,3,2,1,0:T(8,128)(2,1)} fusion(bf16[3,3,16,1024,128]{4,3,2,1,0:T(8,128)(2,1)} %get-tuple-element.191, s32[]{:T(128)} %get-tuple-element.181, s32[]{:T(128)S(6)} %add.125, bf16[16,1024,1024]{1,2,0:T(8,128)(2,1)} %convolution_convert_fusion.2, f32[16,1024,1024]{1,2,0:T(8,128)} %get-tuple-element.151, ...), kind=kOutput, calls=%fused_computation.55.clone.2 | convolution fusion | flops 4448076800 | bytes 209846784 | tf_op jit(solution)/shard_map/while/body/eval_jaxpr/crl,clf->crf/dot_general | solution.py:45
  996.0 64.7 %convert_bitcast_fusion.11 = bf16[1,1,16,1024,128]{4,3,2,1,0:T(8,128)(2,1)} fusion(bf16[3,3,16,1024,128]{4,3,2,1,0:T(8,128)(2,1)} %get-tuple-element.191, s32[]{:T(128)} %get-tuple-element.181, bf16[16,1024,1024]{1,2,0:T(8,128)(2,1)} %convolution_convert_fusion.2, f32[16,1024,1024]{1,2,0:T(8,128)} %get-tuple-element.151, ...), kind=kOutput, calls=%fused_computation.54.clone.2 | convolution fusion | flops 4448076800 | bytes 209846784 | tf_op jit(solution)/shard_map/while/body/eval_jaxpr/crl,crf->clf/dot_general | solution.py:46
  1065.4 34.6 %convert_bitcast_fusion.10 = bf16[1,1,16,1024,128]{4,3,2,1,0:T(8,128)(2,1)} fusion(s32[]{:T(128)} %get-tuple-element.181, f32[16,1024]{1,0:T(8,128)S(1)} %get-tuple-element.150, pred[1024,1024]{0,1:T(8,128)(4,1)} %copy-done, bf16[3,3,16,1024,128]{4,3,2,1,0:T(8,128)(2,1)} %get-tuple-element.191, s32[]{:T(128)S(6)} %add.125, ...), kind=kOutput, calls=%fused_computation.53.clone.3 | convolution fusion | flops 8675935232 | bytes 17892356 | tf_op jit(solution)/shard_map/while/body/eval_jaxpr/crl,crf->clf/dot_general | solution.py:42
  1106.4 36.2 %copy_dynamic-update-slice_fusion.5 = bf16[3,3,16,1024,128]{4,2,1,0,3:T(8,128)(2,1)} fusion(bf16[3,3,16,1024,128]{4,2,1,0,3:T(8,128)(2,1)} %get-tuple-element.182, s32[]{:T(128)} %get-tuple-element.181, bf16[1,3,16,1024,128]{4,3,2,1,0:T(8,128)(2,1)S(1)} %pad_maximum_fusion.2), kind=kLoop, calls=%fused_computation.46.clone.1 | loop fusion | bytes 25166336 | tf_op jit(solution)/shard_map/while/body/jit(dynamic_update_index_in_dim)/dynamic_update_slice | solution.py:67
  1192.6 79.8 %convert_bitcast_fusion.12 = bf16[1,1,16,1024,128]{4,3,2,1,0:T(8,128)(2,1)} fusion(bf16[3,3,16,1024,128]{4,3,2,1,0:T(8,128)(2,1)} %get-tuple-element.191, s32[]{:T(128)} %get-tuple-element.181, s32[]{:T(128)S(6)} %add.125, bf16[16,1024,1024]{1,2,0:T(8,128)(2,1)} %convolution_convert_fusion.2, f32[16,1024,1024]{1,2,0:T(8,128)} %get-tuple-element.151, ...), kind=kOutput, calls=%fused_computation.55.clone.2 | convolution fusion | flops 4448076800 | bytes 209846784 | tf_op jit(solution)/shard_map/while/body/eval_jaxpr/crl,clf->crf/dot_general | solution.py:45
  1272.3 64.7 %convert_bitcast_fusion.11 = bf16[1,1,16,1024,128]{4,3,2,1,0:T(8,128)(2,1)} fusion(bf16[3,3,16,1024,128]{4,3,2,1,0:T(8,128)(2,1)} %get-tuple-element.191, s32[]{:T(128)} %get-tuple-element.181, bf16[16,1024,1024]{1,2,0:T(8,128)(2,1)} %convolution_convert_fusion.2, f32[16,1024,1024]{1,2,0:T(8,128)} %get-tuple-element.151, ...), kind=kOutput, calls=%fused_computation.54.clone.2 | convolution fusion | flops 4448076800 | bytes 209846784 | tf_op jit(solution)/shard_map/while/body/eval_jaxpr/crl,crf->clf/dot_general | solution.py:46
  1341.7 34.6 %convert_bitcast_fusion.10 = bf16[1,1,16,1024,128]{4,3,2,1,0:T(8,128)(2,1)} fusion(s32[]{:T(128)} %get-tuple-element.181, f32[16,1024]{1,0:T(8,128)S(1)} %get-tuple-element.150, pred[1024,1024]{0,1:T(8,128)(4,1)} %copy-done, bf16[3,3,16,1024,128]{4,3,2,1,0:T(8,128)(2,1)} %get-tuple-element.191, s32[]{:T(128)S(6)} %add.125, ...), kind=kOutput, calls=%fused_computation.53.clone.3 | convolution fusion | flops 8675935232 | bytes 17892356 | tf_op jit(solution)/shard_map/while/body/eval_jaxpr/crl,crf->clf/dot_general | solution.py:42
  1382.7 36.2 %copy_dynamic-update-slice_fusion.5 = bf16[3,3,16,1024,128]{4,2,1,0,3:T(8,128)(2,1)} fusion(bf16[3,3,16,1024,128]{4,2,1,0,3:T(8,128)(2,1)} %get-tuple-element.182, s32[]{:T(128)} %get-tuple-element.181, bf16[1,3,16,1024,128]{4,3,2,1,0:T(8,128)(2,1)S(1)} %pad_maximum_fusion.2), kind=kLoop, calls=%fused_computation.46.clone.1 | loop fusion | bytes 25166336 | tf_op jit(solution)/shard_map/while/body/jit(dynamic_update_index_in_dim)/dynamic_update_slice | solution.py:67
  1468.9 79.8 %convert_bitcast_fusion.12 = bf16[1,1,16,1024,128]{4,3,2,1,0:T(8,128)(2,1)} fusion(bf16[3,3,16,1024,128]{4,3,2,1,0:T(8,128)(2,1)} %get-tuple-element.191, s32[]{:T(128)} %get-tuple-element.181, s32[]{:T(128)S(6)} %add.125, bf16[16,1024,1024]{1,2,0:T(8,128)(2,1)} %convolution_convert_fusion.2, f32[16,1024,1024]{1,2,0:T(8,128)} %get-tuple-element.151, ...), kind=kOutput, calls=%fused_computation.55.clone.2 | convolution fusion | flops 4448076800 | bytes 209846784 | tf_op jit(solution)/shard_map/while/body/eval_jaxpr/crl,clf->crf/dot_general | solution.py:45
  1548.6 64.7 %convert_bitcast_fusion.11 = bf16[1,1,16,1024,128]{4,3,2,1,0:T(8,128)(2,1)} fusion(bf16[3,3,16,1024,128]{4,3,2,1,0:T(8,128)(2,1)} %get-tuple-element.191, s32[]{:T(128)} %get-tuple-element.181, bf16[16,1024,1024]{1,2,0:T(8,128)(2,1)} %convolution_convert_fusion.2, f32[16,1024,1024]{1,2,0:T(8,128)} %get-tuple-element.151, ...), kind=kOutput, calls=%fused_computation.54.clone.2 | convolution fusion | flops 4448076800 | bytes 209846784 | tf_op jit(solution)/shard_map/while/body/eval_jaxpr/crl,crf->clf/dot_general | solution.py:46
  1618.0 34.6 %convert_bitcast_fusion.10 = bf16[1,1,16,1024,128]{4,3,2,1,0:T(8,128)(2,1)} fusion(s32[]{:T(128)} %get-tuple-element.181, f32[16,1024]{1,0:T(8,128)S(1)} %get-tuple-element.150, pred[1024,1024]{0,1:T(8,128)(4,1)} %copy-done, bf16[3,3,16,1024,128]{4,3,2,1,0:T(8,128)(2,1)} %get-tuple-element.191, s32[]{:T(128)S(6)} %add.125, ...), kind=kOutput, calls=%fused_computation.53.clone.3 | convolution fusion | flops 8675935232 | bytes 17892356 | tf_op jit(solution)/shard_map/while/body/eval_jaxpr/crl,crf->clf/dot_general | solution.py:42
  1659.0 36.1 %copy_dynamic-update-slice_fusion.5 = bf16[3,3,16,1024,128]{4,2,1,0,3:T(8,128)(2,1)} fusion(bf16[3,3,16,1024,128]{4,2,1,0,3:T(8,128)(2,1)} %get-tuple-element.182, s32[]{:T(128)} %get-tuple-element.181, bf16[1,3,16,1024,128]{4,3,2,1,0:T(8,128)(2,1)S(1)} %pad_maximum_fusion.2), kind=kLoop, calls=%fused_computation.46.clone.1 | loop fusion | bytes 25166336 | tf_op jit(solution)/shard_map/while/body/jit(dynamic_update_index_in_dim)/dynamic_update_slice | solution.py:67
  1750.8 362.4 %all-to-all-done.3 = bf16[3,3,16,1024,128]{4,2,1,0,3:T(8,128)(2,1)} async-done(((bf16[3,3,16,1024,128]{4,2,1,0,3:T(8,128)(2,1)}), bf16[3,3,16,1024,128]{4,2,1,0,3:T(8,128)(2,1)}, u32[]{:S(2)}, u32[]{:S(2)}) %all-to-all-start.3) | async-done | bytes 37748768 | tf_op jit(solution)/shard_map/all_to_all | solution.py:68
  2139.1 94.0 %fusion.76 = f32[2048,3,24,128]{0,3,2,1:T(8,128)} fusion(bf16[24,3,16,128,128]{4,3,1,2,0:T(8,128)(2,1)} %bitcast.275, bf16[16,128,2048]{2,1,0:T(8,128)(2,1)} %param.12, f32[2048]{0:T(1024)S(1)} %copy-done.11, f32[2048]{0:T(1024)S(1)} %copy-done.8, f32[16,128]{1,0:T(8,128)S(1)} %copy-done.6, f32[16,128]{1,0:T(8,128)S(1)} %copy-done.4), kind=kOutput, calls=%fused_computation.82 | convolution fusion | flops 77334577152 | bytes 121667584 | tf_op jit(solution)/shard_map/bsd,htbse->dthe/dot_general | solution.py:70
  2288.5 96.6 %fusion.96 = (f32[2048]{0:T(1024)S(1)}, f32[16,128]{1,0:T(8,128)S(1)}, f32[16,128]{1,0:T(8,128)S(1)}, f32[2048]{0:T(1024)S(1)}, bf16[16,128,2048]{2,1,0:T(8,128)(2,1)}) fusion(bf16[16,128,2048]{2,1,0:T(8,128)(2,1)} %param.12, f32[16,128]{1,0:T(8,128)S(1)} %copy-done.6, f32[16,128]{1,0:T(8,128)S(1)} %copy-done.4, f32[2048]{0:T(1024)S(1)} %copy-done.8, ...), kind=kOutput, calls=%fused_computation.106 | convolution fusion | flops 77359742976 | bytes 92332032 | tf_op jit(solution)/shard_map/htbse,dthe->bsd/dot_general | solution.py:71
  2427.7 920.8 %all-reduce.4.cloned.1.call-done = (f32[2048,3,24,128]{0,3,2,1:T(8,128)}, f32[24,128,2048]{2,1,0:T(8,128)}) async-done(((f32[2048,3,24,128]{0,3,2,1:T(8,128)}, f32[24,128,2048]{2,1,0:T(8,128)}), (f32[2048,3,24,128]{0,3,2,1:T(8,128)}, f32[24,128,2048]{2,1,0:T(8,128)})) %all-reduce.4.cloned.1.call-update) | async-done | bytes 100663312 | tf_op jit(solution)/shard_map/psum | solution.py:75
  3348.5 73.0 %copy.53 = f32[2048,3,24,128]{3,2,1,0:T(8,128)} copy(f32[2048,3,24,128]{0,3,2,1:T(8,128)} %get-tuple-element.95) | data formatting | bytes 150994944
  (87 shorter events, 607.9 us)
Async XLA Ops:
  39.2 15.1 copy-start.7
  39.2 15.1 copy-start.9
  39.2 15.1 copy-start.10
  39.2 139.7 %all-to-all-start.2 = ((bf16[24,16,128,128]{2,3,1,0:T(8,128)(2,1)}), bf16[24,16,128,128]{2,3,1,0:T(8,128)(2,1)}, u32[]{:S(2)}, u32[]{:S(2)}) async-start(bf16[24,16,128,128]{2,3,1,0:T(8,128)(2,1)} %convert_bitcast_fusion.4), calls=%async_computation.2 | async-start | bytes 25165824 | tf_op jit(solution)/shard_map/all_to_all | solution.py:66
  48.0 5.8 copy-start.3
  53.7 0.6 copy-start.5
  178.9 415.8 %all-to-all-start = ((bf16[24,3,16,128,128]{4,3,1,2,0:T(8,128)(2,1)}), bf16[24,3,16,128,128]{4,3,1,2,0:T(8,128)(2,1)}, u32[]{:S(2)}, u32[]{:S(2)}) async-start(bf16[24,3,16,128,128]{4,3,1,2,0:T(8,128)(2,1)} %copy.41), calls=%async_computation | async-start | bytes 75497472 | tf_op jit(solution)/shard_map/all_to_all | solution.py:58
  838.9 862.4 %all-to-all-start.1 = ((bf16[3,16,1024,128]{3,1,0,2:T(8,128)(2,1)}), bf16[3,16,1024,128]{3,1,0,2:T(8,128)(2,1)}, u32[]{:S(2)}, u32[]{:S(2)}) async-start(bf16[3,16,1024,128]{3,1,0,2:T(8,128)(2,1)} %get-tuple-element.47), calls=%async_computation.1 | async-start | bytes 25165824 | tf_op jit(solution)/shard_map/all_to_all | solution.py:60
  866.6 32.9 copy-start
  1142.9 32.9 copy-start
  1419.2 32.9 copy-start
  1701.2 411.9 %all-to-all-start.3 = ((bf16[3,3,16,1024,128]{4,2,1,0,3:T(8,128)(2,1)}), bf16[3,3,16,1024,128]{4,2,1,0,3:T(8,128)(2,1)}, u32[]{:S(2)}, u32[]{:S(2)}) async-start(bf16[3,3,16,1024,128]{4,2,1,0,3:T(8,128)(2,1)} %get-tuple-element.48), calls=%async_computation.3 | async-start | bytes 75497472 | tf_op jit(solution)/shard_map/all_to_all | solution.py:68
  1707.7 1640.8 %all-reduce.4.cloned.1.call-start = ((), (), s32[]{:S(2)}) async-start(), calls=%async_computation.4 | async-start | bytes 201326592 | tf_op jit(solution)/shard_map/psum | solution.py:75
  1707.7 13.4 slice-start
  1707.7 13.4 slice-start.1
  1716.5 4.5 copy-start.1
  2113.2 25.9 copy-start.4
  2113.2 25.9 copy-start.6
  2113.2 25.9 copy-start.8
  2113.2 25.9 copy-start.11
  2233.1 0.7 copy-start.12
  2385.1 15.5 copy-start.2
Sparse Core Ops, SparseCore 0:
  2233.3 1115.1 all-reduce.3
where the time goes:
time: 3450 us
  waiting for transfers between devices  1680 us (49%)
  matrix products  1250 us (36%)
  local copies, waits for them, and re-layouts  343 us (10%)
  other arithmetic  67.8 us (2%)
  loops' own time  38.4 us (1%)
    psum x1, waiting for transfers between devices, local_block(): lax.psum((grad_ln_gain, grad_ln_bias, grad_w_qkv, grad_b_qkv, grad_w_out,...  921 us
    all_to_all x1, waiting for transfers between devices, local_block(): qkv_heads = lax.all_to_all(qkv_local, 'sp', 0, 3, tiled=True)  389 us
    all_to_all x1, waiting for transfers between devices, local_block(): grad_qkv_local = lax.all_to_all(grad_qkv_heads, 'sp', 3, 0, tiled=True)  362 us
    dot_general x3, matrix products, head_attention_bwd(): jnp.einsum('crl,clf->crf', grad_s, qkv_head[1], preferred_element_type=jn...  239 us
    dot_general x3, matrix products, head_attention_bwd(): jnp.einsum('crl,crf->clf', grad_s, qkv_head[0], preferred_element_type=jn...  194 us
    sub x6, matrix products, head_probs(): return jax.nn.softmax(scores, axis=-1)  172 us
    dot_general x3, matrix products, head_attention(): jnp.einsum('crl,clf->crf', prob_low, qkv_head[2], preferred_element_type=...  112 us
    dynamic_update_slice x3, local copies, waits for them, and re-layouts, local_block(): grad_qkv_heads = lax.map(head_attention_bwd, (qkv_heads, grad_attn_heads))  108 us
  transfers between devices with their start and end apart: 5, of which 4 were waited for; matrix products, arithmetic and copies ran while one was open for 34% of the time, Pallas kernels for 0%

commit v1 on v0

v1 whole, which is shorter than its diff:
```python
import functools

import jax
import jax.numpy as jnp
from jax import lax
from jax.experimental import pallas as pl
from jax.experimental.pallas import tpu as pltpu
from jax.sharding import PartitionSpec as P

LN_EPS = 1e-5
F32, BF16 = jnp.float32, jnp.bfloat16
LOG2E = 1.4426950408889634


def dot(a, b, ca, cb):
    return lax.dot_general(a, b, (((ca,), (cb,)), ((), ())), preferred_element_type=F32)


def attention_kernel(blk, scale, qkv_ref, do_ref, o_ref, g_ref, gb_ref, p_ref, ds_ref):
    seq, dh = do_ref.shape
    for i in range(seq // blk):
        lo, hi = i * blk, (i + 1) * blk
        q, k, v = qkv_ref[lo:hi, 0:dh], qkv_ref[0:hi, dh:2 * dh], qkv_ref[0:hi, 2 * dh:3 * dh]
        do = do_ref[lo:hi, :]
        s = dot(k, q, 1, 1)
        rows = lax.broadcasted_iota(jnp.int32, (blk, blk), 0)
        cols = lax.broadcasted_iota(jnp.int32, (blk, blk), 1)
        diag = jnp.where(rows <= cols, s[lo:hi], -1e30)
        s = diag if i == 0 else jnp.concatenate([s[:lo], diag], axis=0)
        m = jnp.max(s, axis=0, keepdims=True)
        e = jnp.exp2((s - m) * (scale * LOG2E))
        p = e * (1.0 / jnp.sum(e, axis=0, keepdims=True))
        pb = p.astype(BF16)
        p_ref[0:hi, lo:hi] = pb
        o_t = dot(v, pb, 0, 0)
        o_ref[lo:hi, :] = o_t.T.astype(BF16)
        delta = jnp.sum(o_t * do.astype(F32).T, axis=0, keepdims=True)
        dp = dot(v, do, 1, 1).astype(BF16).astype(F32)
        ds = (p * (dp - delta)).astype(BF16)
        ds_ref[0:hi, lo:hi] = ds
        g_ref[lo:hi, 0:dh] = (dot(k, ds, 0, 0) * scale).T.astype(BF16)
    for j in range(seq // blk):
        lo, hi = j * blk, (j + 1) * blk
        dk = dot(ds_ref[lo:hi, lo:], qkv_ref[lo:, 0:dh], 1, 0)
        dv = dot(p_ref[lo:hi, lo:], do_ref[lo:, :], 1, 0)
        g_ref[lo:hi, dh:2 * dh] = (dk * scale).astype(BF16)
        g_ref[lo:hi, 2 * dh:3 * dh] = dv.astype(BF16)
    gb_ref[...] = jnp.sum(g_ref[...].astype(F32), axis=0, keepdims=True)[None]


def attention(qkv, grad_o, seq, dh, seqs, into=None, width=0, at=(0, 0)):
    s0, n_seq = seqs[0], seqs[1] - seqs[0]
    n_heads = grad_o.shape[1] // dh
    width = width or n_heads
    rows = n_seq * seq if into is None and width == n_heads else 2 * seq
    flops = n_seq * n_heads * 6 * seq * seq * dh
    in_specs = [pl.BlockSpec((seq, 3 * dh), lambda b, h: (b + s0, h)), pl.BlockSpec((seq, dh), lambda b, h: (b + s0, h))]
    args, alias = [qkv, grad_o], {}
    if into is not None:
        in_specs += [pl.BlockSpec(memory_space=pl.ANY)] * 2
        args += list(into)
        alias = {2: 0, 3: 1}

    def kernel(qkv_ref, do_ref, *refs):
        attention_kernel(seq // 2, dh ** -0.5, qkv_ref, do_ref, *refs[len(args) - 2:])

    o, g, gb = pl.pallas_call(
        kernel,
        grid=(n_seq, n_heads),
        in_specs=in_specs,
        out_specs=[pl.BlockSpec((seq, dh), lambda b, h: (b + at[0], h + at[1])),
                   pl.BlockSpec((seq, 3 * dh), lambda b, h: (b + at[0], h + at[1])),
                   pl.BlockSpec((1, 1, 3 * dh), lambda b, h: (b, 0, h))],
        out_shape=[jax.ShapeDtypeStruct((rows, width * dh), BF16), jax.ShapeDtypeStruct((rows, width * 3 * dh), BF16),
                   jax.ShapeDtypeStruct((n_seq, 1, n_heads * 3 * dh), F32)],
        scratch_shapes=[pltpu.VMEM((seq, seq), BF16)] * 2,
        input_output_aliases=alias,
        cost_estimate=pl.CostEstimate(flops=2 * flops, bytes_accessed=n_seq * n_heads * seq * dh * 16, transcendentals=0),
        name="attention",
    )(*args)
    return o, g, jnp.sum(gb, axis=(0, 1))


def project_kernel(n_units, steps, transposed, has_bias, *refs):
    o_ref, w_ref = refs[-1], refs[n_units]
    i = pl.program_id(0)

    def work(a_ref):
        out = dot(a_ref[...], w_ref[...], 1, 1 if transposed else 0)
        if has_bias:
            out = out + refs[n_units + 1][...]
        o_ref[...] = out.astype(BF16)

    for n in range(n_units):
        pl.when((i >= n * steps) & (i < (n + 1) * steps))(functools.partial(work, refs[n]))


def project(units, w, block, cols, bias=None, transposed=False):
    rows, depth = units[0].shape
    bm = rows if transposed else rows // 2
    steps = rows // bm
    in_specs = [pl.BlockSpec((bm, depth), lambda i, n=n: (jnp.clip(i - n * steps, 0, steps - 1), 0))
                for n in range(len(units))]
    in_specs.append(pl.BlockSpec((cols, depth), lambda i: (block, 0)) if transposed
                    else pl.BlockSpec((depth, cols), lambda i: (0, block)))
    args = list(units) + [w]
    if bias is not None:
        in_specs.append(pl.BlockSpec((1, cols), lambda i: (0, block)))
        args.append(bias)
    total = len(units) * rows
    return pl.pallas_call(
        functools.partial(project_kernel, len(units), steps, transposed, bias is not None),
        grid=(len(units) * steps,),
        in_specs=in_specs,
        out_specs=pl.BlockSpec((bm, cols), lambda i: (i, 0)),
        out_shape=jax.ShapeDtypeStruct((total, cols), BF16),
        cost_estimate=pl.CostEstimate(flops=2 * total * depth * cols, bytes_accessed=2 * total * (depth + cols),
                                      transcendentals=0),
        name="project",
    )(*args)


def weight_grads(order, units, widths, before=None):
    rows, dim = units[0][0].shape
    cols, cols_o = widths
    bd, per_out, total = dim // 8, 2, order.shape[0]
    col = pl.BlockSpec((rows, bd), lambda i, order: (0, order[i]))
    mine = lambda width, at: pl.BlockSpec((rows, width), lambda i, order: at)
    piece = lambda n: pl.BlockSpec((bd, cols + cols_o), lambda i, order: (jnp.clip(i - per_out * n, 0, per_out - 1), 0))
    n_out = total // per_out
    in_specs = [col] * (2 * len(units)) + [mine(cols, unit[4]) for unit in units] + [mine(cols_o, unit[4]) for unit in units]
    args = [unit[n] for n in range(4) for unit in units]
    if before is not None:
        in_specs += [piece(n) for n in range(n_out)]
        args += list(before)

    def kernel(order_ref, *refs):
        inputs, out_refs, acc = refs[:len(args)], refs[len(args):-1], refs[-1]
        u, gy, g, o = (inputs[n * len(units):(n + 1) * len(units)] for n in range(4))
        i = pl.program_id(0)
        acc[:, :cols] = sum(dot(a[...], b[...], 0, 0) for a, b in zip(u, g))
        acc[:, cols:] = sum(dot(a[...], b[...], 0, 0) for a, b in zip(gy, o))

        def write(n):
            out_refs[n][...] = acc[...] if before is None else acc[...] + inputs[4 * len(units) + n][...]

        for n in range(n_out):
            pl.when((i >= n * per_out) & (i < (n + 1) * per_out))(functools.partial(write, n))

    return pl.pallas_call(
        kernel,
        grid_spec=pltpu.PrefetchScalarGridSpec(
            num_scalar_prefetch=1, grid=(total,), in_specs=in_specs, out_specs=[piece(n) for n in range(n_out)],
            scratch_shapes=[pltpu.VMEM((bd, cols + cols_o), F32)]),
        out_shape=[jax.ShapeDtypeStruct((per_out * bd, cols + cols_o), F32)] * n_out,
        cost_estimate=pl.CostEstimate(flops=2 * len(units) * rows * total * bd * (cols + cols_o), bytes_accessed=40 * 2 ** 20,
                                      transcendentals=0),
        name="weight_grads",
    )(order, *args)


def add_last(kept, got_a, got_b, last_a, last_b):
    rows, cols = last_a.shape
    bm = rows // 2
    spec = lambda base, start: pl.BlockSpec((bm, cols), lambda i: (base + jnp.clip(i - start, 0, 1), 0))

    def kernel(kept_ref, a1, b1, a2, b2, a_ref, b_ref):
        i = pl.program_id(0)

        def work(out_ref, first, second):
            out_ref[...] = kept_ref[...] + first[...] + second[...]

        pl.when(i < 2)(lambda: work(a_ref, a1, a2))
        pl.when(i >= 2)(lambda: work(b_ref, b1, b2))

    return pl.pallas_call(
        kernel, grid=(4,),
        in_specs=[pl.BlockSpec((bm, cols), lambda i: (i, 0)), spec(2, 0), spec(2, 2), spec(0, 0), spec(0, 2)],
        out_specs=[spec(0, 0), spec(0, 2)],
        out_shape=[jax.ShapeDtypeStruct(last_a.shape, F32)] * 2,
        cost_estimate=pl.CostEstimate(flops=2 ** 24, bytes_accessed=kept.size * 16, transcendentals=0),
        name="add_last",
    )(kept, got_a, got_b, last_a, last_b)


def assemble(order, pieces):
    rows, cols = pieces[0].shape
    n = len(pieces)

    def kernel(order_ref, *refs):
        def work(m):
            refs[-1][...] = refs[m][...]

        for m in range(n):
            pl.when(pl.program_id(0) == m)(functools.partial(work, m))

    block = pl.BlockSpec((rows, cols), lambda i, order: (0, 0))
    return pl.pallas_call(
        kernel,
        grid_spec=pltpu.PrefetchScalarGridSpec(num_scalar_prefetch=1, grid=(n,), in_specs=[block] * n,
                                               out_specs=pl.BlockSpec((rows, cols), lambda i, order: (order[i], 0))),
        out_shape=jax.ShapeDtypeStruct((n * rows, cols), F32),
        cost_estimate=pl.CostEstimate(flops=2 ** 24, bytes_accessed=n * rows * cols * 8, transcendentals=0),
        name="assemble",
    )(order, *pieces)


def lay_out_kernel(groups, heads, dh, core_ref, w_ref, out_ref):
    def write(core):
        for j in range(groups):
            for h in range(heads):
                for t in range(3):
                    col = ((j * heads + h) * 3 + t) * dh
                    out_ref[:, col:col + dh] = w_ref[:, t, 2 * heads * j + heads * core + h, :]

    pl.when(core_ref[0] == 0)(lambda: write(0))
    pl.when(core_ref[0] == 1)(lambda: write(1))


def lay_out_weights(w_qkv, core, groups, heads):
    dim, _, heads_all, dh = w_qkv.shape
    width = groups * heads * 3 * dh
    blk = 128
    return pl.pallas_call(
        functools.partial(lay_out_kernel, groups, heads, dh),
        grid_spec=pltpu.PrefetchScalarGridSpec(
            num_scalar_prefetch=1, grid=(dim // blk,),
            in_specs=[pl.BlockSpec((blk, 3, heads_all, dh), lambda i, c: (i, 0, 0, 0))],
            out_specs=pl.BlockSpec((blk, width), lambda i, c: (i, 0))),
        out_shape=jax.ShapeDtypeStruct((dim, width), BF16),
        cost_estimate=pl.CostEstimate(flops=dim * width * 400, bytes_accessed=dim * width * 6, transcendentals=0),
        name="lay_out_weights",
    )(core, w_qkv)


def place_kernel(counts, dh, core_ref, *refs):
    qkv_ref, out_ref = refs[-2:]
    heads = sum(counts)

    def write(first):
        h0 = 0
        for n, count in enumerate(counts):
            for side in range(2):
                src = refs[2 * n + (side ^ first)]
                for h in range(count):
                    head = side * heads + h0 + h
                    for t in range(3):
                        qkv_ref[:, t, head, :] = src[:, (h * 3 + t) * dh:(h * 3 + t + 1) * dh]
                    col = (3 * count + h) * dh
                    out_ref[head] = src[:, col:col + dh].T
            h0 += count

    pl.when(core_ref[0] == 0)(lambda: write(0))
    pl.when(core_ref[0] == 1)(lambda: write(1))


def place(into, core, group, heads_all, dim, dh, pairs):
    blk = 256
    args = [a for pair in pairs for a in pair]
    counts = [own.shape[1] // (4 * dh) for own, _ in pairs]
    heads = 2 * sum(counts)
    in_specs = [pl.BlockSpec((blk, a.shape[1]), lambda i, c: (i, 0)) for a in args]
    size, alias = sum(a.size for a in args), {}
    if into is not None:
        in_specs += [pl.BlockSpec(memory_space=pl.ANY)] * 2
        alias = {1 + len(args): 0, 2 + len(args): 1}
        args += list(into)
    return pl.pallas_call(
        functools.partial(place_kernel, counts, dh),
        grid_spec=pltpu.PrefetchScalarGridSpec(
            num_scalar_prefetch=1, grid=(dim // blk,), in_specs=in_specs,
            out_specs=[pl.BlockSpec((blk, 3, heads, dh), lambda i, c: (i, 0, group, 0)),
                       pl.BlockSpec((heads, dh, blk), lambda i, c: (group, 0, i))]),
        out_shape=[jax.ShapeDtypeStruct((dim, 3, heads_all, dh), F32), jax.ShapeDtypeStruct((heads_all, dh, dim), F32)],
        input_output_aliases=alias,
        cost_estimate=pl.CostEstimate(flops=size * 8, bytes_accessed=size * 8, transcendentals=0),
        name="place",
    )(core, *args)


def interleaved(into, piece, at):
    n, *block = piece.shape

    def kernel(in_ref, *refs):
        refs[-1][:, 0] = in_ref[...]

    in_specs, args = [pl.BlockSpec((2, *block), lambda i: (i, 0, 0))], [piece]
    if into is not None:
        in_specs.append(pl.BlockSpec(memory_space=pl.ANY))
        args.append(into)
    return pl.pallas_call(kernel, grid=(n // 2,), in_specs=in_specs,
                          out_specs=pl.BlockSpec((2, 1, *block), lambda i: (i, at, 0, 0)),
                          out_shape=jax.ShapeDtypeStruct((n, 2, *block), piece.dtype),
                          input_output_aliases={} if into is None else {1: 0},
                          cost_estimate=pl.CostEstimate(flops=piece.size, bytes_accessed=4 * piece.size, transcendentals=0),
                          name="interleaved")(*args)


def norm_grads(grad_u, x, gy, gain, s):
    parts, _, part, dim = x.shape

    def kernel(grad_ref, x_ref, gy_ref, gain_ref, gx_ref, sums_ref):
        xf, grad, gyf = x_ref[0, 0].astype(F32), grad_ref[...].astype(F32), gy_ref[...].astype(F32)
        mean_of = lambda a: jnp.sum(a, axis=1, keepdims=True) * (1.0 / dim)
        centered = xf - mean_of(xf)
        inv_std = lax.rsqrt(mean_of(centered * centered) + LN_EPS)
        x_hat = centered * inv_std
        grad_hat = grad * gain_ref[...]
        gx = gyf + inv_std * (grad_hat - mean_of(grad_hat) - x_hat * mean_of(grad_hat * x_hat))
        gx_ref[...] = gx.astype(BF16)

        @pl.when(pl.program_id(0) == 0)
        def _():
            sums_ref[...] = jnp.zeros_like(sums_ref)

        for n, a in enumerate((grad * x_hat, grad, gyf)):
            sums_ref[n:n + 1, :] += jnp.sum(a, axis=0, keepdims=True)

    row = pl.BlockSpec((part, dim), lambda i: (i, 0))
    return pl.pallas_call(
        kernel, grid=(parts,),
        in_specs=[pl.BlockSpec((part, dim), lambda i: (i + parts * s, 0)), pl.BlockSpec((1, 1, part, dim), lambda i: (i, s, 0, 0)),
                  row, pl.BlockSpec((1, dim), lambda i: (0, 0))],
        out_specs=[row, pl.BlockSpec((8, dim), lambda i: (0, 0))],
        out_shape=[jax.ShapeDtypeStruct((parts * part, dim), BF16), jax.ShapeDtypeStruct((8, dim), F32)],
        cost_estimate=pl.CostEstimate(flops=parts * part * dim * 400, bytes_accessed=parts * part * dim * 8, transcendentals=0),
        name="norm_grads",
    )(grad_u, x, gy, gain.reshape(1, dim))


def tie(value, *after):
    return lax.optimization_barrier((value,) + after)[0]


def solution(mesh):
    n_dev = mesh.shape["sp"]
    seq_spec = P(None, "sp", None)
    replicated = P()
    hop = lambda a, bit: lax.ppermute(a, "sp", [(d, d ^ bit) for d in range(n_dev)])
    partner = lambda a: hop(a, 1)
    groups, gh, ch = 3, 4, 2
    steps = groups * gh // ch

    def block(x_in, grad_y, ln_gain, ln_bias, w_qkv, b_qkv, w_out, b_out):
        batch, part, dim = x_in.shape
        heads_all, dh, _ = w_out.shape
        seq = part * n_dev
        device = lax.axis_index("sp")
        core, chip_x, chip_y = (lax.rem(lax.div(device, n), 2) for n in (1, 2, 4))
        core1 = core.reshape(1)

        def exchange(a):
            return lax.all_to_all(a, "sp", 0, 0, tiled=True)

        by_device = lambda a: a.reshape(n_dev, 2, part, dim)
        x_all = exchange(by_device(x_in))
        xs = [x_all[:, s].reshape(seq, dim) for s in range(2)]
        gy_parts = [by_device(grad_y)[:, s] for s in range(2)]
        gys = [exchange(a).reshape(seq, dim) for a in gy_parts]
        w_qkv = tie(w_qkv, *gy_parts)

        w_own = lay_out_weights(w_qkv, core1, groups, gh)
        w_par = lay_out_weights(w_qkv, 1 - core1, groups, gh)
        pick = lambda a, axis, c: lax.dynamic_index_in_dim(a, c, axis, keepdims=False)
        b_own = jnp.transpose(pick(b_qkv.reshape(3, groups, 2, gh, dh), 2, core), (1, 2, 0, 3)).reshape(1, heads_all * 3 * dh // 2)
        wo_of = lambda c: pick(w_out.reshape(groups, 2, gh, dh, dim), 1, c).reshape(heads_all * dh // 2, dim)
        wo_own, wo_par = wo_of(core), wo_of(1 - core)

        def normed(x):
            xf = x.astype(F32)
            centered = xf - jnp.mean(xf, axis=-1, keepdims=True)
            inv_std = lax.rsqrt(jnp.mean(centered * centered, axis=-1, keepdims=True) + LN_EPS)
            x_hat = centered * inv_std
            return (x_hat * ln_gain + ln_bias).astype(BF16), x_hat, inv_std

        u_own = []
        for a in xs:
            u_own.append(normed(a)[0])
        u = u_own + [partner(a) for a in u_own]

        ax = lambda x, y: 2 * x + y
        by = lambda x, y: 4 + 2 * y + x
        x, y = chip_x, chip_y
        order = jnp.stack([ax(1 - x, 1 - y), ax(1 - x, y), by(1 - x, 1 - y), by(x, 1 - y),
                           ax(x, 1 - y), by(1 - x, y), ax(x, y), by(x, y)]).astype(jnp.int32)

        cw, co = ch * 3 * dh, ch * dh
        o_got, g_got, bias = [], [], []
        finals = jnp.stack([ax(x, y), by(x, y), ax(x, 1 - y), by(1 - x, y),
                            ax(1 - x, y), by(x, 1 - y), ax(1 - x, 1 - y), by(1 - x, 1 - y)]).astype(jnp.int32)
        started, sent, halves, blocks, pairs = [], [], [], [], []
        chain = ()

        def after_chain(arrays):
            held = lax.optimization_barrier(tuple(arrays) + tuple(chain))
            return list(held[:len(arrays)])

        def first_add(k):
            kept, got_a, got_b = after_chain(halves[k])
            bd = kept.shape[0] // 2
            send_a, send_b = kept[:bd] + got_a[:bd], kept[bd:] + got_b[:bd]
            sent.append((got_a, got_b, hop(send_a, 4), hop(send_b, 2)))
            return send_a, send_b

        def last_add(k):
            got_a, got_b, last_a, last_b = after_chain(sent[k])
            a, b = add_last(started[k], got_a, got_b, last_a, last_b)
            blocks.append([a, b, hop(a, 4), hop(b, 2)])
            return a, b

        def spread(k):
            a, b = after_chain(blocks[k][:2])
            blocks[k] += [hop(a, 2), hop(b, 4)]

        def forward(k):
            a, b = after_chain(blocks[k][2:4])
            blocks[k][2:4] = [a, b]
            blocks[k] += [hop(a, 2), hop(b, 4)]

        def take(k):
            whole_sum = assemble(finals, after_chain(blocks[k]))
            pairs.append((whole_sum, partner(whole_sum)))
            return (whole_sum,)

        whole = None

        def place_sums(group):
            own = after_chain([pairs[k][0] for k in (2 * group, 2 * group + 1)])
            return place(whole, core1, group, heads_all, dim, dh, [(a, pairs[2 * group + n][1]) for n, a in enumerate(own)])

        for k in range(steps):
            if k == 0:
                qkv = [project([a], w_own, k, cw, b_own) for a in u]
                mine, got, gy_par, bk, chain, part_sums = None, [], [], 0.0, tuple(qkv), None
                for s in range(2):
                    gys[s], = after_chain([gys[s]])
                    gy_par.append(partner(gys[s]))
                    units = []
                    for side, a in enumerate((gys[s], gy_par[s])):
                        grad_o = project([a], wo_own, k, co, transposed=True)
                        if side == 0:
                            mine = attention(qkv[s], grad_o, seq, dh, (0, 1), mine, heads_all // 2, (s, 0))
                            (o_n, g_n), b_n, at = mine[:2], mine[2], (s, 0)
                            mine = mine[:2]
                        else:
                            o_n, g_n, b_n = attention(qkv[2 + s], grad_o, seq, dh, (0, 1))
                            got.append((o_n, g_n))
                            at = (0, 0)
                        units.append((u[2 * side + s], a, g_n, o_n, at))
                        bk = bk + b_n
                    if s == 0:
                        part_sums = weight_grads(order, units, (cw, co))
                        chain = tuple(part_sums)
                gy = gys + gy_par
                send_a, send_b = weight_grads(order[:4], units, (cw, co), part_sums[:2])
                chain = (send_b,)
                rest, = after_chain([part_sums[2]])
                kept, last = weight_grads(order[4:], units, (cw, co), (rest, part_sums[3]))
                chain = (last,)
                o_p, g_p = (jnp.concatenate(after_chain([got[s][n] for s in range(2)]), axis=0) for n in range(2))
            else:
                held = after_chain(u + gy)
                qkv = project(held[:4], w_own, k, cw, b_own)
                grad_o = project(held[4:], wo_own, k, co, transposed=True)
                if k > 1:
                    chain = (qkv, grad_o)
                    if k > 2:
                        spread(k - 2)
                    qkv, grad_o = after_chain([qkv, grad_o])
                o_p, g_p, bk = attention(qkv, grad_o, seq, dh, (2, 4))
                chain = (g_p,)
                if k == 1:
                    chain = first_add(0)
                qkv, = after_chain([qkv])
                *mine, b_n = attention(qkv, grad_o, seq, dh, (0, 2), mine, heads_all // 2, (0, k * ch))
                bk = bk + b_n
                chain = (b_n,)
                if k == 1:
                    chain = last_add(0)
                    spread(0)
                else:
                    chain = first_add(k - 1)
                    if k > 2:
                        forward(k - 2)
                g_p, = after_chain([g_p])
                units = [(u[n], gy[n], mine[1], mine[0], (n, k)) for n in range(2)]
                units += [(u[2 + n], gy[2 + n], g_p, o_p, (n, 0)) for n in range(2)]
                send_a, send_b, kept, last = weight_grads(order, units, (cw, co))
                chain = (last,)
                if k == 1:
                    forward(0)
                else:
                    chain = last_add(k - 1)
            started.append(last)
            halves.append((kept, hop(send_a, 2), hop(send_b, 4)))
            o_got.append(partner(o_p))
            g_got.append(partner(g_p))
            bias.append(bk)

        rows_of = lambda arrays, s: jnp.concatenate([a[s * seq:(s + 1) * seq] for a in arrays], axis=1)
        y_parts = []
        held = after_chain(mine[:1] + o_got)
        for s in range(2):
            proj = dot(held[0][s * seq:(s + 1) * seq], wo_own, 1, 0) + b_out
            proj = dot(rows_of(held[1:], s), wo_par, 1, 0) + proj
            y_parts.append((xs[s].astype(F32) + proj).astype(BF16))
        y_out = None
        for s, y in enumerate(y_parts):
            y_out = interleaved(y_out, exchange(y.reshape(n_dev, part, dim)), s)
        chain = tuple(y_parts)
        spread(steps - 2)
        forward(steps - 2)
        chain = first_add(steps - 1)

        g_mine, = after_chain([mine[1]])
        grad_u = dot(g_mine, w_own, 1, 1)
        chain = (grad_u,)
        chain = last_add(steps - 1)
        spread(steps - 1)
        g_theirs, = after_chain([jnp.concatenate(g_got, axis=1)])
        grad_u = dot(g_theirs, w_par, 1, 1) + grad_u
        chain = (grad_u,)
        forward(steps - 1)
        grad_u, = after_chain([grad_u.astype(BF16)])
        gx_parts, norm_sums = [], []
        for s in range(2):
            gx, found = norm_grads(grad_u, x_all, gys[s], ln_gain, s)
            gx_parts.append(exchange(gx.reshape(n_dev, part, dim)))
            norm_sums.append(found)
            grad_u, = lax.optimization_barrier((grad_u, gx))[:1]

        gb_mine = jnp.transpose(jnp.concatenate(bias).reshape(groups, gh, 3, dh), (2, 0, 1, 3))[:, :, None]
        is_own = (jnp.arange(2) == core)[None, None, :, None, None]
        gb_full = jnp.where(is_own, gb_mine, 0.0).reshape(3 * heads_all * dh)
        norm_sums = (norm_sums[0] + norm_sums[1])[:3].reshape(3 * dim)
        small = jnp.concatenate([norm_sums, gb_full]).reshape(-1, 128)
        small = small + hop(small, 1)
        others = [hop(small, bit) for bit in (2, 4, 6)]

        chain = (gx,)
        for k in range(4):
            chain = take(k)
        whole = place_sums(0)
        chain = tuple(whole)
        chain = take(4)
        whole = place_sums(1)
        others = after_chain(others)
        small = (small + others[0]) + (others[1] + others[2])
        chain = (y_out, small) + tuple(whole)
        chain = take(5)
        grad_x = interleaved(None, after_chain([gx_parts[0]])[0], 0)
        chain = (grad_x,)
        whole = place_sums(2)
        chain = tuple(whole)
        grad_x = interleaved(grad_x, after_chain([gx_parts[1]])[0], 1)
        grad_w_qkv, grad_w_out = whole
        small = small.reshape(-1)
        grad_gain, grad_bias, grad_b_out = small[:dim], small[dim:2 * dim], small[2 * dim:3 * dim]
        grad_b_qkv = small[3 * dim:].reshape(3, heads_all, dh)
        y_out, grad_x = y_out.reshape(batch, part, dim), grad_x.reshape(batch, part, dim)
        return (y_out, grad_x, grad_gain, grad_bias, grad_w_qkv, grad_b_qkv, grad_w_out, grad_b_out)

    return jax.shard_map(block, mesh=mesh, in_specs=(seq_spec, seq_spec) + (replicated,) * 6,
                         out_specs=(seq_spec, seq_spec) + (replicated,) * 6, check_vma=False)
```

time: 3450 us -> 1750 us (0.51)
  waiting for transfers between devices: 1680 us -> 369 us
  matrix products: 1250 us -> 146 us
  Pallas kernels: 0 us -> 862 us
  local copies, waits for them, and re-layouts: 343 us -> 58.8 us
  blocking collectives: 27.1 us -> 148 us
  starting transfers between devices: 28.3 us -> 113 us
  loops' own time: 38.4 us -> 0 us
    dot_general x21 -> x6, matrix products: 1080 us -> 146 us  [dot(): lax.dot_general(a, b, (((ca,), (cb,)), ((), ())), preferred_element_type=...]
    psum x1 -> x0, waiting for transfers between devices: 921 us -> none  [local_block(): lax.psum((grad_ln_gain, grad_ln_bias, grad_w_qkv, grad_b_qkv, grad_w_out,...]
    pallas_call x0 -> x63, Pallas kernels: none -> 862 us  [the longest x18 210 us: project(): pl.pallas_call(functools.partial(project_kernel, len(units), steps, trans...]
    all_to_all x4 -> x5, waiting for transfers between devices: 758 us -> 9.67 us  [exchange(): return lax.all_to_all(a, 'sp', 0, 0, tiled=True)]
    ppermute x0 -> x86, waiting for transfers between devices: none -> 359 us  [solution(): lax.ppermute(a, 'sp', [(d, d ^ bit) for d in range(n_dev)])]
    sub x6 -> x0, matrix products: 172 us -> none  [head_probs(): return jax.nn.softmax(scores, axis=-1)]
    all_to_all x0 -> x2, blocking collectives: none -> 148 us  [exchange(): return lax.all_to_all(a, 'sp', 0, 0, tiled=True)]
    dynamic_update_slice x6 -> x0, local copies, waits for them, and re-layouts: 129 us -> none  [the longest x3 108 us: local_block(): grad_qkv_heads = lax.map(head_attention_bwd, (qkv_heads, grad_attn_heads))]
  transfers between devices with their start and end apart: 5 -> 91, of which waited for: 4 -> 25; matrix products, arithmetic and copies ran while one was open for 34% -> 13% of each run, Pallas kernels for 0% -> 48%
where the time goes in v1:
time: 1750 us; the launch traced here: 1740 us
  Pallas kernels  862 us (49%)
  waiting for transfers between devices  369 us (21%)
  blocking collectives  148 us (8%)
  matrix products  146 us (8%)
  starting transfers between devices  113 us (6%)
  local copies, waits for them, and re-layouts  58.8 us (3%)
  other arithmetic  40.9 us (2%)
    ppermute x86, waiting for transfers between devices, solution(): lax.ppermute(a, 'sp', [(d, d ^ bit) for d in range(n_dev)])  359 us
    pallas_call x18, Pallas kernels, project(): pl.pallas_call(functools.partial(project_kernel, len(units), steps, trans...  210 us
    pallas_call x8, Pallas kernels, weight_grads(): pl.pallas_call(kernel, grid_spec=pltpu.PrefetchScalarGridSpec(num_scalar_...  188 us
    pallas_call x14, Pallas kernels, attention(): pl.pallas_call(kernel, grid=(n_seq, n_heads), in_specs=in_specs, out_spec...  181 us
    all_to_all x2, blocking collectives, exchange(): return lax.all_to_all(a, 'sp', 0, 0, tiled=True)  148 us
    dot_general x6, matrix products, dot(): lax.dot_general(a, b, (((ca,), (cb,)), ((), ())), preferred_element_type=...  146 us
    ppermute x86, starting transfers between devices, solution(): lax.ppermute(a, 'sp', [(d, d ^ bit) for d in range(n_dev)])  92.1 us
    pallas_call x3, Pallas kernels, place(): pl.pallas_call(functools.partial(place_kernel, counts, dh), grid_spec=plt...  89.8 us
  transfers between devices with their start and end apart: 91, of which 25 were waited for; matrix products, arithmetic and copies ran while one was open for 13% of the time, Pallas kernels for 48%

profile of v1, /device:TPU:1, one launch (start us, length us, event | category | flops | bytes accessed | tf_op | source)
XLA Modules:
  0.0 1739.6 jit_solution(2890988398847507634)
XLA Ops:
  0.6 96.7 %all_to_all.35.x_ref = bf16[8,2,128,2048]{3,2,1,0:T(8,128)(2,1)S(1)} all-to-all(bf16[8,2,128,2048]{3,2,1,0:T(8,128)(2,1)} %bitcast.117), channel_id=1, replica_groups=mesh['sp'=8] {'sp'}, dimensions={0} | all-to-all | bytes 16777216 | tf_op jit(solution)/shard_map/all_to_all | solution.py:353
  116.4 33.6 %lay_out_weights.2.refs_1_.refs_4_ = bf16[2048,4608]{1,0:T(8,128)(2,1)} custom-call(s32[1]{0:T(128)} %bitcast.10.core_ref, bf16[2048,3,24,128]{3,2,1,0:T(8,128)(2,1)} %w_ref.1), custom_call_target="tpu_custom_call" | custom-call | flops 3774873600 | bytes 56623104 | tf_op jit(solution)/shard_map/lay_out_weights/pallas_call | solution.py:224
  240.5 33.8 %lay_out_weights.3 = bf16[2048,4608]{1,0:T(8,128)(2,1)} custom-call(s32[1]{0:T(128)S(6)} %sub.63.core_ref, bf16[2048,3,24,128]{3,2,1,0:T(8,128)(2,1)} %w_ref.1), custom_call_target="tpu_custom_call" | custom-call | flops 3774873600 | bytes 56623104 | tf_op jit(solution)/shard_map/lay_out_weights/pallas_call | solution.py:224
  409.8 29.0 %weight_grads.11 = (f32[512,1024]{1,0:T(8,128)}, f32[512,1024]{1,0:T(8,128)}, f32[512,1024]{1,0:T(8,128)}, f32[512,1024]{1,0:T(8,128)}) custom-call(s32[8]{0:T(128)} %stack.50.order_ref, bf16[1024,2048]{1,0:T(8,128)(2,1)} %get-tuple-element.437.refs_0_, bf16[1024,2048]{1,0:T(8,128)(2,1)} %get-tuple-element.438.refs_0_.refs_1_, ...), custom_call_target="tpu_custom_call" | custom-call | flops 17179869184 | bytes 41943040 | tf_op jit(solution)/shard_map/weight_grads/pallas_call | solution.py:150
  452.9 20.3 %project.28.qkv_ref = bf16[4096,768]{1,0:T(8,128)(2,1)} custom-call(bf16[1024,2048]{1,0:T(8,128)(2,1)} %get-tuple-element.437.refs_0_, bf16[1024,2048]{1,0:T(8,128)(2,1)} %get-tuple-element.438.refs_0_.refs_1_, bf16[1024,2048]{1,0:T(8,128)(2,1)} %collective-permute-done.refs_0_.refs_1_.refs_2_, ...), custom_call_target="tpu_custom_call" | custom-call | flops 12884901888 | bytes 23068672 | tf_op jit(solution)/shard_map/project/pallas_call | solution.py:111
  509.4 29.0 %weight_grads.12 = (f32[512,1024]{1,0:T(8,128)}, f32[512,1024]{1,0:T(8,128)}, f32[512,1024]{1,0:T(8,128)}, f32[512,1024]{1,0:T(8,128)}) custom-call(s32[8]{0:T(128)} %stack.50.order_ref, bf16[1024,2048]{1,0:T(8,128)(2,1)} %get-tuple-element.437.refs_0_, bf16[1024,2048]{1,0:T(8,128)(2,1)} %get-tuple-element.438.refs_0_.refs_1_, ...), custom_call_target="tpu_custom_call" | custom-call | flops 17179869184 | bytes 41943040 | tf_op jit(solution)/shard_map/weight_grads/pallas_call | solution.py:150
  557.5 20.5 %project.30.qkv_ref = bf16[4096,768]{1,0:T(8,128)(2,1)} custom-call(bf16[1024,2048]{1,0:T(8,128)(2,1)} %get-tuple-element.437.refs_0_, bf16[1024,2048]{1,0:T(8,128)(2,1)} %get-tuple-element.438.refs_0_.refs_1_, bf16[1024,2048]{1,0:T(8,128)(2,1)} %collective-permute-done.refs_0_.refs_1_.refs_2_, ...), custom_call_target="tpu_custom_call" | custom-call | flops 12884901888 | bytes 23068672 | tf_op jit(solution)/shard_map/project/pallas_call | solution.py:111
  613.8 29.3 %weight_grads.13 = (f32[512,1024]{1,0:T(8,128)}, f32[512,1024]{1,0:T(8,128)}, f32[512,1024]{1,0:T(8,128)}, f32[512,1024]{1,0:T(8,128)}) custom-call(s32[8]{0:T(128)} %stack.50.order_ref, bf16[1024,2048]{1,0:T(8,128)(2,1)} %get-tuple-element.437.refs_0_, bf16[1024,2048]{1,0:T(8,128)(2,1)} %get-tuple-element.438.refs_0_.refs_1_, ...), custom_call_target="tpu_custom_call" | custom-call | flops 17179869184 | bytes 41943040 | tf_op jit(solution)/shard_map/weight_grads/pallas_call | solution.py:150
  718.6 29.0 %weight_grads.14 = (f32[512,1024]{1,0:T(8,128)}, f32[512,1024]{1,0:T(8,128)}, f32[512,1024]{1,0:T(8,128)}, f32[512,1024]{1,0:T(8,128)}) custom-call(s32[8]{0:T(128)} %stack.50.order_ref, bf16[1024,2048]{1,0:T(8,128)(2,1)} %get-tuple-element.437.refs_0_, bf16[1024,2048]{1,0:T(8,128)(2,1)} %get-tuple-element.438.refs_0_.refs_1_, ...), custom_call_target="tpu_custom_call" | custom-call | flops 17179869184 | bytes 41943040 | tf_op jit(solution)/shard_map/weight_grads/pallas_call | solution.py:150
  766.9 20.3 %project.34.qkv_ref = bf16[4096,768]{1,0:T(8,128)(2,1)} custom-call(bf16[1024,2048]{1,0:T(8,128)(2,1)} %get-tuple-element.437.refs_0_, bf16[1024,2048]{1,0:T(8,128)(2,1)} %get-tuple-element.438.refs_0_.refs_1_, bf16[1024,2048]{1,0:T(8,128)(2,1)} %collective-permute-done.refs_0_.refs_1_.refs_2_, ...), custom_call_target="tpu_custom_call" | custom-call | flops 12884901888 | bytes 23068672 | tf_op jit(solution)/shard_map/project/pallas_call | solution.py:111
  876.6 29.1 %weight_grads.15 = (f32[512,1024]{1,0:T(8,128)}, f32[512,1024]{1,0:T(8,128)}, f32[512,1024]{1,0:T(8,128)}, f32[512,1024]{1,0:T(8,128)}) custom-call(s32[8]{0:T(128)} %stack.50.order_ref, bf16[1024,2048]{1,0:T(8,128)(2,1)} %get-tuple-element.437.refs_0_, bf16[1024,2048]{1,0:T(8,128)(2,1)} %get-tuple-element.438.refs_0_.refs_1_, ...), custom_call_target="tpu_custom_call" | custom-call | flops 17179869184 | bytes 41943040 | tf_op jit(solution)/shard_map/weight_grads/pallas_call | solution.py:150
  998.3 49.5 %collective-permute-done.65.refs_3_ = f32[256,1024]{1,0:T(8,128)} collective-permute-done((f32[256,1024]{1,0:T(8,128)}, f32[256,1024]{1,0:T(8,128)}, u32[]{:S(2)}, u32[]{:S(2)}) %collective-permute-start.65) | collective-permute-done | bytes 1048608 | tf_op jit(solution)/shard_map/ppermute | solution.py:339
  1095.7 20.7 %collective-permute-done.38.a2 = f32[256,1024]{1,0:T(8,128)S(1)} collective-permute-done((f32[256,1024]{1,0:T(8,128)S(1)}, f32[256,1024]{1,0:T(8,128)S(1)}, u32[]{:S(2)}, u32[]{:S(2)}) %collective-permute-start.38) | collective-permute-done | bytes 1048608 | tf_op jit(solution)/shard_map/ppermute | solution.py:339
  1117.6 50.0 %fusion.22 = f32[2048,2048]{1,0:T(8,128)} fusion(bf16[2048,4608]{1,0:T(8,128)(2,1)} %get-tuple-element.484.refs_8_.refs_9_, bf16[2048,4608]{1,0:T(8,128)(2,1)} %lay_out_weights.2.refs_1_.refs_4_), kind=kOutput, calls=%fused_computation.90 | convolution fusion | flops 38654705664 | bytes 54525952 | tf_op jit(solution)/shard_map/dot_general | solution.py:16
  1184.2 50.6 %convolution_add_fusion.grad_ref = bf16[2048,2048]{1,0:T(8,128)(2,1)} fusion(f32[2048,2048]{1,0:T(8,128)} %fusion.22, bf16[2048,4608]{1,0:T(8,128)(2,1)} %constant_dynamic-update-slice_fusion, bf16[2048,4608]{1,0:T(8,128)(2,1)} %lay_out_weights.3), kind=kOutput, calls=%fused_computation | convolution fusion | flops 38663094272 | bytes 62914560 | tf_op jit(solution)/shard_map/dot_general | solution.py:16
  1339.8 49.7 %collective-permute-done.43.refs_5_ = f32[256,1024]{1,0:T(8,128)S(1)} collective-permute-done((f32[256,1024]{1,0:T(8,128)S(1)}, f32[256,1024]{1,0:T(8,128)S(1)}, u32[]{:S(2)}, u32[]{:S(2)}) %collective-permute-start.43) | collective-permute-done | bytes 1048608 | tf_op jit(solution)/shard_map/ppermute | solution.py:339
  1391.0 22.3 %collective-permute-done.44.refs_6_ = f32[256,1024]{1,0:T(8,128)S(1)} collective-permute-done((f32[256,1024]{1,0:T(8,128)S(1)}, f32[256,1024]{1,0:T(8,128)S(1)}, u32[]{:S(2)}, u32[]{:S(2)}) %collective-permute-start.44) | collective-permute-done | bytes 1048608 | tf_op jit(solution)/shard_map/ppermute | solution.py:339
  1420.1 31.9 %collective-permute-done.45.refs_7_ = f32[256,1024]{1,0:T(8,128)S(1)} collective-permute-done((f32[256,1024]{1,0:T(8,128)}, f32[256,1024]{1,0:T(8,128)S(1)}, u32[]{:S(2)}, u32[]{:S(2)}) %collective-permute-start.45) | collective-permute-done | bytes 1048608 | tf_op jit(solution)/shard_map/ppermute | solution.py:339
  1487.0 23.5 %collective-permute-done.72.refs_2_ = f32[256,1024]{1,0:T(8,128)S(1)} collective-permute-done((f32[256,1024]{1,0:T(8,128)S(1)}, f32[256,1024]{1,0:T(8,128)S(1)}, u32[]{:S(2)}, u32[]{:S(2)}) %collective-permute-start.72) | collective-permute-done | bytes 1048608 | tf_op jit(solution)/shard_map/ppermute | solution.py:339
  1511.8 21.7 %collective-permute-done.73.refs_3_ = f32[256,1024]{1,0:T(8,128)} collective-permute-done((f32[256,1024]{1,0:T(8,128)S(1)}, f32[256,1024]{1,0:T(8,128)}, u32[]{:S(2)}, u32[]{:S(2)}) %collective-permute-start.73) | collective-permute-done | bytes 1048608 | tf_op jit(solution)/shard_map/ppermute | solution.py:339
  1549.8 29.9 %place.3 = (f32[2048,3,24,128]{3,2,1,0:T(8,128)}, f32[24,128,2048]{2,1,0:T(8,128)}) custom-call(s32[1]{0:T(128)} %bitcast.10.core_ref, f32[2048,1024]{1,0:T(8,128)} %assemble.6.refs_0_, f32[2048,1024]{1,0:T(8,128)} %collective-permute-done.70.refs_1_, f32[2048,1024]{1,0:T(8,128)} %assemble.7.refs_2_, f32[2048,1024]{1,0:T(8,128)} %collective-permute-done.71.refs_3_), custom_call_target="tpu_custom_call" | custom-call | flops 67108864 | bytes 67108864 | tf_op jit(solution)/shard_map/place/pallas_call | solution.py:268
  1594.2 29.9 %place.4 = (f32[2048,3,24,128]{3,2,1,0:T(8,128)}, f32[24,128,2048]{2,1,0:T(8,128)}) custom-call(s32[1]{0:T(128)} %bitcast.10.core_ref, f32[2048,1024]{1,0:T(8,128)} %assemble.8.refs_0_, f32[2048,1024]{1,0:T(8,128)} %collective-permute-done.82.refs_1_, f32[2048,1024]{1,0:T(8,128)} %assemble.9.refs_2_, ...), custom_call_target="tpu_custom_call", output_to_operand_aliasing={{0}: (5, {}), {1}: (6, {})} | custom-call | flops 67108864 | bytes 67108864 | tf_op jit(solution)/shard_map/place/pallas_call | solution.py:268
  1633.0 51.5 %all_to_all.36.in_ref = bf16[8,128,2048]{2,1,0:T(8,128)(2,1)} all-to-all(bf16[8,128,2048]{2,1,0:T(8,128)(2,1)} %bitcast.125), channel_id=1, replica_groups=mesh['sp'=8] {'sp'}, dimensions={0} | all-to-all | bytes 8388608 | tf_op jit(solution)/shard_map/all_to_all | solution.py:353
  1695.1 29.9 %place.5 = (f32[2048,3,24,128]{3,2,1,0:T(8,128)}, f32[24,128,2048]{2,1,0:T(8,128)}) custom-call(s32[1]{0:T(128)} %bitcast.10.core_ref, f32[2048,1024]{1,0:T(8,128)} %assemble.10.refs_0_, f32[2048,1024]{1,0:T(8,128)} %collective-permute-done.84.refs_1_, f32[2048,1024]{1,0:T(8,128)} %assemble.11.refs_2_, ...), custom_call_target="tpu_custom_call", output_to_operand_aliasing={{0}: (5, {}), {1}: (6, {})} | custom-call | flops 67108864 | bytes 67108864 | tf_op jit(solution)/shard_map/place/pallas_call | solution.py:268
  (440 shorter events, 905.8 us)
Async XLA Ops:
  381.3 446.2 %collective-permute-start.30 = (bf16[2048,768]{1,0:T(8,128)(2,1)}, bf16[2048,768]{1,0:T(8,128)(2,1)}, u32[]{:S(2)}, u32[]{:S(2)}) collective-permute-start(bf16[2048,768]{1,0:T(8,128)(2,1)} %pad_maximum_fusion), channel_id=1, source_target_pairs={{0,1},{1,0},{2,3},{3,2},{4,5},{5,4},{6,7},{7,6}} | collective-permute-start | bytes 9437192 | tf_op jit(solution)/shard_map/ppermute | solution.py:339
  408.6 419.2 %collective-permute-start.46 = (f32[256,1024]{1,0:T(8,128)}, f32[256,1024]{1,0:T(8,128)}, u32[]{:S(2)}, u32[]{:S(2)}) collective-permute-start(f32[256,1024]{1,0:T(8,128)} %get-tuple-element.504.refs_0_), channel_id=1, source_target_pairs={{0,4},{1,5},{2,6},{3,7},{4,0},{5,1},{6,2},{7,3}} | collective-permute-start | bytes 3145736 | tf_op jit(solution)/shard_map/ppermute | solution.py:339
  409.6 418.6 %collective-permute-start.47 = (f32[256,1024]{1,0:T(8,128)}, f32[256,1024]{1,0:T(8,128)}, u32[]{:S(2)}, u32[]{:S(2)}) collective-permute-start(f32[256,1024]{1,0:T(8,128)} %get-tuple-element.505.refs_1_), channel_id=1, source_target_pairs={{0,2},{1,3},{2,0},{3,1},{4,6},{5,7},{6,4},{7,5}} | collective-permute-start | bytes 3145736 | tf_op jit(solution)/shard_map/ppermute | solution.py:339
  958.1 90.0 %collective-permute-start.36 = (f32[512,1024]{1,0:T(8,128)}, f32[512,1024]{1,0:T(8,128)}, u32[]{:S(2)}, u32[]{:S(2)}) collective-permute-start(f32[512,1024]{1,0:T(8,128)} %get-tuple-element.479), channel_id=1, source_target_pairs={{0,2},{1,3},{2,0},{3,1},{4,6},{5,7},{6,4},{7,5}} | collective-permute-start | bytes 6291464 | tf_op jit(solution)/shard_map/ppermute | solution.py:339
  959.1 89.3 %collective-permute-start.37 = (f32[512,1024]{1,0:T(8,128)}, f32[512,1024]{1,0:T(8,128)}, u32[]{:S(2)}, u32[]{:S(2)}) collective-permute-start(f32[512,1024]{1,0:T(8,128)} %get-tuple-element.480), channel_id=1, source_target_pairs={{0,4},{1,5},{2,6},{3,7},{4,0},{5,1},{6,2},{7,3}} | collective-permute-start | bytes 6291464 | tf_op jit(solution)/shard_map/ppermute | solution.py:339
  980.5 83.9 %collective-permute-start.33 = (bf16[2048,768]{1,0:T(8,128)(2,1)S(1)}, bf16[2048,768]{1,0:T(8,128)(2,1)}, u32[]{:S(2)}, u32[]{:S(2)}) collective-permute-start(bf16[2048,768]{1,0:T(8,128)(2,1)S(1)} %copy-done.6), channel_id=1, source_target_pairs={{0,1},{1,0},{2,3},{3,2},{4,5},{5,4},{6,7},{7,6}} | collective-permute-start | bytes 9437192 | tf_op jit(solution)/shard_map/ppermute | solution.py:339
  983.0 89.8 %collective-permute-start.34 = (bf16[2048,768]{1,0:T(8,128)(2,1)S(1)}, bf16[2048,768]{1,0:T(8,128)(2,1)}, u32[]{:S(2)}, u32[]{:S(2)}) collective-permute-start(bf16[2048,768]{1,0:T(8,128)(2,1)S(1)} %copy-done.7), channel_id=1, source_target_pairs={{0,1},{1,0},{2,3},{3,2},{4,5},{5,4},{6,7},{7,6}} | collective-permute-start | bytes 9437192 | tf_op jit(solution)/shard_map/ppermute | solution.py:339
  1094.5 83.9 %collective-permute-start.67 = (f32[256,1024]{1,0:T(8,128)S(1)}, f32[256,1024]{1,0:T(8,128)}, u32[]{:S(2)}, u32[]{:S(2)}) collective-permute-start(f32[256,1024]{1,0:T(8,128)S(1)} %copy-done.23), channel_id=1, source_target_pairs={{0,4},{1,5},{2,6},{3,7},{4,0},{5,1},{6,2},{7,3}} | collective-permute-start | bytes 3145736 | tf_op jit(solution)/shard_map/ppermute | solution.py:339
  1176.6 99.1 %collective-permute-start.60 = (f32[256,1024]{1,0:T(8,128)}, f32[256,1024]{1,0:T(8,128)}, u32[]{:S(2)}, u32[]{:S(2)}) collective-permute-start(f32[256,1024]{1,0:T(8,128)} %get-tuple-element.540.refs_0_), channel_id=1, source_target_pairs={{0,2},{1,3},{2,0},{3,1},{4,6},{5,7},{6,4},{7,5}} | collective-permute-start | bytes 3145736 | tf_op jit(solution)/shard_map/ppermute | solution.py:339
  1177.1 103.5 %collective-permute-start.61 = (f32[256,1024]{1,0:T(8,128)}, f32[256,1024]{1,0:T(8,128)}, u32[]{:S(2)}, u32[]{:S(2)}) collective-permute-start(f32[256,1024]{1,0:T(8,128)} %get-tuple-element.541.refs_1_), channel_id=1, source_target_pairs={{0,4},{1,5},{2,6},{3,7},{4,0},{5,1},{6,2},{7,3}} | collective-permute-start | bytes 3145736 | tf_op jit(solution)/shard_map/ppermute | solution.py:339
  1178.3 111.4 %collective-permute-start.62 = (f32[256,1024]{1,0:T(8,128)}, f32[256,1024]{1,0:T(8,128)}, u32[]{:S(2)}, u32[]{:S(2)}) collective-permute-start(f32[256,1024]{1,0:T(8,128)} %collective-permute-done.58.refs_2_), channel_id=1, source_target_pairs={{0,2},{1,3},{2,0},{3,1},{4,6},{5,7},{6,4},{7,5}} | collective-permute-start | bytes 3145736 | tf_op jit(solution)/shard_map/ppermute | solution.py:339
  1179.3 110.9 %collective-permute-start.63 = (f32[256,1024]{1,0:T(8,128)}, f32[256,1024]{1,0:T(8,128)}, u32[]{:S(2)}, u32[]{:S(2)}) collective-permute-start(f32[256,1024]{1,0:T(8,128)} %collective-permute-done.59.refs_3_), channel_id=1, source_target_pairs={{0,4},{1,5},{2,6},{3,7},{4,0},{5,1},{6,2},{7,3}} | collective-permute-start | bytes 3145736 | tf_op jit(solution)/shard_map/ppermute | solution.py:339
  1183.9 115.3 %collective-permute-start.40 = (f32[256,1024]{1,0:T(8,128)S(1)}, f32[256,1024]{1,0:T(8,128)S(1)}, u32[]{:S(2)}, u32[]{:S(2)}) collective-permute-start(f32[256,1024]{1,0:T(8,128)S(1)} %copy-done.21), channel_id=1, source_target_pairs={{0,4},{1,5},{2,6},{3,7},{4,0},{5,1},{6,2},{7,3}} | collective-permute-start | bytes 3145736 | tf_op jit(solution)/shard_map/ppermute | solution.py:339
  1275.7 262.9 %collective-permute-start.70 = (f32[2048,1024]{1,0:T(8,128)}, f32[2048,1024]{1,0:T(8,128)}, u32[]{:S(2)}, u32[]{:S(2)}) collective-permute-start(f32[2048,1024]{1,0:T(8,128)} %assemble.6.refs_0_), channel_id=1, source_target_pairs={{0,1},{1,0},{2,3},{3,2},{4,5},{5,4},{6,7},{7,6}} | collective-permute-start | bytes 25165832 | tf_op jit(solution)/shard_map/ppermute | solution.py:339
  1280.7 258.2 %collective-permute-start.71 = (f32[2048,1024]{1,0:T(8,128)}, f32[2048,1024]{1,0:T(8,128)}, u32[]{:S(2)}, u32[]{:S(2)}) collective-permute-start(f32[2048,1024]{1,0:T(8,128)} %assemble.7.refs_2_), channel_id=1, source_target_pairs={{0,1},{1,0},{2,3},{3,2},{4,5},{5,4},{6,7},{7,6}} | collective-permute-start | bytes 25165832 | tf_op jit(solution)/shard_map/ppermute | solution.py:339
  1289.8 249.2 %collective-permute-start.82 = (f32[2048,1024]{1,0:T(8,128)}, f32[2048,1024]{1,0:T(8,128)}, u32[]{:S(2)}, u32[]{:S(2)}) collective-permute-start(f32[2048,1024]{1,0:T(8,128)} %assemble.8.refs_0_), channel_id=1, source_target_pairs={{0,1},{1,0},{2,3},{3,2},{4,5},{5,4},{6,7},{7,6}} | collective-permute-start | bytes 25165832 | tf_op jit(solution)/shard_map/ppermute | solution.py:339
  1299.2 289.3 %collective-permute-start.83 = (f32[2048,1024]{1,0:T(8,128)}, f32[2048,1024]{1,0:T(8,128)}, u32[]{:S(2)}, u32[]{:S(2)}) collective-permute-start(f32[2048,1024]{1,0:T(8,128)} %assemble.9.refs_2_), channel_id=1, source_target_pairs={{0,1},{1,0},{2,3},{3,2},{4,5},{5,4},{6,7},{7,6}} | collective-permute-start | bytes 25165832 | tf_op jit(solution)/shard_map/ppermute | solution.py:339
  1315.4 100.7 %all-to-all-start.4 = ((bf16[8,128,2048]{2,1,0:T(8,128)(2,1)}), bf16[8,128,2048]{2,1,0:T(8,128)(2,1)}, u32[]{:S(2)}, u32[]{:S(2)}) async-start(bf16[8,128,2048]{2,1,0:T(8,128)(2,1)} %bitcast.126), calls=%async_computation.4 | async-start | bytes 8388608 | tf_op jit(solution)/shard_map/all_to_all | solution.py:353
  1416.1 129.0 %all-to-all-start.3 = ((bf16[8,128,2048]{2,1,0:T(8,128)(2,1)}), bf16[8,128,2048]{2,1,0:T(8,128)(2,1)}, u32[]{:S(2)}, u32[]{:S(2)}) async-start(bf16[8,128,2048]{2,1,0:T(8,128)(2,1)} %bitcast.123), calls=%async_computation.3 | async-start | bytes 8388608 | tf_op jit(solution)/shard_map/all_to_all | solution.py:353
  1537.4 86.8 %collective-permute-start.74 = (f32[256,1024]{1,0:T(8,128)S(1)}, f32[256,1024]{1,0:T(8,128)}, u32[]{:S(2)}, u32[]{:S(2)}) collective-permute-start(f32[256,1024]{1,0:T(8,128)S(1)} %copy-done.28), channel_id=1, source_target_pairs={{0,2},{1,3},{2,0},{3,1},{4,6},{5,7},{6,4},{7,5}} | collective-permute-start | bytes 3145736 | tf_op jit(solution)/shard_map/ppermute | solution.py:339
  1538.6 85.6 %collective-permute-start.75 = (f32[256,1024]{1,0:T(8,128)S(1)}, f32[256,1024]{1,0:T(8,128)}, u32[]{:S(2)}, u32[]{:S(2)}) collective-permute-start(f32[256,1024]{1,0:T(8,128)S(1)} %copy-done.29), channel_id=1, source_target_pairs={{0,4},{1,5},{2,6},{3,7},{4,0},{5,1},{6,2},{7,3}} | collective-permute-start | bytes 3145736 | tf_op jit(solution)/shard_map/ppermute | solution.py:339
  1538.9 85.3 %collective-permute-start.76 = (f32[256,1024]{1,0:T(8,128)S(1)}, f32[256,1024]{1,0:T(8,128)}, u32[]{:S(2)}, u32[]{:S(2)}) collective-permute-start(f32[256,1024]{1,0:T(8,128)S(1)} %collective-permute-done.72.refs_2_), channel_id=1, source_target_pairs={{0,2},{1,3},{2,0},{3,1},{4,6},{5,7},{6,4},{7,5}} | collective-permute-start | bytes 3145736 | tf_op jit(solution)/shard_map/ppermute | solution.py:339
  1539.0 85.3 %collective-permute-start.77 = (f32[256,1024]{1,0:T(8,128)}, f32[256,1024]{1,0:T(8,128)}, u32[]{:S(2)}, u32[]{:S(2)}) collective-permute-start(f32[256,1024]{1,0:T(8,128)} %collective-permute-done.73.refs_3_), channel_id=1, source_target_pairs={{0,4},{1,5},{2,6},{3,7},{4,0},{5,1},{6,2},{7,3}} | collective-permute-start | bytes 3145736 | tf_op jit(solution)/shard_map/ppermute | solution.py:339
  1588.5 106.6 %collective-permute-start.84 = (f32[2048,1024]{1,0:T(8,128)}, f32[2048,1024]{1,0:T(8,128)}, u32[]{:S(2)}, u32[]{:S(2)}) collective-permute-start(f32[2048,1024]{1,0:T(8,128)} %assemble.10.refs_0_), channel_id=1, source_target_pairs={{0,1},{1,0},{2,3},{3,2},{4,5},{5,4},{6,7},{7,6}} | collective-permute-start | bytes 25165832 | tf_op jit(solution)/shard_map/ppermute | solution.py:339
  (139 other events, 4672.9 us)

commit v2 on v1

--- a/solution.py
+++ b/solution.py
@@ -10,6 +10,10 @@
 LN_EPS = 1e-5
 F32, BF16 = jnp.float32, jnp.bfloat16
 LOG2E = 1.4426950408889634
+
+
+def cost(flops, bytes_accessed):
+    return pl.CostEstimate(flops=flops, bytes_accessed=bytes_accessed, transcendentals=0)
 
 
 def dot(a, b, ca, cb):
@@ -45,7 +49,7 @@
         dv = dot(p_ref[lo:hi, lo:], do_ref[lo:, :], 1, 0)
         g_ref[lo:hi, dh:2 * dh] = (dk * scale).astype(BF16)
         g_ref[lo:hi, 2 * dh:3 * dh] = dv.astype(BF16)
-    gb_ref[...] = jnp.sum(g_ref[...].astype(F32), axis=0, keepdims=True)[None]
+    gb_ref[:] = jnp.sum(g_ref[:].astype(F32), axis=0, keepdims=True)[None]
 
 
 def attention(qkv, grad_o, seq, dh, seqs, into=None, width=0, at=(0, 0)):
@@ -75,7 +79,7 @@
                    jax.ShapeDtypeStruct((n_seq, 1, n_heads * 3 * dh), F32)],
         scratch_shapes=[pltpu.VMEM((seq, seq), BF16)] * 2,
         input_output_aliases=alias,
-        cost_estimate=pl.CostEstimate(flops=2 * flops, bytes_accessed=n_seq * n_heads * seq * dh * 16, transcendentals=0),
+        cost_estimate=cost(2 * flops, n_seq * n_heads * seq * dh * 16),
         name="attention",
     )(*args)
     return o, g, jnp.sum(gb, axis=(0, 1))
@@ -86,10 +90,10 @@
     i = pl.program_id(0)
 
     def work(a_ref):
-        out = dot(a_ref[...], w_ref[...], 1, 1 if transposed else 0)
+        out = dot(a_ref[:], w_ref[:], 1, 1 if transposed else 0)
         if has_bias:
-            out = out + refs[n_units + 1][...]
-        o_ref[...] = out.astype(BF16)
+            out = out + refs[n_units + 1][:]
+        o_ref[:] = out.astype(BF16)
 
     for n in range(n_units):
         pl.when((i >= n * steps) & (i < (n + 1) * steps))(functools.partial(work, refs[n]))
@@ -114,8 +118,7 @@
         in_specs=in_specs,
         out_specs=pl.BlockSpec((bm, cols), lambda i: (i, 0)),
         out_shape=jax.ShapeDtypeStruct((total, cols), BF16),
-        cost_estimate=pl.CostEstimate(flops=2 * total * depth * cols, bytes_accessed=2 * total * (depth + cols),
-                                      transcendentals=0),
+        cost_estimate=cost(2 * total * depth * cols, 2 * total * (depth + cols)),
         name="project",
     )(*args)
 
@@ -138,11 +141,11 @@
         inputs, out_refs, acc = refs[:len(args)], refs[len(args):-1], refs[-1]
         u, gy, g, o = (inputs[n * len(units):(n + 1) * len(units)] for n in range(4))
         i = pl.program_id(0)
-        acc[:, :cols] = sum(dot(a[...], b[...], 0, 0) for a, b in zip(u, g))
-        acc[:, cols:] = sum(dot(a[...], b[...], 0, 0) for a, b in zip(gy, o))
+        acc[:, :cols] = sum(dot(a[:], b[:], 0, 0) for a, b in zip(u, g))
+        acc[:, cols:] = sum(dot(a[:], b[:], 0, 0) for a, b in zip(gy, o))
 
         def write(n):
-            out_refs[n][...] = acc[...] if before is None else acc[...] + inputs[4 * len(units) + n][...]
+            out_refs[n][:] = acc[:] if before is None else acc[:] + inputs[4 * len(units) + n][:]
 
         for n in range(n_out):
             pl.when((i >= n * per_out) & (i < (n + 1) * per_out))(functools.partial(write, n))
@@ -153,8 +156,7 @@
             num_scalar_prefetch=1, grid=(total,), in_specs=in_specs, out_specs=[piece(n) for n in range(n_out)],
             scratch_shapes=[pltpu.VMEM((bd, cols + cols_o), F32)]),
         out_shape=[jax.ShapeDtypeStruct((per_out * bd, cols + cols_o), F32)] * n_out,
-        cost_estimate=pl.CostEstimate(flops=2 * len(units) * rows * total * bd * (cols + cols_o), bytes_accessed=40 * 2 ** 20,
-                                      transcendentals=0),
+        cost_estimate=cost(2 * len(units) * rows * total * bd * (cols + cols_o), 40 * 2 ** 20),
         name="weight_grads",
     )(order, *args)
 
@@ -168,7 +170,7 @@
         i = pl.program_id(0)
 
         def work(out_ref, first, second):
-            out_ref[...] = kept_ref[...] + first[...] + second[...]
+            out_ref[:] = kept_ref[:] + first[:] + second[:]
 
         pl.when(i < 2)(lambda: work(a_ref, a1, a2))
         pl.when(i >= 2)(lambda: work(b_ref, b1, b2))
@@ -178,7 +180,7 @@
         in_specs=[pl.BlockSpec((bm, cols), lambda i: (i, 0)), spec(2, 0), spec(2, 2), spec(0, 0), spec(0, 2)],
         out_specs=[spec(0, 0), spec(0, 2)],
         out_shape=[jax.ShapeDtypeStruct(last_a.shape, F32)] * 2,
-        cost_estimate=pl.CostEstimate(flops=2 ** 24, bytes_accessed=kept.size * 16, transcendentals=0),
+        cost_estimate=cost(2 ** 24, kept.size * 16),
         name="add_last",
     )(kept, got_a, got_b, last_a, last_b)
 
@@ -189,7 +191,7 @@
 
     def kernel(order_ref, *refs):
         def work(m):
-            refs[-1][...] = refs[m][...]
+            refs[-1][:] = refs[m][:]
 
         for m in range(n):
             pl.when(pl.program_id(0) == m)(functools.partial(work, m))
@@ -200,7 +202,7 @@
         grid_spec=pltpu.PrefetchScalarGridSpec(num_scalar_prefetch=1, grid=(n,), in_specs=[block] * n,
                                                out_specs=pl.BlockSpec((rows, cols), lambda i, order: (order[i], 0))),
         out_shape=jax.ShapeDtypeStruct((n * rows, cols), F32),
-        cost_estimate=pl.CostEstimate(flops=2 ** 24, bytes_accessed=n * rows * cols * 8, transcendentals=0),
+        cost_estimate=cost(2 ** 24, n * rows * cols * 8),
         name="assemble",
     )(order, *pieces)
 
@@ -228,7 +230,7 @@
             in_specs=[pl.BlockSpec((blk, 3, heads_all, dh), lambda i, c: (i, 0, 0, 0))],
             out_specs=pl.BlockSpec((blk, width), lambda i, c: (i, 0))),
         out_shape=jax.ShapeDtypeStruct((dim, width), BF16),
-        cost_estimate=pl.CostEstimate(flops=dim * width * 400, bytes_accessed=dim * width * 6, transcendentals=0),
+        cost_estimate=cost(dim * width * 400, dim * width * 6),
         name="lay_out_weights",
     )(core, w_qkv)
 
@@ -273,7 +275,7 @@
                        pl.BlockSpec((heads, dh, blk), lambda i, c: (group, 0, i))]),
         out_shape=[jax.ShapeDtypeStruct((dim, 3, heads_all, dh), F32), jax.ShapeDtypeStruct((heads_all, dh, dim), F32)],
         input_output_aliases=alias,
-        cost_estimate=pl.CostEstimate(flops=size * 8, bytes_accessed=size * 8, transcendentals=0),
+        cost_estimate=cost(size * 8, size * 8),
         name="place",
     )(core, *args)
 
@@ -282,7 +284,7 @@
     n, *block = piece.shape
 
     def kernel(in_ref, *refs):
-        refs[-1][:, 0] = in_ref[...]
+        refs[-1][:, 0] = in_ref[:]
 
     in_specs, args = [pl.BlockSpec((2, *block), lambda i: (i, 0, 0))], [piece]
     if into is not None:
@@ -292,7 +294,7 @@
                           out_specs=pl.BlockSpec((2, 1, *block), lambda i: (i, at, 0, 0)),
                           out_shape=jax.ShapeDtypeStruct((n, 2, *block), piece.dtype),
                           input_output_aliases={} if into is None else {1: 0},
-                          cost_estimate=pl.CostEstimate(flops=piece.size, bytes_accessed=4 * piece.size, transcendentals=0),
+                          cost_estimate=cost(piece.size, 4 * piece.size),
                           name="interleaved")(*args)
 
 
@@ -300,18 +302,18 @@
     parts, _, part, dim = x.shape
 
     def kernel(grad_ref, x_ref, gy_ref, gain_ref, gx_ref, sums_ref):
-        xf, grad, gyf = x_ref[0, 0].astype(F32), grad_ref[...].astype(F32), gy_ref[...].astype(F32)
+        xf, grad, gyf = x_ref[0, 0].astype(F32), grad_ref[:].astype(F32), gy_ref[:].astype(F32)
         mean_of = lambda a: jnp.sum(a, axis=1, keepdims=True) * (1.0 / dim)
         centered = xf - mean_of(xf)
         inv_std = lax.rsqrt(mean_of(centered * centered) + LN_EPS)
         x_hat = centered * inv_std
-        grad_hat = grad * gain_ref[...]
+        grad_hat = grad * gain_ref[:]
         gx = gyf + inv_std * (grad_hat - mean_of(grad_hat) - x_hat * mean_of(grad_hat * x_hat))
-        gx_ref[...] = gx.astype(BF16)
+        gx_ref[:] = gx.astype(BF16)
 
         @pl.when(pl.program_id(0) == 0)
         def _():
-            sums_ref[...] = jnp.zeros_like(sums_ref)
+            sums_ref[:] = jnp.zeros_like(sums_ref)
 
         for n, a in enumerate((grad * x_hat, grad, gyf)):
             sums_ref[n:n + 1, :] += jnp.sum(a, axis=0, keepdims=True)
@@ -323,7 +325,7 @@
                   row, pl.BlockSpec((1, dim), lambda i: (0, 0))],
         out_specs=[row, pl.BlockSpec((8, dim), lambda i: (0, 0))],
         out_shape=[jax.ShapeDtypeStruct((parts * part, dim), BF16), jax.ShapeDtypeStruct((8, dim), F32)],
-        cost_estimate=pl.CostEstimate(flops=parts * part * dim * 400, bytes_accessed=parts * part * dim * 8, transcendentals=0),
+        cost_estimate=cost(parts * part * dim * 400, parts * part * dim * 8),
         name="norm_grads",
     )(grad_u, x, gy, gain.reshape(1, dim))
 
@@ -504,17 +506,19 @@
             proj = dot(held[0][s * seq:(s + 1) * seq], wo_own, 1, 0) + b_out
             proj = dot(rows_of(held[1:], s), wo_par, 1, 0) + proj
             y_parts.append((xs[s].astype(F32) + proj).astype(BF16))
-        y_out = None
-        for s, y in enumerate(y_parts):
-            y_out = interleaved(y_out, exchange(y.reshape(n_dev, part, dim)), s)
+        y_moved = [exchange(y.reshape(n_dev, part, dim)) for y in y_parts]
         chain = tuple(y_parts)
         spread(steps - 2)
+        for k in range(2):
+            chain = take(k)
         forward(steps - 2)
         chain = first_add(steps - 1)
 
         g_mine, = after_chain([mine[1]])
         grad_u = dot(g_mine, w_own, 1, 1)
         chain = (grad_u,)
+        whole = place_sums(0)
+        chain = tuple(whole)
         chain = last_add(steps - 1)
         spread(steps - 1)
         g_theirs, = after_chain([jnp.concatenate(g_got, axis=1)])
@@ -538,20 +542,20 @@
         others = [hop(small, bit) for bit in (2, 4, 6)]
 
         chain = (gx,)
-        for k in range(4):
+        for k in range(2, 4):
             chain = take(k)
-        whole = place_sums(0)
+        whole = place_sums(1)
         chain = tuple(whole)
         chain = take(4)
-        whole = place_sums(1)
+        y_out = interleaved(interleaved(None, after_chain([y_moved[0]])[0], 0), y_moved[1], 1)
+        chain = (y_out, small)
         others = after_chain(others)
         small = (small + others[0]) + (others[1] + others[2])
-        chain = (y_out, small) + tuple(whole)
         chain = take(5)
-        grad_x = interleaved(None, after_chain([gx_parts[0]])[0], 0)
-        chain = (grad_x,)
         whole = place_sums(2)
         chain = tuple(whole)
+        grad_x = interleaved(None, after_chain([gx_parts[0]])[0], 0)
+        chain = (grad_x, small)
         grad_x = interleaved(grad_x, after_chain([gx_parts[1]])[0], 1)
         grad_w_qkv, grad_w_out = whole
         small = small.reshape(-1)

time: 1750 us -> 1720 us (0.983)
    ppermute x86, waiting for transfers between devices: 359 us -> 308 us  [solution(): lax.ppermute(a, 'sp', [(d, d ^ bit) for d in range(n_dev)])]
    all_to_all x5, waiting for transfers between devices: 9.67 us -> 44.2 us  [exchange(): return lax.all_to_all(a, 'sp', 0, 0, tiled=True)]
  transfers between devices with their start and end apart: 91 -> 91, of which waited for: 25 -> 20; matrix products, arithmetic and copies ran while one was open for 13% -> 13% of each run, Pallas kernels for 48% -> 47%
where the time goes in v2:
time: 1720 us
  Pallas kernels  861 us (50%)
  waiting for transfers between devices  353 us (21%)
  blocking collectives  148 us (9%)
  matrix products  144 us (8%)
  starting transfers between devices  116 us (7%)
  local copies, waits for them, and re-layouts  49.9 us (3%)
  other arithmetic  42.3 us (2%)
    ppermute x86, waiting for transfers between devices, solution(): lax.ppermute(a, 'sp', [(d, d ^ bit) for d in range(n_dev)])  308 us
    pallas_call x18, Pallas kernels, project(): pl.pallas_call(functools.partial(project_kernel, len(units), steps, trans...  210 us
    pallas_call x8, Pallas kernels, weight_grads(): pl.pallas_call(kernel, grid_spec=pltpu.PrefetchScalarGridSpec(num_scalar_...  188 us
    pallas_call x14, Pallas kernels, attention(): pl.pallas_call(kernel, grid=(n_seq, n_heads), in_specs=in_specs, out_spec...  181 us
    all_to_all x2, blocking collectives, exchange(): return lax.all_to_all(a, 'sp', 0, 0, tiled=True)  148 us
    dot_general x6, matrix products, dot(): lax.dot_general(a, b, (((ca,), (cb,)), ((), ())), preferred_element_type=...  144 us
    ppermute x86, starting transfers between devices, solution(): lax.ppermute(a, 'sp', [(d, d ^ bit) for d in range(n_dev)])  92.9 us
    pallas_call x3, Pallas kernels, place(): pl.pallas_call(functools.partial(place_kernel, counts, dh), grid_spec=plt...  89.9 us
  transfers between devices with their start and end apart: 91, of which 20 were waited for; matrix products, arithmetic and copies ran while one was open for 13% of the time, Pallas kernels for 47%

profile of v2, /device:TPU:1, one launch (start us, length us, event | category | flops | bytes accessed | tf_op | source)
XLA Modules:
  0.0 1715.7 jit_solution(8110333657838308031)
XLA Ops:
  0.6 96.7 %all_to_all.35.x_ref = bf16[8,2,128,2048]{3,2,1,0:T(8,128)(2,1)S(1)} all-to-all(bf16[8,2,128,2048]{3,2,1,0:T(8,128)(2,1)} %bitcast.117), channel_id=1, replica_groups=mesh['sp'=8] {'sp'}, dimensions={0} | all-to-all | bytes 16777216 | tf_op jit(solution)/shard_map/all_to_all | solution.py:355
  116.2 33.6 %lay_out_weights.2.refs_1_.refs_4_ = bf16[2048,4608]{1,0:T(8,128)(2,1)} custom-call(s32[1]{0:T(128)} %bitcast.10.core_ref, bf16[2048,3,24,128]{3,2,1,0:T(8,128)(2,1)} %w_ref.1), custom_call_target="tpu_custom_call" | custom-call | flops 3774873600 | bytes 56623104 | tf_op jit(solution)/shard_map/lay_out_weights/pallas_call | solution.py:226
  375.8 29.0 %weight_grads.11 = (f32[512,1024]{1,0:T(8,128)}, f32[512,1024]{1,0:T(8,128)}, f32[512,1024]{1,0:T(8,128)}, f32[512,1024]{1,0:T(8,128)}) custom-call(s32[8]{0:T(128)} %stack.50.order_ref, bf16[1024,2048]{1,0:T(8,128)(2,1)} %get-tuple-element.438.refs_0_, bf16[1024,2048]{1,0:T(8,128)(2,1)} %get-tuple-element.439.refs_0_.refs_1_, ...), custom_call_target="tpu_custom_call" | custom-call | flops 17179869184 | bytes 41943040 | tf_op jit(solution)/shard_map/weight_grads/pallas_call | solution.py:153
  418.7 20.5 %project.28.qkv_ref = bf16[4096,768]{1,0:T(8,128)(2,1)} custom-call(bf16[1024,2048]{1,0:T(8,128)(2,1)} %get-tuple-element.438.refs_0_, bf16[1024,2048]{1,0:T(8,128)(2,1)} %get-tuple-element.439.refs_0_.refs_1_, bf16[1024,2048]{1,0:T(8,128)(2,1)} %collective-permute-done.refs_0_.refs_1_.refs_2_, ...), custom_call_target="tpu_custom_call" | custom-call | flops 12884901888 | bytes 23068672 | tf_op jit(solution)/shard_map/project/pallas_call | solution.py:115
  475.0 29.5 %weight_grads.12 = (f32[512,1024]{1,0:T(8,128)}, f32[512,1024]{1,0:T(8,128)}, f32[512,1024]{1,0:T(8,128)}, f32[512,1024]{1,0:T(8,128)}) custom-call(s32[8]{0:T(128)} %stack.50.order_ref, bf16[1024,2048]{1,0:T(8,128)(2,1)} %get-tuple-element.438.refs_0_, bf16[1024,2048]{1,0:T(8,128)(2,1)} %get-tuple-element.439.refs_0_.refs_1_, ...), custom_call_target="tpu_custom_call" | custom-call | flops 17179869184 | bytes 41943040 | tf_op jit(solution)/shard_map/weight_grads/pallas_call | solution.py:153
  579.8 29.1 %weight_grads.13 = (f32[512,1024]{1,0:T(8,128)}, f32[512,1024]{1,0:T(8,128)}, f32[512,1024]{1,0:T(8,128)}, f32[512,1024]{1,0:T(8,128)}) custom-call(s32[8]{0:T(128)} %stack.50.order_ref, bf16[1024,2048]{1,0:T(8,128)(2,1)} %get-tuple-element.438.refs_0_, bf16[1024,2048]{1,0:T(8,128)(2,1)} %get-tuple-element.439.refs_0_.refs_1_, ...), custom_call_target="tpu_custom_call" | custom-call | flops 17179869184 | bytes 41943040 | tf_op jit(solution)/shard_map/weight_grads/pallas_call | solution.py:153
  684.6 29.0 %weight_grads.14 = (f32[512,1024]{1,0:T(8,128)}, f32[512,1024]{1,0:T(8,128)}, f32[512,1024]{1,0:T(8,128)}, f32[512,1024]{1,0:T(8,128)}) custom-call(s32[8]{0:T(128)} %stack.50.order_ref, bf16[1024,2048]{1,0:T(8,128)(2,1)} %get-tuple-element.438.refs_0_, bf16[1024,2048]{1,0:T(8,128)(2,1)} %get-tuple-element.439.refs_0_.refs_1_, ...), custom_call_target="tpu_custom_call" | custom-call | flops 17179869184 | bytes 41943040 | tf_op jit(solution)/shard_map/weight_grads/pallas_call | solution.py:153
  834.0 29.1 %weight_grads.15 = (f32[512,1024]{1,0:T(8,128)}, f32[512,1024]{1,0:T(8,128)}, f32[512,1024]{1,0:T(8,128)}, f32[512,1024]{1,0:T(8,128)}) custom-call(s32[8]{0:T(128)} %stack.50.order_ref, bf16[1024,2048]{1,0:T(8,128)(2,1)} %get-tuple-element.438.refs_0_, bf16[1024,2048]{1,0:T(8,128)(2,1)} %get-tuple-element.439.refs_0_.refs_1_, ...), custom_call_target="tpu_custom_call" | custom-call | flops 17179869184 | bytes 41943040 | tf_op jit(solution)/shard_map/weight_grads/pallas_call | solution.py:153
  976.2 23.5 %collective-permute-done.48.refs_2_ = f32[256,1024]{1,0:T(8,128)} collective-permute-done((f32[256,1024]{1,0:T(8,128)}, f32[256,1024]{1,0:T(8,128)}, u32[]{:S(2)}, u32[]{:S(2)}) %collective-permute-start.48) | collective-permute-done | bytes 1048608 | tf_op jit(solution)/shard_map/ppermute | solution.py:341
  999.9 24.0 %collective-permute-done.49.refs_3_ = f32[256,1024]{1,0:T(8,128)} collective-permute-done((f32[256,1024]{1,0:T(8,128)}, f32[256,1024]{1,0:T(8,128)}, u32[]{:S(2)}, u32[]{:S(2)}) %collective-permute-start.49) | collective-permute-done | bytes 1048608 | tf_op jit(solution)/shard_map/ppermute | solution.py:341
  1025.4 21.7 %collective-permute-done.66.refs_2_ = f32[256,1024]{1,0:T(8,128)S(1)} collective-permute-done((f32[256,1024]{1,0:T(8,128)}, f32[256,1024]{1,0:T(8,128)S(1)}, u32[]{:S(2)}, u32[]{:S(2)}) %collective-permute-start.66) | collective-permute-done | bytes 1048608 | tf_op jit(solution)/shard_map/ppermute | solution.py:341
  1051.8 33.6 %lay_out_weights.3 = bf16[2048,4608]{1,0:T(8,128)(2,1)} custom-call(s32[1]{0:T(128)S(6)} %sub.63.core_ref, bf16[2048,3,24,128]{3,2,1,0:T(8,128)(2,1)} %w_ref.1), custom_call_target="tpu_custom_call" | custom-call | flops 3774873600 | bytes 56623104 | tf_op jit(solution)/shard_map/lay_out_weights/pallas_call | solution.py:226
  1104.5 50.0 %fusion.22 = f32[2048,2048]{1,0:T(8,128)} fusion(bf16[2048,4608]{1,0:T(8,128)(2,1)} %get-tuple-element.517.refs_8_.refs_9_, bf16[2048,4608]{1,0:T(8,128)(2,1)} %lay_out_weights.2.refs_1_.refs_4_), kind=kOutput, calls=%fused_computation.90 | convolution fusion | flops 38654705664 | bytes 54525952 | tf_op jit(solution)/shard_map/dot_general | solution.py:20
  1158.4 30.0 %place.3 = (f32[2048,3,24,128]{3,2,1,0:T(8,128)}, f32[24,128,2048]{2,1,0:T(8,128)}) custom-call(s32[1]{0:T(128)} %bitcast.10.core_ref, f32[2048,1024]{1,0:T(8,128)} %assemble.6.refs_0_, f32[2048,1024]{1,0:T(8,128)} %collective-permute-done.64.refs_1_, f32[2048,1024]{1,0:T(8,128)} %assemble.7.refs_2_, f32[2048,1024]{1,0:T(8,128)} %collective-permute-done.65.refs_3_), custom_call_target="tpu_custom_call" | custom-call | flops 67108864 | bytes 67108864 | tf_op jit(solution)/shard_map/place/pallas_call | solution.py:270
  1197.6 50.8 %convolution_add_fusion.grad_ref = bf16[2048,2048]{1,0:T(8,128)(2,1)} fusion(f32[2048,2048]{1,0:T(8,128)} %fusion.22, bf16[2048,4608]{1,0:T(8,128)(2,1)} %constant_dynamic-update-slice_fusion, bf16[2048,4608]{1,0:T(8,128)(2,1)} %lay_out_weights.3), kind=kOutput, calls=%fused_computation | convolution fusion | flops 38663094272 | bytes 62914560 | tf_op jit(solution)/shard_map/dot_general | solution.py:20
  1299.2 44.2 %all-to-all-done.4.in_ref = bf16[8,128,2048]{2,1,0:T(8,128)(2,1)} async-done(((bf16[8,128,2048]{2,1,0:T(8,128)(2,1)}), bf16[8,128,2048]{2,1,0:T(8,128)(2,1)}, u32[]{:S(2)}, u32[]{:S(2)}) %all-to-all-start.4) | async-done | bytes 4194336 | tf_op jit(solution)/shard_map/all_to_all | solution.py:355
  1352.1 26.7 %collective-permute-done.30.refs_2_ = f32[256,1024]{1,0:T(8,128)} collective-permute-done((f32[256,1024]{1,0:T(8,128)S(1)}, f32[256,1024]{1,0:T(8,128)}, u32[]{:S(2)}, u32[]{:S(2)}) %collective-permute-start.30) | collective-permute-done | bytes 1048608 | tf_op jit(solution)/shard_map/ppermute | solution.py:341
  1379.5 41.0 %collective-permute-done.31.refs_3_ = f32[256,1024]{1,0:T(8,128)} collective-permute-done((f32[256,1024]{1,0:T(8,128)S(1)}, f32[256,1024]{1,0:T(8,128)}, u32[]{:S(2)}, u32[]{:S(2)}) %collective-permute-start.31) | collective-permute-done | bytes 1048608 | tf_op jit(solution)/shard_map/ppermute | solution.py:341
  1421.8 21.2 %collective-permute-done.44.refs_4_ = f32[256,1024]{1,0:T(8,128)} collective-permute-done((f32[256,1024]{1,0:T(8,128)S(1)}, f32[256,1024]{1,0:T(8,128)}, u32[]{:S(2)}, u32[]{:S(2)}) %collective-permute-start.44) | collective-permute-done | bytes 1048608 | tf_op jit(solution)/shard_map/ppermute | solution.py:341
  1458.5 30.9 %collective-permute-done.75.refs_3_ = f32[256,1024]{1,0:T(8,128)S(1)} collective-permute-done((f32[256,1024]{1,0:T(8,128)}, f32[256,1024]{1,0:T(8,128)S(1)}, u32[]{:S(2)}, u32[]{:S(2)}) %collective-permute-start.75) | collective-permute-done | bytes 1048608 | tf_op jit(solution)/shard_map/ppermute | solution.py:341
  1493.6 29.9 %place.4 = (f32[2048,3,24,128]{3,2,1,0:T(8,128)}, f32[24,128,2048]{2,1,0:T(8,128)}) custom-call(s32[1]{0:T(128)} %bitcast.10.core_ref, f32[2048,1024]{1,0:T(8,128)} %assemble.8.refs_0_, f32[2048,1024]{1,0:T(8,128)} %collective-permute-done.72.refs_1_, f32[2048,1024]{1,0:T(8,128)} %assemble.9.refs_2_, ...), custom_call_target="tpu_custom_call", output_to_operand_aliasing={{0}: (5, {}), {1}: (6, {})} | custom-call | flops 67108864 | bytes 67108864 | tf_op jit(solution)/shard_map/place/pallas_call | solution.py:270
  1569.0 51.5 %all_to_all.36.in_ref = bf16[8,128,2048]{2,1,0:T(8,128)(2,1)} all-to-all(bf16[8,128,2048]{2,1,0:T(8,128)(2,1)} %bitcast.128), channel_id=1, replica_groups=mesh['sp'=8] {'sp'}, dimensions={0} | all-to-all | bytes 8388608 | tf_op jit(solution)/shard_map/all_to_all | solution.py:355
  1627.6 46.9 %collective-permute-done.85 = f32[120,128]{1,0:T(8,128)S(1)} collective-permute-done((f32[120,128]{1,0:T(8,128)S(1)}, f32[120,128]{1,0:T(8,128)S(1)}, u32[]{:S(2)}, u32[]{:S(2)}) %collective-permute-start.85) | collective-permute-done | bytes 61472 | tf_op jit(solution)/shard_map/ppermute | solution.py:341
  1676.1 29.9 %place.5 = (f32[2048,3,24,128]{3,2,1,0:T(8,128)}, f32[24,128,2048]{2,1,0:T(8,128)}) custom-call(s32[1]{0:T(128)} %bitcast.10.core_ref, f32[2048,1024]{1,0:T(8,128)} %assemble.10.refs_0_, f32[2048,1024]{1,0:T(8,128)} %collective-permute-done.81.refs_1_, f32[2048,1024]{1,0:T(8,128)} %assemble.11.refs_2_, ...), custom_call_target="tpu_custom_call", output_to_operand_aliasing={{0}: (5, {}), {1}: (6, {})} | custom-call | flops 67108864 | bytes 67108864 | tf_op jit(solution)/shard_map/place/pallas_call | solution.py:270
  (421 shorter events, 861.2 us)
Async XLA Ops:
  346.9 469.4 %collective-permute-start.20 = (bf16[2048,256]{1,0:T(8,128)(2,1)}, bf16[2048,256]{1,0:T(8,128)(2,1)}, u32[]{:S(2)}, u32[]{:S(2)}) collective-permute-start(bf16[2048,256]{1,0:T(8,128)(2,1)} %pad_maximum_fusion.1), channel_id=1, source_target_pairs={{0,1},{1,0},{2,3},{3,2},{4,5},{5,4},{6,7},{7,6}} | collective-permute-start | bytes 3145736 | tf_op jit(solution)/shard_map/ppermute | solution.py:341
  374.4 412.8 %collective-permute-start.38 = (f32[256,1024]{1,0:T(8,128)}, f32[256,1024]{1,0:T(8,128)}, u32[]{:S(2)}, u32[]{:S(2)}) collective-permute-start(f32[256,1024]{1,0:T(8,128)} %get-tuple-element.485.refs_0_), channel_id=1, source_target_pairs={{0,4},{1,5},{2,6},{3,7},{4,0},{5,1},{6,2},{7,3}} | collective-permute-start | bytes 3145736 | tf_op jit(solution)/shard_map/ppermute | solution.py:341
  374.6 413.0 %collective-permute-start.39 = (f32[256,1024]{1,0:T(8,128)}, f32[256,1024]{1,0:T(8,128)}, u32[]{:S(2)}, u32[]{:S(2)}) collective-permute-start(f32[256,1024]{1,0:T(8,128)} %get-tuple-element.486.refs_1_), channel_id=1, source_target_pairs={{0,2},{1,3},{2,0},{3,1},{4,6},{5,7},{6,4},{7,5}} | collective-permute-start | bytes 3145736 | tf_op jit(solution)/shard_map/ppermute | solution.py:341
  972.2 131.0 %collective-permute-start.65 = (f32[2048,1024]{1,0:T(8,128)}, f32[2048,1024]{1,0:T(8,128)}, u32[]{:S(2)}, u32[]{:S(2)}) collective-permute-start(f32[2048,1024]{1,0:T(8,128)} %assemble.7.refs_2_), channel_id=1, source_target_pairs={{0,1},{1,0},{2,3},{3,2},{4,5},{5,4},{6,7},{7,6}} | collective-permute-start | bytes 25165832 | tf_op jit(solution)/shard_map/ppermute | solution.py:341
  974.2 130.0 %collective-permute-start.64 = (f32[2048,1024]{1,0:T(8,128)}, f32[2048,1024]{1,0:T(8,128)}, u32[]{:S(2)}, u32[]{:S(2)}) collective-permute-start(f32[2048,1024]{1,0:T(8,128)} %assemble.6.refs_0_), channel_id=1, source_target_pairs={{0,1},{1,0},{2,3},{3,2},{4,5},{5,4},{6,7},{7,6}} | collective-permute-start | bytes 25165832 | tf_op jit(solution)/shard_map/ppermute | solution.py:341
  975.9 74.8 %collective-permute-start.58 = (bf16[2048,768]{1,0:T(8,128)(2,1)}, bf16[2048,768]{1,0:T(8,128)(2,1)}, u32[]{:S(2)}, u32[]{:S(2)}) collective-permute-start(bf16[2048,768]{1,0:T(8,128)(2,1)} %get-tuple-element.428.refs_10_.refs_11_), channel_id=1, source_target_pairs={{0,1},{1,0},{2,3},{3,2},{4,5},{5,4},{6,7},{7,6}} | collective-permute-start | bytes 9437192 | tf_op jit(solution)/shard_map/ppermute | solution.py:341
  1096.1 99.1 %collective-permute-start.50 = (f32[256,1024]{1,0:T(8,128)S(1)}, f32[256,1024]{1,0:T(8,128)}, u32[]{:S(2)}, u32[]{:S(2)}) collective-permute-start(f32[256,1024]{1,0:T(8,128)S(1)} %copy-done.21), channel_id=1, source_target_pairs={{0,2},{1,3},{2,0},{3,1},{4,6},{5,7},{6,4},{7,5}} | collective-permute-start | bytes 3145736 | tf_op jit(solution)/shard_map/ppermute | solution.py:341
  1097.0 98.5 %collective-permute-start.51 = (f32[256,1024]{1,0:T(8,128)}, f32[256,1024]{1,0:T(8,128)}, u32[]{:S(2)}, u32[]{:S(2)}) collective-permute-start(f32[256,1024]{1,0:T(8,128)} %get-tuple-element.534.refs_1_), channel_id=1, source_target_pairs={{0,4},{1,5},{2,6},{3,7},{4,0},{5,1},{6,2},{7,3}} | collective-permute-start | bytes 3145736 | tf_op jit(solution)/shard_map/ppermute | solution.py:341
  1102.8 93.7 %collective-permute-start.52 = (f32[256,1024]{1,0:T(8,128)}, f32[256,1024]{1,0:T(8,128)}, u32[]{:S(2)}, u32[]{:S(2)}) collective-permute-start(f32[256,1024]{1,0:T(8,128)} %collective-permute-done.48.refs_2_), channel_id=1, source_target_pairs={{0,2},{1,3},{2,0},{3,1},{4,6},{5,7},{6,4},{7,5}} | collective-permute-start | bytes 3145736 | tf_op jit(solution)/shard_map/ppermute | solution.py:341
  1103.3 85.1 %collective-permute-start.63 = (f32[256,1024]{1,0:T(8,128)}, f32[256,1024]{1,0:T(8,128)}, u32[]{:S(2)}, u32[]{:S(2)}) collective-permute-start(f32[256,1024]{1,0:T(8,128)} %get-tuple-element.610), channel_id=1, source_target_pairs={{0,2},{1,3},{2,0},{3,1},{4,6},{5,7},{6,4},{7,5}} | collective-permute-start | bytes 3145736 | tf_op jit(solution)/shard_map/ppermute | solution.py:341
  1104.2 85.3 %collective-permute-start.62 = (f32[256,1024]{1,0:T(8,128)}, f32[256,1024]{1,0:T(8,128)}, u32[]{:S(2)}, u32[]{:S(2)}) collective-permute-start(f32[256,1024]{1,0:T(8,128)} %get-tuple-element.611), channel_id=1, source_target_pairs={{0,4},{1,5},{2,6},{3,7},{4,0},{5,1},{6,2},{7,3}} | collective-permute-start | bytes 3145736 | tf_op jit(solution)/shard_map/ppermute | solution.py:341
  1188.4 83.4 %collective-permute-start.53 = (f32[256,1024]{1,0:T(8,128)}, f32[256,1024]{1,0:T(8,128)}, u32[]{:S(2)}, u32[]{:S(2)}) collective-permute-start(f32[256,1024]{1,0:T(8,128)} %collective-permute-done.49.refs_3_), channel_id=1, source_target_pairs={{0,4},{1,5},{2,6},{3,7},{4,0},{5,1},{6,2},{7,3}} | collective-permute-start | bytes 3145736 | tf_op jit(solution)/shard_map/ppermute | solution.py:341
  1189.6 90.9 %collective-permute-start.68 = (f32[256,1024]{1,0:T(8,128)S(1)}, f32[256,1024]{1,0:T(8,128)}, u32[]{:S(2)}, u32[]{:S(2)}) collective-permute-start(f32[256,1024]{1,0:T(8,128)S(1)} %copy-done.22), channel_id=1, source_target_pairs={{0,2},{1,3},{2,0},{3,1},{4,6},{5,7},{6,4},{7,5}} | collective-permute-start | bytes 3145736 | tf_op jit(solution)/shard_map/ppermute | solution.py:341
  1195.2 85.2 %collective-permute-start.69 = (f32[256,1024]{1,0:T(8,128)S(1)}, f32[256,1024]{1,0:T(8,128)S(1)}, u32[]{:S(2)}, u32[]{:S(2)}) collective-permute-start(f32[256,1024]{1,0:T(8,128)S(1)} %copy-done.23), channel_id=1, source_target_pairs={{0,4},{1,5},{2,6},{3,7},{4,0},{5,1},{6,2},{7,3}} | collective-permute-start | bytes 3145736 | tf_op jit(solution)/shard_map/ppermute | solution.py:341
  1195.5 84.9 %collective-permute-start.70 = (f32[256,1024]{1,0:T(8,128)}, f32[256,1024]{1,0:T(8,128)}, u32[]{:S(2)}, u32[]{:S(2)}) collective-permute-start(f32[256,1024]{1,0:T(8,128)} %copy-done.25), channel_id=1, source_target_pairs={{0,2},{1,3},{2,0},{3,1},{4,6},{5,7},{6,4},{7,5}} | collective-permute-start | bytes 3145736 | tf_op jit(solution)/shard_map/ppermute | solution.py:341
  1196.5 84.0 %collective-permute-start.71 = (f32[256,1024]{1,0:T(8,128)}, f32[256,1024]{1,0:T(8,128)}, u32[]{:S(2)}, u32[]{:S(2)}) collective-permute-start(f32[256,1024]{1,0:T(8,128)} %copy-done.26), channel_id=1, source_target_pairs={{0,4},{1,5},{2,6},{3,7},{4,0},{5,1},{6,2},{7,3}} | collective-permute-start | bytes 3145736 | tf_op jit(solution)/shard_map/ppermute | solution.py:341
  1290.1 201.6 %collective-permute-start.73 = (f32[2048,1024]{1,0:T(8,128)}, f32[2048,1024]{1,0:T(8,128)}, u32[]{:S(2)}, u32[]{:S(2)}) collective-permute-start(f32[2048,1024]{1,0:T(8,128)} %assemble.9.refs_2_), channel_id=1, source_target_pairs={{0,1},{1,0},{2,3},{3,2},{4,5},{5,4},{6,7},{7,6}} | collective-permute-start | bytes 25165832 | tf_op jit(solution)/shard_map/ppermute | solution.py:341
  1293.9 198.5 %collective-permute-start.72 = (f32[2048,1024]{1,0:T(8,128)}, f32[2048,1024]{1,0:T(8,128)}, u32[]{:S(2)}, u32[]{:S(2)}) collective-permute-start(f32[2048,1024]{1,0:T(8,128)} %assemble.8.refs_0_), channel_id=1, source_target_pairs={{0,1},{1,0},{2,3},{3,2},{4,5},{5,4},{6,7},{7,6}} | collective-permute-start | bytes 25165832 | tf_op jit(solution)/shard_map/ppermute | solution.py:341
  1297.8 81.0 %collective-permute-start.30 = (f32[256,1024]{1,0:T(8,128)S(1)}, f32[256,1024]{1,0:T(8,128)}, u32[]{:S(2)}, u32[]{:S(2)}) collective-permute-start(f32[256,1024]{1,0:T(8,128)S(1)} %copy-done.19), channel_id=1, source_target_pairs={{0,4},{1,5},{2,6},{3,7},{4,0},{5,1},{6,2},{7,3}} | collective-permute-start | bytes 3145736 | tf_op jit(solution)/shard_map/ppermute | solution.py:341
  1343.6 193.4 %all-to-all-start.3 = ((bf16[8,128,2048]{2,1,0:T(8,128)(2,1)}), bf16[8,128,2048]{2,1,0:T(8,128)(2,1)}, u32[]{:S(2)}, u32[]{:S(2)}) async-start(bf16[8,128,2048]{2,1,0:T(8,128)(2,1)} %bitcast.125), calls=%async_computation.3 | async-start | bytes 8388608 | tf_op jit(solution)/shard_map/all_to_all | solution.py:355
  1352.0 90.9 %collective-permute-start.44 = (f32[256,1024]{1,0:T(8,128)S(1)}, f32[256,1024]{1,0:T(8,128)}, u32[]{:S(2)}, u32[]{:S(2)}) collective-permute-start(f32[256,1024]{1,0:T(8,128)S(1)} %copy-done.19), channel_id=1, source_target_pairs={{0,2},{1,3},{2,0},{3,1},{4,6},{5,7},{6,4},{7,5}} | collective-permute-start | bytes 3145736 | tf_op jit(solution)/shard_map/ppermute | solution.py:341
  1566.3 109.8 %collective-permute-start.82 = (f32[2048,1024]{1,0:T(8,128)}, f32[2048,1024]{1,0:T(8,128)}, u32[]{:S(2)}, u32[]{:S(2)}) collective-permute-start(f32[2048,1024]{1,0:T(8,128)} %assemble.11.refs_2_), channel_id=1, source_target_pairs={{0,1},{1,0},{2,3},{3,2},{4,5},{5,4},{6,7},{7,6}} | collective-permute-start | bytes 25165832 | tf_op jit(solution)/shard_map/ppermute | solution.py:341
  1569.0 107.1 %collective-permute-start.81 = (f32[2048,1024]{1,0:T(8,128)}, f32[2048,1024]{1,0:T(8,128)}, u32[]{:S(2)}, u32[]{:S(2)}) collective-permute-start(f32[2048,1024]{1,0:T(8,128)} %assemble.10.refs_0_), channel_id=1, source_target_pairs={{0,1},{1,0},{2,3},{3,2},{4,5},{5,4},{6,7},{7,6}} | collective-permute-start | bytes 25165832 | tf_op jit(solution)/shard_map/ppermute | solution.py:341
  1620.6 90.2 %all-to-all-start.5 = ((bf16[8,128,2048]{2,1,0:T(8,128)(2,1)}), bf16[8,128,2048]{2,1,0:T(8,128)(2,1)}, u32[]{:S(2)}, u32[]{:S(2)}) async-start(bf16[8,128,2048]{2,1,0:T(8,128)(2,1)} %bitcast.127), calls=%async_computation.5 | async-start | bytes 8388608 | tf_op jit(solution)/shard_map/all_to_all | solution.py:355
  (129 other events, 4689.9 us)

commit v3 on v2

--- a/solution.py
+++ b/solution.py
@@ -524,7 +524,6 @@
         g_theirs, = after_chain([jnp.concatenate(g_got, axis=1)])
         grad_u = dot(g_theirs, w_par, 1, 1) + grad_u
         chain = (grad_u,)
-        forward(steps - 1)
         grad_u, = after_chain([grad_u.astype(BF16)])
         gx_parts, norm_sums = [], []
         for s in range(2):
@@ -542,20 +541,21 @@
         others = [hop(small, bit) for bit in (2, 4, 6)]
 
         chain = (gx,)
-        for k in range(2, 4):
+        forward(steps - 1)
+        for k in range(2, 5):
             chain = take(k)
+        y_out = interleaved(interleaved(None, after_chain([y_moved[0]])[0], 0), y_moved[1], 1)
+        chain = (y_out,)
+        chain = take(5)
         whole = place_sums(1)
         chain = tuple(whole)
-        chain = take(4)
-        y_out = interleaved(interleaved(None, after_chain([y_moved[0]])[0], 0), y_moved[1], 1)
-        chain = (y_out, small)
         others = after_chain(others)
         small = (small + others[0]) + (others[1] + others[2])
-        chain = take(5)
+        chain = (small,)
         whole = place_sums(2)
         chain = tuple(whole)
         grad_x = interleaved(None, after_chain([gx_parts[0]])[0], 0)
-        chain = (grad_x, small)
+        chain = (grad_x,)
         grad_x = interleaved(grad_x, after_chain([gx_parts[1]])[0], 1)
         grad_w_qkv, grad_w_out = whole
         small = small.reshape(-1)

time: 1720 us -> 1620 us (0.942)
  waiting for transfers between devices: 353 us -> 240 us
    ppermute x86, waiting for transfers between devices: 308 us -> 240 us  [solution(): lax.ppermute(a, 'sp', [(d, d ^ bit) for d in range(n_dev)])]
    all_to_all x5, waiting for transfers between devices: 44.2 us -> 0.01 us  [exchange(): return lax.all_to_all(a, 'sp', 0, 0, tiled=True)]
  transfers between devices with their start and end apart: 91 -> 91, of which waited for: 20 -> 22; matrix products, arithmetic and copies ran while one was open for 13% -> 14% of each run, Pallas kernels for 47% -> 52%
where the time goes in v3:
time: 1620 us; the launch traced here: 1610 us
  Pallas kernels  861 us (53%)
  waiting for transfers between devices  240 us (15%)
  blocking collectives  148 us (9%)
  matrix products  143 us (9%)
  starting transfers between devices  115 us (7%)
  local copies, waits for them, and re-layouts  62.6 us (4%)
  other arithmetic  41.7 us (3%)
    ppermute x86, waiting for transfers between devices, solution(): lax.ppermute(a, 'sp', [(d, d ^ bit) for d in range(n_dev)])  240 us
    pallas_call x18, Pallas kernels, project(): pl.pallas_call(functools.partial(project_kernel, len(units), steps, trans...  210 us
    pallas_call x8, Pallas kernels, weight_grads(): pl.pallas_call(kernel, grid_spec=pltpu.PrefetchScalarGridSpec(num_scalar_...  188 us
    pallas_call x14, Pallas kernels, attention(): pl.pallas_call(kernel, grid=(n_seq, n_heads), in_specs=in_specs, out_spec...  181 us
    all_to_all x2, blocking collectives, exchange(): return lax.all_to_all(a, 'sp', 0, 0, tiled=True)  148 us
    dot_general x6, matrix products, dot(): lax.dot_general(a, b, (((ca,), (cb,)), ((), ())), preferred_element_type=...  143 us
    ppermute x86, starting transfers between devices, solution(): lax.ppermute(a, 'sp', [(d, d ^ bit) for d in range(n_dev)])  90.4 us
    pallas_call x3, Pallas kernels, place(): pl.pallas_call(functools.partial(place_kernel, counts, dh), grid_spec=plt...  89.8 us
  transfers between devices with their start and end apart: 91, of which 22 were waited for; matrix products, arithmetic and copies ran while one was open for 14% of the time, Pallas kernels for 52%

profile of v3, /device:TPU:1, one launch (start us, length us, event | category | flops | bytes accessed | tf_op | source)
XLA Modules:
  0.0 1613.4 jit_solution(14053273324657422396)
XLA Ops:
  0.6 96.7 %all_to_all.35.x_ref = bf16[8,2,128,2048]{3,2,1,0:T(8,128)(2,1)S(1)} all-to-all(bf16[8,2,128,2048]{3,2,1,0:T(8,128)(2,1)} %bitcast.117), channel_id=1, replica_groups=mesh['sp'=8] {'sp'}, dimensions={0} | all-to-all | bytes 16777216 | tf_op jit(solution)/shard_map/all_to_all | solution.py:355
  116.2 33.6 %lay_out_weights.2.refs_1_.refs_4_ = bf16[2048,4608]{1,0:T(8,128)(2,1)} custom-call(s32[1]{0:T(128)} %bitcast.10.core_ref, bf16[2048,3,24,128]{3,2,1,0:T(8,128)(2,1)} %w_ref.1), custom_call_target="tpu_custom_call" | custom-call | flops 3774873600 | bytes 56623104 | tf_op jit(solution)/shard_map/lay_out_weights/pallas_call | solution.py:226
  305.2 20.3 %project.26.qkv_ref = bf16[4096,768]{1,0:T(8,128)(2,1)} custom-call(bf16[1024,2048]{1,0:T(8,128)(2,1)} %get-tuple-element.438.refs_0_, bf16[1024,2048]{1,0:T(8,128)(2,1)} %get-tuple-element.439.refs_0_.refs_1_, bf16[1024,2048]{1,0:T(8,128)(2,1)} %collective-permute-done.refs_0_.refs_1_.refs_2_, ...), custom_call_target="tpu_custom_call" | custom-call | flops 12884901888 | bytes 23068672 | tf_op jit(solution)/shard_map/project/pallas_call | solution.py:115
  375.9 29.0 %weight_grads.11 = (f32[512,1024]{1,0:T(8,128)}, f32[512,1024]{1,0:T(8,128)}, f32[512,1024]{1,0:T(8,128)}, f32[512,1024]{1,0:T(8,128)}) custom-call(s32[8]{0:T(128)} %stack.50.order_ref, bf16[1024,2048]{1,0:T(8,128)(2,1)} %get-tuple-element.438.refs_0_, bf16[1024,2048]{1,0:T(8,128)(2,1)} %get-tuple-element.439.refs_0_.refs_1_, ...), custom_call_target="tpu_custom_call" | custom-call | flops 17179869184 | bytes 41943040 | tf_op jit(solution)/shard_map/weight_grads/pallas_call | solution.py:153
  418.5 20.5 %project.28.qkv_ref = bf16[4096,768]{1,0:T(8,128)(2,1)} custom-call(bf16[1024,2048]{1,0:T(8,128)(2,1)} %get-tuple-element.438.refs_0_, bf16[1024,2048]{1,0:T(8,128)(2,1)} %get-tuple-element.439.refs_0_.refs_1_, bf16[1024,2048]{1,0:T(8,128)(2,1)} %collective-permute-done.refs_0_.refs_1_.refs_2_, ...), custom_call_target="tpu_custom_call" | custom-call | flops 12884901888 | bytes 23068672 | tf_op jit(solution)/shard_map/project/pallas_call | solution.py:115
  475.2 29.4 %weight_grads.12 = (f32[512,1024]{1,0:T(8,128)}, f32[512,1024]{1,0:T(8,128)}, f32[512,1024]{1,0:T(8,128)}, f32[512,1024]{1,0:T(8,128)}) custom-call(s32[8]{0:T(128)} %stack.50.order_ref, bf16[1024,2048]{1,0:T(8,128)(2,1)} %get-tuple-element.438.refs_0_, bf16[1024,2048]{1,0:T(8,128)(2,1)} %get-tuple-element.439.refs_0_.refs_1_, ...), custom_call_target="tpu_custom_call" | custom-call | flops 17179869184 | bytes 41943040 | tf_op jit(solution)/shard_map/weight_grads/pallas_call | solution.py:153
  523.3 20.3 %project.30.qkv_ref = bf16[4096,768]{1,0:T(8,128)(2,1)} custom-call(bf16[1024,2048]{1,0:T(8,128)(2,1)} %get-tuple-element.438.refs_0_, bf16[1024,2048]{1,0:T(8,128)(2,1)} %get-tuple-element.439.refs_0_.refs_1_, bf16[1024,2048]{1,0:T(8,128)(2,1)} %collective-permute-done.refs_0_.refs_1_.refs_2_, ...), custom_call_target="tpu_custom_call" | custom-call | flops 12884901888 | bytes 23068672 | tf_op jit(solution)/shard_map/project/pallas_call | solution.py:115
  579.9 29.0 %weight_grads.13 = (f32[512,1024]{1,0:T(8,128)}, f32[512,1024]{1,0:T(8,128)}, f32[512,1024]{1,0:T(8,128)}, f32[512,1024]{1,0:T(8,128)}) custom-call(s32[8]{0:T(128)} %stack.50.order_ref, bf16[1024,2048]{1,0:T(8,128)(2,1)} %get-tuple-element.438.refs_0_, bf16[1024,2048]{1,0:T(8,128)(2,1)} %get-tuple-element.439.refs_0_.refs_1_, ...), custom_call_target="tpu_custom_call" | custom-call | flops 17179869184 | bytes 41943040 | tf_op jit(solution)/shard_map/weight_grads/pallas_call | solution.py:153
  627.9 20.3 %project.32.qkv_ref = bf16[4096,768]{1,0:T(8,128)(2,1)} custom-call(bf16[1024,2048]{1,0:T(8,128)(2,1)} %get-tuple-element.438.refs_0_, bf16[1024,2048]{1,0:T(8,128)(2,1)} %get-tuple-element.439.refs_0_.refs_1_, bf16[1024,2048]{1,0:T(8,128)(2,1)} %collective-permute-done.refs_0_.refs_1_.refs_2_, ...), custom_call_target="tpu_custom_call" | custom-call | flops 12884901888 | bytes 23068672 | tf_op jit(solution)/shard_map/project/pallas_call | solution.py:115
  684.7 29.1 %weight_grads.14 = (f32[512,1024]{1,0:T(8,128)}, f32[512,1024]{1,0:T(8,128)}, f32[512,1024]{1,0:T(8,128)}, f32[512,1024]{1,0:T(8,128)}) custom-call(s32[8]{0:T(128)} %stack.50.order_ref, bf16[1024,2048]{1,0:T(8,128)(2,1)} %get-tuple-element.438.refs_0_, bf16[1024,2048]{1,0:T(8,128)(2,1)} %get-tuple-element.439.refs_0_.refs_1_, ...), custom_call_target="tpu_custom_call" | custom-call | flops 17179869184 | bytes 41943040 | tf_op jit(solution)/shard_map/weight_grads/pallas_call | solution.py:153
  732.5 20.5 %project.34.qkv_ref = bf16[4096,768]{1,0:T(8,128)(2,1)} custom-call(bf16[1024,2048]{1,0:T(8,128)(2,1)} %get-tuple-element.438.refs_0_, bf16[1024,2048]{1,0:T(8,128)(2,1)} %get-tuple-element.439.refs_0_.refs_1_, bf16[1024,2048]{1,0:T(8,128)(2,1)} %collective-permute-done.refs_0_.refs_1_.refs_2_, ...), custom_call_target="tpu_custom_call" | custom-call | flops 12884901888 | bytes 23068672 | tf_op jit(solution)/shard_map/project/pallas_call | solution.py:115
  834.0 29.0 %weight_grads.15 = (f32[512,1024]{1,0:T(8,128)}, f32[512,1024]{1,0:T(8,128)}, f32[512,1024]{1,0:T(8,128)}, f32[512,1024]{1,0:T(8,128)}) custom-call(s32[8]{0:T(128)} %stack.50.order_ref, bf16[1024,2048]{1,0:T(8,128)(2,1)} %get-tuple-element.438.refs_0_, bf16[1024,2048]{1,0:T(8,128)(2,1)} %get-tuple-element.439.refs_0_.refs_1_, ...), custom_call_target="tpu_custom_call" | custom-call | flops 17179869184 | bytes 41943040 | tf_op jit(solution)/shard_map/weight_grads/pallas_call | solution.py:153
  917.2 21.0 %collective-permute-done.34.refs_4_ = f32[256,1024]{1,0:T(8,128)} collective-permute-done((f32[256,1024]{1,0:T(8,128)}, f32[256,1024]{1,0:T(8,128)}, u32[]{:S(2)}, u32[]{:S(2)}) %collective-permute-start.34) | collective-permute-done | bytes 1048608 | tf_op jit(solution)/shard_map/ppermute | solution.py:341
  975.4 21.9 %collective-permute-done.56.refs_4_ = f32[256,1024]{1,0:T(8,128)S(1)} collective-permute-done((f32[256,1024]{1,0:T(8,128)}, f32[256,1024]{1,0:T(8,128)S(1)}, u32[]{:S(2)}, u32[]{:S(2)}) %collective-permute-start.56) | collective-permute-done | bytes 1048608 | tf_op jit(solution)/shard_map/ppermute | solution.py:341
  998.7 22.2 %collective-permute-done.54.refs_2_ = f32[256,1024]{1,0:T(8,128)S(1)} collective-permute-done((f32[256,1024]{1,0:T(8,128)}, f32[256,1024]{1,0:T(8,128)S(1)}, u32[]{:S(2)}, u32[]{:S(2)}) %collective-permute-start.54) | collective-permute-done | bytes 1048608 | tf_op jit(solution)/shard_map/ppermute | solution.py:341
  1023.4 42.8 %collective-permute-done.66.a1 = f32[512,1024]{1,0:T(8,128)S(1)} collective-permute-done((f32[512,1024]{1,0:T(8,128)}, f32[512,1024]{1,0:T(8,128)S(1)}, u32[]{:S(2)}, u32[]{:S(2)}) %collective-permute-start.66) | collective-permute-done | bytes 2097184 | tf_op jit(solution)/shard_map/ppermute | solution.py:341
  1111.7 33.6 %lay_out_weights.3 = bf16[2048,4608]{1,0:T(8,128)(2,1)} custom-call(s32[1]{0:T(128)S(6)} %sub.63.core_ref, bf16[2048,3,24,128]{3,2,1,0:T(8,128)(2,1)} %w_ref.1), custom_call_target="tpu_custom_call" | custom-call | flops 3774873600 | bytes 56623104 | tf_op jit(solution)/shard_map/lay_out_weights/pallas_call | solution.py:226
  1166.6 49.9 %fusion.22 = f32[2048,2048]{1,0:T(8,128)} fusion(bf16[2048,4608]{1,0:T(8,128)(2,1)} %get-tuple-element.521.refs_8_.refs_9_, bf16[2048,4608]{1,0:T(8,128)(2,1)} %lay_out_weights.2.refs_1_.refs_4_), kind=kOutput, calls=%fused_computation.90 | convolution fusion | flops 38654705664 | bytes 54525952 | tf_op jit(solution)/shard_map/dot_general | solution.py:20
  1216.5 29.9 %place.3 = (f32[2048,3,24,128]{3,2,1,0:T(8,128)}, f32[24,128,2048]{2,1,0:T(8,128)}) custom-call(s32[1]{0:T(128)} %bitcast.10.core_ref, f32[2048,1024]{1,0:T(8,128)} %assemble.6.refs_0_, f32[2048,1024]{1,0:T(8,128)} %collective-permute-done.70.refs_1_, f32[2048,1024]{1,0:T(8,128)} %assemble.7.refs_2_, f32[2048,1024]{1,0:T(8,128)} %collective-permute-done.71.refs_3_), custom_call_target="tpu_custom_call" | custom-call | flops 67108864 | bytes 67108864 | tf_op jit(solution)/shard_map/place/pallas_call | solution.py:270
  1299.6 21.3 %collective-permute-done.72.refs_2_ = f32[256,1024]{1,0:T(8,128)} collective-permute-done((f32[256,1024]{1,0:T(8,128)}, f32[256,1024]{1,0:T(8,128)}, u32[]{:S(2)}, u32[]{:S(2)}) %collective-permute-start.72) | collective-permute-done | bytes 1048608 | tf_op jit(solution)/shard_map/ppermute | solution.py:341
  1322.3 50.4 %convolution_add_fusion.grad_ref = bf16[2048,2048]{1,0:T(8,128)(2,1)} fusion(f32[2048,2048]{1,0:T(8,128)} %fusion.22, bf16[2048,4608]{1,0:T(8,128)(2,1)} %constant_dynamic-update-slice_fusion, bf16[2048,4608]{1,0:T(8,128)(2,1)} %lay_out_weights.3), kind=kOutput, calls=%fused_computation | convolution fusion | flops 38663094272 | bytes 62914560 | tf_op jit(solution)/shard_map/dot_general | solution.py:20
  1466.0 51.0 %all_to_all.36.in_ref = bf16[8,128,2048]{2,1,0:T(8,128)(2,1)} all-to-all(bf16[8,128,2048]{2,1,0:T(8,128)(2,1)} %bitcast.128), channel_id=1, replica_groups=mesh['sp'=8] {'sp'}, dimensions={0} | all-to-all | bytes 8388608 | tf_op jit(solution)/shard_map/all_to_all | solution.py:355
  1526.5 29.9 %place.4 = (f32[2048,3,24,128]{3,2,1,0:T(8,128)}, f32[24,128,2048]{2,1,0:T(8,128)}) custom-call(s32[1]{0:T(128)} %bitcast.10.core_ref, f32[2048,1024]{1,0:T(8,128)} %assemble.8.refs_0_, f32[2048,1024]{1,0:T(8,128)} %collective-permute-done.82.refs_1_, f32[2048,1024]{1,0:T(8,128)} %assemble.9.refs_2_, ...), custom_call_target="tpu_custom_call", output_to_operand_aliasing={{0}: (5, {}), {1}: (6, {})} | custom-call | flops 67108864 | bytes 67108864 | tf_op jit(solution)/shard_map/place/pallas_call | solution.py:270
  1573.8 29.9 %place.5 = (f32[2048,3,24,128]{3,2,1,0:T(8,128)}, f32[24,128,2048]{2,1,0:T(8,128)}) custom-call(s32[1]{0:T(128)} %bitcast.10.core_ref, f32[2048,1024]{1,0:T(8,128)} %assemble.10.refs_0_, f32[2048,1024]{1,0:T(8,128)} %collective-permute-done.84.refs_1_, f32[2048,1024]{1,0:T(8,128)} %assemble.11.refs_2_, ...), custom_call_target="tpu_custom_call", output_to_operand_aliasing={{0}: (5, {}), {1}: (6, {})} | custom-call | flops 67108864 | bytes 67108864 | tf_op jit(solution)/shard_map/place/pallas_call | solution.py:270
  (423 shorter events, 829.7 us)
Async XLA Ops:
  347.0 470.7 %collective-permute-start.20 = (bf16[2048,256]{1,0:T(8,128)(2,1)}, bf16[2048,256]{1,0:T(8,128)(2,1)}, u32[]{:S(2)}, u32[]{:S(2)}) collective-permute-start(bf16[2048,256]{1,0:T(8,128)(2,1)} %pad_maximum_fusion.1), channel_id=1, source_target_pairs={{0,1},{1,0},{2,3},{3,2},{4,5},{5,4},{6,7},{7,6}} | collective-permute-start | bytes 3145736 | tf_op jit(solution)/shard_map/ppermute | solution.py:341
  374.4 413.0 %collective-permute-start.38 = (f32[256,1024]{1,0:T(8,128)}, f32[256,1024]{1,0:T(8,128)}, u32[]{:S(2)}, u32[]{:S(2)}) collective-permute-start(f32[256,1024]{1,0:T(8,128)} %get-tuple-element.485.refs_0_), channel_id=1, source_target_pairs={{0,4},{1,5},{2,6},{3,7},{4,0},{5,1},{6,2},{7,3}} | collective-permute-start | bytes 3145736 | tf_op jit(solution)/shard_map/ppermute | solution.py:341
  375.5 412.2 %collective-permute-start.39 = (f32[256,1024]{1,0:T(8,128)}, f32[256,1024]{1,0:T(8,128)}, u32[]{:S(2)}, u32[]{:S(2)}) collective-permute-start(f32[256,1024]{1,0:T(8,128)} %get-tuple-element.486.refs_1_), channel_id=1, source_target_pairs={{0,2},{1,3},{2,0},{3,1},{4,6},{5,7},{6,4},{7,5}} | collective-permute-start | bytes 3145736 | tf_op jit(solution)/shard_map/ppermute | solution.py:341
  970.7 194.4 %collective-permute-start.71 = (f32[2048,1024]{1,0:T(8,128)}, f32[2048,1024]{1,0:T(8,128)}, u32[]{:S(2)}, u32[]{:S(2)}) collective-permute-start(f32[2048,1024]{1,0:T(8,128)} %assemble.7.refs_2_), channel_id=1, source_target_pairs={{0,1},{1,0},{2,3},{3,2},{4,5},{5,4},{6,7},{7,6}} | collective-permute-start | bytes 25165832 | tf_op jit(solution)/shard_map/ppermute | solution.py:341
  972.8 193.5 %collective-permute-start.70 = (f32[2048,1024]{1,0:T(8,128)}, f32[2048,1024]{1,0:T(8,128)}, u32[]{:S(2)}, u32[]{:S(2)}) collective-permute-start(f32[2048,1024]{1,0:T(8,128)} %assemble.6.refs_0_), channel_id=1, source_target_pairs={{0,1},{1,0},{2,3},{3,2},{4,5},{5,4},{6,7},{7,6}} | collective-permute-start | bytes 25165832 | tf_op jit(solution)/shard_map/ppermute | solution.py:341
  1088.7 74.2 %collective-permute-start.59 = (f32[256,1024]{1,0:T(8,128)}, f32[256,1024]{1,0:T(8,128)}, u32[]{:S(2)}, u32[]{:S(2)}) collective-permute-start(f32[256,1024]{1,0:T(8,128)} %collective-permute-done.55.refs_3_), channel_id=1, source_target_pairs={{0,4},{1,5},{2,6},{3,7},{4,0},{5,1},{6,2},{7,3}} | collective-permute-start | bytes 3145736 | tf_op jit(solution)/shard_map/ppermute | solution.py:341
  1090.6 72.4 %collective-permute-start.68 = (f32[256,1024]{1,0:T(8,128)}, f32[256,1024]{1,0:T(8,128)}, u32[]{:S(2)}, u32[]{:S(2)}) collective-permute-start(f32[256,1024]{1,0:T(8,128)} %get-tuple-element.611), channel_id=1, source_target_pairs={{0,4},{1,5},{2,6},{3,7},{4,0},{5,1},{6,2},{7,3}} | collective-permute-start | bytes 3145736 | tf_op jit(solution)/shard_map/ppermute | solution.py:341
  1156.0 123.9 %all-to-all-start.4 = ((bf16[8,128,2048]{2,1,0:T(8,128)(2,1)}), bf16[8,128,2048]{2,1,0:T(8,128)(2,1)}, u32[]{:S(2)}, u32[]{:S(2)}) async-start(bf16[8,128,2048]{2,1,0:T(8,128)(2,1)} %bitcast.126), calls=%async_computation.4 | async-start | bytes 8388608 | tf_op jit(solution)/shard_map/all_to_all | solution.py:355
  1162.9 88.7 %collective-permute-start.64 = (bf16[2048,768]{1,0:T(8,128)(2,1)S(1)}, bf16[2048,768]{1,0:T(8,128)(2,1)}, u32[]{:S(2)}, u32[]{:S(2)}) collective-permute-start(bf16[2048,768]{1,0:T(8,128)(2,1)S(1)} %copy-done.5), channel_id=1, source_target_pairs={{0,1},{1,0},{2,3},{3,2},{4,5},{5,4},{6,7},{7,6}} | collective-permute-start | bytes 9437192 | tf_op jit(solution)/shard_map/ppermute | solution.py:341
  1163.0 88.5 %collective-permute-start.50 = (f32[256,1024]{1,0:T(8,128)}, f32[256,1024]{1,0:T(8,128)}, u32[]{:S(2)}, u32[]{:S(2)}) collective-permute-start(f32[256,1024]{1,0:T(8,128)} %get-tuple-element.545.refs_0_), channel_id=1, source_target_pairs={{0,2},{1,3},{2,0},{3,1},{4,6},{5,7},{6,4},{7,5}} | collective-permute-start | bytes 3145736 | tf_op jit(solution)/shard_map/ppermute | solution.py:341
  1164.7 91.7 %collective-permute-start.65 = (bf16[2048,768]{1,0:T(8,128)(2,1)}, bf16[2048,768]{1,0:T(8,128)(2,1)}, u32[]{:S(2)}, u32[]{:S(2)}) collective-permute-start(bf16[2048,768]{1,0:T(8,128)(2,1)} %get-tuple-element.462.refs_10_.refs_11_), channel_id=1, source_target_pairs={{0,1},{1,0},{2,3},{3,2},{4,5},{5,4},{6,7},{7,6}} | collective-permute-start | bytes 9437192 | tf_op jit(solution)/shard_map/ppermute | solution.py:341
  1165.1 87.9 %collective-permute-start.30 = (f32[256,1024]{1,0:T(8,128)}, f32[256,1024]{1,0:T(8,128)}, u32[]{:S(2)}, u32[]{:S(2)}) collective-permute-start(f32[256,1024]{1,0:T(8,128)} %get-tuple-element.553.refs_0_), channel_id=1, source_target_pairs={{0,4},{1,5},{2,6},{3,7},{4,0},{5,1},{6,2},{7,3}} | collective-permute-start | bytes 3145736 | tf_op jit(solution)/shard_map/ppermute | solution.py:341
  1166.3 88.9 %collective-permute-start.31 = (f32[256,1024]{1,0:T(8,128)}, f32[256,1024]{1,0:T(8,128)}, u32[]{:S(2)}, u32[]{:S(2)}) collective-permute-start(f32[256,1024]{1,0:T(8,128)} %get-tuple-element.554.refs_1_), channel_id=1, source_target_pairs={{0,2},{1,3},{2,0},{3,1},{4,6},{5,7},{6,4},{7,5}} | collective-permute-start | bytes 3145736 | tf_op jit(solution)/shard_map/ppermute | solution.py:341
  1275.8 120.2 %collective-permute-start.44 = (f32[256,1024]{1,0:T(8,128)S(1)}, f32[256,1024]{1,0:T(8,128)}, u32[]{:S(2)}, u32[]{:S(2)}) collective-permute-start(f32[256,1024]{1,0:T(8,128)S(1)} %copy-done.20), channel_id=1, source_target_pairs={{0,2},{1,3},{2,0},{3,1},{4,6},{5,7},{6,4},{7,5}} | collective-permute-start | bytes 3145736 | tf_op jit(solution)/shard_map/ppermute | solution.py:341
  1278.6 118.7 %collective-permute-start.45 = (f32[256,1024]{1,0:T(8,128)S(1)}, f32[256,1024]{1,0:T(8,128)}, u32[]{:S(2)}, u32[]{:S(2)}) collective-permute-start(f32[256,1024]{1,0:T(8,128)S(1)} %copy-done.21), channel_id=1, source_target_pairs={{0,4},{1,5},{2,6},{3,7},{4,0},{5,1},{6,2},{7,3}} | collective-permute-start | bytes 3145736 | tf_op jit(solution)/shard_map/ppermute | solution.py:341
  1279.9 154.1 %all-to-all-start.3 = ((bf16[8,128,2048]{2,1,0:T(8,128)(2,1)}), bf16[8,128,2048]{2,1,0:T(8,128)(2,1)}, u32[]{:S(2)}, u32[]{:S(2)}) async-start(bf16[8,128,2048]{2,1,0:T(8,128)(2,1)} %bitcast.125), calls=%async_computation.3 | async-start | bytes 8388608 | tf_op jit(solution)/shard_map/all_to_all | solution.py:355
  1298.4 99.2 %collective-permute-start.46 = (f32[256,1024]{1,0:T(8,128)}, f32[256,1024]{1,0:T(8,128)}, u32[]{:S(2)}, u32[]{:S(2)}) collective-permute-start(f32[256,1024]{1,0:T(8,128)} %collective-permute-done.30.refs_2_), channel_id=1, source_target_pairs={{0,2},{1,3},{2,0},{3,1},{4,6},{5,7},{6,4},{7,5}} | collective-permute-start | bytes 3145736 | tf_op jit(solution)/shard_map/ppermute | solution.py:341
  1320.9 94.6 %collective-permute-start.47 = (f32[256,1024]{1,0:T(8,128)}, f32[256,1024]{1,0:T(8,128)}, u32[]{:S(2)}, u32[]{:S(2)}) collective-permute-start(f32[256,1024]{1,0:T(8,128)} %collective-permute-done.31.refs_3_), channel_id=1, source_target_pairs={{0,4},{1,5},{2,6},{3,7},{4,0},{5,1},{6,2},{7,3}} | collective-permute-start | bytes 3145736 | tf_op jit(solution)/shard_map/ppermute | solution.py:341
  1321.0 99.5 %collective-permute-start.74 = (f32[256,1024]{1,0:T(8,128)S(1)}, f32[256,1024]{1,0:T(8,128)}, u32[]{:S(2)}, u32[]{:S(2)}) collective-permute-start(f32[256,1024]{1,0:T(8,128)S(1)} %copy-done.27), channel_id=1, source_target_pairs={{0,2},{1,3},{2,0},{3,1},{4,6},{5,7},{6,4},{7,5}} | collective-permute-start | bytes 3145736 | tf_op jit(solution)/shard_map/ppermute | solution.py:341
  1415.5 109.7 %collective-permute-start.83 = (f32[2048,1024]{1,0:T(8,128)}, f32[2048,1024]{1,0:T(8,128)}, u32[]{:S(2)}, u32[]{:S(2)}) collective-permute-start(f32[2048,1024]{1,0:T(8,128)} %assemble.9.refs_2_), channel_id=1, source_target_pairs={{0,1},{1,0},{2,3},{3,2},{4,5},{5,4},{6,7},{7,6}} | collective-permute-start | bytes 25165832 | tf_op jit(solution)/shard_map/ppermute | solution.py:341
  1420.5 105.9 %collective-permute-start.82 = (f32[2048,1024]{1,0:T(8,128)}, f32[2048,1024]{1,0:T(8,128)}, u32[]{:S(2)}, u32[]{:S(2)}) collective-permute-start(f32[2048,1024]{1,0:T(8,128)} %assemble.8.refs_0_), channel_id=1, source_target_pairs={{0,1},{1,0},{2,3},{3,2},{4,5},{5,4},{6,7},{7,6}} | collective-permute-start | bytes 25165832 | tf_op jit(solution)/shard_map/ppermute | solution.py:341
  1438.7 135.1 %collective-permute-start.84 = (f32[2048,1024]{1,0:T(8,128)}, f32[2048,1024]{1,0:T(8,128)}, u32[]{:S(2)}, u32[]{:S(2)}) collective-permute-start(f32[2048,1024]{1,0:T(8,128)} %assemble.10.refs_0_), channel_id=1, source_target_pairs={{0,1},{1,0},{2,3},{3,2},{4,5},{5,4},{6,7},{7,6}} | collective-permute-start | bytes 25165832 | tf_op jit(solution)/shard_map/ppermute | solution.py:341
  1464.5 109.4 %collective-permute-start.85 = (f32[2048,1024]{1,0:T(8,128)}, f32[2048,1024]{1,0:T(8,128)}, u32[]{:S(2)}, u32[]{:S(2)}) collective-permute-start(f32[2048,1024]{1,0:T(8,128)} %assemble.11.refs_2_), channel_id=1, source_target_pairs={{0,1},{1,0},{2,3},{3,2},{4,5},{5,4},{6,7},{7,6}} | collective-permute-start | bytes 25165832 | tf_op jit(solution)/shard_map/ppermute | solution.py:341
  1517.2 91.3 %all-to-all-start.5 = ((bf16[8,128,2048]{2,1,0:T(8,128)(2,1)}), bf16[8,128,2048]{2,1,0:T(8,128)(2,1)}, u32[]{:S(2)}, u32[]{:S(2)}) async-start(bf16[8,128,2048]{2,1,0:T(8,128)(2,1)} %bitcast.127), calls=%async_computation.5 | async-start | bytes 8388608 | tf_op jit(solution)/shard_map/all_to_all | solution.py:355
  (130 other events, 3888.8 us)

commit v4 on v3

--- a/solution.py
+++ b/solution.py
@@ -24,7 +24,7 @@
     seq, dh = do_ref.shape
     for i in range(seq // blk):
         lo, hi = i * blk, (i + 1) * blk
-        q, k, v = qkv_ref[lo:hi, 0:dh], qkv_ref[0:hi, dh:2 * dh], qkv_ref[0:hi, 2 * dh:3 * dh]
+        q, k, v = qkv_ref[lo:hi, :dh], qkv_ref[:hi, dh:2 * dh], qkv_ref[:hi, 2 * dh:3 * dh]
         do = do_ref[lo:hi, :]
         s = dot(k, q, 1, 1)
         rows = lax.broadcasted_iota(jnp.int32, (blk, blk), 0)
@@ -35,30 +35,30 @@
         e = jnp.exp2((s - m) * (scale * LOG2E))
         p = e * (1.0 / jnp.sum(e, axis=0, keepdims=True))
         pb = p.astype(BF16)
-        p_ref[0:hi, lo:hi] = pb
+        p_ref[:hi, lo:hi] = pb
         o_t = dot(v, pb, 0, 0)
         o_ref[lo:hi, :] = o_t.T.astype(BF16)
         delta = jnp.sum(o_t * do.astype(F32).T, axis=0, keepdims=True)
         dp = dot(v, do, 1, 1).astype(BF16).astype(F32)
         ds = (p * (dp - delta)).astype(BF16)
-        ds_ref[0:hi, lo:hi] = ds
-        g_ref[lo:hi, 0:dh] = (dot(k, ds, 0, 0) * scale).T.astype(BF16)
+        ds_ref[:hi, lo:hi] = ds
+        g_ref[lo:hi, :dh] = (dot(k, ds, 0, 0) * scale).T.astype(BF16)
     for j in range(seq // blk):
         lo, hi = j * blk, (j + 1) * blk
-        dk = dot(ds_ref[lo:hi, lo:], qkv_ref[lo:, 0:dh], 1, 0)
+        dk = dot(ds_ref[lo:hi, lo:], qkv_ref[lo:, :dh], 1, 0)
         dv = dot(p_ref[lo:hi, lo:], do_ref[lo:, :], 1, 0)
         g_ref[lo:hi, dh:2 * dh] = (dk * scale).astype(BF16)
         g_ref[lo:hi, 2 * dh:3 * dh] = dv.astype(BF16)
     gb_ref[:] = jnp.sum(g_ref[:].astype(F32), axis=0, keepdims=True)[None]
 
 
-def attention(qkv, grad_o, seq, dh, seqs, into=None, width=0, at=(0, 0)):
+def attention(qkv, grad_o, seq, dh, seqs, first=0, into=None, width=0, at=(0, 0)):
     s0, n_seq = seqs[0], seqs[1] - seqs[0]
-    n_heads = grad_o.shape[1] // dh
+    n_heads = qkv.shape[1] // (3 * dh)
     width = width or n_heads
     rows = n_seq * seq if into is None and width == n_heads else 2 * seq
     flops = n_seq * n_heads * 6 * seq * seq * dh
-    in_specs = [pl.BlockSpec((seq, 3 * dh), lambda b, h: (b + s0, h)), pl.BlockSpec((seq, dh), lambda b, h: (b + s0, h))]
+    in_specs = [pl.BlockSpec((seq, 3 * dh), lambda b, h: (b + s0, h)), pl.BlockSpec((seq, dh), lambda b, h: (b + s0, h + first))]
     args, alias = [qkv, grad_o], {}
     if into is not None:
         in_specs += [pl.BlockSpec(memory_space=pl.ANY)] * 2
@@ -156,7 +156,7 @@
             num_scalar_prefetch=1, grid=(total,), in_specs=in_specs, out_specs=[piece(n) for n in range(n_out)],
             scratch_shapes=[pltpu.VMEM((bd, cols + cols_o), F32)]),
         out_shape=[jax.ShapeDtypeStruct((per_out * bd, cols + cols_o), F32)] * n_out,
-        cost_estimate=cost(2 * len(units) * rows * total * bd * (cols + cols_o), 40 * 2 ** 20),
+        cost_estimate=cost(2 * len(units) * rows * total * bd * (cols + cols_o), len(units) * rows * dim * 8),
         name="weight_grads",
     )(order, *args)
 
@@ -165,6 +165,7 @@
     rows, cols = last_a.shape
     bm = rows // 2
     spec = lambda base, start: pl.BlockSpec((bm, cols), lambda i: (base + jnp.clip(i - start, 0, 1), 0))
+    own = [spec(0, 0), spec(0, 2)]
 
     def kernel(kept_ref, a1, b1, a2, b2, a_ref, b_ref):
         i = pl.program_id(0)
@@ -177,10 +178,10 @@
 
     return pl.pallas_call(
         kernel, grid=(4,),
-        in_specs=[pl.BlockSpec((bm, cols), lambda i: (i, 0)), spec(2, 0), spec(2, 2), spec(0, 0), spec(0, 2)],
-        out_specs=[spec(0, 0), spec(0, 2)],
+        in_specs=[pl.BlockSpec((bm, cols), lambda i: (i, 0)), spec(2, 0), spec(2, 2), *own],
+        out_specs=own,
         out_shape=[jax.ShapeDtypeStruct(last_a.shape, F32)] * 2,
-        cost_estimate=cost(2 ** 24, kept.size * 16),
+        cost_estimate=cost(kept.size, 16 * kept.size),
         name="add_last",
     )(kept, got_a, got_b, last_a, last_b)
 
@@ -202,7 +203,7 @@
         grid_spec=pltpu.PrefetchScalarGridSpec(num_scalar_prefetch=1, grid=(n,), in_specs=[block] * n,
                                                out_specs=pl.BlockSpec((rows, cols), lambda i, order: (order[i], 0))),
         out_shape=jax.ShapeDtypeStruct((n * rows, cols), F32),
-        cost_estimate=cost(2 ** 24, n * rows * cols * 8),
+        cost_estimate=cost(n * rows * cols, n * rows * cols * 8),
         name="assemble",
     )(order, *pieces)
 
@@ -298,10 +299,12 @@
                           name="interleaved")(*args)
 
 
-def norm_grads(grad_u, x, gy, gain, s):
+def norm_grads(grad_u, x, gy, gain, s, into):
     parts, _, part, dim = x.shape
-
-    def kernel(grad_ref, x_ref, gy_ref, gain_ref, gx_ref, sums_ref):
+    extra = [] if into is None else [into]
+
+    def kernel(grad_ref, x_ref, gy_ref, gain_ref, *refs):
+        gx_ref, sums_ref = refs[-2:]
         xf, grad, gyf = x_ref[0, 0].astype(F32), grad_ref[:].astype(F32), gy_ref[:].astype(F32)
         mean_of = lambda a: jnp.sum(a, axis=1, keepdims=True) * (1.0 / dim)
         centered = xf - mean_of(xf)
@@ -309,7 +312,7 @@
         x_hat = centered * inv_std
         grad_hat = grad * gain_ref[:]
         gx = gyf + inv_std * (grad_hat - mean_of(grad_hat) - x_hat * mean_of(grad_hat * x_hat))
-        gx_ref[:] = gx.astype(BF16)
+        gx_ref[0, 0] = gx.astype(BF16)
 
         @pl.when(pl.program_id(0) == 0)
         def _():
@@ -318,16 +321,26 @@
         for n, a in enumerate((grad * x_hat, grad, gyf)):
             sums_ref[n:n + 1, :] += jnp.sum(a, axis=0, keepdims=True)
 
-    row = pl.BlockSpec((part, dim), lambda i: (i, 0))
+    piece = pl.BlockSpec((1, 1, part, dim), lambda i: (i, s, 0, 0))
     return pl.pallas_call(
         kernel, grid=(parts,),
-        in_specs=[pl.BlockSpec((part, dim), lambda i: (i + parts * s, 0)), pl.BlockSpec((1, 1, part, dim), lambda i: (i, s, 0, 0)),
-                  row, pl.BlockSpec((1, dim), lambda i: (0, 0))],
-        out_specs=[row, pl.BlockSpec((8, dim), lambda i: (0, 0))],
-        out_shape=[jax.ShapeDtypeStruct((parts * part, dim), BF16), jax.ShapeDtypeStruct((8, dim), F32)],
+        in_specs=[pl.BlockSpec((part, dim), lambda i: (i + parts * s, 0)), piece, pl.BlockSpec((part, dim), lambda i: (i, 0)),
+                  pl.BlockSpec((1, dim), lambda i: (0, 0))] + [pl.BlockSpec(memory_space=pl.ANY)] * len(extra),
+        out_specs=[piece, pl.BlockSpec((8, dim), lambda i: (0, 0))],
+        out_shape=[jax.ShapeDtypeStruct(x.shape, BF16), jax.ShapeDtypeStruct((8, dim), F32)],
+        input_output_aliases={4: 0} if extra else {},
         cost_estimate=cost(parts * part * dim * 400, parts * part * dim * 8),
         name="norm_grads",
-    )(grad_u, x, gy, gain.reshape(1, dim))
+    )(grad_u, x, gy, gain.reshape(1, dim), *extra)
+
+
+def copied(a):
+    def kernel(in_ref, out_ref):
+        out_ref[:] = in_ref[:]
+
+    block = pl.BlockSpec((2, *a.shape[1:]), lambda i: (i, 0, 0))
+    return pl.pallas_call(kernel, grid=(a.shape[0] // 2,), in_specs=[block], out_specs=block,
+                          out_shape=jax.ShapeDtypeStruct(a.shape, a.dtype), cost_estimate=cost(a.size, 4 * a.size), name="copied")(a)
 
 
 def tie(value, *after):
@@ -441,7 +454,7 @@
                     for side, a in enumerate((gys[s], gy_par[s])):
                         grad_o = project([a], wo_own, k, co, transposed=True)
                         if side == 0:
-                            mine = attention(qkv[s], grad_o, seq, dh, (0, 1), mine, heads_all // 2, (s, 0))
+                            mine = attention(qkv[s], grad_o, seq, dh, (0, 1), 0, mine, heads_all // 2, (s, 0))
                             (o_n, g_n), b_n, at = mine[:2], mine[2], (s, 0)
                             mine = mine[:2]
                         else:
@@ -463,18 +476,21 @@
             else:
                 held = after_chain(u + gy)
                 qkv = project(held[:4], w_own, k, cw, b_own)
-                grad_o = project(held[4:], wo_own, k, co, transposed=True)
-                if k > 1:
-                    chain = (qkv, grad_o)
-                    if k > 2:
-                        spread(k - 2)
-                    qkv, grad_o = after_chain([qkv, grad_o])
-                o_p, g_p, bk = attention(qkv, grad_o, seq, dh, (2, 4))
+                if k == 1:
+                    grad_o = project(held[4:], wo_own, k, co, transposed=True)
+                elif k % 2 == 0:
+                    grad_o = project(held[4:], wo_own, k // 2, 2 * co, transposed=True)
+                first = ch * (k % 2) if k > 1 else 0
+                chain = (qkv, grad_o)
+                if k > 2:
+                    spread(k - 2)
+                elif k == 1:
+                    chain = first_add(0)
+                qkv, grad_o = after_chain([qkv, grad_o])
+                o_p, g_p, bk = attention(qkv, grad_o, seq, dh, (2, 4), first)
                 chain = (g_p,)
-                if k == 1:
-                    chain = first_add(0)
                 qkv, = after_chain([qkv])
-                *mine, b_n = attention(qkv, grad_o, seq, dh, (0, 2), mine, heads_all // 2, (0, k * ch))
+                *mine, b_n = attention(qkv, grad_o, seq, dh, (0, 2), first, mine, heads_all // 2, (0, k * ch))
                 bk = bk + b_n
                 chain = (b_n,)
                 if k == 1:
@@ -501,11 +517,11 @@
 
         rows_of = lambda arrays, s: jnp.concatenate([a[s * seq:(s + 1) * seq] for a in arrays], axis=1)
         y_parts = []
-        held = after_chain(mine[:1] + o_got)
+        held = after_chain(mine[:1] + o_got + [x_all])
         for s in range(2):
             proj = dot(held[0][s * seq:(s + 1) * seq], wo_own, 1, 0) + b_out
-            proj = dot(rows_of(held[1:], s), wo_par, 1, 0) + proj
-            y_parts.append((xs[s].astype(F32) + proj).astype(BF16))
+            proj = dot(rows_of(held[1:-1], s), wo_par, 1, 0) + proj
+            y_parts.append((held[-1][:, s].reshape(seq, dim).astype(F32) + proj).astype(BF16))
         y_moved = [exchange(y.reshape(n_dev, part, dim)) for y in y_parts]
         chain = tuple(y_parts)
         spread(steps - 2)
@@ -525,12 +541,11 @@
         grad_u = dot(g_theirs, w_par, 1, 1) + grad_u
         chain = (grad_u,)
         grad_u, = after_chain([grad_u.astype(BF16)])
-        gx_parts, norm_sums = [], []
+        gx, norm_sums = None, []
         for s in range(2):
-            gx, found = norm_grads(grad_u, x_all, gys[s], ln_gain, s)
-            gx_parts.append(exchange(gx.reshape(n_dev, part, dim)))
+            gx, found = norm_grads(grad_u, x_all, gys[s], ln_gain, s, gx)
             norm_sums.append(found)
-            grad_u, = lax.optimization_barrier((grad_u, gx))[:1]
+        gx_moved = exchange(gx)
 
         gb_mine = jnp.transpose(jnp.concatenate(bias).reshape(groups, gh, 3, dh), (2, 0, 1, 3))[:, :, None]
         is_own = (jnp.arange(2) == core)[None, None, :, None, None]
@@ -549,19 +564,16 @@
         chain = take(5)
         whole = place_sums(1)
         chain = tuple(whole)
-        others = after_chain(others)
-        small = (small + others[0]) + (others[1] + others[2])
-        chain = (small,)
         whole = place_sums(2)
         chain = tuple(whole)
-        grad_x = interleaved(None, after_chain([gx_parts[0]])[0], 0)
-        chain = (grad_x,)
-        grad_x = interleaved(grad_x, after_chain([gx_parts[1]])[0], 1)
+        near, far, across = after_chain(others)
+        small = (small + near) + (far + across)
+        grad_x = copied(after_chain([gx_moved])[0].reshape(batch, part, dim))
         grad_w_qkv, grad_w_out = whole
         small = small.reshape(-1)
         grad_gain, grad_bias, grad_b_out = small[:dim], small[dim:2 * dim], small[2 * dim:3 * dim]
         grad_b_qkv = small[3 * dim:].reshape(3, heads_all, dh)
-        y_out, grad_x = y_out.reshape(batch, part, dim), grad_x.reshape(batch, part, dim)
+        y_out = y_out.reshape(batch, part, dim)
         return (y_out, grad_x, grad_gain, grad_bias, grad_w_qkv, grad_b_qkv, grad_w_out, grad_b_out)
 
     return jax.shard_map(block, mesh=mesh, in_specs=(seq_spec, seq_spec) + (replicated,) * 6,

time: 1620 us -> 1590 us (0.981)
  blocking collectives: 148 us -> 96.7 us
  other arithmetic: 41.7 us -> 59.8 us
  starting transfers between devices: 115 us -> 133 us
    all_to_all x2 -> x1, blocking collectives: 148 us -> 96.7 us  [exchange(): return lax.all_to_all(a, 'sp', 0, 0, tiled=True)]
    pallas_call x18 -> x16, Pallas kernels: 210 us -> 196 us  [project(): pl.pallas_call(functools.partial(project_kernel, len(units), steps, trans...]
  transfers between devices with their start and end apart: 91 -> 91, of which waited for: 22 -> 17; matrix products, arithmetic and copies ran while one was open for 14% -> 15% of each run, Pallas kernels for 52% -> 51%
where the time goes in v4:
time: 1590 us; the launch traced here: 1580 us
  Pallas kernels  847 us (53%)
  waiting for transfers between devices  237 us (15%)
  matrix products  146 us (9%)
  starting transfers between devices  133 us (8%)
  blocking collectives  96.7 us (6%)
  other arithmetic  59.8 us (4%)
  local copies, waits for them, and re-layouts  58.5 us (4%)
    ppermute x86, waiting for transfers between devices, solution(): lax.ppermute(a, 'sp', [(d, d ^ bit) for d in range(n_dev)])  237 us
    pallas_call x16, Pallas kernels, project(): pl.pallas_call(functools.partial(project_kernel, len(units), steps, trans...  196 us
    pallas_call x8, Pallas kernels, weight_grads(): pl.pallas_call(kernel, grid_spec=pltpu.PrefetchScalarGridSpec(num_scalar_...  188 us
    pallas_call x14, Pallas kernels, attention(): pl.pallas_call(kernel, grid=(n_seq, n_heads), in_specs=in_specs, out_spec...  181 us
    dot_general x6, matrix products, dot(): lax.dot_general(a, b, (((ca,), (cb,)), ((), ())), preferred_element_type=...  146 us
    ppermute x86, starting transfers between devices, solution(): lax.ppermute(a, 'sp', [(d, d ^ bit) for d in range(n_dev)])  106 us
    all_to_all x1, blocking collectives, exchange(): return lax.all_to_all(a, 'sp', 0, 0, tiled=True)  96.7 us
    pallas_call x3, Pallas kernels, place(): pl.pallas_call(functools.partial(place_kernel, counts, dh), grid_spec=plt...  90.2 us
  transfers between devices with their start and end apart: 91, of which 17 were waited for; matrix products, arithmetic and copies ran while one was open for 15% of the time, Pallas kernels for 51%

profile of v4, /device:TPU:1, one launch (start us, length us, event | category | flops | bytes accessed | tf_op | source)
XLA Modules:
  0.0 1579.3 jit_solution(2235156786463932760)
XLA Ops:
  0.7 96.7 %all_to_all.30.x_ref = bf16[8,2,128,2048]{3,2,1,0:T(8,128)(2,1)S(1)} all-to-all(bf16[8,2,128,2048]{3,2,1,0:T(8,128)(2,1)} %bitcast.114), channel_id=1, replica_groups=mesh['sp'=8] {'sp'}, dimensions={0} | all-to-all | bytes 16777216 | tf_op jit(solution)/shard_map/all_to_all | solution.py:368
  134.5 33.6 %lay_out_weights.2.refs_1_.refs_4_ = bf16[2048,4608]{1,0:T(8,128)(2,1)} custom-call(s32[1]{0:T(128)} %bitcast.10.core_ref, bf16[2048,3,24,128]{3,2,1,0:T(8,128)(2,1)} %w_ref.1), custom_call_target="tpu_custom_call" | custom-call | flops 3774873600 | bytes 56623104 | tf_op jit(solution)/shard_map/lay_out_weights/pallas_call | solution.py:227
  325.4 20.3 %project.24.qkv_ref = bf16[4096,768]{1,0:T(8,128)(2,1)} custom-call(bf16[1024,2048]{1,0:T(8,128)(2,1)} %get-tuple-element.429.refs_0_, bf16[1024,2048]{1,0:T(8,128)(2,1)} %get-tuple-element.430.refs_0_.refs_1_, bf16[1024,2048]{1,0:T(8,128)(2,1)} %collective-permute-done.refs_0_.refs_1_.refs_2_, ...), custom_call_target="tpu_custom_call" | custom-call | flops 12884901888 | bytes 23068672 | tf_op jit(solution)/shard_map/project/pallas_call | solution.py:115
  388.8 29.0 %weight_grads.11 = (f32[512,1024]{1,0:T(8,128)}, f32[512,1024]{1,0:T(8,128)}, f32[512,1024]{1,0:T(8,128)}, f32[512,1024]{1,0:T(8,128)}) custom-call(s32[8]{0:T(128)} %stack.50.order_ref, bf16[1024,2048]{1,0:T(8,128)(2,1)} %get-tuple-element.429.refs_0_, bf16[1024,2048]{1,0:T(8,128)(2,1)} %get-tuple-element.430.refs_0_.refs_1_, ...), custom_call_target="tpu_custom_call" | custom-call | flops 17179869184 | bytes 67108864 | tf_op jit(solution)/shard_map/weight_grads/pallas_call | solution.py:153
  418.4 20.5 %project.26.qkv_ref = bf16[4096,768]{1,0:T(8,128)(2,1)} custom-call(bf16[1024,2048]{1,0:T(8,128)(2,1)} %get-tuple-element.429.refs_0_, bf16[1024,2048]{1,0:T(8,128)(2,1)} %get-tuple-element.430.refs_0_.refs_1_, bf16[1024,2048]{1,0:T(8,128)(2,1)} %collective-permute-done.refs_0_.refs_1_.refs_2_, ...), custom_call_target="tpu_custom_call" | custom-call | flops 12884901888 | bytes 23068672 | tf_op jit(solution)/shard_map/project/pallas_call | solution.py:115
  493.4 29.0 %weight_grads.12 = (f32[512,1024]{1,0:T(8,128)}, f32[512,1024]{1,0:T(8,128)}, f32[512,1024]{1,0:T(8,128)}, f32[512,1024]{1,0:T(8,128)}) custom-call(s32[8]{0:T(128)} %stack.50.order_ref, bf16[1024,2048]{1,0:T(8,128)(2,1)} %get-tuple-element.429.refs_0_, bf16[1024,2048]{1,0:T(8,128)(2,1)} %get-tuple-element.430.refs_0_.refs_1_, ...), custom_call_target="tpu_custom_call" | custom-call | flops 17179869184 | bytes 67108864 | tf_op jit(solution)/shard_map/weight_grads/pallas_call | solution.py:153
  528.1 20.5 %project.28.qkv_ref = bf16[4096,768]{1,0:T(8,128)(2,1)} custom-call(bf16[1024,2048]{1,0:T(8,128)(2,1)} %get-tuple-element.429.refs_0_, bf16[1024,2048]{1,0:T(8,128)(2,1)} %get-tuple-element.430.refs_0_.refs_1_, bf16[1024,2048]{1,0:T(8,128)(2,1)} %collective-permute-done.refs_0_.refs_1_.refs_2_, ...), custom_call_target="tpu_custom_call" | custom-call | flops 12884901888 | bytes 23068672 | tf_op jit(solution)/shard_map/project/pallas_call | solution.py:115
  585.6 29.2 %weight_grads.13 = (f32[512,1024]{1,0:T(8,128)}, f32[512,1024]{1,0:T(8,128)}, f32[512,1024]{1,0:T(8,128)}, f32[512,1024]{1,0:T(8,128)}) custom-call(s32[8]{0:T(128)} %stack.50.order_ref, bf16[1024,2048]{1,0:T(8,128)(2,1)} %get-tuple-element.429.refs_0_, bf16[1024,2048]{1,0:T(8,128)(2,1)} %get-tuple-element.430.refs_0_.refs_1_, ...), custom_call_target="tpu_custom_call" | custom-call | flops 17179869184 | bytes 67108864 | tf_op jit(solution)/shard_map/weight_grads/pallas_call | solution.py:153
  620.5 20.3 %project.29.qkv_ref = bf16[4096,768]{1,0:T(8,128)(2,1)} custom-call(bf16[1024,2048]{1,0:T(8,128)(2,1)} %get-tuple-element.429.refs_0_, bf16[1024,2048]{1,0:T(8,128)(2,1)} %get-tuple-element.430.refs_0_.refs_1_, bf16[1024,2048]{1,0:T(8,128)(2,1)} %collective-permute-done.refs_0_.refs_1_.refs_2_, ...), custom_call_target="tpu_custom_call" | custom-call | flops 12884901888 | bytes 23068672 | tf_op jit(solution)/shard_map/project/pallas_call | solution.py:115
  695.4 29.0 %weight_grads.14 = (f32[512,1024]{1,0:T(8,128)}, f32[512,1024]{1,0:T(8,128)}, f32[512,1024]{1,0:T(8,128)}, f32[512,1024]{1,0:T(8,128)}) custom-call(s32[8]{0:T(128)} %stack.50.order_ref, bf16[1024,2048]{1,0:T(8,128)(2,1)} %get-tuple-element.429.refs_0_, bf16[1024,2048]{1,0:T(8,128)(2,1)} %get-tuple-element.430.refs_0_.refs_1_, ...), custom_call_target="tpu_custom_call" | custom-call | flops 17179869184 | bytes 67108864 | tf_op jit(solution)/shard_map/weight_grads/pallas_call | solution.py:153
  730.1 20.3 %project.31.qkv_ref = bf16[4096,768]{1,0:T(8,128)(2,1)} custom-call(bf16[1024,2048]{1,0:T(8,128)(2,1)} %get-tuple-element.429.refs_0_, bf16[1024,2048]{1,0:T(8,128)(2,1)} %get-tuple-element.430.refs_0_.refs_1_, bf16[1024,2048]{1,0:T(8,128)(2,1)} %collective-permute-done.refs_0_.refs_1_.refs_2_, ...), custom_call_target="tpu_custom_call" | custom-call | flops 12884901888 | bytes 23068672 | tf_op jit(solution)/shard_map/project/pallas_call | solution.py:115
  831.0 29.0 %weight_grads.15 = (f32[512,1024]{1,0:T(8,128)}, f32[512,1024]{1,0:T(8,128)}, f32[512,1024]{1,0:T(8,128)}, f32[512,1024]{1,0:T(8,128)}) custom-call(s32[8]{0:T(128)} %stack.50.order_ref, bf16[1024,2048]{1,0:T(8,128)(2,1)} %get-tuple-element.429.refs_0_, bf16[1024,2048]{1,0:T(8,128)(2,1)} %get-tuple-element.430.refs_0_.refs_1_, ...), custom_call_target="tpu_custom_call" | custom-call | flops 17179869184 | bytes 67108864 | tf_op jit(solution)/shard_map/weight_grads/pallas_call | solution.py:153
  915.5 19.6 %collective-permute-done.34.refs_4_ = f32[256,1024]{1,0:T(8,128)} collective-permute-done((f32[256,1024]{1,0:T(8,128)}, f32[256,1024]{1,0:T(8,128)}, u32[]{:S(2)}, u32[]{:S(2)}) %collective-permute-start.34) | collective-permute-done | bytes 1048608 | tf_op jit(solution)/shard_map/ppermute | solution.py:354
  1006.0 20.8 %collective-permute-done.56.refs_4_ = f32[256,1024]{1,0:T(8,128)S(1)} collective-permute-done((f32[256,1024]{1,0:T(8,128)}, f32[256,1024]{1,0:T(8,128)S(1)}, u32[]{:S(2)}, u32[]{:S(2)}) %collective-permute-start.56) | collective-permute-done | bytes 1048608 | tf_op jit(solution)/shard_map/ppermute | solution.py:354
  1030.6 20.4 %collective-permute-done.58.refs_6_ = f32[256,1024]{1,0:T(8,128)S(1)} collective-permute-done((f32[256,1024]{1,0:T(8,128)}, f32[256,1024]{1,0:T(8,128)S(1)}, u32[]{:S(2)}, u32[]{:S(2)}) %collective-permute-start.58) | collective-permute-done | bytes 1048608 | tf_op jit(solution)/shard_map/ppermute | solution.py:354
  1053.7 20.0 %collective-permute-done.48.refs_2_ = f32[256,1024]{1,0:T(8,128)} collective-permute-done((f32[256,1024]{1,0:T(8,128)}, f32[256,1024]{1,0:T(8,128)}, u32[]{:S(2)}, u32[]{:S(2)}) %collective-permute-start.48) | collective-permute-done | bytes 1048608 | tf_op jit(solution)/shard_map/ppermute | solution.py:354
  1081.8 38.2 %collective-permute-done.66.a1 = f32[512,1024]{1,0:T(8,128)} collective-permute-done((f32[512,1024]{1,0:T(8,128)}, f32[512,1024]{1,0:T(8,128)}, u32[]{:S(2)}, u32[]{:S(2)}) %collective-permute-start.66) | collective-permute-done | bytes 2097184 | tf_op jit(solution)/shard_map/ppermute | solution.py:354
  1121.2 33.6 %lay_out_weights.3 = bf16[2048,4608]{1,0:T(8,128)(2,1)} custom-call(s32[1]{0:T(128)S(6)} %sub.63.core_ref, bf16[2048,3,24,128]{3,2,1,0:T(8,128)(2,1)} %w_ref.1), custom_call_target="tpu_custom_call" | custom-call | flops 3774873600 | bytes 56623104 | tf_op jit(solution)/shard_map/lay_out_weights/pallas_call | solution.py:227
  1192.2 49.9 %fusion.20 = f32[2048,2048]{1,0:T(8,128)} fusion(bf16[2048,4608]{1,0:T(8,128)(2,1)} %get-tuple-element.509.refs_8_.refs_9_, bf16[2048,4608]{1,0:T(8,128)(2,1)} %lay_out_weights.2.refs_1_.refs_4_), kind=kOutput, calls=%fused_computation.88 | convolution fusion | flops 38654705664 | bytes 54525952 | tf_op jit(solution)/shard_map/dot_general | solution.py:20
  1244.1 30.3 %place.3 = (f32[2048,3,24,128]{3,2,1,0:T(8,128)}, f32[24,128,2048]{2,1,0:T(8,128)}) custom-call(s32[1]{0:T(128)} %bitcast.10.core_ref, f32[2048,1024]{1,0:T(8,128)} %assemble.6.refs_0_, f32[2048,1024]{1,0:T(8,128)} %collective-permute-done.70.refs_1_, f32[2048,1024]{1,0:T(8,128)} %assemble.7.refs_2_, f32[2048,1024]{1,0:T(8,128)} %collective-permute-done.71.refs_3_), custom_call_target="tpu_custom_call" | custom-call | flops 67108864 | bytes 67108864 | tf_op jit(solution)/shard_map/place/pallas_call | solution.py:271
  1311.5 50.4 %convolution_add_fusion.grad_ref = bf16[2048,2048]{1,0:T(8,128)(2,1)} fusion(f32[2048,2048]{1,0:T(8,128)} %fusion.20, bf16[2048,4608]{1,0:T(8,128)(2,1)} %constant_dynamic-update-slice_fusion, bf16[2048,4608]{1,0:T(8,128)(2,1)} %lay_out_weights.3), kind=kOutput, calls=%fused_computation | convolution fusion | flops 38663094272 | bytes 62914560 | tf_op jit(solution)/shard_map/dot_general | solution.py:20
  1487.9 29.9 %place.4 = (f32[2048,3,24,128]{3,2,1,0:T(8,128)}, f32[24,128,2048]{2,1,0:T(8,128)}) custom-call(s32[1]{0:T(128)} %bitcast.10.core_ref, f32[2048,1024]{1,0:T(8,128)} %assemble.8.refs_0_, f32[2048,1024]{1,0:T(8,128)} %collective-permute-done.78.refs_1_, f32[2048,1024]{1,0:T(8,128)} %assemble.9.refs_2_, ...), custom_call_target="tpu_custom_call", output_to_operand_aliasing={{0}: (5, {}), {1}: (6, {})} | custom-call | flops 67108864 | bytes 67108864 | tf_op jit(solution)/shard_map/place/pallas_call | solution.py:271
  1517.8 29.9 %place.5 = (f32[2048,3,24,128]{3,2,1,0:T(8,128)}, f32[24,128,2048]{2,1,0:T(8,128)}) custom-call(s32[1]{0:T(128)} %bitcast.10.core_ref, f32[2048,1024]{1,0:T(8,128)} %assemble.10.refs_0_, f32[2048,1024]{1,0:T(8,128)} %collective-permute-done.80.refs_1_, f32[2048,1024]{1,0:T(8,128)} %assemble.11.refs_2_, ...), custom_call_target="tpu_custom_call", output_to_operand_aliasing={{0}: (5, {}), {1}: (6, {})} | custom-call | flops 67108864 | bytes 67108864 | tf_op jit(solution)/shard_map/place/pallas_call | solution.py:271
  1547.8 19.0 %collective-permute-done.83 = f32[120,128]{1,0:T(8,128)S(1)} collective-permute-done((f32[120,128]{1,0:T(8,128)S(1)}, f32[120,128]{1,0:T(8,128)S(1)}, u32[]{:S(2)}, u32[]{:S(2)}) %collective-permute-start.83) | collective-permute-done | bytes 61472 | tf_op jit(solution)/shard_map/ppermute | solution.py:354
  (411 shorter events, 837.9 us)
Async XLA Ops:
  312.1 503.4 %collective-permute-start.20 = (bf16[2048,256]{1,0:T(8,128)(2,1)}, bf16[2048,256]{1,0:T(8,128)(2,1)}, u32[]{:S(2)}, u32[]{:S(2)}) collective-permute-start(bf16[2048,256]{1,0:T(8,128)(2,1)} %pad_maximum_fusion.1), channel_id=1, source_target_pairs={{0,1},{1,0},{2,3},{3,2},{4,5},{5,4},{6,7},{7,6}} | collective-permute-start | bytes 3145736 | tf_op jit(solution)/shard_map/ppermute | solution.py:354
  386.4 401.4 %collective-permute-start.38 = (f32[256,1024]{1,0:T(8,128)}, f32[256,1024]{1,0:T(8,128)}, u32[]{:S(2)}, u32[]{:S(2)}) collective-permute-start(f32[256,1024]{1,0:T(8,128)} %get-tuple-element.473.refs_0_), channel_id=1, source_target_pairs={{0,4},{1,5},{2,6},{3,7},{4,0},{5,1},{6,2},{7,3}} | collective-permute-start | bytes 3145736 | tf_op jit(solution)/shard_map/ppermute | solution.py:354
  387.7 400.4 %collective-permute-start.39 = (f32[256,1024]{1,0:T(8,128)}, f32[256,1024]{1,0:T(8,128)}, u32[]{:S(2)}, u32[]{:S(2)}) collective-permute-start(f32[256,1024]{1,0:T(8,128)} %get-tuple-element.474.refs_1_), channel_id=1, source_target_pairs={{0,2},{1,3},{2,0},{3,1},{4,6},{5,7},{6,4},{7,5}} | collective-permute-start | bytes 3145736 | tf_op jit(solution)/shard_map/ppermute | solution.py:354
  913.9 78.1 %collective-permute-start.62 = (bf16[2048,768]{1,0:T(8,128)(2,1)}, bf16[2048,768]{1,0:T(8,128)(2,1)}, u32[]{:S(2)}, u32[]{:S(2)}) collective-permute-start(bf16[2048,768]{1,0:T(8,128)(2,1)} %get-tuple-element.363.refs_10_.refs_11_), channel_id=1, source_target_pairs={{0,1},{1,0},{2,3},{3,2},{4,5},{5,4},{6,7},{7,6}} | collective-permute-start | bytes 9437192 | tf_op jit(solution)/shard_map/ppermute | solution.py:354
  959.2 92.6 %collective-permute-start.63 = (bf16[2048,768]{1,0:T(8,128)(2,1)}, bf16[2048,768]{1,0:T(8,128)(2,1)}, u32[]{:S(2)}, u32[]{:S(2)}) collective-permute-start(bf16[2048,768]{1,0:T(8,128)(2,1)} %get-tuple-element.389.refs_10_.refs_11_), channel_id=1, source_target_pairs={{0,1},{1,0},{2,3},{3,2},{4,5},{5,4},{6,7},{7,6}} | collective-permute-start | bytes 9437192 | tf_op jit(solution)/shard_map/ppermute | solution.py:354
  982.1 208.6 %collective-permute-start.70 = (f32[2048,1024]{1,0:T(8,128)}, f32[2048,1024]{1,0:T(8,128)}, u32[]{:S(2)}, u32[]{:S(2)}) collective-permute-start(f32[2048,1024]{1,0:T(8,128)} %assemble.6.refs_0_), channel_id=1, source_target_pairs={{0,1},{1,0},{2,3},{3,2},{4,5},{5,4},{6,7},{7,6}} | collective-permute-start | bytes 25165832 | tf_op jit(solution)/shard_map/ppermute | solution.py:354
  992.0 198.8 %collective-permute-start.71 = (f32[2048,1024]{1,0:T(8,128)}, f32[2048,1024]{1,0:T(8,128)}, u32[]{:S(2)}, u32[]{:S(2)}) collective-permute-start(f32[2048,1024]{1,0:T(8,128)} %assemble.7.refs_2_), channel_id=1, source_target_pairs={{0,1},{1,0},{2,3},{3,2},{4,5},{5,4},{6,7},{7,6}} | collective-permute-start | bytes 25165832 | tf_op jit(solution)/shard_map/ppermute | solution.py:354
  1078.1 109.7 %collective-permute-start.65 = (bf16[2048,768]{1,0:T(8,128)(2,1)}, bf16[2048,768]{1,0:T(8,128)(2,1)S(1)}, u32[]{:S(2)}, u32[]{:S(2)}) collective-permute-start(bf16[2048,768]{1,0:T(8,128)(2,1)} %get-tuple-element.449.refs_10_.refs_11_), channel_id=1, source_target_pairs={{0,1},{1,0},{2,3},{3,2},{4,5},{5,4},{6,7},{7,6}} | collective-permute-start | bytes 9437192 | tf_op jit(solution)/shard_map/ppermute | solution.py:354
  1175.5 103.9 %all-to-all-start.4 = ((bf16[8,128,2048]{2,1,0:T(8,128)(2,1)}), bf16[8,128,2048]{2,1,0:T(8,128)(2,1)}, u32[]{:S(2)}, u32[]{:S(2)}) async-start(bf16[8,128,2048]{2,1,0:T(8,128)(2,1)} %bitcast.125), calls=%async_computation.4 | async-start | bytes 8388608 | tf_op jit(solution)/shard_map/all_to_all | solution.py:368
  1187.8 97.6 %collective-permute-start.59 = (f32[256,1024]{1,0:T(8,128)}, f32[256,1024]{1,0:T(8,128)}, u32[]{:S(2)}, u32[]{:S(2)}) collective-permute-start(f32[256,1024]{1,0:T(8,128)} %collective-permute-done.55.refs_3_), channel_id=1, source_target_pairs={{0,4},{1,5},{2,6},{3,7},{4,0},{5,1},{6,2},{7,3}} | collective-permute-start | bytes 3145736 | tf_op jit(solution)/shard_map/ppermute | solution.py:354
  1189.2 97.6 %collective-permute-start.50 = (f32[256,1024]{1,0:T(8,128)}, f32[256,1024]{1,0:T(8,128)}, u32[]{:S(2)}, u32[]{:S(2)}) collective-permute-start(f32[256,1024]{1,0:T(8,128)} %get-tuple-element.532.refs_0_), channel_id=1, source_target_pairs={{0,2},{1,3},{2,0},{3,1},{4,6},{5,7},{6,4},{7,5}} | collective-permute-start | bytes 3145736 | tf_op jit(solution)/shard_map/ppermute | solution.py:354
  1190.4 97.6 %collective-permute-start.51 = (f32[256,1024]{1,0:T(8,128)}, f32[256,1024]{1,0:T(8,128)}, u32[]{:S(2)}, u32[]{:S(2)}) collective-permute-start(f32[256,1024]{1,0:T(8,128)} %get-tuple-element.533.refs_1_), channel_id=1, source_target_pairs={{0,4},{1,5},{2,6},{3,7},{4,0},{5,1},{6,2},{7,3}} | collective-permute-start | bytes 3145736 | tf_op jit(solution)/shard_map/ppermute | solution.py:354
  1190.7 97.6 %collective-permute-start.52 = (f32[256,1024]{1,0:T(8,128)}, f32[256,1024]{1,0:T(8,128)}, u32[]{:S(2)}, u32[]{:S(2)}) collective-permute-start(f32[256,1024]{1,0:T(8,128)} %collective-permute-done.48.refs_2_), channel_id=1, source_target_pairs={{0,2},{1,3},{2,0},{3,1},{4,6},{5,7},{6,4},{7,5}} | collective-permute-start | bytes 3145736 | tf_op jit(solution)/shard_map/ppermute | solution.py:354
  1190.8 108.6 %collective-permute-start.53 = (f32[256,1024]{1,0:T(8,128)}, f32[256,1024]{1,0:T(8,128)}, u32[]{:S(2)}, u32[]{:S(2)}) collective-permute-start(f32[256,1024]{1,0:T(8,128)} %collective-permute-done.49.refs_3_), channel_id=1, source_target_pairs={{0,4},{1,5},{2,6},{3,7},{4,0},{5,1},{6,2},{7,3}} | collective-permute-start | bytes 3145736 | tf_op jit(solution)/shard_map/ppermute | solution.py:354
  1279.5 168.6 %all-to-all-start.3 = ((bf16[8,128,2048]{2,1,0:T(8,128)(2,1)}), bf16[8,128,2048]{2,1,0:T(8,128)(2,1)}, u32[]{:S(2)}, u32[]{:S(2)}) async-start(bf16[8,128,2048]{2,1,0:T(8,128)(2,1)} %bitcast.124), calls=%async_computation.3 | async-start | bytes 8388608 | tf_op jit(solution)/shard_map/all_to_all | solution.py:368
  1285.4 126.8 %collective-permute-start.44 = (f32[256,1024]{1,0:T(8,128)S(1)}, f32[256,1024]{1,0:T(8,128)}, u32[]{:S(2)}, u32[]{:S(2)}) collective-permute-start(f32[256,1024]{1,0:T(8,128)S(1)} %copy-done.15), channel_id=1, source_target_pairs={{0,2},{1,3},{2,0},{3,1},{4,6},{5,7},{6,4},{7,5}} | collective-permute-start | bytes 3145736 | tf_op jit(solution)/shard_map/ppermute | solution.py:354
  1286.8 126.5 %collective-permute-start.45 = (f32[256,1024]{1,0:T(8,128)S(1)}, f32[256,1024]{1,0:T(8,128)}, u32[]{:S(2)}, u32[]{:S(2)}) collective-permute-start(f32[256,1024]{1,0:T(8,128)S(1)} %copy-done.16), channel_id=1, source_target_pairs={{0,4},{1,5},{2,6},{3,7},{4,0},{5,1},{6,2},{7,3}} | collective-permute-start | bytes 3145736 | tf_op jit(solution)/shard_map/ppermute | solution.py:354
  1288.0 126.5 %collective-permute-start.46 = (f32[256,1024]{1,0:T(8,128)}, f32[256,1024]{1,0:T(8,128)}, u32[]{:S(2)}, u32[]{:S(2)}) collective-permute-start(f32[256,1024]{1,0:T(8,128)} %collective-permute-done.30.refs_2_), channel_id=1, source_target_pairs={{0,2},{1,3},{2,0},{3,1},{4,6},{5,7},{6,4},{7,5}} | collective-permute-start | bytes 3145736 | tf_op jit(solution)/shard_map/ppermute | solution.py:354
  1288.3 100.9 %collective-permute-start.72 = (f32[256,1024]{1,0:T(8,128)S(1)}, f32[256,1024]{1,0:T(8,128)}, u32[]{:S(2)}, u32[]{:S(2)}) collective-permute-start(f32[256,1024]{1,0:T(8,128)S(1)} %copy-done.20), channel_id=1, source_target_pairs={{0,4},{1,5},{2,6},{3,7},{4,0},{5,1},{6,2},{7,3}} | collective-permute-start | bytes 3145736 | tf_op jit(solution)/shard_map/ppermute | solution.py:354
  1299.3 100.9 %collective-permute-start.73 = (f32[256,1024]{1,0:T(8,128)}, f32[256,1024]{1,0:T(8,128)}, u32[]{:S(2)}, u32[]{:S(2)}) collective-permute-start(f32[256,1024]{1,0:T(8,128)} %get-tuple-element.554.refs_1_), channel_id=1, source_target_pairs={{0,2},{1,3},{2,0},{3,1},{4,6},{5,7},{6,4},{7,5}} | collective-permute-start | bytes 3145736 | tf_op jit(solution)/shard_map/ppermute | solution.py:354
  1469.5 100.6 %all-to-all-start.5 = ((bf16[8,2,128,2048]{3,2,1,0:T(8,128)(2,1)}), bf16[8,2,128,2048]{3,2,1,0:T(8,128)(2,1)}, u32[]{:S(2)}, u32[]{:S(2)}) async-start(bf16[8,2,128,2048]{3,2,1,0:T(8,128)(2,1)} %get-tuple-element.523), calls=%async_computation.5 | async-start | bytes 16777216 | tf_op jit(solution)/shard_map/all_to_all | solution.py:368
  1485.2 81.5 %collective-permute-start.83 = (f32[120,128]{1,0:T(8,128)S(1)}, f32[120,128]{1,0:T(8,128)S(1)}, u32[]{:S(2)}, u32[]{:S(2)}) collective-permute-start(f32[120,128]{1,0:T(8,128)S(1)} %fusion.16), channel_id=1, source_target_pairs={{0,2},{1,3},{2,0},{3,1},{4,6},{5,7},{6,4},{7,5}} | collective-permute-start | bytes 184328 | tf_op jit(solution)/shard_map/ppermute | solution.py:354
  1485.3 81.4 %collective-permute-start.84 = (f32[120,128]{1,0:T(8,128)S(1)}, f32[120,128]{1,0:T(8,128)S(1)}, u32[]{:S(2)}, u32[]{:S(2)}) collective-permute-start(f32[120,128]{1,0:T(8,128)S(1)} %fusion.16), channel_id=1, source_target_pairs={{0,4},{1,5},{2,6},{3,7},{4,0},{5,1},{6,2},{7,3}} | collective-permute-start | bytes 184328 | tf_op jit(solution)/shard_map/ppermute | solution.py:354
  1486.7 82.2 %collective-permute-start.85 = (f32[120,128]{1,0:T(8,128)S(1)}, f32[120,128]{1,0:T(8,128)S(1)}, u32[]{:S(2)}, u32[]{:S(2)}) collective-permute-start(f32[120,128]{1,0:T(8,128)S(1)} %fusion.16), channel_id=1, source_target_pairs={{0,6},{1,7},{2,4},{3,5},{4,2},{5,3},{6,0},{7,1}} | collective-permute-start | bytes 184328 | tf_op jit(solution)/shard_map/ppermute | solution.py:354
  (124 other events, 3726.9 us)

commit v5 on v4

--- a/solution.py
+++ b/solution.py
@@ -181,7 +181,7 @@
         in_specs=[pl.BlockSpec((bm, cols), lambda i: (i, 0)), spec(2, 0), spec(2, 2), *own],
         out_specs=own,
         out_shape=[jax.ShapeDtypeStruct(last_a.shape, F32)] * 2,
-        cost_estimate=cost(kept.size, 16 * kept.size),
+        cost_estimate=cost(kept.size, kept.size),
         name="add_last",
     )(kept, got_a, got_b, last_a, last_b)
 
@@ -203,7 +203,7 @@
         grid_spec=pltpu.PrefetchScalarGridSpec(num_scalar_prefetch=1, grid=(n,), in_specs=[block] * n,
                                                out_specs=pl.BlockSpec((rows, cols), lambda i, order: (order[i], 0))),
         out_shape=jax.ShapeDtypeStruct((n * rows, cols), F32),
-        cost_estimate=cost(n * rows * cols, n * rows * cols * 8),
+        cost_estimate=cost(n * rows * cols, n * rows * cols),
         name="assemble",
     )(order, *pieces)
 
@@ -276,7 +276,7 @@
                        pl.BlockSpec((heads, dh, blk), lambda i, c: (group, 0, i))]),
         out_shape=[jax.ShapeDtypeStruct((dim, 3, heads_all, dh), F32), jax.ShapeDtypeStruct((heads_all, dh, dim), F32)],
         input_output_aliases=alias,
-        cost_estimate=cost(size * 8, size * 8),
+        cost_estimate=cost(size, size),
         name="place",
     )(core, *args)
 
@@ -295,8 +295,29 @@
                           out_specs=pl.BlockSpec((2, 1, *block), lambda i: (i, at, 0, 0)),
                           out_shape=jax.ShapeDtypeStruct((n, 2, *block), piece.dtype),
                           input_output_aliases={} if into is None else {1: 0},
-                          cost_estimate=cost(piece.size, 4 * piece.size),
+                          cost_estimate=cost(piece.size, piece.size),
                           name="interleaved")(*args)
+
+
+def norm_rows(x):
+    x = x.astype(F32)
+    centered = x - jnp.mean(x, axis=1, keepdims=True)
+    inv_std = lax.rsqrt(jnp.mean(centered * centered, axis=1, keepdims=True) + LN_EPS)
+    return centered * inv_std, inv_std
+
+
+def norm(x, gain, bias, s):
+    parts, _, part, dim = x.shape
+
+    def kernel(x_ref, gain_ref, bias_ref, u_ref):
+        u_ref[:] = (norm_rows(x_ref[0, 0])[0] * gain_ref[:] + bias_ref[:]).astype(BF16)
+
+    row = pl.BlockSpec((1, dim), lambda i: (0, 0))
+    return pl.pallas_call(
+        kernel, grid=(parts,), in_specs=[pl.BlockSpec((1, 1, part, dim), lambda i: (i, s, 0, 0)), row, row],
+        out_specs=pl.BlockSpec((part, dim), lambda i: (i, 0)), out_shape=jax.ShapeDtypeStruct((parts * part, dim), BF16),
+        cost_estimate=cost(x.size, x.size), name="norm",
+    )(x, gain.reshape(1, dim), bias.reshape(1, dim))
 
 
 def norm_grads(grad_u, x, gy, gain, s, into):
@@ -305,11 +326,9 @@
 
     def kernel(grad_ref, x_ref, gy_ref, gain_ref, *refs):
         gx_ref, sums_ref = refs[-2:]
-        xf, grad, gyf = x_ref[0, 0].astype(F32), grad_ref[:].astype(F32), gy_ref[:].astype(F32)
-        mean_of = lambda a: jnp.sum(a, axis=1, keepdims=True) * (1.0 / dim)
-        centered = xf - mean_of(xf)
-        inv_std = lax.rsqrt(mean_of(centered * centered) + LN_EPS)
-        x_hat = centered * inv_std
+        x_hat, inv_std = norm_rows(x_ref[0, 0])
+        grad, gyf = grad_ref[:].astype(F32), gy_ref[:].astype(F32)
+        mean_of = lambda a: jnp.mean(a, axis=1, keepdims=True)
         grad_hat = grad * gain_ref[:]
         gx = gyf + inv_std * (grad_hat - mean_of(grad_hat) - x_hat * mean_of(grad_hat * x_hat))
         gx_ref[0, 0] = gx.astype(BF16)
@@ -329,7 +348,7 @@
         out_specs=[piece, pl.BlockSpec((8, dim), lambda i: (0, 0))],
         out_shape=[jax.ShapeDtypeStruct(x.shape, BF16), jax.ShapeDtypeStruct((8, dim), F32)],
         input_output_aliases={4: 0} if extra else {},
-        cost_estimate=cost(parts * part * dim * 400, parts * part * dim * 8),
+        cost_estimate=cost(x.size, x.size),
         name="norm_grads",
     )(grad_u, x, gy, gain.reshape(1, dim), *extra)
 
@@ -340,7 +359,7 @@
 
     block = pl.BlockSpec((2, *a.shape[1:]), lambda i: (i, 0, 0))
     return pl.pallas_call(kernel, grid=(a.shape[0] // 2,), in_specs=[block], out_specs=block,
-                          out_shape=jax.ShapeDtypeStruct(a.shape, a.dtype), cost_estimate=cost(a.size, 4 * a.size), name="copied")(a)
+                          out_shape=jax.ShapeDtypeStruct(a.shape, a.dtype), cost_estimate=cost(a.size, a.size), name="copied")(a)
 
 
 def tie(value, *after):
@@ -355,6 +374,7 @@
     partner = lambda a: hop(a, 1)
     groups, gh, ch = 3, 4, 2
     steps = groups * gh // ch
+    end = steps - 1
 
     def block(x_in, grad_y, ln_gain, ln_bias, w_qkv, b_qkv, w_out, b_out):
         batch, part, dim = x_in.shape
@@ -369,7 +389,6 @@
 
         by_device = lambda a: a.reshape(n_dev, 2, part, dim)
         x_all = exchange(by_device(x_in))
-        xs = [x_all[:, s].reshape(seq, dim) for s in range(2)]
         gy_parts = [by_device(grad_y)[:, s] for s in range(2)]
         gys = [exchange(a).reshape(seq, dim) for a in gy_parts]
         w_qkv = tie(w_qkv, *gy_parts)
@@ -381,16 +400,9 @@
         wo_of = lambda c: pick(w_out.reshape(groups, 2, gh, dh, dim), 1, c).reshape(heads_all * dh // 2, dim)
         wo_own, wo_par = wo_of(core), wo_of(1 - core)
 
-        def normed(x):
-            xf = x.astype(F32)
-            centered = xf - jnp.mean(xf, axis=-1, keepdims=True)
-            inv_std = lax.rsqrt(jnp.mean(centered * centered, axis=-1, keepdims=True) + LN_EPS)
-            x_hat = centered * inv_std
-            return (x_hat * ln_gain + ln_bias).astype(BF16), x_hat, inv_std
-
         u_own = []
-        for a in xs:
-            u_own.append(normed(a)[0])
+        for s in range(2):
+            u_own.append(norm(x_all, ln_gain, ln_bias, s))
         u = u_own + [partner(a) for a in u_own]
 
         ax = lambda x, y: 2 * x + y
@@ -428,8 +440,8 @@
             blocks[k] += [hop(a, 2), hop(b, 4)]
 
         def forward(k):
-            a, b = after_chain(blocks[k][2:4])
-            blocks[k][2:4] = [a, b]
+            mine = slice(2, 4)
+            a, b = blocks[k][mine] = after_chain(blocks[k][mine])
             blocks[k] += [hop(a, 2), hop(b, 4)]
 
         def take(k):
@@ -498,8 +510,6 @@
                     spread(0)
                 else:
                     chain = first_add(k - 1)
-                    if k > 2:
-                        forward(k - 2)
                 g_p, = after_chain([g_p])
                 units = [(u[n], gy[n], mine[1], mine[0], (n, k)) for n in range(2)]
                 units += [(u[2 + n], gy[2 + n], g_p, o_p, (n, 0)) for n in range(2)]
@@ -508,6 +518,9 @@
                 if k == 1:
                     forward(0)
                 else:
+                    if k > 2:
+                        forward(k - 2)
+                        chain = take(k - 3)
                     chain = last_add(k - 1)
             started.append(last)
             halves.append((kept, hop(send_a, 2), hop(send_b, 4)))
@@ -524,19 +537,15 @@
             y_parts.append((held[-1][:, s].reshape(seq, dim).astype(F32) + proj).astype(BF16))
         y_moved = [exchange(y.reshape(n_dev, part, dim)) for y in y_parts]
         chain = tuple(y_parts)
-        spread(steps - 2)
-        for k in range(2):
-            chain = take(k)
-        forward(steps - 2)
-        chain = first_add(steps - 1)
+        spread(end - 1)
+        forward(end - 1)
+        chain = first_add(end)
 
         g_mine, = after_chain([mine[1]])
         grad_u = dot(g_mine, w_own, 1, 1)
         chain = (grad_u,)
-        whole = place_sums(0)
-        chain = tuple(whole)
-        chain = last_add(steps - 1)
-        spread(steps - 1)
+        chain = last_add(end)
+        spread(end)
         g_theirs, = after_chain([jnp.concatenate(g_got, axis=1)])
         grad_u = dot(g_theirs, w_par, 1, 1) + grad_u
         chain = (grad_u,)
@@ -556,9 +565,11 @@
         others = [hop(small, bit) for bit in (2, 4, 6)]
 
         chain = (gx,)
-        forward(steps - 1)
-        for k in range(2, 5):
-            chain = take(k)
+        forward(end)
+        chain = take(3)
+        whole = place_sums(0)
+        chain = tuple(whole)
+        chain = take(4)
         y_out = interleaved(interleaved(None, after_chain([y_moved[0]])[0], 0), y_moved[1], 1)
         chain = (y_out,)
         chain = take(5)

time: 1590 us -> 1520 us (0.956)
  waiting for transfers between devices: 237 us -> 139 us
  starting transfers between devices: 133 us -> 166 us
  other arithmetic: 59.8 us -> 32.6 us
  Pallas kernels: 847 us -> 863 us
    ppermute x86, waiting for transfers between devices: 237 us -> 139 us  [solution(): lax.ppermute(a, 'sp', [(d, d ^ bit) for d in range(n_dev)])]
    ppermute x86, starting transfers between devices: 106 us -> 145 us  [solution(): lax.ppermute(a, 'sp', [(d, d ^ bit) for d in range(n_dev)])]
    convert_element_type x2 -> x0, other arithmetic: 21.3 us -> none  [the longest x1 11.8 us: normed(): xf = x.astype(F32)]
    unnamed x125 -> x105, local copies, waits for them, and re-layouts: 32.3 us -> 31.6 us
  transfers between devices with their start and end apart: 91 -> 91, of which waited for: 17 -> 13; matrix products, arithmetic and copies ran while one was open for 15% -> 15% of each run, Pallas kernels for 51% -> 54%
where the time goes in v5:
time: 1520 us; the launch traced here: 1510 us
  Pallas kernels  863 us (57%)
  starting transfers between devices  166 us (11%)
  matrix products  145 us (10%)
  waiting for transfers between devices  139 us (9%)
  blocking collectives  97.9 us (6%)
  local copies, waits for them, and re-layouts  64.2 us (4%)
  other arithmetic  32.6 us (2%)
    pallas_call x16, Pallas kernels, project(): pl.pallas_call(functools.partial(project_kernel, len(units), steps, trans...  196 us
    pallas_call x8, Pallas kernels, weight_grads(): pl.pallas_call(kernel, grid_spec=pltpu.PrefetchScalarGridSpec(num_scalar_...  188 us
    pallas_call x14, Pallas kernels, attention(): pl.pallas_call(kernel, grid=(n_seq, n_heads), in_specs=in_specs, out_spec...  181 us
    ppermute x86, starting transfers between devices, solution(): lax.ppermute(a, 'sp', [(d, d ^ bit) for d in range(n_dev)])  145 us
    dot_general x6, matrix products, dot(): lax.dot_general(a, b, (((ca,), (cb,)), ((), ())), preferred_element_type=...  145 us
    ppermute x86, waiting for transfers between devices, solution(): lax.ppermute(a, 'sp', [(d, d ^ bit) for d in range(n_dev)])  139 us
    all_to_all x1, blocking collectives, exchange(): return lax.all_to_all(a, 'sp', 0, 0, tiled=True)  97.9 us
    pallas_call x3, Pallas kernels, place(): pl.pallas_call(functools.partial(place_kernel, counts, dh), grid_spec=plt...  89.9 us
  transfers between devices with their start and end apart: 91, of which 13 were waited for; matrix products, arithmetic and copies ran while one was open for 15% of the time, Pallas kernels for 54%

profile of v5, /device:TPU:1, one launch (start us, length us, event | category | flops | bytes accessed | tf_op | source)
XLA Modules:
  0.0 1507.9 jit_solution(1122379635661172800)
XLA Ops:
  0.6 97.9 %all_to_all.30.x_ref = bf16[8,2,128,2048]{3,2,1,0:T(8,128)(2,1)} all-to-all(bf16[8,2,128,2048]{3,2,1,0:T(8,128)(2,1)} %bitcast.85), channel_id=1, replica_groups=mesh['sp'=8] {'sp'}, dimensions={0} | all-to-all | bytes 16777216 | tf_op jit(solution)/shard_map/all_to_all | solution.py:388
  126.1 33.6 %lay_out_weights.2.refs_1_.refs_4_ = bf16[2048,4608]{1,0:T(8,128)(2,1)} custom-call(s32[1]{0:T(128)} %bitcast.6.core_ref, bf16[2048,3,24,128]{3,2,1,0:T(8,128)(2,1)} %w_ref.1), custom_call_target="tpu_custom_call" | custom-call | flops 3774873600 | bytes 56623104 | tf_op jit(solution)/shard_map/lay_out_weights/pallas_call | solution.py:227
  230.3 18.5 %weight_grads.8 = (f32[512,1024]{1,0:T(8,128)}, f32[512,1024]{1,0:T(8,128)}, f32[512,1024]{1,0:T(8,128)}, f32[512,1024]{1,0:T(8,128)}) custom-call(s32[8]{0:T(128)} %stack.50.order_ref, bf16[1024,2048]{1,0:T(8,128)(2,1)} %norm.2.refs_0_, bf16[1024,2048]{1,0:T(8,128)(2,1)} %collective-permute-done.refs_0_.refs_1_.refs_2_, ...), custom_call_target="tpu_custom_call" | custom-call | flops 8589934592 | bytes 33554432 | tf_op jit(solution)/shard_map/weight_grads/pallas_call | solution.py:153
  317.2 20.3 %project.24.qkv_ref = bf16[4096,768]{1,0:T(8,128)(2,1)} custom-call(bf16[1024,2048]{1,0:T(8,128)(2,1)} %norm.2.refs_0_, bf16[1024,2048]{1,0:T(8,128)(2,1)} %norm.3.refs_0_.refs_1_, bf16[1024,2048]{1,0:T(8,128)(2,1)} %collective-permute-done.refs_0_.refs_1_.refs_2_, bf16[1024,2048]{1,0:T(8,128)(2,1)} %collective-permute-done.1.refs_0_.refs_1_.refs_3_, ...), custom_call_target="tpu_custom_call" | custom-call | flops 12884901888 | bytes 23068672 | tf_op jit(solution)/shard_map/project/pallas_call | solution.py:115
  380.7 29.2 %weight_grads.11 = (f32[512,1024]{1,0:T(8,128)}, f32[512,1024]{1,0:T(8,128)}, f32[512,1024]{1,0:T(8,128)}, f32[512,1024]{1,0:T(8,128)}) custom-call(s32[8]{0:T(128)} %stack.50.order_ref, bf16[1024,2048]{1,0:T(8,128)(2,1)} %norm.2.refs_0_, bf16[1024,2048]{1,0:T(8,128)(2,1)} %norm.3.refs_0_.refs_1_, ...), custom_call_target="tpu_custom_call" | custom-call | flops 17179869184 | bytes 67108864 | tf_op jit(solution)/shard_map/weight_grads/pallas_call | solution.py:153
  410.9 20.5 %project.26.qkv_ref = bf16[4096,768]{1,0:T(8,128)(2,1)} custom-call(bf16[1024,2048]{1,0:T(8,128)(2,1)} %norm.2.refs_0_, bf16[1024,2048]{1,0:T(8,128)(2,1)} %norm.3.refs_0_.refs_1_, bf16[1024,2048]{1,0:T(8,128)(2,1)} %collective-permute-done.refs_0_.refs_1_.refs_2_, bf16[1024,2048]{1,0:T(8,128)(2,1)} %collective-permute-done.1.refs_0_.refs_1_.refs_3_, ...), custom_call_target="tpu_custom_call" | custom-call | flops 12884901888 | bytes 23068672 | tf_op jit(solution)/shard_map/project/pallas_call | solution.py:115
  487.4 29.0 %weight_grads.12 = (f32[512,1024]{1,0:T(8,128)}, f32[512,1024]{1,0:T(8,128)}, f32[512,1024]{1,0:T(8,128)}, f32[512,1024]{1,0:T(8,128)}) custom-call(s32[8]{0:T(128)} %stack.50.order_ref, bf16[1024,2048]{1,0:T(8,128)(2,1)} %norm.2.refs_0_, bf16[1024,2048]{1,0:T(8,128)(2,1)} %norm.3.refs_0_.refs_1_, ...), custom_call_target="tpu_custom_call" | custom-call | flops 17179869184 | bytes 67108864 | tf_op jit(solution)/shard_map/weight_grads/pallas_call | solution.py:153
  525.2 21.3 %collective-permute-done.11.b2 = f32[256,1024]{1,0:T(8,128)} collective-permute-done((f32[256,1024]{1,0:T(8,128)}, f32[256,1024]{1,0:T(8,128)}, u32[]{:S(2)}, u32[]{:S(2)}) %collective-permute-start.11) | collective-permute-done | bytes 1048608 | tf_op jit(solution)/shard_map/ppermute | solution.py:373
  552.7 20.5 %project.28.qkv_ref = bf16[4096,768]{1,0:T(8,128)(2,1)} custom-call(bf16[1024,2048]{1,0:T(8,128)(2,1)} %norm.2.refs_0_, bf16[1024,2048]{1,0:T(8,128)(2,1)} %norm.3.refs_0_.refs_1_, bf16[1024,2048]{1,0:T(8,128)(2,1)} %collective-permute-done.refs_0_.refs_1_.refs_2_, bf16[1024,2048]{1,0:T(8,128)(2,1)} %collective-permute-done.1.refs_0_.refs_1_.refs_3_, ...), custom_call_target="tpu_custom_call" | custom-call | flops 12884901888 | bytes 23068672 | tf_op jit(solution)/shard_map/project/pallas_call | solution.py:115
  610.8 29.2 %weight_grads.13 = (f32[512,1024]{1,0:T(8,128)}, f32[512,1024]{1,0:T(8,128)}, f32[512,1024]{1,0:T(8,128)}, f32[512,1024]{1,0:T(8,128)}) custom-call(s32[8]{0:T(128)} %stack.50.order_ref, bf16[1024,2048]{1,0:T(8,128)(2,1)} %norm.2.refs_0_, bf16[1024,2048]{1,0:T(8,128)(2,1)} %norm.3.refs_0_.refs_1_, ...), custom_call_target="tpu_custom_call" | custom-call | flops 17179869184 | bytes 67108864 | tf_op jit(solution)/shard_map/weight_grads/pallas_call | solution.py:153
  674.1 20.3 %project.29.qkv_ref = bf16[4096,768]{1,0:T(8,128)(2,1)} custom-call(bf16[1024,2048]{1,0:T(8,128)(2,1)} %norm.2.refs_0_, bf16[1024,2048]{1,0:T(8,128)(2,1)} %norm.3.refs_0_.refs_1_, bf16[1024,2048]{1,0:T(8,128)(2,1)} %collective-permute-done.refs_0_.refs_1_.refs_2_, bf16[1024,2048]{1,0:T(8,128)(2,1)} %collective-permute-done.1.refs_0_.refs_1_.refs_3_, ...), custom_call_target="tpu_custom_call" | custom-call | flops 12884901888 | bytes 23068672 | tf_op jit(solution)/shard_map/project/pallas_call | solution.py:115
  694.4 17.4 %project.30.do_ref = bf16[4096,512]{1,0:T(8,128)(2,1)} custom-call(bf16[1024,2048]{1,0:T(8,128)(2,1)} %bitcast.5.refs_0_.refs_2_.refs_4_.gy_ref, bf16[1024,2048]{1,0:T(8,128)(2,1)} %bitcast.11.refs_0_.refs_2_.refs_1_.refs_5_.gy_ref, bf16[1024,2048]{1,0:T(8,128)(2,1)} %collective-permute-done.2.refs_0_.refs_3_.refs_2_.refs_6_, ...), custom_call_target="tpu_custom_call" | custom-call | flops 8589934592 | bytes 20971520 | tf_op jit(solution)/shard_map/project/pallas_call | solution.py:115
  750.0 29.0 %weight_grads.14 = (f32[512,1024]{1,0:T(8,128)}, f32[512,1024]{1,0:T(8,128)}, f32[512,1024]{1,0:T(8,128)}, f32[512,1024]{1,0:T(8,128)}) custom-call(s32[8]{0:T(128)} %stack.50.order_ref, bf16[1024,2048]{1,0:T(8,128)(2,1)} %norm.2.refs_0_, bf16[1024,2048]{1,0:T(8,128)(2,1)} %norm.3.refs_0_.refs_1_, ...), custom_call_target="tpu_custom_call" | custom-call | flops 17179869184 | bytes 67108864 | tf_op jit(solution)/shard_map/weight_grads/pallas_call | solution.py:153
  812.4 20.3 %project.31.qkv_ref = bf16[4096,768]{1,0:T(8,128)(2,1)} custom-call(bf16[1024,2048]{1,0:T(8,128)(2,1)} %norm.2.refs_0_, bf16[1024,2048]{1,0:T(8,128)(2,1)} %norm.3.refs_0_.refs_1_, bf16[1024,2048]{1,0:T(8,128)(2,1)} %collective-permute-done.refs_0_.refs_1_.refs_2_, bf16[1024,2048]{1,0:T(8,128)(2,1)} %collective-permute-done.1.refs_0_.refs_1_.refs_3_, ...), custom_call_target="tpu_custom_call" | custom-call | flops 12884901888 | bytes 23068672 | tf_op jit(solution)/shard_map/project/pallas_call | solution.py:115
  873.5 24.1 %collective-permute-start.33 = (bf16[2048,256]{1,0:T(8,128)(2,1)}, bf16[2048,256]{1,0:T(8,128)(2,1)}, u32[]{:S(2)}, u32[]{:S(2)}) collective-permute-start(bf16[2048,256]{1,0:T(8,128)(2,1)} %get-tuple-element.341.refs_14_.refs_15_), channel_id=1, source_target_pairs={{0,1},{1,0},{2,3},{3,2},{4,5},{5,4},{6,7},{7,6}} | collective-permute-start | bytes 3145736 | tf_op jit(solution)/shard_map/ppermute | solution.py:373
  927.6 29.0 %weight_grads.15 = (f32[512,1024]{1,0:T(8,128)}, f32[512,1024]{1,0:T(8,128)}, f32[512,1024]{1,0:T(8,128)}, f32[512,1024]{1,0:T(8,128)}) custom-call(s32[8]{0:T(128)} %stack.50.order_ref, bf16[1024,2048]{1,0:T(8,128)(2,1)} %norm.2.refs_0_, bf16[1024,2048]{1,0:T(8,128)(2,1)} %norm.3.refs_0_.refs_1_, ...), custom_call_target="tpu_custom_call" | custom-call | flops 17179869184 | bytes 67108864 | tf_op jit(solution)/shard_map/weight_grads/pallas_call | solution.py:153
  1049.2 33.8 %lay_out_weights.3 = bf16[2048,4608]{1,0:T(8,128)(2,1)} custom-call(s32[1]{0:T(128)S(6)} %sub.11.core_ref, bf16[2048,3,24,128]{3,2,1,0:T(8,128)(2,1)} %w_ref.1), custom_call_target="tpu_custom_call" | custom-call | flops 3774873600 | bytes 56623104 | tf_op jit(solution)/shard_map/lay_out_weights/pallas_call | solution.py:227
  1102.3 49.9 %fusion.8 = f32[2048,2048]{1,0:T(8,128)} fusion(bf16[2048,4608]{1,0:T(8,128)(2,1)} %get-tuple-element.517.refs_8_.refs_9_, bf16[2048,4608]{1,0:T(8,128)(2,1)} %lay_out_weights.2.refs_1_.refs_4_), kind=kOutput, calls=%fused_computation.66 | convolution fusion | flops 38654705664 | bytes 54525952 | tf_op jit(solution)/shard_map/dot_general | solution.py:20
  1170.7 20.6 %collective-permute-done.49.refs_3_ = f32[256,1024]{1,0:T(8,128)} collective-permute-done((f32[256,1024]{1,0:T(8,128)}, f32[256,1024]{1,0:T(8,128)}, u32[]{:S(2)}, u32[]{:S(2)}) %collective-permute-start.49) | collective-permute-done | bytes 1048608 | tf_op jit(solution)/shard_map/ppermute | solution.py:373
  1249.9 50.4 %convolution_add_fusion.grad_ref = bf16[2048,2048]{1,0:T(8,128)(2,1)} fusion(f32[2048,2048]{1,0:T(8,128)} %fusion.8, bf16[2048,4608]{1,0:T(8,128)(2,1)} %constant_dynamic-update-slice_fusion, bf16[2048,4608]{1,0:T(8,128)(2,1)} %lay_out_weights.3), kind=kOutput, calls=%fused_computation | convolution fusion | flops 38663094272 | bytes 62914560 | tf_op jit(solution)/shard_map/dot_general | solution.py:20
  1340.0 30.1 %place.3 = (f32[2048,3,24,128]{3,2,1,0:T(8,128)}, f32[24,128,2048]{2,1,0:T(8,128)}) custom-call(s32[1]{0:T(128)} %bitcast.6.core_ref, f32[2048,1024]{1,0:T(8,128)} %assemble.6.refs_0_, f32[2048,1024]{1,0:T(8,128)} %collective-permute-done.70.refs_1_, f32[2048,1024]{1,0:T(8,128)} %assemble.7.refs_2_, f32[2048,1024]{1,0:T(8,128)} %collective-permute-done.71.refs_3_), custom_call_target="tpu_custom_call" | custom-call | flops 8388608 | bytes 8388608 | tf_op jit(solution)/shard_map/place/pallas_call | solution.py:271
  1418.0 29.9 %place.4 = (f32[2048,3,24,128]{3,2,1,0:T(8,128)}, f32[24,128,2048]{2,1,0:T(8,128)}) custom-call(s32[1]{0:T(128)} %bitcast.6.core_ref, f32[2048,1024]{1,0:T(8,128)} %assemble.8.refs_0_, f32[2048,1024]{1,0:T(8,128)} %collective-permute-done.78.refs_1_, f32[2048,1024]{1,0:T(8,128)} %assemble.9.refs_2_, ...), custom_call_target="tpu_custom_call", output_to_operand_aliasing={{0}: (5, {}), {1}: (6, {})} | custom-call | flops 8388608 | bytes 8388608 | tf_op jit(solution)/shard_map/place/pallas_call | solution.py:271
  1447.9 29.9 %place.5 = (f32[2048,3,24,128]{3,2,1,0:T(8,128)}, f32[24,128,2048]{2,1,0:T(8,128)}) custom-call(s32[1]{0:T(128)} %bitcast.6.core_ref, f32[2048,1024]{1,0:T(8,128)} %assemble.10.refs_0_, f32[2048,1024]{1,0:T(8,128)} %collective-permute-done.80.refs_1_, f32[2048,1024]{1,0:T(8,128)} %assemble.11.refs_2_, ...), custom_call_target="tpu_custom_call", output_to_operand_aliasing={{0}: (5, {}), {1}: (6, {})} | custom-call | flops 8388608 | bytes 8388608 | tf_op jit(solution)/shard_map/place/pallas_call | solution.py:271
  1477.9 17.5 %collective-permute-done.83 = f32[120,128]{1,0:T(8,128)S(1)} collective-permute-done((f32[120,128]{1,0:T(8,128)S(1)}, f32[120,128]{1,0:T(8,128)S(1)}, u32[]{:S(2)}, u32[]{:S(2)}) %collective-permute-start.83) | collective-permute-done | bytes 61472 | tf_op jit(solution)/shard_map/ppermute | solution.py:373
  (382 shorter events, 784.1 us)
Async XLA Ops:
  378.8 101.3 %collective-permute-start.18 = (f32[256,1024]{1,0:T(8,128)}, f32[256,1024]{1,0:T(8,128)}, u32[]{:S(2)}, u32[]{:S(2)}) collective-permute-start(f32[256,1024]{1,0:T(8,128)} %get-tuple-element.400.refs_0_), channel_id=1, source_target_pairs={{0,4},{1,5},{2,6},{3,7},{4,0},{5,1},{6,2},{7,3}} | collective-permute-start | bytes 3145736 | tf_op jit(solution)/shard_map/ppermute | solution.py:373
  380.0 101.3 %collective-permute-start.19 = (f32[256,1024]{1,0:T(8,128)}, f32[256,1024]{1,0:T(8,128)S(1)}, u32[]{:S(2)}, u32[]{:S(2)}) collective-permute-start(f32[256,1024]{1,0:T(8,128)} %get-tuple-element.401.refs_1_), channel_id=1, source_target_pairs={{0,2},{1,3},{2,0},{3,1},{4,6},{5,7},{6,4},{7,5}} | collective-permute-start | bytes 3145736 | tf_op jit(solution)/shard_map/ppermute | solution.py:373
  479.4 129.7 %collective-permute-start.20 = (f32[256,1024]{1,0:T(8,128)}, f32[256,1024]{1,0:T(8,128)}, u32[]{:S(2)}, u32[]{:S(2)}) collective-permute-start(f32[256,1024]{1,0:T(8,128)} %get-tuple-element.400.refs_0_), channel_id=1, source_target_pairs={{0,2},{1,3},{2,0},{3,1},{4,6},{5,7},{6,4},{7,5}} | collective-permute-start | bytes 3145736 | tf_op jit(solution)/shard_map/ppermute | solution.py:373
  480.1 130.1 %collective-permute-start.21 = (f32[256,1024]{1,0:T(8,128)}, f32[256,1024]{1,0:T(8,128)}, u32[]{:S(2)}, u32[]{:S(2)}) collective-permute-start(f32[256,1024]{1,0:T(8,128)} %get-tuple-element.401.refs_1_), channel_id=1, source_target_pairs={{0,4},{1,5},{2,6},{3,7},{4,0},{5,1},{6,2},{7,3}} | collective-permute-start | bytes 3145736 | tf_op jit(solution)/shard_map/ppermute | solution.py:373
  481.3 129.3 %collective-permute-start.22 = (f32[256,1024]{1,0:T(8,128)}, f32[256,1024]{1,0:T(8,128)}, u32[]{:S(2)}, u32[]{:S(2)}) collective-permute-start(f32[256,1024]{1,0:T(8,128)} %collective-permute-done.18.refs_2_), channel_id=1, source_target_pairs={{0,2},{1,3},{2,0},{3,1},{4,6},{5,7},{6,4},{7,5}} | collective-permute-start | bytes 3145736 | tf_op jit(solution)/shard_map/ppermute | solution.py:373
  640.0 107.7 %collective-permute-start.28 = (f32[256,1024]{1,0:T(8,128)S(1)}, f32[256,1024]{1,0:T(8,128)}, u32[]{:S(2)}, u32[]{:S(2)}) collective-permute-start(f32[256,1024]{1,0:T(8,128)S(1)} %copy-done.13), channel_id=1, source_target_pairs={{0,2},{1,3},{2,0},{3,1},{4,6},{5,7},{6,4},{7,5}} | collective-permute-start | bytes 3145736 | tf_op jit(solution)/shard_map/ppermute | solution.py:373
  644.1 103.8 %collective-permute-start.29 = (f32[256,1024]{1,0:T(8,128)}, f32[256,1024]{1,0:T(8,128)}, u32[]{:S(2)}, u32[]{:S(2)}) collective-permute-start(f32[256,1024]{1,0:T(8,128)} %get-tuple-element.440.refs_1_), channel_id=1, source_target_pairs={{0,4},{1,5},{2,6},{3,7},{4,0},{5,1},{6,2},{7,3}} | collective-permute-start | bytes 3145736 | tf_op jit(solution)/shard_map/ppermute | solution.py:373
  644.2 98.4 %collective-permute-start.14 = (f32[512,1024]{1,0:T(8,128)}, f32[512,1024]{1,0:T(8,128)S(1)}, u32[]{:S(2)}, u32[]{:S(2)}) collective-permute-start(f32[512,1024]{1,0:T(8,128)} %get-tuple-element.394), channel_id=1, source_target_pairs={{0,2},{1,3},{2,0},{3,1},{4,6},{5,7},{6,4},{7,5}} | collective-permute-start | bytes 6291464 | tf_op jit(solution)/shard_map/ppermute | solution.py:373
  666.7 81.8 %collective-permute-start.30 = (f32[256,1024]{1,0:T(8,128)}, f32[256,1024]{1,0:T(8,128)}, u32[]{:S(2)}, u32[]{:S(2)}) collective-permute-start(f32[256,1024]{1,0:T(8,128)} %collective-permute-done.26.refs_2_), channel_id=1, source_target_pairs={{0,2},{1,3},{2,0},{3,1},{4,6},{5,7},{6,4},{7,5}} | collective-permute-start | bytes 3145736 | tf_op jit(solution)/shard_map/ppermute | solution.py:373
  779.0 91.1 %collective-permute-start.32 = (bf16[2048,256]{1,0:T(8,128)(2,1)}, bf16[2048,256]{1,0:T(8,128)(2,1)}, u32[]{:S(2)}, u32[]{:S(2)}) collective-permute-start(bf16[2048,256]{1,0:T(8,128)(2,1)} %pad_maximum_fusion.1), channel_id=1, source_target_pairs={{0,1},{1,0},{2,3},{3,2},{4,5},{5,4},{6,7},{7,6}} | collective-permute-start | bytes 3145736 | tf_op jit(solution)/shard_map/ppermute | solution.py:373
  873.5 97.2 %collective-permute-start.33 = (bf16[2048,256]{1,0:T(8,128)(2,1)}, bf16[2048,256]{1,0:T(8,128)(2,1)}, u32[]{:S(2)}, u32[]{:S(2)}) collective-permute-start(bf16[2048,256]{1,0:T(8,128)(2,1)} %get-tuple-element.341.refs_14_.refs_15_), channel_id=1, source_target_pairs={{0,1},{1,0},{2,3},{3,2},{4,5},{5,4},{6,7},{7,6}} | collective-permute-start | bytes 3145736 | tf_op jit(solution)/shard_map/ppermute | solution.py:373
  1093.6 121.7 %all-to-all-start.4 = ((bf16[8,128,2048]{2,1,0:T(8,128)(2,1)}), bf16[8,128,2048]{2,1,0:T(8,128)(2,1)}, u32[]{:S(2)}, u32[]{:S(2)}) async-start(bf16[8,128,2048]{2,1,0:T(8,128)(2,1)} %bitcast.92), calls=%async_computation.4 | async-start | bytes 8388608 | tf_op jit(solution)/shard_map/all_to_all | solution.py:388
  1099.1 93.4 %collective-permute-start.65 = (bf16[2048,768]{1,0:T(8,128)(2,1)}, bf16[2048,768]{1,0:T(8,128)(2,1)}, u32[]{:S(2)}, u32[]{:S(2)}) collective-permute-start(bf16[2048,768]{1,0:T(8,128)(2,1)} %get-tuple-element.477.refs_10_.refs_11_), channel_id=1, source_target_pairs={{0,1},{1,0},{2,3},{3,2},{4,5},{5,4},{6,7},{7,6}} | collective-permute-start | bytes 9437192 | tf_op jit(solution)/shard_map/ppermute | solution.py:373
  1102.1 89.2 %collective-permute-start.49 = (f32[256,1024]{1,0:T(8,128)}, f32[256,1024]{1,0:T(8,128)}, u32[]{:S(2)}, u32[]{:S(2)}) collective-permute-start(f32[256,1024]{1,0:T(8,128)} %get-tuple-element.541.refs_1_), channel_id=1, source_target_pairs={{0,2},{1,3},{2,0},{3,1},{4,6},{5,7},{6,4},{7,5}} | collective-permute-start | bytes 3145736 | tf_op jit(solution)/shard_map/ppermute | solution.py:373
  1208.0 116.9 %collective-permute-start.70 = (f32[2048,1024]{1,0:T(8,128)}, f32[2048,1024]{1,0:T(8,128)}, u32[]{:S(2)}, u32[]{:S(2)}) collective-permute-start(f32[2048,1024]{1,0:T(8,128)} %assemble.6.refs_0_), channel_id=1, source_target_pairs={{0,1},{1,0},{2,3},{3,2},{4,5},{5,4},{6,7},{7,6}} | collective-permute-start | bytes 25165832 | tf_op jit(solution)/shard_map/ppermute | solution.py:373
  1213.7 126.2 %collective-permute-start.71 = (f32[2048,1024]{1,0:T(8,128)}, f32[2048,1024]{1,0:T(8,128)}, u32[]{:S(2)}, u32[]{:S(2)}) collective-permute-start(f32[2048,1024]{1,0:T(8,128)} %assemble.7.refs_2_), channel_id=1, source_target_pairs={{0,1},{1,0},{2,3},{3,2},{4,5},{5,4},{6,7},{7,6}} | collective-permute-start | bytes 25165832 | tf_op jit(solution)/shard_map/ppermute | solution.py:373
  1215.3 168.2 %all-to-all-start.3 = ((bf16[8,128,2048]{2,1,0:T(8,128)(2,1)}), bf16[8,128,2048]{2,1,0:T(8,128)(2,1)}, u32[]{:S(2)}, u32[]{:S(2)}) async-start(bf16[8,128,2048]{2,1,0:T(8,128)(2,1)} %bitcast.91), calls=%async_computation.3 | async-start | bytes 8388608 | tf_op jit(solution)/shard_map/all_to_all | solution.py:388
  1219.0 104.7 %collective-permute-start.52 = (f32[256,1024]{1,0:T(8,128)}, f32[256,1024]{1,0:T(8,128)}, u32[]{:S(2)}, u32[]{:S(2)}) collective-permute-start(f32[256,1024]{1,0:T(8,128)} %collective-permute-done.48.refs_2_), channel_id=1, source_target_pairs={{0,2},{1,3},{2,0},{3,1},{4,6},{5,7},{6,4},{7,5}} | collective-permute-start | bytes 3145736 | tf_op jit(solution)/shard_map/ppermute | solution.py:373
  1237.1 87.4 %collective-permute-start.53 = (f32[256,1024]{1,0:T(8,128)}, f32[256,1024]{1,0:T(8,128)}, u32[]{:S(2)}, u32[]{:S(2)}) collective-permute-start(f32[256,1024]{1,0:T(8,128)} %collective-permute-done.49.refs_3_), channel_id=1, source_target_pairs={{0,4},{1,5},{2,6},{3,7},{4,0},{5,1},{6,2},{7,3}} | collective-permute-start | bytes 3145736 | tf_op jit(solution)/shard_map/ppermute | solution.py:373
  1238.4 96.1 %collective-permute-start.74 = (f32[256,1024]{1,0:T(8,128)S(1)}, f32[256,1024]{1,0:T(8,128)}, u32[]{:S(2)}, u32[]{:S(2)}) collective-permute-start(f32[256,1024]{1,0:T(8,128)S(1)} %copy-done.14), channel_id=1, source_target_pairs={{0,2},{1,3},{2,0},{3,1},{4,6},{5,7},{6,4},{7,5}} | collective-permute-start | bytes 3145736 | tf_op jit(solution)/shard_map/ppermute | solution.py:373
  1334.5 82.2 %collective-permute-start.78 = (f32[2048,1024]{1,0:T(8,128)}, f32[2048,1024]{1,0:T(8,128)}, u32[]{:S(2)}, u32[]{:S(2)}) collective-permute-start(f32[2048,1024]{1,0:T(8,128)} %assemble.8.refs_0_), channel_id=1, source_target_pairs={{0,1},{1,0},{2,3},{3,2},{4,5},{5,4},{6,7},{7,6}} | collective-permute-start | bytes 25165832 | tf_op jit(solution)/shard_map/ppermute | solution.py:373
  1397.7 101.1 %all-to-all-start.5 = ((bf16[8,2,128,2048]{3,2,1,0:T(8,128)(2,1)}), bf16[8,2,128,2048]{3,2,1,0:T(8,128)(2,1)}, u32[]{:S(2)}, u32[]{:S(2)}) async-start(bf16[8,2,128,2048]{3,2,1,0:T(8,128)(2,1)} %get-tuple-element.527), calls=%async_computation.5 | async-start | bytes 16777216 | tf_op jit(solution)/shard_map/all_to_all | solution.py:388
  1415.3 80.0 %collective-permute-start.83 = (f32[120,128]{1,0:T(8,128)S(1)}, f32[120,128]{1,0:T(8,128)S(1)}, u32[]{:S(2)}, u32[]{:S(2)}) collective-permute-start(f32[120,128]{1,0:T(8,128)S(1)} %fusion.4), channel_id=1, source_target_pairs={{0,2},{1,3},{2,0},{3,1},{4,6},{5,7},{6,4},{7,5}} | collective-permute-start | bytes 184328 | tf_op jit(solution)/shard_map/ppermute | solution.py:373
  1416.7 80.8 %collective-permute-start.85 = (f32[120,128]{1,0:T(8,128)S(1)}, f32[120,128]{1,0:T(8,128)S(1)}, u32[]{:S(2)}, u32[]{:S(2)}) collective-permute-start(f32[120,128]{1,0:T(8,128)S(1)} %fusion.4), channel_id=1, source_target_pairs={{0,6},{1,7},{2,4},{3,5},{4,2},{5,3},{6,0},{7,1}} | collective-permute-start | bytes 184328 | tf_op jit(solution)/shard_map/ppermute | solution.py:373
  (114 other events, 4387.8 us)

commit v6 on v5

--- a/solution.py
+++ b/solution.py
@@ -101,7 +101,7 @@
 
 def project(units, w, block, cols, bias=None, transposed=False):
     rows, depth = units[0].shape
-    bm = rows if transposed else rows // 2
+    bm = rows // 2 if not transposed else rows if len(units) > 1 else rows // 4
     steps = rows // bm
     in_specs = [pl.BlockSpec((bm, depth), lambda i, n=n: (jnp.clip(i - n * steps, 0, steps - 1), 0))
                 for n in range(len(units))]
@@ -521,7 +521,8 @@
                     if k > 2:
                         forward(k - 2)
                         chain = take(k - 3)
-                    chain = last_add(k - 1)
+                    if k < end:
+                        chain = last_add(k - 1)
             started.append(last)
             halves.append((kept, hop(send_a, 2), hop(send_b, 4)))
             o_got.append(partner(o_p))
@@ -529,17 +530,22 @@
             bias.append(bk)
 
         rows_of = lambda arrays, s: jnp.concatenate([a[s * seq:(s + 1) * seq] for a in arrays], axis=1)
-        y_parts = []
-        held = after_chain(mine[:1] + o_got + [x_all])
+        y_moved = []
         for s in range(2):
+            held = after_chain(mine[:1] + o_got + [x_all])
             proj = dot(held[0][s * seq:(s + 1) * seq], wo_own, 1, 0) + b_out
             proj = dot(rows_of(held[1:-1], s), wo_par, 1, 0) + proj
-            y_parts.append((held[-1][:, s].reshape(seq, dim).astype(F32) + proj).astype(BF16))
-        y_moved = [exchange(y.reshape(n_dev, part, dim)) for y in y_parts]
-        chain = tuple(y_parts)
+            y = (held[-1][:, s].reshape(seq, dim).astype(F32) + proj).astype(BF16)
+            y_moved.append(exchange(y.reshape(n_dev, part, dim)))
+            chain = (y,)
+            if s == 0:
+                chain = last_add(end - 1)
         spread(end - 1)
+        chain = first_add(end)
+        chain = take(3)
+        whole = place_sums(0)
+        chain = tuple(whole)
         forward(end - 1)
-        chain = first_add(end)
 
         g_mine, = after_chain([mine[1]])
         grad_u = dot(g_mine, w_own, 1, 1)
@@ -562,19 +568,17 @@
         norm_sums = (norm_sums[0] + norm_sums[1])[:3].reshape(3 * dim)
         small = jnp.concatenate([norm_sums, gb_full]).reshape(-1, 128)
         small = small + hop(small, 1)
-        others = [hop(small, bit) for bit in (2, 4, 6)]
 
         chain = (gx,)
         forward(end)
-        chain = take(3)
-        whole = place_sums(0)
-        chain = tuple(whole)
         chain = take(4)
         y_out = interleaved(interleaved(None, after_chain([y_moved[0]])[0], 0), y_moved[1], 1)
         chain = (y_out,)
         chain = take(5)
         whole = place_sums(1)
         chain = tuple(whole)
+        small, = after_chain([small])
+        others = [hop(small, bit) for bit in (2, 4, 6)]
         whole = place_sums(2)
         chain = tuple(whole)
         near, far, across = after_chain(others)

time: 1520 us -> 1540 us (1.013)
  waiting for transfers between devices: 139 us -> 172 us
  starting transfers between devices: 166 us -> 146 us
    ppermute x86, waiting for transfers between devices: 139 us -> 172 us  [solution(): lax.ppermute(a, 'sp', [(d, d ^ bit) for d in range(n_dev)])]
    ppermute x86, starting transfers between devices: 145 us -> 118 us  [solution(): lax.ppermute(a, 'sp', [(d, d ^ bit) for d in range(n_dev)])]
    unnamed x105 -> x118, local copies, waits for them, and re-layouts: 31.6 us -> 36.4 us
  transfers between devices with their start and end apart: 91 -> 91, of which waited for: 13 -> 19; matrix products, arithmetic and copies ran while one was open for 15% -> 15% of each run, Pallas kernels for 54% -> 54%
where the time goes in v6:
time: 1540 us; the launch traced here: 1530 us
  Pallas kernels  867 us (56%)
  waiting for transfers between devices  172 us (11%)
  starting transfers between devices  146 us (9%)
  matrix products  144 us (9%)
  blocking collectives  98 us (6%)
  local copies, waits for them, and re-layouts  64.2 us (4%)
  other arithmetic  35.4 us (2%)
    pallas_call x16, Pallas kernels, project(): pl.pallas_call(functools.partial(project_kernel, len(units), steps, trans...  198 us
    pallas_call x8, Pallas kernels, weight_grads(): pl.pallas_call(kernel, grid_spec=pltpu.PrefetchScalarGridSpec(num_scalar_...  189 us
    pallas_call x14, Pallas kernels, attention(): pl.pallas_call(kernel, grid=(n_seq, n_heads), in_specs=in_specs, out_spec...  182 us
    ppermute x86, waiting for transfers between devices, solution(): lax.ppermute(a, 'sp', [(d, d ^ bit) for d in range(n_dev)])  172 us
    dot_general x6, matrix products, dot(): lax.dot_general(a, b, (((ca,), (cb,)), ((), ())), preferred_element_type=...  144 us
    ppermute x86, starting transfers between devices, solution(): lax.ppermute(a, 'sp', [(d, d ^ bit) for d in range(n_dev)])  118 us
    all_to_all x1, blocking collectives, exchange(): return lax.all_to_all(a, 'sp', 0, 0, tiled=True)  98 us
    pallas_call x3, Pallas kernels, place(): pl.pallas_call(functools.partial(place_kernel, counts, dh), grid_spec=plt...  89.8 us
  transfers between devices with their start and end apart: 91, of which 19 were waited for; matrix products, arithmetic and copies ran while one was open for 15% of the time, Pallas kernels for 54%

profile of v6, /device:TPU:1, one launch (start us, length us, event | category | flops | bytes accessed | tf_op | source)
XLA Modules:
  0.0 1528.1 jit_solution(7552682729620919691)
XLA Ops:
  0.6 98.0 %all_to_all.30.x_ref = bf16[8,2,128,2048]{3,2,1,0:T(8,128)(2,1)} all-to-all(bf16[8,2,128,2048]{3,2,1,0:T(8,128)(2,1)} %bitcast.87), channel_id=1, replica_groups=mesh['sp'=8] {'sp'}, dimensions={0} | all-to-all | bytes 16777216 | tf_op jit(solution)/shard_map/all_to_all | solution.py:388
  126.1 33.6 %lay_out_weights.2.refs_1_.refs_4_ = bf16[2048,4608]{1,0:T(8,128)(2,1)} custom-call(s32[1]{0:T(128)} %bitcast.6.core_ref, bf16[2048,3,24,128]{3,2,1,0:T(8,128)(2,1)} %w_ref.1), custom_call_target="tpu_custom_call" | custom-call | flops 3774873600 | bytes 56623104 | tf_op jit(solution)/shard_map/lay_out_weights/pallas_call | solution.py:227
  231.6 18.5 %weight_grads.8 = (f32[512,1024]{1,0:T(8,128)}, f32[512,1024]{1,0:T(8,128)}, f32[512,1024]{1,0:T(8,128)}, f32[512,1024]{1,0:T(8,128)}) custom-call(s32[8]{0:T(128)} %stack.50.order_ref, bf16[1024,2048]{1,0:T(8,128)(2,1)} %norm.2.refs_0_, bf16[1024,2048]{1,0:T(8,128)(2,1)} %collective-permute-done.refs_0_.refs_1_.refs_2_, ...), custom_call_target="tpu_custom_call" | custom-call | flops 8589934592 | bytes 33554432 | tf_op jit(solution)/shard_map/weight_grads/pallas_call | solution.py:153
  318.6 20.3 %project.24.qkv_ref = bf16[4096,768]{1,0:T(8,128)(2,1)} custom-call(bf16[1024,2048]{1,0:T(8,128)(2,1)} %norm.2.refs_0_, bf16[1024,2048]{1,0:T(8,128)(2,1)} %norm.3.refs_0_.refs_1_, bf16[1024,2048]{1,0:T(8,128)(2,1)} %collective-permute-done.refs_0_.refs_1_.refs_2_, bf16[1024,2048]{1,0:T(8,128)(2,1)} %collective-permute-done.1.refs_0_.refs_1_.refs_3_, ...), custom_call_target="tpu_custom_call" | custom-call | flops 12884901888 | bytes 23068672 | tf_op jit(solution)/shard_map/project/pallas_call | solution.py:115
  381.8 29.0 %weight_grads.11 = (f32[512,1024]{1,0:T(8,128)}, f32[512,1024]{1,0:T(8,128)}, f32[512,1024]{1,0:T(8,128)}, f32[512,1024]{1,0:T(8,128)}) custom-call(s32[8]{0:T(128)} %stack.50.order_ref, bf16[1024,2048]{1,0:T(8,128)(2,1)} %norm.2.refs_0_, bf16[1024,2048]{1,0:T(8,128)(2,1)} %norm.3.refs_0_.refs_1_, ...), custom_call_target="tpu_custom_call" | custom-call | flops 17179869184 | bytes 67108864 | tf_op jit(solution)/shard_map/weight_grads/pallas_call | solution.py:153
  412.4 20.5 %project.26.qkv_ref = bf16[4096,768]{1,0:T(8,128)(2,1)} custom-call(bf16[1024,2048]{1,0:T(8,128)(2,1)} %norm.2.refs_0_, bf16[1024,2048]{1,0:T(8,128)(2,1)} %norm.3.refs_0_.refs_1_, bf16[1024,2048]{1,0:T(8,128)(2,1)} %collective-permute-done.refs_0_.refs_1_.refs_2_, bf16[1024,2048]{1,0:T(8,128)(2,1)} %collective-permute-done.1.refs_0_.refs_1_.refs_3_, ...), custom_call_target="tpu_custom_call" | custom-call | flops 12884901888 | bytes 23068672 | tf_op jit(solution)/shard_map/project/pallas_call | solution.py:115
  489.0 29.1 %weight_grads.12 = (f32[512,1024]{1,0:T(8,128)}, f32[512,1024]{1,0:T(8,128)}, f32[512,1024]{1,0:T(8,128)}, f32[512,1024]{1,0:T(8,128)}) custom-call(s32[8]{0:T(128)} %stack.50.order_ref, bf16[1024,2048]{1,0:T(8,128)(2,1)} %norm.2.refs_0_, bf16[1024,2048]{1,0:T(8,128)(2,1)} %norm.3.refs_0_.refs_1_, ...), custom_call_target="tpu_custom_call" | custom-call | flops 17179869184 | bytes 67108864 | tf_op jit(solution)/shard_map/weight_grads/pallas_call | solution.py:153
  527.3 21.3 %collective-permute-done.11.b2 = f32[256,1024]{1,0:T(8,128)} collective-permute-done((f32[256,1024]{1,0:T(8,128)}, f32[256,1024]{1,0:T(8,128)}, u32[]{:S(2)}, u32[]{:S(2)}) %collective-permute-start.11) | collective-permute-done | bytes 1048608 | tf_op jit(solution)/shard_map/ppermute | solution.py:373
  553.9 20.5 %project.28.qkv_ref = bf16[4096,768]{1,0:T(8,128)(2,1)} custom-call(bf16[1024,2048]{1,0:T(8,128)(2,1)} %norm.2.refs_0_, bf16[1024,2048]{1,0:T(8,128)(2,1)} %norm.3.refs_0_.refs_1_, bf16[1024,2048]{1,0:T(8,128)(2,1)} %collective-permute-done.refs_0_.refs_1_.refs_2_, bf16[1024,2048]{1,0:T(8,128)(2,1)} %collective-permute-done.1.refs_0_.refs_1_.refs_3_, ...), custom_call_target="tpu_custom_call" | custom-call | flops 12884901888 | bytes 23068672 | tf_op jit(solution)/shard_map/project/pallas_call | solution.py:115
  613.1 29.4 %weight_grads.13 = (f32[512,1024]{1,0:T(8,128)}, f32[512,1024]{1,0:T(8,128)}, f32[512,1024]{1,0:T(8,128)}, f32[512,1024]{1,0:T(8,128)}) custom-call(s32[8]{0:T(128)} %stack.50.order_ref, bf16[1024,2048]{1,0:T(8,128)(2,1)} %norm.2.refs_0_, bf16[1024,2048]{1,0:T(8,128)(2,1)} %norm.3.refs_0_.refs_1_, ...), custom_call_target="tpu_custom_call" | custom-call | flops 17179869184 | bytes 67108864 | tf_op jit(solution)/shard_map/weight_grads/pallas_call | solution.py:153
  675.3 20.3 %project.29.qkv_ref = bf16[4096,768]{1,0:T(8,128)(2,1)} custom-call(bf16[1024,2048]{1,0:T(8,128)(2,1)} %norm.2.refs_0_, bf16[1024,2048]{1,0:T(8,128)(2,1)} %norm.3.refs_0_.refs_1_, bf16[1024,2048]{1,0:T(8,128)(2,1)} %collective-permute-done.refs_0_.refs_1_.refs_2_, bf16[1024,2048]{1,0:T(8,128)(2,1)} %collective-permute-done.1.refs_0_.refs_1_.refs_3_, ...), custom_call_target="tpu_custom_call" | custom-call | flops 12884901888 | bytes 23068672 | tf_op jit(solution)/shard_map/project/pallas_call | solution.py:115
  752.2 29.3 %weight_grads.14 = (f32[512,1024]{1,0:T(8,128)}, f32[512,1024]{1,0:T(8,128)}, f32[512,1024]{1,0:T(8,128)}, f32[512,1024]{1,0:T(8,128)}) custom-call(s32[8]{0:T(128)} %stack.50.order_ref, bf16[1024,2048]{1,0:T(8,128)(2,1)} %norm.2.refs_0_, bf16[1024,2048]{1,0:T(8,128)(2,1)} %norm.3.refs_0_.refs_1_, ...), custom_call_target="tpu_custom_call" | custom-call | flops 17179869184 | bytes 67108864 | tf_op jit(solution)/shard_map/weight_grads/pallas_call | solution.py:153
  786.6 26.6 %collective-permute-start.32 = (bf16[2048,256]{1,0:T(8,128)(2,1)}, bf16[2048,256]{1,0:T(8,128)(2,1)}, u32[]{:S(2)}, u32[]{:S(2)}) collective-permute-start(bf16[2048,256]{1,0:T(8,128)(2,1)} %pad_maximum_fusion.1), channel_id=1, source_target_pairs={{0,1},{1,0},{2,3},{3,2},{4,5},{5,4},{6,7},{7,6}} | collective-permute-start | bytes 3145736 | tf_op jit(solution)/shard_map/ppermute | solution.py:373
  828.8 20.5 %project.31.qkv_ref = bf16[4096,768]{1,0:T(8,128)(2,1)} custom-call(bf16[1024,2048]{1,0:T(8,128)(2,1)} %norm.2.refs_0_, bf16[1024,2048]{1,0:T(8,128)(2,1)} %norm.3.refs_0_.refs_1_, bf16[1024,2048]{1,0:T(8,128)(2,1)} %collective-permute-done.refs_0_.refs_1_.refs_2_, bf16[1024,2048]{1,0:T(8,128)(2,1)} %collective-permute-done.1.refs_0_.refs_1_.refs_3_, ...), custom_call_target="tpu_custom_call" | custom-call | flops 12884901888 | bytes 23068672 | tf_op jit(solution)/shard_map/project/pallas_call | solution.py:115
  885.5 25.8 %collective-permute-start.33 = (bf16[2048,256]{1,0:T(8,128)(2,1)S(1)}, bf16[2048,256]{1,0:T(8,128)(2,1)}, u32[]{:S(2)}, u32[]{:S(2)}) collective-permute-start(bf16[2048,256]{1,0:T(8,128)(2,1)S(1)} %copy-done.11), channel_id=1, source_target_pairs={{0,1},{1,0},{2,3},{3,2},{4,5},{5,4},{6,7},{7,6}} | collective-permute-start | bytes 3145736 | tf_op jit(solution)/shard_map/ppermute | solution.py:373
  912.4 29.7 %weight_grads.15 = (f32[512,1024]{1,0:T(8,128)}, f32[512,1024]{1,0:T(8,128)}, f32[512,1024]{1,0:T(8,128)}, f32[512,1024]{1,0:T(8,128)}) custom-call(s32[8]{0:T(128)} %stack.50.order_ref, bf16[1024,2048]{1,0:T(8,128)(2,1)} %norm.2.refs_0_, bf16[1024,2048]{1,0:T(8,128)(2,1)} %norm.3.refs_0_.refs_1_, ...), custom_call_target="tpu_custom_call" | custom-call | flops 17179869184 | bytes 67108864 | tf_op jit(solution)/shard_map/weight_grads/pallas_call | solution.py:153
  1072.3 33.6 %lay_out_weights.3 = bf16[2048,4608]{1,0:T(8,128)(2,1)} custom-call(s32[1]{0:T(128)S(6)} %sub.11.core_ref, bf16[2048,3,24,128]{3,2,1,0:T(8,128)(2,1)} %w_ref.1), custom_call_target="tpu_custom_call" | custom-call | flops 3774873600 | bytes 56623104 | tf_op jit(solution)/shard_map/lay_out_weights/pallas_call | solution.py:227
  1137.4 29.9 %place.3 = (f32[2048,3,24,128]{3,2,1,0:T(8,128)}, f32[24,128,2048]{2,1,0:T(8,128)}) custom-call(s32[1]{0:T(128)} %bitcast.6.core_ref, f32[2048,1024]{1,0:T(8,128)} %assemble.6.refs_0_, f32[2048,1024]{1,0:T(8,128)} %collective-permute-done.58.refs_1_, f32[2048,1024]{1,0:T(8,128)} %assemble.7.refs_2_, f32[2048,1024]{1,0:T(8,128)} %collective-permute-done.59.refs_3_), custom_call_target="tpu_custom_call" | custom-call | flops 8388608 | bytes 8388608 | tf_op jit(solution)/shard_map/place/pallas_call | solution.py:271
  1168.6 50.1 %fusion.7 = f32[2048,2048]{1,0:T(8,128)} fusion(bf16[2048,4608]{1,0:T(8,128)(2,1)} %get-tuple-element.546.refs_8_.refs_9_, bf16[2048,4608]{1,0:T(8,128)(2,1)} %lay_out_weights.2.refs_1_.refs_4_), kind=kOutput, calls=%fused_computation.65 | convolution fusion | flops 38654705664 | bytes 54525952 | tf_op jit(solution)/shard_map/dot_general | solution.py:20
  1271.8 50.4 %convolution_add_fusion.grad_ref = bf16[2048,2048]{1,0:T(8,128)(2,1)} fusion(f32[2048,2048]{1,0:T(8,128)} %fusion.7, bf16[2048,4608]{1,0:T(8,128)(2,1)} %constant_dynamic-update-slice_fusion, bf16[2048,4608]{1,0:T(8,128)(2,1)} %lay_out_weights.3), kind=kOutput, calls=%fused_computation | convolution fusion | flops 38663094272 | bytes 62914560 | tf_op jit(solution)/shard_map/dot_general | solution.py:20
  1352.7 31.3 %collective-permute-done.74.refs_4_ = f32[256,1024]{1,0:T(8,128)} collective-permute-done((f32[256,1024]{1,0:T(8,128)S(1)}, f32[256,1024]{1,0:T(8,128)}, u32[]{:S(2)}, u32[]{:S(2)}) %collective-permute-start.74) | collective-permute-done | bytes 1048608 | tf_op jit(solution)/shard_map/ppermute | solution.py:373
  1433.0 29.9 %place.4 = (f32[2048,3,24,128]{3,2,1,0:T(8,128)}, f32[24,128,2048]{2,1,0:T(8,128)}) custom-call(s32[1]{0:T(128)} %bitcast.6.core_ref, f32[2048,1024]{1,0:T(8,128)} %assemble.8.refs_0_, f32[2048,1024]{1,0:T(8,128)} %collective-permute-done.78.refs_1_, f32[2048,1024]{1,0:T(8,128)} %assemble.9.refs_2_, ...), custom_call_target="tpu_custom_call", output_to_operand_aliasing={{0}: (5, {}), {1}: (6, {})} | custom-call | flops 8388608 | bytes 8388608 | tf_op jit(solution)/shard_map/place/pallas_call | solution.py:271
  1465.6 29.9 %place.5 = (f32[2048,3,24,128]{3,2,1,0:T(8,128)}, f32[24,128,2048]{2,1,0:T(8,128)}) custom-call(s32[1]{0:T(128)} %bitcast.6.core_ref, f32[2048,1024]{1,0:T(8,128)} %assemble.10.refs_0_, f32[2048,1024]{1,0:T(8,128)} %collective-permute-done.80.refs_1_, f32[2048,1024]{1,0:T(8,128)} %assemble.11.refs_2_, ...), custom_call_target="tpu_custom_call", output_to_operand_aliasing={{0}: (5, {}), {1}: (6, {})} | custom-call | flops 8388608 | bytes 8388608 | tf_op jit(solution)/shard_map/place/pallas_call | solution.py:271
  1495.5 20.0 %collective-permute-done.83 = f32[120,128]{1,0:T(8,128)S(1)} collective-permute-done((f32[120,128]{1,0:T(8,128)S(1)}, f32[120,128]{1,0:T(8,128)S(1)}, u32[]{:S(2)}, u32[]{:S(2)}) %collective-permute-start.83) | collective-permute-done | bytes 61472 | tf_op jit(solution)/shard_map/ppermute | solution.py:373
  (400 shorter events, 778.6 us)
Async XLA Ops:
  380.4 101.1 %collective-permute-start.18 = (f32[256,1024]{1,0:T(8,128)}, f32[256,1024]{1,0:T(8,128)}, u32[]{:S(2)}, u32[]{:S(2)}) collective-permute-start(f32[256,1024]{1,0:T(8,128)} %get-tuple-element.409.refs_0_), channel_id=1, source_target_pairs={{0,4},{1,5},{2,6},{3,7},{4,0},{5,1},{6,2},{7,3}} | collective-permute-start | bytes 3145736 | tf_op jit(solution)/shard_map/ppermute | solution.py:373
  380.7 101.8 %collective-permute-start.19 = (f32[256,1024]{1,0:T(8,128)}, f32[256,1024]{1,0:T(8,128)S(1)}, u32[]{:S(2)}, u32[]{:S(2)}) collective-permute-start(f32[256,1024]{1,0:T(8,128)} %get-tuple-element.410.refs_1_), channel_id=1, source_target_pairs={{0,2},{1,3},{2,0},{3,1},{4,6},{5,7},{6,4},{7,5}} | collective-permute-start | bytes 3145736 | tf_op jit(solution)/shard_map/ppermute | solution.py:373
  481.1 129.3 %collective-permute-start.20 = (f32[256,1024]{1,0:T(8,128)}, f32[256,1024]{1,0:T(8,128)}, u32[]{:S(2)}, u32[]{:S(2)}) collective-permute-start(f32[256,1024]{1,0:T(8,128)} %get-tuple-element.409.refs_0_), channel_id=1, source_target_pairs={{0,2},{1,3},{2,0},{3,1},{4,6},{5,7},{6,4},{7,5}} | collective-permute-start | bytes 3145736 | tf_op jit(solution)/shard_map/ppermute | solution.py:373
  481.5 130.3 %collective-permute-start.21 = (f32[256,1024]{1,0:T(8,128)}, f32[256,1024]{1,0:T(8,128)}, u32[]{:S(2)}, u32[]{:S(2)}) collective-permute-start(f32[256,1024]{1,0:T(8,128)} %get-tuple-element.410.refs_1_), channel_id=1, source_target_pairs={{0,4},{1,5},{2,6},{3,7},{4,0},{5,1},{6,2},{7,3}} | collective-permute-start | bytes 3145736 | tf_op jit(solution)/shard_map/ppermute | solution.py:373
  482.5 129.3 %collective-permute-start.22 = (f32[256,1024]{1,0:T(8,128)}, f32[256,1024]{1,0:T(8,128)}, u32[]{:S(2)}, u32[]{:S(2)}) collective-permute-start(f32[256,1024]{1,0:T(8,128)} %collective-permute-done.18.refs_2_), channel_id=1, source_target_pairs={{0,2},{1,3},{2,0},{3,1},{4,6},{5,7},{6,4},{7,5}} | collective-permute-start | bytes 3145736 | tf_op jit(solution)/shard_map/ppermute | solution.py:373
  642.5 106.8 %collective-permute-start.28 = (f32[256,1024]{1,0:T(8,128)S(1)}, f32[256,1024]{1,0:T(8,128)}, u32[]{:S(2)}, u32[]{:S(2)}) collective-permute-start(f32[256,1024]{1,0:T(8,128)S(1)} %copy-done.15), channel_id=1, source_target_pairs={{0,2},{1,3},{2,0},{3,1},{4,6},{5,7},{6,4},{7,5}} | collective-permute-start | bytes 3145736 | tf_op jit(solution)/shard_map/ppermute | solution.py:373
  646.0 104.1 %collective-permute-start.29 = (f32[256,1024]{1,0:T(8,128)}, f32[256,1024]{1,0:T(8,128)}, u32[]{:S(2)}, u32[]{:S(2)}) collective-permute-start(f32[256,1024]{1,0:T(8,128)} %get-tuple-element.449.refs_1_), channel_id=1, source_target_pairs={{0,4},{1,5},{2,6},{3,7},{4,0},{5,1},{6,2},{7,3}} | collective-permute-start | bytes 3145736 | tf_op jit(solution)/shard_map/ppermute | solution.py:373
  647.3 96.9 %collective-permute-start.14 = (f32[512,1024]{1,0:T(8,128)}, f32[512,1024]{1,0:T(8,128)S(1)}, u32[]{:S(2)}, u32[]{:S(2)}) collective-permute-start(f32[512,1024]{1,0:T(8,128)} %get-tuple-element.403), channel_id=1, source_target_pairs={{0,2},{1,3},{2,0},{3,1},{4,6},{5,7},{6,4},{7,5}} | collective-permute-start | bytes 6291464 | tf_op jit(solution)/shard_map/ppermute | solution.py:373
  786.6 98.9 %collective-permute-start.32 = (bf16[2048,256]{1,0:T(8,128)(2,1)}, bf16[2048,256]{1,0:T(8,128)(2,1)}, u32[]{:S(2)}, u32[]{:S(2)}) collective-permute-start(bf16[2048,256]{1,0:T(8,128)(2,1)} %pad_maximum_fusion.1), channel_id=1, source_target_pairs={{0,1},{1,0},{2,3},{3,2},{4,5},{5,4},{6,7},{7,6}} | collective-permute-start | bytes 3145736 | tf_op jit(solution)/shard_map/ppermute | solution.py:373
  822.2 89.2 %collective-permute-start.44 = (f32[256,1024]{1,0:T(8,128)}, f32[256,1024]{1,0:T(8,128)}, u32[]{:S(2)}, u32[]{:S(2)}) collective-permute-start(f32[256,1024]{1,0:T(8,128)} %get-tuple-element.488.refs_0_), channel_id=1, source_target_pairs={{0,2},{1,3},{2,0},{3,1},{4,6},{5,7},{6,4},{7,5}} | collective-permute-start | bytes 3145736 | tf_op jit(solution)/shard_map/ppermute | solution.py:373
  822.6 88.7 %collective-permute-start.45 = (f32[256,1024]{1,0:T(8,128)}, f32[256,1024]{1,0:T(8,128)}, u32[]{:S(2)}, u32[]{:S(2)}) collective-permute-start(f32[256,1024]{1,0:T(8,128)} %get-tuple-element.489.refs_1_), channel_id=1, source_target_pairs={{0,4},{1,5},{2,6},{3,7},{4,0},{5,1},{6,2},{7,3}} | collective-permute-start | bytes 3145736 | tf_op jit(solution)/shard_map/ppermute | solution.py:373
  950.9 186.0 %collective-permute-start.58 = (f32[2048,1024]{1,0:T(8,128)}, f32[2048,1024]{1,0:T(8,128)}, u32[]{:S(2)}, u32[]{:S(2)}) collective-permute-start(f32[2048,1024]{1,0:T(8,128)} %assemble.6.refs_0_), channel_id=1, source_target_pairs={{0,1},{1,0},{2,3},{3,2},{4,5},{5,4},{6,7},{7,6}} | collective-permute-start | bytes 25165832 | tf_op jit(solution)/shard_map/ppermute | solution.py:373
  951.4 185.7 %collective-permute-start.59 = (f32[2048,1024]{1,0:T(8,128)}, f32[2048,1024]{1,0:T(8,128)}, u32[]{:S(2)}, u32[]{:S(2)}) collective-permute-start(f32[2048,1024]{1,0:T(8,128)} %assemble.7.refs_2_), channel_id=1, source_target_pairs={{0,1},{1,0},{2,3},{3,2},{4,5},{5,4},{6,7},{7,6}} | collective-permute-start | bytes 25165832 | tf_op jit(solution)/shard_map/ppermute | solution.py:373
  1071.7 95.6 %collective-permute-start.70 = (f32[256,1024]{1,0:T(8,128)}, f32[256,1024]{1,0:T(8,128)}, u32[]{:S(2)}, u32[]{:S(2)}) collective-permute-start(f32[256,1024]{1,0:T(8,128)} %get-tuple-element.607), channel_id=1, source_target_pairs={{0,4},{1,5},{2,6},{3,7},{4,0},{5,1},{6,2},{7,3}} | collective-permute-start | bytes 3145736 | tf_op jit(solution)/shard_map/ppermute | solution.py:373
  1116.6 132.6 %all-to-all-start.4 = ((bf16[8,128,2048]{2,1,0:T(8,128)(2,1)}), bf16[8,128,2048]{2,1,0:T(8,128)(2,1)}, u32[]{:S(2)}, u32[]{:S(2)}) async-start(bf16[8,128,2048]{2,1,0:T(8,128)(2,1)} %bitcast.92), calls=%async_computation.4 | async-start | bytes 8388608 | tf_op jit(solution)/shard_map/all_to_all | solution.py:388
  1127.5 97.5 %collective-permute-start.66 = (bf16[2048,768]{1,0:T(8,128)(2,1)S(1)}, bf16[2048,768]{1,0:T(8,128)(2,1)}, u32[]{:S(2)}, u32[]{:S(2)}) collective-permute-start(bf16[2048,768]{1,0:T(8,128)(2,1)S(1)} %copy-done.3), channel_id=1, source_target_pairs={{0,1},{1,0},{2,3},{3,2},{4,5},{5,4},{6,7},{7,6}} | collective-permute-start | bytes 9437192 | tf_op jit(solution)/shard_map/ppermute | solution.py:373
  1127.7 97.5 %collective-permute-start.67 = (bf16[2048,768]{1,0:T(8,128)(2,1)}, bf16[2048,768]{1,0:T(8,128)(2,1)}, u32[]{:S(2)}, u32[]{:S(2)}) collective-permute-start(bf16[2048,768]{1,0:T(8,128)(2,1)} %get-tuple-element.398.refs_10_.refs_11_), channel_id=1, source_target_pairs={{0,1},{1,0},{2,3},{3,2},{4,5},{5,4},{6,7},{7,6}} | collective-permute-start | bytes 9437192 | tf_op jit(solution)/shard_map/ppermute | solution.py:373
  1137.0 101.2 %collective-permute-start.69 = (bf16[2048,768]{1,0:T(8,128)(2,1)}, bf16[2048,768]{1,0:T(8,128)(2,1)}, u32[]{:S(2)}, u32[]{:S(2)}) collective-permute-start(bf16[2048,768]{1,0:T(8,128)(2,1)} %get-tuple-element.486.refs_10_.refs_11_), channel_id=1, source_target_pairs={{0,1},{1,0},{2,3},{3,2},{4,5},{5,4},{6,7},{7,6}} | collective-permute-start | bytes 9437192 | tf_op jit(solution)/shard_map/ppermute | solution.py:373
  1238.2 107.4 %collective-permute-start.60 = (f32[256,1024]{1,0:T(8,128)}, f32[256,1024]{1,0:T(8,128)}, u32[]{:S(2)}, u32[]{:S(2)}) collective-permute-start(f32[256,1024]{1,0:T(8,128)} %get-tuple-element.557.refs_0_), channel_id=1, source_target_pairs={{0,2},{1,3},{2,0},{3,1},{4,6},{5,7},{6,4},{7,5}} | collective-permute-start | bytes 3145736 | tf_op jit(solution)/shard_map/ppermute | solution.py:373
  1243.0 103.0 %collective-permute-start.61 = (f32[256,1024]{1,0:T(8,128)S(1)}, f32[256,1024]{1,0:T(8,128)}, u32[]{:S(2)}, u32[]{:S(2)}) collective-permute-start(f32[256,1024]{1,0:T(8,128)S(1)} %copy-done.14), channel_id=1, source_target_pairs={{0,4},{1,5},{2,6},{3,7},{4,0},{5,1},{6,2},{7,3}} | collective-permute-start | bytes 3145736 | tf_op jit(solution)/shard_map/ppermute | solution.py:373
  1249.0 98.1 %collective-permute-start.62 = (f32[256,1024]{1,0:T(8,128)}, f32[256,1024]{1,0:T(8,128)}, u32[]{:S(2)}, u32[]{:S(2)}) collective-permute-start(f32[256,1024]{1,0:T(8,128)} %collective-permute-done.48.refs_2_), channel_id=1, source_target_pairs={{0,2},{1,3},{2,0},{3,1},{4,6},{5,7},{6,4},{7,5}} | collective-permute-start | bytes 3145736 | tf_op jit(solution)/shard_map/ppermute | solution.py:373
  1249.9 150.7 %all-to-all-start.3 = ((bf16[8,128,2048]{2,1,0:T(8,128)(2,1)}), bf16[8,128,2048]{2,1,0:T(8,128)(2,1)}, u32[]{:S(2)}, u32[]{:S(2)}) async-start(bf16[8,128,2048]{2,1,0:T(8,128)(2,1)} %bitcast.91), calls=%async_computation.3 | async-start | bytes 8388608 | tf_op jit(solution)/shard_map/all_to_all | solution.py:388
  1271.6 112.4 %collective-permute-start.74 = (f32[256,1024]{1,0:T(8,128)S(1)}, f32[256,1024]{1,0:T(8,128)}, u32[]{:S(2)}, u32[]{:S(2)}) collective-permute-start(f32[256,1024]{1,0:T(8,128)S(1)} %copy-done.17), channel_id=1, source_target_pairs={{0,2},{1,3},{2,0},{3,1},{4,6},{5,7},{6,4},{7,5}} | collective-permute-start | bytes 3145736 | tf_op jit(solution)/shard_map/ppermute | solution.py:373
  1418.3 100.6 %all-to-all-start.5 = ((bf16[8,2,128,2048]{3,2,1,0:T(8,128)(2,1)}), bf16[8,2,128,2048]{3,2,1,0:T(8,128)(2,1)}, u32[]{:S(2)}, u32[]{:S(2)}) async-start(bf16[8,2,128,2048]{3,2,1,0:T(8,128)(2,1)} %get-tuple-element.556), calls=%async_computation.5 | async-start | bytes 16777216 | tf_op jit(solution)/shard_map/all_to_all | solution.py:388
  (120 other events, 4359.6 us)

commit v7 on v6

--- a/solution.py
+++ b/solution.py
@@ -101,7 +101,7 @@
 
 def project(units, w, block, cols, bias=None, transposed=False):
     rows, depth = units[0].shape
-    bm = rows // 2 if not transposed else rows if len(units) > 1 else rows // 4
+    bm = rows if transposed else rows // 2
     steps = rows // bm
     in_specs = [pl.BlockSpec((bm, depth), lambda i, n=n: (jnp.clip(i - n * steps, 0, steps - 1), 0))
                 for n in range(len(units))]
@@ -572,16 +572,15 @@
         chain = (gx,)
         forward(end)
         chain = take(4)
+        whole = place_sums(1)
+        chain = tuple(whole)
+        chain = take(5)
         y_out = interleaved(interleaved(None, after_chain([y_moved[0]])[0], 0), y_moved[1], 1)
         chain = (y_out,)
-        chain = take(5)
-        whole = place_sums(1)
-        chain = tuple(whole)
+        whole = place_sums(2)
+        chain = tuple(whole) + (gx_moved,)
         small, = after_chain([small])
-        others = [hop(small, bit) for bit in (2, 4, 6)]
-        whole = place_sums(2)
-        chain = tuple(whole)
-        near, far, across = after_chain(others)
+        near, far, across = [hop(small, bit) for bit in (2, 4, 6)]
         small = (small + near) + (far + across)
         grad_x = copied(after_chain([gx_moved])[0].reshape(batch, part, dim))
         grad_w_qkv, grad_w_out = whole

time: 1540 us -> 1550 us (level)
    all_to_all x5, waiting for transfers between devices: 0.01 us -> 40.1 us  [exchange(): return lax.all_to_all(a, 'sp', 0, 0, tiled=True)]
    ppermute x86, waiting for transfers between devices: 172 us -> 136 us  [solution(): lax.ppermute(a, 'sp', [(d, d ^ bit) for d in range(n_dev)])]
  transfers between devices with their start and end apart: 91 -> 91, of which waited for: 19 -> 16; matrix products, arithmetic and copies ran while one was open for 15% -> 15% of each run, Pallas kernels for 54% -> 54%
where the time goes in v7:
time: 1550 us; the launch traced here: 1530 us
  Pallas kernels  864 us (56%)
  waiting for transfers between devices  176 us (11%)
  starting transfers between devices  151 us (10%)
  matrix products  144 us (9%)
  blocking collectives  98 us (6%)
  local copies, waits for them, and re-layouts  63 us (4%)
  other arithmetic  35.2 us (2%)
    pallas_call x16, Pallas kernels, project(): pl.pallas_call(functools.partial(project_kernel, len(units), steps, trans...  196 us
    pallas_call x8, Pallas kernels, weight_grads(): pl.pallas_call(kernel, grid_spec=pltpu.PrefetchScalarGridSpec(num_scalar_...  189 us
    pallas_call x14, Pallas kernels, attention(): pl.pallas_call(kernel, grid=(n_seq, n_heads), in_specs=in_specs, out_spec...  182 us
    dot_general x6, matrix products, dot(): lax.dot_general(a, b, (((ca,), (cb,)), ((), ())), preferred_element_type=...  144 us
    ppermute x86, waiting for transfers between devices, solution(): lax.ppermute(a, 'sp', [(d, d ^ bit) for d in range(n_dev)])  136 us
    ppermute x86, starting transfers between devices, solution(): lax.ppermute(a, 'sp', [(d, d ^ bit) for d in range(n_dev)])  122 us
    all_to_all x1, blocking collectives, exchange(): return lax.all_to_all(a, 'sp', 0, 0, tiled=True)  98 us
    pallas_call x3, Pallas kernels, place(): pl.pallas_call(functools.partial(place_kernel, counts, dh), grid_spec=plt...  89.9 us
  transfers between devices with their start and end apart: 91, of which 16 were waited for; matrix products, arithmetic and copies ran while one was open for 15% of the time, Pallas kernels for 54%

profile of v7, /device:TPU:1, one launch (start us, length us, event | category | flops | bytes accessed | tf_op | source)
XLA Modules:
  0.0 1532.3 jit_solution(12334558710210754425)
XLA Ops:
  0.6 98.0 %all_to_all.30.x_ref = bf16[8,2,128,2048]{3,2,1,0:T(8,128)(2,1)} all-to-all(bf16[8,2,128,2048]{3,2,1,0:T(8,128)(2,1)} %bitcast.87), channel_id=1, replica_groups=mesh['sp'=8] {'sp'}, dimensions={0} | all-to-all | bytes 16777216 | tf_op jit(solution)/shard_map/all_to_all | solution.py:388
  126.1 33.6 %lay_out_weights.2.refs_1_.refs_4_ = bf16[2048,4608]{1,0:T(8,128)(2,1)} custom-call(s32[1]{0:T(128)} %bitcast.6.core_ref, bf16[2048,3,24,128]{3,2,1,0:T(8,128)(2,1)} %w_ref.1), custom_call_target="tpu_custom_call" | custom-call | flops 3774873600 | bytes 56623104 | tf_op jit(solution)/shard_map/lay_out_weights/pallas_call | solution.py:227
  230.6 18.5 %weight_grads.8 = (f32[512,1024]{1,0:T(8,128)}, f32[512,1024]{1,0:T(8,128)}, f32[512,1024]{1,0:T(8,128)}, f32[512,1024]{1,0:T(8,128)}) custom-call(s32[8]{0:T(128)} %stack.50.order_ref, bf16[1024,2048]{1,0:T(8,128)(2,1)} %norm.2.refs_0_, bf16[1024,2048]{1,0:T(8,128)(2,1)} %collective-permute-done.refs_0_.refs_1_.refs_2_, ...), custom_call_target="tpu_custom_call" | custom-call | flops 8589934592 | bytes 33554432 | tf_op jit(solution)/shard_map/weight_grads/pallas_call | solution.py:153
  316.2 20.3 %project.24.qkv_ref = bf16[4096,768]{1,0:T(8,128)(2,1)} custom-call(bf16[1024,2048]{1,0:T(8,128)(2,1)} %norm.2.refs_0_, bf16[1024,2048]{1,0:T(8,128)(2,1)} %norm.3.refs_0_.refs_1_, bf16[1024,2048]{1,0:T(8,128)(2,1)} %collective-permute-done.refs_0_.refs_1_.refs_2_, bf16[1024,2048]{1,0:T(8,128)(2,1)} %collective-permute-done.1.refs_0_.refs_1_.refs_3_, ...), custom_call_target="tpu_custom_call" | custom-call | flops 12884901888 | bytes 23068672 | tf_op jit(solution)/shard_map/project/pallas_call | solution.py:115
  379.5 29.0 %weight_grads.11 = (f32[512,1024]{1,0:T(8,128)}, f32[512,1024]{1,0:T(8,128)}, f32[512,1024]{1,0:T(8,128)}, f32[512,1024]{1,0:T(8,128)}) custom-call(s32[8]{0:T(128)} %stack.50.order_ref, bf16[1024,2048]{1,0:T(8,128)(2,1)} %norm.2.refs_0_, bf16[1024,2048]{1,0:T(8,128)(2,1)} %norm.3.refs_0_.refs_1_, ...), custom_call_target="tpu_custom_call" | custom-call | flops 17179869184 | bytes 67108864 | tf_op jit(solution)/shard_map/weight_grads/pallas_call | solution.py:153
  410.2 20.5 %project.26.qkv_ref = bf16[4096,768]{1,0:T(8,128)(2,1)} custom-call(bf16[1024,2048]{1,0:T(8,128)(2,1)} %norm.2.refs_0_, bf16[1024,2048]{1,0:T(8,128)(2,1)} %norm.3.refs_0_.refs_1_, bf16[1024,2048]{1,0:T(8,128)(2,1)} %collective-permute-done.refs_0_.refs_1_.refs_2_, bf16[1024,2048]{1,0:T(8,128)(2,1)} %collective-permute-done.1.refs_0_.refs_1_.refs_3_, ...), custom_call_target="tpu_custom_call" | custom-call | flops 12884901888 | bytes 23068672 | tf_op jit(solution)/shard_map/project/pallas_call | solution.py:115
  486.8 29.2 %weight_grads.12 = (f32[512,1024]{1,0:T(8,128)}, f32[512,1024]{1,0:T(8,128)}, f32[512,1024]{1,0:T(8,128)}, f32[512,1024]{1,0:T(8,128)}) custom-call(s32[8]{0:T(128)} %stack.50.order_ref, bf16[1024,2048]{1,0:T(8,128)(2,1)} %norm.2.refs_0_, bf16[1024,2048]{1,0:T(8,128)(2,1)} %norm.3.refs_0_.refs_1_, ...), custom_call_target="tpu_custom_call" | custom-call | flops 17179869184 | bytes 67108864 | tf_op jit(solution)/shard_map/weight_grads/pallas_call | solution.py:153
  525.1 21.3 %collective-permute-done.11.b2 = f32[256,1024]{1,0:T(8,128)} collective-permute-done((f32[256,1024]{1,0:T(8,128)}, f32[256,1024]{1,0:T(8,128)}, u32[]{:S(2)}, u32[]{:S(2)}) %collective-permute-start.11) | collective-permute-done | bytes 1048608 | tf_op jit(solution)/shard_map/ppermute | solution.py:373
  551.7 20.5 %project.28.qkv_ref = bf16[4096,768]{1,0:T(8,128)(2,1)} custom-call(bf16[1024,2048]{1,0:T(8,128)(2,1)} %norm.2.refs_0_, bf16[1024,2048]{1,0:T(8,128)(2,1)} %norm.3.refs_0_.refs_1_, bf16[1024,2048]{1,0:T(8,128)(2,1)} %collective-permute-done.refs_0_.refs_1_.refs_2_, bf16[1024,2048]{1,0:T(8,128)(2,1)} %collective-permute-done.1.refs_0_.refs_1_.refs_3_, ...), custom_call_target="tpu_custom_call" | custom-call | flops 12884901888 | bytes 23068672 | tf_op jit(solution)/shard_map/project/pallas_call | solution.py:115
  610.9 29.4 %weight_grads.13 = (f32[512,1024]{1,0:T(8,128)}, f32[512,1024]{1,0:T(8,128)}, f32[512,1024]{1,0:T(8,128)}, f32[512,1024]{1,0:T(8,128)}) custom-call(s32[8]{0:T(128)} %stack.50.order_ref, bf16[1024,2048]{1,0:T(8,128)(2,1)} %norm.2.refs_0_, bf16[1024,2048]{1,0:T(8,128)(2,1)} %norm.3.refs_0_.refs_1_, ...), custom_call_target="tpu_custom_call" | custom-call | flops 17179869184 | bytes 67108864 | tf_op jit(solution)/shard_map/weight_grads/pallas_call | solution.py:153
  672.8 20.3 %project.29.qkv_ref = bf16[4096,768]{1,0:T(8,128)(2,1)} custom-call(bf16[1024,2048]{1,0:T(8,128)(2,1)} %norm.2.refs_0_, bf16[1024,2048]{1,0:T(8,128)(2,1)} %norm.3.refs_0_.refs_1_, bf16[1024,2048]{1,0:T(8,128)(2,1)} %collective-permute-done.refs_0_.refs_1_.refs_2_, bf16[1024,2048]{1,0:T(8,128)(2,1)} %collective-permute-done.1.refs_0_.refs_1_.refs_3_, ...), custom_call_target="tpu_custom_call" | custom-call | flops 12884901888 | bytes 23068672 | tf_op jit(solution)/shard_map/project/pallas_call | solution.py:115
  749.5 29.2 %weight_grads.14 = (f32[512,1024]{1,0:T(8,128)}, f32[512,1024]{1,0:T(8,128)}, f32[512,1024]{1,0:T(8,128)}, f32[512,1024]{1,0:T(8,128)}) custom-call(s32[8]{0:T(128)} %stack.50.order_ref, bf16[1024,2048]{1,0:T(8,128)(2,1)} %norm.2.refs_0_, bf16[1024,2048]{1,0:T(8,128)(2,1)} %norm.3.refs_0_.refs_1_, ...), custom_call_target="tpu_custom_call" | custom-call | flops 17179869184 | bytes 67108864 | tf_op jit(solution)/shard_map/weight_grads/pallas_call | solution.py:153
  784.2 26.6 %collective-permute-start.32 = (bf16[2048,256]{1,0:T(8,128)(2,1)}, bf16[2048,256]{1,0:T(8,128)(2,1)}, u32[]{:S(2)}, u32[]{:S(2)}) collective-permute-start(bf16[2048,256]{1,0:T(8,128)(2,1)} %pad_maximum_fusion.1), channel_id=1, source_target_pairs={{0,1},{1,0},{2,3},{3,2},{4,5},{5,4},{6,7},{7,6}} | collective-permute-start | bytes 3145736 | tf_op jit(solution)/shard_map/ppermute | solution.py:373
  826.4 20.5 %project.31.qkv_ref = bf16[4096,768]{1,0:T(8,128)(2,1)} custom-call(bf16[1024,2048]{1,0:T(8,128)(2,1)} %norm.2.refs_0_, bf16[1024,2048]{1,0:T(8,128)(2,1)} %norm.3.refs_0_.refs_1_, bf16[1024,2048]{1,0:T(8,128)(2,1)} %collective-permute-done.refs_0_.refs_1_.refs_2_, bf16[1024,2048]{1,0:T(8,128)(2,1)} %collective-permute-done.1.refs_0_.refs_1_.refs_3_, ...), custom_call_target="tpu_custom_call" | custom-call | flops 12884901888 | bytes 23068672 | tf_op jit(solution)/shard_map/project/pallas_call | solution.py:115
  883.0 26.0 %collective-permute-start.33 = (bf16[2048,256]{1,0:T(8,128)(2,1)S(1)}, bf16[2048,256]{1,0:T(8,128)(2,1)}, u32[]{:S(2)}, u32[]{:S(2)}) collective-permute-start(bf16[2048,256]{1,0:T(8,128)(2,1)S(1)} %copy-done.11), channel_id=1, source_target_pairs={{0,1},{1,0},{2,3},{3,2},{4,5},{5,4},{6,7},{7,6}} | collective-permute-start | bytes 3145736 | tf_op jit(solution)/shard_map/ppermute | solution.py:373
  910.0 29.4 %weight_grads.15 = (f32[512,1024]{1,0:T(8,128)}, f32[512,1024]{1,0:T(8,128)}, f32[512,1024]{1,0:T(8,128)}, f32[512,1024]{1,0:T(8,128)}) custom-call(s32[8]{0:T(128)} %stack.50.order_ref, bf16[1024,2048]{1,0:T(8,128)(2,1)} %norm.2.refs_0_, bf16[1024,2048]{1,0:T(8,128)(2,1)} %norm.3.refs_0_.refs_1_, ...), custom_call_target="tpu_custom_call" | custom-call | flops 17179869184 | bytes 67108864 | tf_op jit(solution)/shard_map/weight_grads/pallas_call | solution.py:153
  1069.8 33.6 %lay_out_weights.3 = bf16[2048,4608]{1,0:T(8,128)(2,1)} custom-call(s32[1]{0:T(128)S(6)} %sub.11.core_ref, bf16[2048,3,24,128]{3,2,1,0:T(8,128)(2,1)} %w_ref.1), custom_call_target="tpu_custom_call" | custom-call | flops 3774873600 | bytes 56623104 | tf_op jit(solution)/shard_map/lay_out_weights/pallas_call | solution.py:227
  1134.7 29.9 %place.3 = (f32[2048,3,24,128]{3,2,1,0:T(8,128)}, f32[24,128,2048]{2,1,0:T(8,128)}) custom-call(s32[1]{0:T(128)} %bitcast.6.core_ref, f32[2048,1024]{1,0:T(8,128)} %assemble.6.refs_0_, f32[2048,1024]{1,0:T(8,128)} %collective-permute-done.58.refs_1_, f32[2048,1024]{1,0:T(8,128)} %assemble.7.refs_2_, f32[2048,1024]{1,0:T(8,128)} %collective-permute-done.59.refs_3_), custom_call_target="tpu_custom_call" | custom-call | flops 8388608 | bytes 8388608 | tf_op jit(solution)/shard_map/place/pallas_call | solution.py:271
  1166.0 50.1 %fusion.7 = f32[2048,2048]{1,0:T(8,128)} fusion(bf16[2048,4608]{1,0:T(8,128)(2,1)} %get-tuple-element.537.refs_8_.refs_9_, bf16[2048,4608]{1,0:T(8,128)(2,1)} %lay_out_weights.2.refs_1_.refs_4_), kind=kOutput, calls=%fused_computation.65 | convolution fusion | flops 38654705664 | bytes 54525952 | tf_op jit(solution)/shard_map/dot_general | solution.py:20
  1272.4 19.0 %collective-permute-done.61.refs_3_ = f32[256,1024]{1,0:T(8,128)S(1)} collective-permute-done((f32[256,1024]{1,0:T(8,128)}, f32[256,1024]{1,0:T(8,128)S(1)}, u32[]{:S(2)}, u32[]{:S(2)}) %collective-permute-start.61) | collective-permute-done | bytes 1048608 | tf_op jit(solution)/shard_map/ppermute | solution.py:373
  1291.6 50.6 %convolution_add_fusion.grad_ref = bf16[2048,2048]{1,0:T(8,128)(2,1)} fusion(f32[2048,2048]{1,0:T(8,128)} %fusion.7, bf16[2048,4608]{1,0:T(8,128)(2,1)} %constant_dynamic-update-slice_fusion, bf16[2048,4608]{1,0:T(8,128)(2,1)} %lay_out_weights.3), kind=kOutput, calls=%fused_computation | convolution fusion | flops 38663094272 | bytes 62914560 | tf_op jit(solution)/shard_map/dot_general | solution.py:20
  1381.7 30.1 %place.4 = (f32[2048,3,24,128]{3,2,1,0:T(8,128)}, f32[24,128,2048]{2,1,0:T(8,128)}) custom-call(s32[1]{0:T(128)} %bitcast.6.core_ref, f32[2048,1024]{1,0:T(8,128)} %assemble.8.refs_0_, f32[2048,1024]{1,0:T(8,128)} %collective-permute-done.78.refs_1_, f32[2048,1024]{1,0:T(8,128)} %assemble.9.refs_2_, ...), custom_call_target="tpu_custom_call", output_to_operand_aliasing={{0}: (5, {}), {1}: (6, {})} | custom-call | flops 8388608 | bytes 8388608 | tf_op jit(solution)/shard_map/place/pallas_call | solution.py:271
  1447.3 29.9 %place.5 = (f32[2048,3,24,128]{3,2,1,0:T(8,128)}, f32[24,128,2048]{2,1,0:T(8,128)}) custom-call(s32[1]{0:T(128)} %bitcast.6.core_ref, f32[2048,1024]{1,0:T(8,128)} %assemble.10.refs_0_, f32[2048,1024]{1,0:T(8,128)} %collective-permute-done.80.refs_1_, f32[2048,1024]{1,0:T(8,128)} %assemble.11.refs_2_, ...), custom_call_target="tpu_custom_call", output_to_operand_aliasing={{0}: (5, {}), {1}: (6, {})} | custom-call | flops 8388608 | bytes 8388608 | tf_op jit(solution)/shard_map/place/pallas_call | solution.py:271
  1477.2 40.1 %all-to-all-done.5 = bf16[8,2,128,2048]{3,2,1,0:T(8,128)(2,1)} async-done(((bf16[8,2,128,2048]{3,2,1,0:T(8,128)(2,1)}), bf16[8,2,128,2048]{3,2,1,0:T(8,128)(2,1)}, u32[]{:S(2)}, u32[]{:S(2)}) %all-to-all-start.5) | async-done | bytes 8388640 | tf_op jit(solution)/shard_map/all_to_all | solution.py:388
  (400 shorter events, 774.8 us)
Async XLA Ops:
  378.3 101.1 %collective-permute-start.18 = (f32[256,1024]{1,0:T(8,128)}, f32[256,1024]{1,0:T(8,128)}, u32[]{:S(2)}, u32[]{:S(2)}) collective-permute-start(f32[256,1024]{1,0:T(8,128)} %get-tuple-element.406.refs_0_), channel_id=1, source_target_pairs={{0,4},{1,5},{2,6},{3,7},{4,0},{5,1},{6,2},{7,3}} | collective-permute-start | bytes 3145736 | tf_op jit(solution)/shard_map/ppermute | solution.py:373
  378.5 101.6 %collective-permute-start.19 = (f32[256,1024]{1,0:T(8,128)}, f32[256,1024]{1,0:T(8,128)S(1)}, u32[]{:S(2)}, u32[]{:S(2)}) collective-permute-start(f32[256,1024]{1,0:T(8,128)} %get-tuple-element.407.refs_1_), channel_id=1, source_target_pairs={{0,2},{1,3},{2,0},{3,1},{4,6},{5,7},{6,4},{7,5}} | collective-permute-start | bytes 3145736 | tf_op jit(solution)/shard_map/ppermute | solution.py:373
  478.9 129.3 %collective-permute-start.20 = (f32[256,1024]{1,0:T(8,128)}, f32[256,1024]{1,0:T(8,128)}, u32[]{:S(2)}, u32[]{:S(2)}) collective-permute-start(f32[256,1024]{1,0:T(8,128)} %get-tuple-element.406.refs_0_), channel_id=1, source_target_pairs={{0,2},{1,3},{2,0},{3,1},{4,6},{5,7},{6,4},{7,5}} | collective-permute-start | bytes 3145736 | tf_op jit(solution)/shard_map/ppermute | solution.py:373
  479.3 130.0 %collective-permute-start.21 = (f32[256,1024]{1,0:T(8,128)}, f32[256,1024]{1,0:T(8,128)}, u32[]{:S(2)}, u32[]{:S(2)}) collective-permute-start(f32[256,1024]{1,0:T(8,128)} %get-tuple-element.407.refs_1_), channel_id=1, source_target_pairs={{0,4},{1,5},{2,6},{3,7},{4,0},{5,1},{6,2},{7,3}} | collective-permute-start | bytes 3145736 | tf_op jit(solution)/shard_map/ppermute | solution.py:373
  480.1 129.3 %collective-permute-start.22 = (f32[256,1024]{1,0:T(8,128)}, f32[256,1024]{1,0:T(8,128)}, u32[]{:S(2)}, u32[]{:S(2)}) collective-permute-start(f32[256,1024]{1,0:T(8,128)} %collective-permute-done.18.refs_2_), channel_id=1, source_target_pairs={{0,2},{1,3},{2,0},{3,1},{4,6},{5,7},{6,4},{7,5}} | collective-permute-start | bytes 3145736 | tf_op jit(solution)/shard_map/ppermute | solution.py:373
  640.3 106.3 %collective-permute-start.28 = (f32[256,1024]{1,0:T(8,128)S(1)}, f32[256,1024]{1,0:T(8,128)}, u32[]{:S(2)}, u32[]{:S(2)}) collective-permute-start(f32[256,1024]{1,0:T(8,128)S(1)} %copy-done.15), channel_id=1, source_target_pairs={{0,2},{1,3},{2,0},{3,1},{4,6},{5,7},{6,4},{7,5}} | collective-permute-start | bytes 3145736 | tf_op jit(solution)/shard_map/ppermute | solution.py:373
  643.8 104.1 %collective-permute-start.29 = (f32[256,1024]{1,0:T(8,128)}, f32[256,1024]{1,0:T(8,128)}, u32[]{:S(2)}, u32[]{:S(2)}) collective-permute-start(f32[256,1024]{1,0:T(8,128)} %get-tuple-element.446.refs_1_), channel_id=1, source_target_pairs={{0,4},{1,5},{2,6},{3,7},{4,0},{5,1},{6,2},{7,3}} | collective-permute-start | bytes 3145736 | tf_op jit(solution)/shard_map/ppermute | solution.py:373
  645.1 96.3 %collective-permute-start.14 = (f32[512,1024]{1,0:T(8,128)}, f32[512,1024]{1,0:T(8,128)S(1)}, u32[]{:S(2)}, u32[]{:S(2)}) collective-permute-start(f32[512,1024]{1,0:T(8,128)} %get-tuple-element.400), channel_id=1, source_target_pairs={{0,2},{1,3},{2,0},{3,1},{4,6},{5,7},{6,4},{7,5}} | collective-permute-start | bytes 6291464 | tf_op jit(solution)/shard_map/ppermute | solution.py:373
  784.2 98.8 %collective-permute-start.32 = (bf16[2048,256]{1,0:T(8,128)(2,1)}, bf16[2048,256]{1,0:T(8,128)(2,1)}, u32[]{:S(2)}, u32[]{:S(2)}) collective-permute-start(bf16[2048,256]{1,0:T(8,128)(2,1)} %pad_maximum_fusion.1), channel_id=1, source_target_pairs={{0,1},{1,0},{2,3},{3,2},{4,5},{5,4},{6,7},{7,6}} | collective-permute-start | bytes 3145736 | tf_op jit(solution)/shard_map/ppermute | solution.py:373
  819.5 89.4 %collective-permute-start.44 = (f32[256,1024]{1,0:T(8,128)}, f32[256,1024]{1,0:T(8,128)}, u32[]{:S(2)}, u32[]{:S(2)}) collective-permute-start(f32[256,1024]{1,0:T(8,128)} %get-tuple-element.485.refs_0_), channel_id=1, source_target_pairs={{0,2},{1,3},{2,0},{3,1},{4,6},{5,7},{6,4},{7,5}} | collective-permute-start | bytes 3145736 | tf_op jit(solution)/shard_map/ppermute | solution.py:373
  948.2 186.1 %collective-permute-start.58 = (f32[2048,1024]{1,0:T(8,128)}, f32[2048,1024]{1,0:T(8,128)}, u32[]{:S(2)}, u32[]{:S(2)}) collective-permute-start(f32[2048,1024]{1,0:T(8,128)} %assemble.6.refs_0_), channel_id=1, source_target_pairs={{0,1},{1,0},{2,3},{3,2},{4,5},{5,4},{6,7},{7,6}} | collective-permute-start | bytes 25165832 | tf_op jit(solution)/shard_map/ppermute | solution.py:373
  948.6 185.8 %collective-permute-start.59 = (f32[2048,1024]{1,0:T(8,128)}, f32[2048,1024]{1,0:T(8,128)}, u32[]{:S(2)}, u32[]{:S(2)}) collective-permute-start(f32[2048,1024]{1,0:T(8,128)} %assemble.7.refs_2_), channel_id=1, source_target_pairs={{0,1},{1,0},{2,3},{3,2},{4,5},{5,4},{6,7},{7,6}} | collective-permute-start | bytes 25165832 | tf_op jit(solution)/shard_map/ppermute | solution.py:373
  1069.4 95.3 %collective-permute-start.50 = (f32[256,1024]{1,0:T(8,128)}, f32[256,1024]{1,0:T(8,128)}, u32[]{:S(2)}, u32[]{:S(2)}) collective-permute-start(f32[256,1024]{1,0:T(8,128)} %get-tuple-element.601), channel_id=1, source_target_pairs={{0,4},{1,5},{2,6},{3,7},{4,0},{5,1},{6,2},{7,3}} | collective-permute-start | bytes 3145736 | tf_op jit(solution)/shard_map/ppermute | solution.py:373
  1114.1 132.6 %all-to-all-start.4 = ((bf16[8,128,2048]{2,1,0:T(8,128)(2,1)}), bf16[8,128,2048]{2,1,0:T(8,128)(2,1)}, u32[]{:S(2)}, u32[]{:S(2)}) async-start(bf16[8,128,2048]{2,1,0:T(8,128)(2,1)} %bitcast.92), calls=%async_computation.4 | async-start | bytes 8388608 | tf_op jit(solution)/shard_map/all_to_all | solution.py:388
  1124.9 97.5 %collective-permute-start.64 = (bf16[2048,768]{1,0:T(8,128)(2,1)S(1)}, bf16[2048,768]{1,0:T(8,128)(2,1)}, u32[]{:S(2)}, u32[]{:S(2)}) collective-permute-start(bf16[2048,768]{1,0:T(8,128)(2,1)S(1)} %copy-done.3), channel_id=1, source_target_pairs={{0,1},{1,0},{2,3},{3,2},{4,5},{5,4},{6,7},{7,6}} | collective-permute-start | bytes 9437192 | tf_op jit(solution)/shard_map/ppermute | solution.py:373
  1125.1 97.5 %collective-permute-start.65 = (bf16[2048,768]{1,0:T(8,128)(2,1)}, bf16[2048,768]{1,0:T(8,128)(2,1)}, u32[]{:S(2)}, u32[]{:S(2)}) collective-permute-start(bf16[2048,768]{1,0:T(8,128)(2,1)} %get-tuple-element.395.refs_10_.refs_11_), channel_id=1, source_target_pairs={{0,1},{1,0},{2,3},{3,2},{4,5},{5,4},{6,7},{7,6}} | collective-permute-start | bytes 9437192 | tf_op jit(solution)/shard_map/ppermute | solution.py:373
  1134.2 89.6 %collective-permute-start.66 = (bf16[2048,768]{1,0:T(8,128)(2,1)}, bf16[2048,768]{1,0:T(8,128)(2,1)}, u32[]{:S(2)}, u32[]{:S(2)}) collective-permute-start(bf16[2048,768]{1,0:T(8,128)(2,1)} %get-tuple-element.441.refs_10_.refs_11_), channel_id=1, source_target_pairs={{0,1},{1,0},{2,3},{3,2},{4,5},{5,4},{6,7},{7,6}} | collective-permute-start | bytes 9437192 | tf_op jit(solution)/shard_map/ppermute | solution.py:373
  1134.4 89.7 %collective-permute-start.67 = (bf16[2048,768]{1,0:T(8,128)(2,1)}, bf16[2048,768]{1,0:T(8,128)(2,1)}, u32[]{:S(2)}, u32[]{:S(2)}) collective-permute-start(bf16[2048,768]{1,0:T(8,128)(2,1)} %get-tuple-element.483.refs_10_.refs_11_), channel_id=1, source_target_pairs={{0,1},{1,0},{2,3},{3,2},{4,5},{5,4},{6,7},{7,6}} | collective-permute-start | bytes 9437192 | tf_op jit(solution)/shard_map/ppermute | solution.py:373
  1240.5 127.8 %collective-permute-start.78 = (f32[2048,1024]{1,0:T(8,128)}, f32[2048,1024]{1,0:T(8,128)}, u32[]{:S(2)}, u32[]{:S(2)}) collective-permute-start(f32[2048,1024]{1,0:T(8,128)} %assemble.8.refs_0_), channel_id=1, source_target_pairs={{0,1},{1,0},{2,3},{3,2},{4,5},{5,4},{6,7},{7,6}} | collective-permute-start | bytes 25165832 | tf_op jit(solution)/shard_map/ppermute | solution.py:373
  1246.5 119.2 %collective-permute-start.75 = (f32[256,1024]{1,0:T(8,128)S(1)}, f32[256,1024]{1,0:T(8,128)}, u32[]{:S(2)}, u32[]{:S(2)}) collective-permute-start(f32[256,1024]{1,0:T(8,128)S(1)} %copy-done.14), channel_id=1, source_target_pairs={{0,4},{1,5},{2,6},{3,7},{4,0},{5,1},{6,2},{7,3}} | collective-permute-start | bytes 3145736 | tf_op jit(solution)/shard_map/ppermute | solution.py:373
  1246.7 176.5 %all-to-all-start.3 = ((bf16[8,128,2048]{2,1,0:T(8,128)(2,1)}), bf16[8,128,2048]{2,1,0:T(8,128)(2,1)}, u32[]{:S(2)}, u32[]{:S(2)}) async-start(bf16[8,128,2048]{2,1,0:T(8,128)(2,1)} %bitcast.91), calls=%async_computation.3 | async-start | bytes 8388608 | tf_op jit(solution)/shard_map/all_to_all | solution.py:388
  1268.9 108.4 %collective-permute-start.79 = (f32[2048,1024]{1,0:T(8,128)}, f32[2048,1024]{1,0:T(8,128)}, u32[]{:S(2)}, u32[]{:S(2)}) collective-permute-start(f32[2048,1024]{1,0:T(8,128)} %assemble.9.refs_2_), channel_id=1, source_target_pairs={{0,1},{1,0},{2,3},{3,2},{4,5},{5,4},{6,7},{7,6}} | collective-permute-start | bytes 25165832 | tf_op jit(solution)/shard_map/ppermute | solution.py:373
  1272.2 93.8 %collective-permute-start.76 = (f32[256,1024]{1,0:T(8,128)}, f32[256,1024]{1,0:T(8,128)}, u32[]{:S(2)}, u32[]{:S(2)}) collective-permute-start(f32[256,1024]{1,0:T(8,128)} %collective-permute-done.72.refs_2_), channel_id=1, source_target_pairs={{0,2},{1,3},{2,0},{3,1},{4,6},{5,7},{6,4},{7,5}} | collective-permute-start | bytes 3145736 | tf_op jit(solution)/shard_map/ppermute | solution.py:373
  1423.2 94.1 %all-to-all-start.5 = ((bf16[8,2,128,2048]{3,2,1,0:T(8,128)(2,1)}), bf16[8,2,128,2048]{3,2,1,0:T(8,128)(2,1)}, u32[]{:S(2)}, u32[]{:S(2)}) async-start(bf16[8,2,128,2048]{3,2,1,0:T(8,128)(2,1)} %get-tuple-element.549), calls=%async_computation.5 | async-start | bytes 16777216 | tf_op jit(solution)/shard_map/all_to_all | solution.py:388
  (120 other events, 4208.9 us)

commit v8 on v6

--- a/solution.py
+++ b/solution.py
@@ -101,7 +101,7 @@
 
 def project(units, w, block, cols, bias=None, transposed=False):
     rows, depth = units[0].shape
-    bm = rows // 2 if not transposed else rows if len(units) > 1 else rows // 4
+    bm = rows if transposed else rows // 2
     steps = rows // bm
     in_specs = [pl.BlockSpec((bm, depth), lambda i, n=n: (jnp.clip(i - n * steps, 0, steps - 1), 0))
                 for n in range(len(units))]
@@ -357,8 +357,8 @@
     def kernel(in_ref, out_ref):
         out_ref[:] = in_ref[:]
 
-    block = pl.BlockSpec((2, *a.shape[1:]), lambda i: (i, 0, 0))
-    return pl.pallas_call(kernel, grid=(a.shape[0] // 2,), in_specs=[block], out_specs=block,
+    block = pl.BlockSpec((4, *a.shape[1:]), lambda i: (i, 0, 0))
+    return pl.pallas_call(kernel, grid=(a.shape[0] // 4,), in_specs=[block], out_specs=block,
                           out_shape=jax.ShapeDtypeStruct(a.shape, a.dtype), cost_estimate=cost(a.size, a.size), name="copied")(a)
 
 
@@ -488,11 +488,15 @@
             else:
                 held = after_chain(u + gy)
                 qkv = project(held[:4], w_own, k, cw, b_own)
-                if k == 1:
+                first = 0
+                if k < 4:
                     grad_o = project(held[4:], wo_own, k, co, transposed=True)
-                elif k % 2 == 0:
-                    grad_o = project(held[4:], wo_own, k // 2, 2 * co, transposed=True)
-                first = ch * (k % 2) if k > 1 else 0
+                elif k == 4:
+                    grad_o = project(held[4:], wo_own, 2, 2 * co, transposed=True)
+                else:
+                    first = ch
+                if k == 3:
+                    g_got = after_chain(g_got)
                 chain = (qkv, grad_o)
                 if k > 2:
                     spread(k - 2)

time: 1540 us -> 1580 us (1.026)
  waiting for transfers between devices: 172 us -> 236 us
  starting transfers between devices: 146 us -> 125 us
    ppermute x86, waiting for transfers between devices: 172 us -> 236 us  [solution(): lax.ppermute(a, 'sp', [(d, d ^ bit) for d in range(n_dev)])]
    unnamed x118 -> x110, local copies, waits for them, and re-layouts: 36.4 us -> 28.4 us
    pallas_call x16 -> x17, Pallas kernels: 198 us -> 203 us  [project(): pl.pallas_call(functools.partial(project_kernel, len(units), steps, trans...]
  transfers between devices with their start and end apart: 91 -> 91, of which waited for: 19 -> 19; matrix products, arithmetic and copies ran while one was open for 15% -> 15% of each run, Pallas kernels for 54% -> 53%
where the time goes in v8:
time: 1580 us; the launch traced here: 1560 us
  Pallas kernels  869 us (55%)
  waiting for transfers between devices  236 us (15%)
  matrix products  144 us (9%)
  starting transfers between devices  125 us (8%)
  blocking collectives  98 us (6%)
  local copies, waits for them, and re-layouts  56 us (4%)
  other arithmetic  33.3 us (2%)
    ppermute x86, waiting for transfers between devices, solution(): lax.ppermute(a, 'sp', [(d, d ^ bit) for d in range(n_dev)])  236 us
    pallas_call x17, Pallas kernels, project(): pl.pallas_call(functools.partial(project_kernel, len(units), steps, trans...  203 us
    pallas_call x8, Pallas kernels, weight_grads(): pl.pallas_call(kernel, grid_spec=pltpu.PrefetchScalarGridSpec(num_scalar_...  189 us
    pallas_call x14, Pallas kernels, attention(): pl.pallas_call(kernel, grid=(n_seq, n_heads), in_specs=in_specs, out_spec...  181 us
    dot_general x6, matrix products, dot(): lax.dot_general(a, b, (((ca,), (cb,)), ((), ())), preferred_element_type=...  144 us
    ppermute x86, starting transfers between devices, solution(): lax.ppermute(a, 'sp', [(d, d ^ bit) for d in range(n_dev)])  102 us
    all_to_all x1, blocking collectives, exchange(): return lax.all_to_all(a, 'sp', 0, 0, tiled=True)  98 us
    pallas_call x3, Pallas kernels, place(): pl.pallas_call(functools.partial(place_kernel, counts, dh), grid_spec=plt...  89.8 us
  transfers between devices with their start and end apart: 91, of which 19 were waited for; matrix products, arithmetic and copies ran while one was open for 15% of the time, Pallas kernels for 53%

profile of v8, /device:TPU:1, one launch (start us, length us, event | category | flops | bytes accessed | tf_op | source)
XLA Modules:
  0.0 1562.4 jit_solution(775408994908443681)
XLA Ops:
  0.6 98.0 %all_to_all.30.x_ref = bf16[8,2,128,2048]{3,2,1,0:T(8,128)(2,1)} all-to-all(bf16[8,2,128,2048]{3,2,1,0:T(8,128)(2,1)} %bitcast.88), channel_id=1, replica_groups=mesh['sp'=8] {'sp'}, dimensions={0} | all-to-all | bytes 16777216 | tf_op jit(solution)/shard_map/all_to_all | solution.py:388
  126.1 33.6 %lay_out_weights.2.refs_1_.refs_4_ = bf16[2048,4608]{1,0:T(8,128)(2,1)} custom-call(s32[1]{0:T(128)} %bitcast.6.core_ref, bf16[2048,3,24,128]{3,2,1,0:T(8,128)(2,1)} %w_ref.1), custom_call_target="tpu_custom_call" | custom-call | flops 3774873600 | bytes 56623104 | tf_op jit(solution)/shard_map/lay_out_weights/pallas_call | solution.py:227
  316.0 20.3 %project.25.qkv_ref = bf16[4096,768]{1,0:T(8,128)(2,1)} custom-call(bf16[1024,2048]{1,0:T(8,128)(2,1)} %norm.2.refs_0_, bf16[1024,2048]{1,0:T(8,128)(2,1)} %norm.3.refs_0_.refs_1_, bf16[1024,2048]{1,0:T(8,128)(2,1)} %collective-permute-done.refs_0_.refs_1_.refs_2_, bf16[1024,2048]{1,0:T(8,128)(2,1)} %collective-permute-done.1.refs_0_.refs_1_.refs_3_, ...), custom_call_target="tpu_custom_call" | custom-call | flops 12884901888 | bytes 23068672 | tf_op jit(solution)/shard_map/project/pallas_call | solution.py:115
  379.2 29.2 %weight_grads.11 = (f32[512,1024]{1,0:T(8,128)}, f32[512,1024]{1,0:T(8,128)}, f32[512,1024]{1,0:T(8,128)}, f32[512,1024]{1,0:T(8,128)}) custom-call(s32[8]{0:T(128)} %stack.50.order_ref, bf16[1024,2048]{1,0:T(8,128)(2,1)} %norm.2.refs_0_, bf16[1024,2048]{1,0:T(8,128)(2,1)} %norm.3.refs_0_.refs_1_, ...), custom_call_target="tpu_custom_call" | custom-call | flops 17179869184 | bytes 67108864 | tf_op jit(solution)/shard_map/weight_grads/pallas_call | solution.py:153
  422.6 20.3 %project.27.qkv_ref = bf16[4096,768]{1,0:T(8,128)(2,1)} custom-call(bf16[1024,2048]{1,0:T(8,128)(2,1)} %norm.2.refs_0_, bf16[1024,2048]{1,0:T(8,128)(2,1)} %norm.3.refs_0_.refs_1_, bf16[1024,2048]{1,0:T(8,128)(2,1)} %collective-permute-done.refs_0_.refs_1_.refs_2_, bf16[1024,2048]{1,0:T(8,128)(2,1)} %collective-permute-done.1.refs_0_.refs_1_.refs_3_, ...), custom_call_target="tpu_custom_call" | custom-call | flops 12884901888 | bytes 23068672 | tf_op jit(solution)/shard_map/project/pallas_call | solution.py:115
  481.9 29.1 %weight_grads.12 = (f32[512,1024]{1,0:T(8,128)}, f32[512,1024]{1,0:T(8,128)}, f32[512,1024]{1,0:T(8,128)}, f32[512,1024]{1,0:T(8,128)}) custom-call(s32[8]{0:T(128)} %stack.50.order_ref, bf16[1024,2048]{1,0:T(8,128)(2,1)} %norm.2.refs_0_, bf16[1024,2048]{1,0:T(8,128)(2,1)} %norm.3.refs_0_.refs_1_, ...), custom_call_target="tpu_custom_call" | custom-call | flops 17179869184 | bytes 67108864 | tf_op jit(solution)/shard_map/weight_grads/pallas_call | solution.py:153
  520.1 21.1 %collective-permute-done.11.b2 = f32[256,1024]{1,0:T(8,128)} collective-permute-done((f32[256,1024]{1,0:T(8,128)}, f32[256,1024]{1,0:T(8,128)}, u32[]{:S(2)}, u32[]{:S(2)}) %collective-permute-start.11) | collective-permute-done | bytes 1048608 | tf_op jit(solution)/shard_map/ppermute | solution.py:373
  558.6 20.5 %project.29.qkv_ref = bf16[4096,768]{1,0:T(8,128)(2,1)} custom-call(bf16[1024,2048]{1,0:T(8,128)(2,1)} %norm.2.refs_0_, bf16[1024,2048]{1,0:T(8,128)(2,1)} %norm.3.refs_0_.refs_1_, bf16[1024,2048]{1,0:T(8,128)(2,1)} %collective-permute-done.refs_0_.refs_1_.refs_2_, bf16[1024,2048]{1,0:T(8,128)(2,1)} %collective-permute-done.1.refs_0_.refs_1_.refs_3_, ...), custom_call_target="tpu_custom_call" | custom-call | flops 12884901888 | bytes 23068672 | tf_op jit(solution)/shard_map/project/pallas_call | solution.py:115
  617.7 29.6 %weight_grads.13 = (f32[512,1024]{1,0:T(8,128)}, f32[512,1024]{1,0:T(8,128)}, f32[512,1024]{1,0:T(8,128)}, f32[512,1024]{1,0:T(8,128)}) custom-call(s32[8]{0:T(128)} %stack.50.order_ref, bf16[1024,2048]{1,0:T(8,128)(2,1)} %norm.2.refs_0_, bf16[1024,2048]{1,0:T(8,128)(2,1)} %norm.3.refs_0_.refs_1_, ...), custom_call_target="tpu_custom_call" | custom-call | flops 17179869184 | bytes 67108864 | tf_op jit(solution)/shard_map/weight_grads/pallas_call | solution.py:153
  686.9 20.3 %project.31.qkv_ref = bf16[4096,768]{1,0:T(8,128)(2,1)} custom-call(bf16[1024,2048]{1,0:T(8,128)(2,1)} %norm.2.refs_0_, bf16[1024,2048]{1,0:T(8,128)(2,1)} %norm.3.refs_0_.refs_1_, bf16[1024,2048]{1,0:T(8,128)(2,1)} %collective-permute-done.refs_0_.refs_1_.refs_2_, bf16[1024,2048]{1,0:T(8,128)(2,1)} %collective-permute-done.1.refs_0_.refs_1_.refs_3_, ...), custom_call_target="tpu_custom_call" | custom-call | flops 12884901888 | bytes 23068672 | tf_op jit(solution)/shard_map/project/pallas_call | solution.py:115
  762.8 29.1 %weight_grads.14 = (f32[512,1024]{1,0:T(8,128)}, f32[512,1024]{1,0:T(8,128)}, f32[512,1024]{1,0:T(8,128)}, f32[512,1024]{1,0:T(8,128)}) custom-call(s32[8]{0:T(128)} %stack.50.order_ref, bf16[1024,2048]{1,0:T(8,128)(2,1)} %norm.2.refs_0_, bf16[1024,2048]{1,0:T(8,128)(2,1)} %norm.3.refs_0_.refs_1_, ...), custom_call_target="tpu_custom_call" | custom-call | flops 17179869184 | bytes 67108864 | tf_op jit(solution)/shard_map/weight_grads/pallas_call | solution.py:153
  804.0 21.0 %collective-permute-done.42.refs_2_ = f32[256,1024]{1,0:T(8,128)} collective-permute-done((f32[256,1024]{1,0:T(8,128)}, f32[256,1024]{1,0:T(8,128)}, u32[]{:S(2)}, u32[]{:S(2)}) %collective-permute-start.42) | collective-permute-done | bytes 1048608 | tf_op jit(solution)/shard_map/ppermute | solution.py:373
  826.0 33.6 %lay_out_weights.3 = bf16[2048,4608]{1,0:T(8,128)(2,1)} custom-call(s32[1]{0:T(128)S(6)} %sub.11.core_ref, bf16[2048,3,24,128]{3,2,1,0:T(8,128)(2,1)} %w_ref.1), custom_call_target="tpu_custom_call" | custom-call | flops 3774873600 | bytes 56623104 | tf_op jit(solution)/shard_map/lay_out_weights/pallas_call | solution.py:227
  886.8 20.5 %project.33.qkv_ref = bf16[4096,768]{1,0:T(8,128)(2,1)} custom-call(bf16[1024,2048]{1,0:T(8,128)(2,1)} %norm.2.refs_0_, bf16[1024,2048]{1,0:T(8,128)(2,1)} %norm.3.refs_0_.refs_1_, bf16[1024,2048]{1,0:T(8,128)(2,1)} %collective-permute-done.refs_0_.refs_1_.refs_2_, bf16[1024,2048]{1,0:T(8,128)(2,1)} %collective-permute-done.1.refs_0_.refs_1_.refs_3_, ...), custom_call_target="tpu_custom_call" | custom-call | flops 12884901888 | bytes 23068672 | tf_op jit(solution)/shard_map/project/pallas_call | solution.py:115
  944.9 29.4 %weight_grads.15 = (f32[512,1024]{1,0:T(8,128)}, f32[512,1024]{1,0:T(8,128)}, f32[512,1024]{1,0:T(8,128)}, f32[512,1024]{1,0:T(8,128)}) custom-call(s32[8]{0:T(128)} %stack.50.order_ref, bf16[1024,2048]{1,0:T(8,128)(2,1)} %norm.2.refs_0_, bf16[1024,2048]{1,0:T(8,128)(2,1)} %norm.3.refs_0_.refs_1_, ...), custom_call_target="tpu_custom_call" | custom-call | flops 17179869184 | bytes 67108864 | tf_op jit(solution)/shard_map/weight_grads/pallas_call | solution.py:153
  1055.4 44.3 %collective-permute-done.52.refs_4_ = f32[256,1024]{1,0:T(8,128)} collective-permute-done((f32[256,1024]{1,0:T(8,128)S(1)}, f32[256,1024]{1,0:T(8,128)}, u32[]{:S(2)}, u32[]{:S(2)}) %collective-permute-start.52) | collective-permute-done | bytes 1048608 | tf_op jit(solution)/shard_map/ppermute | solution.py:373
  1100.1 44.4 %collective-permute-done.56.a1 = f32[512,1024]{1,0:T(8,128)S(1)} collective-permute-done((f32[512,1024]{1,0:T(8,128)}, f32[512,1024]{1,0:T(8,128)S(1)}, u32[]{:S(2)}, u32[]{:S(2)}) %collective-permute-start.56) | collective-permute-done | bytes 2097184 | tf_op jit(solution)/shard_map/ppermute | solution.py:373
  1181.0 29.9 %place.3 = (f32[2048,3,24,128]{3,2,1,0:T(8,128)}, f32[24,128,2048]{2,1,0:T(8,128)}) custom-call(s32[1]{0:T(128)} %bitcast.6.core_ref, f32[2048,1024]{1,0:T(8,128)} %assemble.6.refs_0_, f32[2048,1024]{1,0:T(8,128)} %collective-permute-done.58.refs_1_, f32[2048,1024]{1,0:T(8,128)} %assemble.7.refs_2_, f32[2048,1024]{1,0:T(8,128)} %collective-permute-done.59.refs_3_), custom_call_target="tpu_custom_call" | custom-call | flops 8388608 | bytes 8388608 | tf_op jit(solution)/shard_map/place/pallas_call | solution.py:271
  1210.9 50.1 %fusion.7 = f32[2048,2048]{1,0:T(8,128)} fusion(bf16[2048,4608]{1,0:T(8,128)(2,1)} %get-tuple-element.560.refs_8_.refs_9_, bf16[2048,4608]{1,0:T(8,128)(2,1)} %lay_out_weights.2.refs_1_.refs_4_), kind=kOutput, calls=%fused_computation.65 | convolution fusion | flops 38654705664 | bytes 54525952 | tf_op jit(solution)/shard_map/dot_general | solution.py:20
  1309.5 50.4 %convolution_add_fusion.grad_ref = bf16[2048,2048]{1,0:T(8,128)(2,1)} fusion(f32[2048,2048]{1,0:T(8,128)} %fusion.7, bf16[2048,4608]{1,0:T(8,128)(2,1)} %constant_dynamic-update-slice_fusion, bf16[2048,4608]{1,0:T(8,128)(2,1)} %lay_out_weights.3), kind=kOutput, calls=%fused_computation | convolution fusion | flops 38663094272 | bytes 62914560 | tf_op jit(solution)/shard_map/dot_general | solution.py:20
  1399.1 22.1 %collective-permute-done.74.refs_4_ = f32[256,1024]{1,0:T(8,128)} collective-permute-done((f32[256,1024]{1,0:T(8,128)S(1)}, f32[256,1024]{1,0:T(8,128)}, u32[]{:S(2)}, u32[]{:S(2)}) %collective-permute-start.74) | collective-permute-done | bytes 1048608 | tf_op jit(solution)/shard_map/ppermute | solution.py:373
  1469.4 29.9 %place.4 = (f32[2048,3,24,128]{3,2,1,0:T(8,128)}, f32[24,128,2048]{2,1,0:T(8,128)}) custom-call(s32[1]{0:T(128)} %bitcast.6.core_ref, f32[2048,1024]{1,0:T(8,128)} %assemble.8.refs_0_, f32[2048,1024]{1,0:T(8,128)} %collective-permute-done.78.refs_1_, f32[2048,1024]{1,0:T(8,128)} %assemble.9.refs_2_, ...), custom_call_target="tpu_custom_call", output_to_operand_aliasing={{0}: (5, {}), {1}: (6, {})} | custom-call | flops 8388608 | bytes 8388608 | tf_op jit(solution)/shard_map/place/pallas_call | solution.py:271
  1502.0 29.9 %place.5 = (f32[2048,3,24,128]{3,2,1,0:T(8,128)}, f32[24,128,2048]{2,1,0:T(8,128)}) custom-call(s32[1]{0:T(128)} %bitcast.6.core_ref, f32[2048,1024]{1,0:T(8,128)} %assemble.10.refs_0_, f32[2048,1024]{1,0:T(8,128)} %collective-permute-done.80.refs_1_, f32[2048,1024]{1,0:T(8,128)} %assemble.11.refs_2_, ...), custom_call_target="tpu_custom_call", output_to_operand_aliasing={{0}: (5, {}), {1}: (6, {})} | custom-call | flops 8388608 | bytes 8388608 | tf_op jit(solution)/shard_map/place/pallas_call | solution.py:271
  1531.9 19.8 %collective-permute-done.83 = f32[120,128]{1,0:T(8,128)S(1)} collective-permute-done((f32[120,128]{1,0:T(8,128)S(1)}, f32[120,128]{1,0:T(8,128)S(1)}, u32[]{:S(2)}, u32[]{:S(2)}) %collective-permute-start.83) | collective-permute-done | bytes 61472 | tf_op jit(solution)/shard_map/ppermute | solution.py:373
  (393 shorter events, 783.9 us)
Async XLA Ops:
  378.1 96.4 %collective-permute-start.18 = (f32[256,1024]{1,0:T(8,128)}, f32[256,1024]{1,0:T(8,128)}, u32[]{:S(2)}, u32[]{:S(2)}) collective-permute-start(f32[256,1024]{1,0:T(8,128)} %get-tuple-element.420.refs_0_), channel_id=1, source_target_pairs={{0,4},{1,5},{2,6},{3,7},{4,0},{5,1},{6,2},{7,3}} | collective-permute-start | bytes 3145736 | tf_op jit(solution)/shard_map/ppermute | solution.py:373
  378.3 96.7 %collective-permute-start.19 = (f32[256,1024]{1,0:T(8,128)}, f32[256,1024]{1,0:T(8,128)}, u32[]{:S(2)}, u32[]{:S(2)}) collective-permute-start(f32[256,1024]{1,0:T(8,128)} %get-tuple-element.421.refs_1_), channel_id=1, source_target_pairs={{0,2},{1,3},{2,0},{3,1},{4,6},{5,7},{6,4},{7,5}} | collective-permute-start | bytes 3145736 | tf_op jit(solution)/shard_map/ppermute | solution.py:373
  474.0 141.0 %collective-permute-start.20 = (f32[256,1024]{1,0:T(8,128)S(1)}, f32[256,1024]{1,0:T(8,128)}, u32[]{:S(2)}, u32[]{:S(2)}) collective-permute-start(f32[256,1024]{1,0:T(8,128)S(1)} %copy-done.15), channel_id=1, source_target_pairs={{0,2},{1,3},{2,0},{3,1},{4,6},{5,7},{6,4},{7,5}} | collective-permute-start | bytes 3145736 | tf_op jit(solution)/shard_map/ppermute | solution.py:373
  474.4 141.4 %collective-permute-start.21 = (f32[256,1024]{1,0:T(8,128)}, f32[256,1024]{1,0:T(8,128)}, u32[]{:S(2)}, u32[]{:S(2)}) collective-permute-start(f32[256,1024]{1,0:T(8,128)} %get-tuple-element.421.refs_1_), channel_id=1, source_target_pairs={{0,4},{1,5},{2,6},{3,7},{4,0},{5,1},{6,2},{7,3}} | collective-permute-start | bytes 3145736 | tf_op jit(solution)/shard_map/ppermute | solution.py:373
  475.1 141.2 %collective-permute-start.22 = (f32[256,1024]{1,0:T(8,128)}, f32[256,1024]{1,0:T(8,128)}, u32[]{:S(2)}, u32[]{:S(2)}) collective-permute-start(f32[256,1024]{1,0:T(8,128)} %collective-permute-done.18.refs_2_), channel_id=1, source_target_pairs={{0,2},{1,3},{2,0},{3,1},{4,6},{5,7},{6,4},{7,5}} | collective-permute-start | bytes 3145736 | tf_op jit(solution)/shard_map/ppermute | solution.py:373
  518.7 91.1 %collective-permute-start.12 = (f32[512,1024]{1,0:T(8,128)}, f32[512,1024]{1,0:T(8,128)S(1)}, u32[]{:S(2)}, u32[]{:S(2)}) collective-permute-start(f32[512,1024]{1,0:T(8,128)} %get-tuple-element.403), channel_id=1, source_target_pairs={{0,2},{1,3},{2,0},{3,1},{4,6},{5,7},{6,4},{7,5}} | collective-permute-start | bytes 6291464 | tf_op jit(solution)/shard_map/ppermute | solution.py:373
  650.7 110.0 %collective-permute-start.64 = (bf16[2048,768]{1,0:T(8,128)(2,1)}, bf16[2048,768]{1,0:T(8,128)(2,1)}, u32[]{:S(2)}, u32[]{:S(2)}) collective-permute-start(bf16[2048,768]{1,0:T(8,128)(2,1)} %pad_maximum_fusion), channel_id=1, source_target_pairs={{0,1},{1,0},{2,3},{3,2},{4,5},{5,4},{6,7},{7,6}} | collective-permute-start | bytes 9437192 | tf_op jit(solution)/shard_map/ppermute | solution.py:373
  665.4 96.0 %collective-permute-start.65 = (bf16[2048,768]{1,0:T(8,128)(2,1)}, bf16[2048,768]{1,0:T(8,128)(2,1)}, u32[]{:S(2)}, u32[]{:S(2)}) collective-permute-start(bf16[2048,768]{1,0:T(8,128)(2,1)} %get-tuple-element.355.refs_10_.refs_11_), channel_id=1, source_target_pairs={{0,1},{1,0},{2,3},{3,2},{4,5},{5,4},{6,7},{7,6}} | collective-permute-start | bytes 9437192 | tf_op jit(solution)/shard_map/ppermute | solution.py:373
  674.0 129.9 %collective-permute-start.66 = (bf16[2048,768]{1,0:T(8,128)(2,1)S(1)}, bf16[2048,768]{1,0:T(8,128)(2,1)}, u32[]{:S(2)}, u32[]{:S(2)}) collective-permute-start(bf16[2048,768]{1,0:T(8,128)(2,1)S(1)} %copy-done.4), channel_id=1, source_target_pairs={{0,1},{1,0},{2,3},{3,2},{4,5},{5,4},{6,7},{7,6}} | collective-permute-start | bytes 9437192 | tf_op jit(solution)/shard_map/ppermute | solution.py:373
  803.9 103.4 %collective-permute-start.38 = (f32[512,1024]{1,0:T(8,128)}, f32[512,1024]{1,0:T(8,128)S(1)}, u32[]{:S(2)}, u32[]{:S(2)}) collective-permute-start(f32[512,1024]{1,0:T(8,128)} %get-tuple-element.486), channel_id=1, source_target_pairs={{0,2},{1,3},{2,0},{3,1},{4,6},{5,7},{6,4},{7,5}} | collective-permute-start | bytes 6291464 | tf_op jit(solution)/shard_map/ppermute | solution.py:373
  983.3 196.5 %collective-permute-start.58 = (f32[2048,1024]{1,0:T(8,128)}, f32[2048,1024]{1,0:T(8,128)}, u32[]{:S(2)}, u32[]{:S(2)}) collective-permute-start(f32[2048,1024]{1,0:T(8,128)} %assemble.6.refs_0_), channel_id=1, source_target_pairs={{0,1},{1,0},{2,3},{3,2},{4,5},{5,4},{6,7},{7,6}} | collective-permute-start | bytes 25165832 | tf_op jit(solution)/shard_map/ppermute | solution.py:373
  983.3 197.6 %collective-permute-start.59 = (f32[2048,1024]{1,0:T(8,128)}, f32[2048,1024]{1,0:T(8,128)}, u32[]{:S(2)}, u32[]{:S(2)}) collective-permute-start(f32[2048,1024]{1,0:T(8,128)} %assemble.7.refs_2_), channel_id=1, source_target_pairs={{0,1},{1,0},{2,3},{3,2},{4,5},{5,4},{6,7},{7,6}} | collective-permute-start | bytes 25165832 | tf_op jit(solution)/shard_map/ppermute | solution.py:373
  1019.7 267.4 %all-to-all-start.4 = ((bf16[8,128,2048]{2,1,0:T(8,128)(2,1)}), bf16[8,128,2048]{2,1,0:T(8,128)(2,1)}, u32[]{:S(2)}, u32[]{:S(2)}) async-start(bf16[8,128,2048]{2,1,0:T(8,128)(2,1)} %bitcast.93), calls=%async_computation.4 | async-start | bytes 8388608 | tf_op jit(solution)/shard_map/all_to_all | solution.py:388
  1031.0 113.5 %collective-permute-start.56 = (f32[512,1024]{1,0:T(8,128)}, f32[512,1024]{1,0:T(8,128)S(1)}, u32[]{:S(2)}, u32[]{:S(2)}) collective-permute-start(f32[512,1024]{1,0:T(8,128)} %get-tuple-element.534), channel_id=1, source_target_pairs={{0,2},{1,3},{2,0},{3,1},{4,6},{5,7},{6,4},{7,5}} | collective-permute-start | bytes 6291464 | tf_op jit(solution)/shard_map/ppermute | solution.py:373
  1032.2 112.9 %collective-permute-start.57 = (f32[512,1024]{1,0:T(8,128)}, f32[512,1024]{1,0:T(8,128)}, u32[]{:S(2)}, u32[]{:S(2)}) collective-permute-start(f32[512,1024]{1,0:T(8,128)} %get-tuple-element.535), channel_id=1, source_target_pairs={{0,4},{1,5},{2,6},{3,7},{4,0},{5,1},{6,2},{7,3}} | collective-permute-start | bytes 6291464 | tf_op jit(solution)/shard_map/ppermute | solution.py:373
  1160.5 107.3 %collective-permute-start.67 = (bf16[2048,768]{1,0:T(8,128)(2,1)S(1)}, bf16[2048,768]{1,0:T(8,128)(2,1)}, u32[]{:S(2)}, u32[]{:S(2)}) collective-permute-start(bf16[2048,768]{1,0:T(8,128)(2,1)S(1)} %copy-done.3), channel_id=1, source_target_pairs={{0,1},{1,0},{2,3},{3,2},{4,5},{5,4},{6,7},{7,6}} | collective-permute-start | bytes 9437192 | tf_op jit(solution)/shard_map/ppermute | solution.py:373
  1167.3 101.7 %collective-permute-start.68 = (bf16[2048,768]{1,0:T(8,128)(2,1)}, bf16[2048,768]{1,0:T(8,128)(2,1)}, u32[]{:S(2)}, u32[]{:S(2)}) collective-permute-start(bf16[2048,768]{1,0:T(8,128)(2,1)} %get-tuple-element.455.refs_10_.refs_11_), channel_id=1, source_target_pairs={{0,1},{1,0},{2,3},{3,2},{4,5},{5,4},{6,7},{7,6}} | collective-permute-start | bytes 9437192 | tf_op jit(solution)/shard_map/ppermute | solution.py:373
  1170.4 110.2 %collective-permute-start.69 = (bf16[2048,768]{1,0:T(8,128)(2,1)}, bf16[2048,768]{1,0:T(8,128)(2,1)}, u32[]{:S(2)}, u32[]{:S(2)}) collective-permute-start(bf16[2048,768]{1,0:T(8,128)(2,1)} %get-tuple-element.497.refs_10_.refs_11_), channel_id=1, source_target_pairs={{0,1},{1,0},{2,3},{3,2},{4,5},{5,4},{6,7},{7,6}} | collective-permute-start | bytes 9437192 | tf_op jit(solution)/shard_map/ppermute | solution.py:373
  1280.6 102.8 %collective-permute-start.60 = (f32[256,1024]{1,0:T(8,128)}, f32[256,1024]{1,0:T(8,128)}, u32[]{:S(2)}, u32[]{:S(2)}) collective-permute-start(f32[256,1024]{1,0:T(8,128)} %get-tuple-element.571.refs_0_), channel_id=1, source_target_pairs={{0,2},{1,3},{2,0},{3,1},{4,6},{5,7},{6,4},{7,5}} | collective-permute-start | bytes 3145736 | tf_op jit(solution)/shard_map/ppermute | solution.py:373
  1285.8 98.9 %collective-permute-start.61 = (f32[256,1024]{1,0:T(8,128)}, f32[256,1024]{1,0:T(8,128)}, u32[]{:S(2)}, u32[]{:S(2)}) collective-permute-start(f32[256,1024]{1,0:T(8,128)} %get-tuple-element.572.refs_1_), channel_id=1, source_target_pairs={{0,4},{1,5},{2,6},{3,7},{4,0},{5,1},{6,2},{7,3}} | collective-permute-start | bytes 3145736 | tf_op jit(solution)/shard_map/ppermute | solution.py:373
  1286.6 98.4 %collective-permute-start.62 = (f32[256,1024]{1,0:T(8,128)}, f32[256,1024]{1,0:T(8,128)}, u32[]{:S(2)}, u32[]{:S(2)}) collective-permute-start(f32[256,1024]{1,0:T(8,128)} %collective-permute-done.48.refs_2_), channel_id=1, source_target_pairs={{0,2},{1,3},{2,0},{3,1},{4,6},{5,7},{6,4},{7,5}} | collective-permute-start | bytes 3145736 | tf_op jit(solution)/shard_map/ppermute | solution.py:373
  1287.2 150.5 %all-to-all-start.3 = ((bf16[8,128,2048]{2,1,0:T(8,128)(2,1)}), bf16[8,128,2048]{2,1,0:T(8,128)(2,1)}, u32[]{:S(2)}, u32[]{:S(2)}) async-start(bf16[8,128,2048]{2,1,0:T(8,128)(2,1)} %bitcast.92), calls=%async_computation.3 | async-start | bytes 8388608 | tf_op jit(solution)/shard_map/all_to_all | solution.py:388
  1308.9 112.3 %collective-permute-start.74 = (f32[256,1024]{1,0:T(8,128)S(1)}, f32[256,1024]{1,0:T(8,128)}, u32[]{:S(2)}, u32[]{:S(2)}) collective-permute-start(f32[256,1024]{1,0:T(8,128)S(1)} %copy-done.16), channel_id=1, source_target_pairs={{0,2},{1,3},{2,0},{3,1},{4,6},{5,7},{6,4},{7,5}} | collective-permute-start | bytes 3145736 | tf_op jit(solution)/shard_map/ppermute | solution.py:373
  1454.5 100.6 %all-to-all-start.5 = ((bf16[8,2,128,2048]{3,2,1,0:T(8,128)(2,1)}), bf16[8,2,128,2048]{3,2,1,0:T(8,128)(2,1)}, u32[]{:S(2)}, u32[]{:S(2)}) async-start(bf16[8,2,128,2048]{3,2,1,0:T(8,128)(2,1)} %get-tuple-element.570), calls=%async_computation.5 | async-start | bytes 16777216 | tf_op jit(solution)/shard_map/all_to_all | solution.py:388
  (116 other events, 4850.5 us)

commit v9 on v8

--- a/solution.py
+++ b/solution.py
@@ -495,8 +495,6 @@
                     grad_o = project(held[4:], wo_own, 2, 2 * co, transposed=True)
                 else:
                     first = ch
-                if k == 3:
-                    g_got = after_chain(g_got)
                 chain = (qkv, grad_o)
                 if k > 2:
                     spread(k - 2)
@@ -524,6 +522,7 @@
                 else:
                     if k > 2:
                         forward(k - 2)
+                    if 2 < k < end:
                         chain = take(k - 3)
                     if k < end:
                         chain = last_add(k - 1)
@@ -545,18 +544,19 @@
             if s == 0:
                 chain = last_add(end - 1)
         spread(end - 1)
+        g_theirs = jnp.concatenate(after_chain(g_got), axis=1)
+        chain = (g_theirs,)
         chain = first_add(end)
-        chain = take(3)
         whole = place_sums(0)
         chain = tuple(whole)
-        forward(end - 1)
 
         g_mine, = after_chain([mine[1]])
         grad_u = dot(g_mine, w_own, 1, 1)
         chain = (grad_u,)
+        forward(end - 1)
         chain = last_add(end)
         spread(end)
-        g_theirs, = after_chain([jnp.concatenate(g_got, axis=1)])
+        g_theirs, = after_chain([g_theirs])
         grad_u = dot(g_theirs, w_par, 1, 1) + grad_u
         chain = (grad_u,)
         grad_u, = after_chain([grad_u.astype(BF16)])
@@ -575,17 +575,18 @@
 
         chain = (gx,)
         forward(end)
-        chain = take(4)
+        for k in range(2, 5):
+            chain = take(k)
+        whole = place_sums(1)
+        chain = tuple(whole)
+        small, = after_chain([small])
+        near, far, across = [hop(small, bit) for bit in (2, 4, 6)]
         y_out = interleaved(interleaved(None, after_chain([y_moved[0]])[0], 0), y_moved[1], 1)
         chain = (y_out,)
         chain = take(5)
-        whole = place_sums(1)
-        chain = tuple(whole)
-        small, = after_chain([small])
-        others = [hop(small, bit) for bit in (2, 4, 6)]
         whole = place_sums(2)
         chain = tuple(whole)
-        near, far, across = after_chain(others)
+        near, far, across = after_chain([near, far, across])
         small = (small + near) + (far + across)
         grad_x = copied(after_chain([gx_moved])[0].reshape(batch, part, dim))
         grad_w_qkv, grad_w_out = whole

time: 1580 us -> 1660 us (1.051)
  waiting for transfers between devices: 236 us -> 331 us
    ppermute x86, waiting for transfers between devices: 236 us -> 288 us  [solution(): lax.ppermute(a, 'sp', [(d, d ^ bit) for d in range(n_dev)])]
    all_to_all x5, waiting for transfers between devices: 0.01 us -> 43 us  [exchange(): return lax.all_to_all(a, 'sp', 0, 0, tiled=True)]
  transfers between devices with their start and end apart: 91 -> 91, of which waited for: 19 -> 17; matrix products, arithmetic and copies ran while one was open for 15% -> 13% of each run, Pallas kernels for 53% -> 50%
where the time goes in v9:
time: 1660 us; the launch traced here: 1650 us
  Pallas kernels  870 us (52%)
  waiting for transfers between devices  331 us (20%)
  matrix products  144 us (9%)
  starting transfers between devices  111 us (7%)
  blocking collectives  97.9 us (6%)
  local copies, waits for them, and re-layouts  58.7 us (4%)
  other arithmetic  31.8 us (2%)
    ppermute x86, waiting for transfers between devices, solution(): lax.ppermute(a, 'sp', [(d, d ^ bit) for d in range(n_dev)])  288 us
    pallas_call x17, Pallas kernels, project(): pl.pallas_call(functools.partial(project_kernel, len(units), steps, trans...  203 us
    pallas_call x8, Pallas kernels, weight_grads(): pl.pallas_call(kernel, grid_spec=pltpu.PrefetchScalarGridSpec(num_scalar_...  189 us
    pallas_call x14, Pallas kernels, attention(): pl.pallas_call(kernel, grid=(n_seq, n_heads), in_specs=in_specs, out_spec...  181 us
    dot_general x6, matrix products, dot(): lax.dot_general(a, b, (((ca,), (cb,)), ((), ())), preferred_element_type=...  144 us
    all_to_all x1, blocking collectives, exchange(): return lax.all_to_all(a, 'sp', 0, 0, tiled=True)  97.9 us
    pallas_call x3, Pallas kernels, place(): pl.pallas_call(functools.partial(place_kernel, counts, dh), grid_spec=plt...  90.2 us
    ppermute x86, starting transfers between devices, solution(): lax.ppermute(a, 'sp', [(d, d ^ bit) for d in range(n_dev)])  87.5 us
  transfers between devices with their start and end apart: 91, of which 17 were waited for; matrix products, arithmetic and copies ran while one was open for 13% of the time, Pallas kernels for 50%

profile of v9, /device:TPU:1, one launch (start us, length us, event | category | flops | bytes accessed | tf_op | source)
XLA Modules:
  0.0 1645.7 jit_solution(6533242821412538816)
XLA Ops:
  0.6 97.9 %all_to_all.30.x_ref = bf16[8,2,128,2048]{3,2,1,0:T(8,128)(2,1)} all-to-all(bf16[8,2,128,2048]{3,2,1,0:T(8,128)(2,1)} %bitcast.88), channel_id=1, replica_groups=mesh['sp'=8] {'sp'}, dimensions={0} | all-to-all | bytes 16777216 | tf_op jit(solution)/shard_map/all_to_all | solution.py:388
  126.1 33.6 %lay_out_weights.2.refs_1_.refs_4_ = bf16[2048,4608]{1,0:T(8,128)(2,1)} custom-call(s32[1]{0:T(128)} %bitcast.6.core_ref, bf16[2048,3,24,128]{3,2,1,0:T(8,128)(2,1)} %w_ref.1), custom_call_target="tpu_custom_call" | custom-call | flops 3774873600 | bytes 56623104 | tf_op jit(solution)/shard_map/lay_out_weights/pallas_call | solution.py:227
  250.6 33.8 %lay_out_weights.3 = bf16[2048,4608]{1,0:T(8,128)(2,1)} custom-call(s32[1]{0:T(128)S(6)} %sub.11.core_ref, bf16[2048,3,24,128]{3,2,1,0:T(8,128)(2,1)} %w_ref.1), custom_call_target="tpu_custom_call" | custom-call | flops 3774873600 | bytes 56623104 | tf_op jit(solution)/shard_map/lay_out_weights/pallas_call | solution.py:227
  354.2 20.8 %project.25.qkv_ref = bf16[4096,768]{1,0:T(8,128)(2,1)} custom-call(bf16[1024,2048]{1,0:T(8,128)(2,1)} %norm.2.refs_0_, bf16[1024,2048]{1,0:T(8,128)(2,1)} %norm.3.refs_0_.refs_1_, bf16[1024,2048]{1,0:T(8,128)(2,1)} %collective-permute-done.refs_0_.refs_1_.refs_2_, bf16[1024,2048]{1,0:T(8,128)(2,1)} %collective-permute-done.1.refs_0_.refs_1_.refs_3_, ...), custom_call_target="tpu_custom_call" | custom-call | flops 12884901888 | bytes 23068672 | tf_op jit(solution)/shard_map/project/pallas_call | solution.py:115
  427.4 29.0 %weight_grads.11 = (f32[512,1024]{1,0:T(8,128)}, f32[512,1024]{1,0:T(8,128)}, f32[512,1024]{1,0:T(8,128)}, f32[512,1024]{1,0:T(8,128)}) custom-call(s32[8]{0:T(128)} %stack.50.order_ref, bf16[1024,2048]{1,0:T(8,128)(2,1)} %norm.2.refs_0_, bf16[1024,2048]{1,0:T(8,128)(2,1)} %norm.3.refs_0_.refs_1_, ...), custom_call_target="tpu_custom_call" | custom-call | flops 17179869184 | bytes 67108864 | tf_op jit(solution)/shard_map/weight_grads/pallas_call | solution.py:153
  470.3 20.3 %project.27.qkv_ref = bf16[4096,768]{1,0:T(8,128)(2,1)} custom-call(bf16[1024,2048]{1,0:T(8,128)(2,1)} %norm.2.refs_0_, bf16[1024,2048]{1,0:T(8,128)(2,1)} %norm.3.refs_0_.refs_1_, bf16[1024,2048]{1,0:T(8,128)(2,1)} %collective-permute-done.refs_0_.refs_1_.refs_2_, bf16[1024,2048]{1,0:T(8,128)(2,1)} %collective-permute-done.1.refs_0_.refs_1_.refs_3_, ...), custom_call_target="tpu_custom_call" | custom-call | flops 12884901888 | bytes 23068672 | tf_op jit(solution)/shard_map/project/pallas_call | solution.py:115
  529.0 29.1 %weight_grads.12 = (f32[512,1024]{1,0:T(8,128)}, f32[512,1024]{1,0:T(8,128)}, f32[512,1024]{1,0:T(8,128)}, f32[512,1024]{1,0:T(8,128)}) custom-call(s32[8]{0:T(128)} %stack.50.order_ref, bf16[1024,2048]{1,0:T(8,128)(2,1)} %norm.2.refs_0_, bf16[1024,2048]{1,0:T(8,128)(2,1)} %norm.3.refs_0_.refs_1_, ...), custom_call_target="tpu_custom_call" | custom-call | flops 17179869184 | bytes 67108864 | tf_op jit(solution)/shard_map/weight_grads/pallas_call | solution.py:153
  567.4 21.1 %collective-permute-done.11.b2 = f32[256,1024]{1,0:T(8,128)} collective-permute-done((f32[256,1024]{1,0:T(8,128)}, f32[256,1024]{1,0:T(8,128)}, u32[]{:S(2)}, u32[]{:S(2)}) %collective-permute-start.11) | collective-permute-done | bytes 1048608 | tf_op jit(solution)/shard_map/ppermute | solution.py:373
  606.8 20.7 %project.29.qkv_ref = bf16[4096,768]{1,0:T(8,128)(2,1)} custom-call(bf16[1024,2048]{1,0:T(8,128)(2,1)} %norm.2.refs_0_, bf16[1024,2048]{1,0:T(8,128)(2,1)} %norm.3.refs_0_.refs_1_, bf16[1024,2048]{1,0:T(8,128)(2,1)} %collective-permute-done.refs_0_.refs_1_.refs_2_, bf16[1024,2048]{1,0:T(8,128)(2,1)} %collective-permute-done.1.refs_0_.refs_1_.refs_3_, ...), custom_call_target="tpu_custom_call" | custom-call | flops 12884901888 | bytes 23068672 | tf_op jit(solution)/shard_map/project/pallas_call | solution.py:115
  665.3 29.4 %weight_grads.13 = (f32[512,1024]{1,0:T(8,128)}, f32[512,1024]{1,0:T(8,128)}, f32[512,1024]{1,0:T(8,128)}, f32[512,1024]{1,0:T(8,128)}) custom-call(s32[8]{0:T(128)} %stack.50.order_ref, bf16[1024,2048]{1,0:T(8,128)(2,1)} %norm.2.refs_0_, bf16[1024,2048]{1,0:T(8,128)(2,1)} %norm.3.refs_0_.refs_1_, ...), custom_call_target="tpu_custom_call" | custom-call | flops 17179869184 | bytes 67108864 | tf_op jit(solution)/shard_map/weight_grads/pallas_call | solution.py:153
  726.3 20.3 %project.31.qkv_ref = bf16[4096,768]{1,0:T(8,128)(2,1)} custom-call(bf16[1024,2048]{1,0:T(8,128)(2,1)} %norm.2.refs_0_, bf16[1024,2048]{1,0:T(8,128)(2,1)} %norm.3.refs_0_.refs_1_, bf16[1024,2048]{1,0:T(8,128)(2,1)} %collective-permute-done.refs_0_.refs_1_.refs_2_, bf16[1024,2048]{1,0:T(8,128)(2,1)} %collective-permute-done.1.refs_0_.refs_1_.refs_3_, ...), custom_call_target="tpu_custom_call" | custom-call | flops 12884901888 | bytes 23068672 | tf_op jit(solution)/shard_map/project/pallas_call | solution.py:115
  802.9 29.4 %weight_grads.14 = (f32[512,1024]{1,0:T(8,128)}, f32[512,1024]{1,0:T(8,128)}, f32[512,1024]{1,0:T(8,128)}, f32[512,1024]{1,0:T(8,128)}) custom-call(s32[8]{0:T(128)} %stack.50.order_ref, bf16[1024,2048]{1,0:T(8,128)(2,1)} %norm.2.refs_0_, bf16[1024,2048]{1,0:T(8,128)(2,1)} %norm.3.refs_0_.refs_1_, ...), custom_call_target="tpu_custom_call" | custom-call | flops 17179869184 | bytes 67108864 | tf_op jit(solution)/shard_map/weight_grads/pallas_call | solution.py:153
  870.8 20.3 %project.33.qkv_ref = bf16[4096,768]{1,0:T(8,128)(2,1)} custom-call(bf16[1024,2048]{1,0:T(8,128)(2,1)} %norm.2.refs_0_, bf16[1024,2048]{1,0:T(8,128)(2,1)} %norm.3.refs_0_.refs_1_, bf16[1024,2048]{1,0:T(8,128)(2,1)} %collective-permute-done.refs_0_.refs_1_.refs_2_, bf16[1024,2048]{1,0:T(8,128)(2,1)} %collective-permute-done.1.refs_0_.refs_1_.refs_3_, ...), custom_call_target="tpu_custom_call" | custom-call | flops 12884901888 | bytes 23068672 | tf_op jit(solution)/shard_map/project/pallas_call | solution.py:115
  929.5 29.2 %weight_grads.15 = (f32[512,1024]{1,0:T(8,128)}, f32[512,1024]{1,0:T(8,128)}, f32[512,1024]{1,0:T(8,128)}, f32[512,1024]{1,0:T(8,128)}) custom-call(s32[8]{0:T(128)} %stack.50.order_ref, bf16[1024,2048]{1,0:T(8,128)(2,1)} %norm.2.refs_0_, bf16[1024,2048]{1,0:T(8,128)(2,1)} %norm.3.refs_0_.refs_1_, ...), custom_call_target="tpu_custom_call" | custom-call | flops 17179869184 | bytes 67108864 | tf_op jit(solution)/shard_map/weight_grads/pallas_call | solution.py:153
  1099.2 30.3 %place.3 = (f32[2048,3,24,128]{3,2,1,0:T(8,128)}, f32[24,128,2048]{2,1,0:T(8,128)}) custom-call(s32[1]{0:T(128)} %bitcast.6.core_ref, f32[2048,1024]{1,0:T(8,128)} %assemble.6.refs_0_, f32[2048,1024]{1,0:T(8,128)} %collective-permute-done.58.refs_1_, f32[2048,1024]{1,0:T(8,128)} %assemble.7.refs_2_, f32[2048,1024]{1,0:T(8,128)} %collective-permute-done.59.refs_3_), custom_call_target="tpu_custom_call" | custom-call | flops 8388608 | bytes 8388608 | tf_op jit(solution)/shard_map/place/pallas_call | solution.py:271
  1129.6 50.0 %fusion.7 = f32[2048,2048]{1,0:T(8,128)} fusion(bf16[2048,4608]{1,0:T(8,128)(2,1)} %get-tuple-element.542.refs_8_.refs_9_, bf16[2048,4608]{1,0:T(8,128)(2,1)} %lay_out_weights.2.refs_1_.refs_4_), kind=kOutput, calls=%fused_computation.65 | convolution fusion | flops 38654705664 | bytes 54525952 | tf_op jit(solution)/shard_map/dot_general | solution.py:20
  1188.8 50.6 %convolution_add_fusion.grad_ref = bf16[2048,2048]{1,0:T(8,128)(2,1)} fusion(f32[2048,2048]{1,0:T(8,128)} %fusion.7, bf16[2048,4608]{1,0:T(8,128)(2,1)} %copy-done.38, bf16[2048,4608]{1,0:T(8,128)(2,1)} %lay_out_weights.3), kind=kOutput, calls=%fused_computation | convolution fusion | flops 38663094272 | bytes 62914560 | tf_op jit(solution)/shard_map/dot_general | solution.py:20
  1292.6 43.0 %all-to-all-done.4.in_ref = bf16[8,128,2048]{2,1,0:T(8,128)(2,1)} async-done(((bf16[8,128,2048]{2,1,0:T(8,128)(2,1)}), bf16[8,128,2048]{2,1,0:T(8,128)(2,1)}, u32[]{:S(2)}, u32[]{:S(2)}) %all-to-all-start.4) | async-done | bytes 4194336 | tf_op jit(solution)/shard_map/all_to_all | solution.py:388
  1362.0 65.4 %collective-permute-done.68.refs_4_ = f32[256,1024]{1,0:T(8,128)S(1)} collective-permute-done((f32[256,1024]{1,0:T(8,128)S(1)}, f32[256,1024]{1,0:T(8,128)S(1)}, u32[]{:S(2)}, u32[]{:S(2)}) %collective-permute-start.68) | collective-permute-done | bytes 1048608 | tf_op jit(solution)/shard_map/ppermute | solution.py:373
  1428.9 20.9 %collective-permute-done.75.refs_3_ = f32[256,1024]{1,0:T(8,128)} collective-permute-done((f32[256,1024]{1,0:T(8,128)}, f32[256,1024]{1,0:T(8,128)}, u32[]{:S(2)}, u32[]{:S(2)}) %collective-permute-start.75) | collective-permute-done | bytes 1048608 | tf_op jit(solution)/shard_map/ppermute | solution.py:373
  1451.7 20.5 %collective-permute-done.70.refs_6_ = f32[256,1024]{1,0:T(8,128)S(1)} collective-permute-done((f32[256,1024]{1,0:T(8,128)}, f32[256,1024]{1,0:T(8,128)S(1)}, u32[]{:S(2)}, u32[]{:S(2)}) %collective-permute-start.70) | collective-permute-done | bytes 1048608 | tf_op jit(solution)/shard_map/ppermute | solution.py:373
  1487.5 29.9 %place.4 = (f32[2048,3,24,128]{3,2,1,0:T(8,128)}, f32[24,128,2048]{2,1,0:T(8,128)}) custom-call(s32[1]{0:T(128)} %bitcast.6.core_ref, f32[2048,1024]{1,0:T(8,128)} %assemble.8.refs_0_, f32[2048,1024]{1,0:T(8,128)} %collective-permute-done.72.refs_1_, f32[2048,1024]{1,0:T(8,128)} %assemble.9.refs_2_, ...), custom_call_target="tpu_custom_call", output_to_operand_aliasing={{0}: (5, {}), {1}: (6, {})} | custom-call | flops 8388608 | bytes 8388608 | tf_op jit(solution)/shard_map/place/pallas_call | solution.py:271
  1555.0 29.9 %place.5 = (f32[2048,3,24,128]{3,2,1,0:T(8,128)}, f32[24,128,2048]{2,1,0:T(8,128)}) custom-call(s32[1]{0:T(128)} %bitcast.6.core_ref, f32[2048,1024]{1,0:T(8,128)} %assemble.10.refs_0_, f32[2048,1024]{1,0:T(8,128)} %collective-permute-done.80.refs_1_, f32[2048,1024]{1,0:T(8,128)} %assemble.11.refs_2_, ...), custom_call_target="tpu_custom_call", output_to_operand_aliasing={{0}: (5, {}), {1}: (6, {})} | custom-call | flops 8388608 | bytes 8388608 | tf_op jit(solution)/shard_map/place/pallas_call | solution.py:271
  1584.9 50.1 %collective-permute-done.83 = f32[120,128]{1,0:T(8,128)S(1)} collective-permute-done((f32[120,128]{1,0:T(8,128)S(1)}, f32[120,128]{1,0:T(8,128)S(1)}, u32[]{:S(2)}, u32[]{:S(2)}) %collective-permute-start.83) | collective-permute-done | bytes 61472 | tf_op jit(solution)/shard_map/ppermute | solution.py:373
  (427 shorter events, 818.1 us)
Async XLA Ops:
  426.0 95.6 %collective-permute-start.18 = (f32[256,1024]{1,0:T(8,128)}, f32[256,1024]{1,0:T(8,128)}, u32[]{:S(2)}, u32[]{:S(2)}) collective-permute-start(f32[256,1024]{1,0:T(8,128)} %get-tuple-element.423.refs_0_), channel_id=1, source_target_pairs={{0,4},{1,5},{2,6},{3,7},{4,0},{5,1},{6,2},{7,3}} | collective-permute-start | bytes 3145736 | tf_op jit(solution)/shard_map/ppermute | solution.py:373
  427.2 95.8 %collective-permute-start.19 = (f32[256,1024]{1,0:T(8,128)}, f32[256,1024]{1,0:T(8,128)}, u32[]{:S(2)}, u32[]{:S(2)}) collective-permute-start(f32[256,1024]{1,0:T(8,128)} %get-tuple-element.424.refs_1_), channel_id=1, source_target_pairs={{0,2},{1,3},{2,0},{3,1},{4,6},{5,7},{6,4},{7,5}} | collective-permute-start | bytes 3145736 | tf_op jit(solution)/shard_map/ppermute | solution.py:373
  521.5 142.0 %collective-permute-start.20 = (f32[256,1024]{1,0:T(8,128)S(1)}, f32[256,1024]{1,0:T(8,128)}, u32[]{:S(2)}, u32[]{:S(2)}) collective-permute-start(f32[256,1024]{1,0:T(8,128)S(1)} %copy-done.24), channel_id=1, source_target_pairs={{0,2},{1,3},{2,0},{3,1},{4,6},{5,7},{6,4},{7,5}} | collective-permute-start | bytes 3145736 | tf_op jit(solution)/shard_map/ppermute | solution.py:373
  521.6 142.2 %collective-permute-start.21 = (f32[256,1024]{1,0:T(8,128)}, f32[256,1024]{1,0:T(8,128)}, u32[]{:S(2)}, u32[]{:S(2)}) collective-permute-start(f32[256,1024]{1,0:T(8,128)} %get-tuple-element.424.refs_1_), channel_id=1, source_target_pairs={{0,4},{1,5},{2,6},{3,7},{4,0},{5,1},{6,2},{7,3}} | collective-permute-start | bytes 3145736 | tf_op jit(solution)/shard_map/ppermute | solution.py:373
  523.0 140.9 %collective-permute-start.22 = (f32[256,1024]{1,0:T(8,128)}, f32[256,1024]{1,0:T(8,128)}, u32[]{:S(2)}, u32[]{:S(2)}) collective-permute-start(f32[256,1024]{1,0:T(8,128)} %collective-permute-done.18.refs_2_), channel_id=1, source_target_pairs={{0,2},{1,3},{2,0},{3,1},{4,6},{5,7},{6,4},{7,5}} | collective-permute-start | bytes 3145736 | tf_op jit(solution)/shard_map/ppermute | solution.py:373
  565.9 92.2 %collective-permute-start.12 = (f32[512,1024]{1,0:T(8,128)}, f32[512,1024]{1,0:T(8,128)S(1)}, u32[]{:S(2)}, u32[]{:S(2)}) collective-permute-start(f32[512,1024]{1,0:T(8,128)} %get-tuple-element.406), channel_id=1, source_target_pairs={{0,2},{1,3},{2,0},{3,1},{4,6},{5,7},{6,4},{7,5}} | collective-permute-start | bytes 6291464 | tf_op jit(solution)/shard_map/ppermute | solution.py:373
  694.7 105.5 %collective-permute-start.28 = (f32[256,1024]{1,0:T(8,128)}, f32[256,1024]{1,0:T(8,128)}, u32[]{:S(2)}, u32[]{:S(2)}) collective-permute-start(f32[256,1024]{1,0:T(8,128)} %get-tuple-element.462.refs_0_), channel_id=1, source_target_pairs={{0,2},{1,3},{2,0},{3,1},{4,6},{5,7},{6,4},{7,5}} | collective-permute-start | bytes 3145736 | tf_op jit(solution)/shard_map/ppermute | solution.py:373
  698.4 103.1 %collective-permute-start.29 = (f32[256,1024]{1,0:T(8,128)}, f32[256,1024]{1,0:T(8,128)}, u32[]{:S(2)}, u32[]{:S(2)}) collective-permute-start(f32[256,1024]{1,0:T(8,128)} %get-tuple-element.463.refs_1_), channel_id=1, source_target_pairs={{0,4},{1,5},{2,6},{3,7},{4,0},{5,1},{6,2},{7,3}} | collective-permute-start | bytes 3145736 | tf_op jit(solution)/shard_map/ppermute | solution.py:373
  698.7 96.3 %collective-permute-start.14 = (f32[512,1024]{1,0:T(8,128)}, f32[512,1024]{1,0:T(8,128)S(1)}, u32[]{:S(2)}, u32[]{:S(2)}) collective-permute-start(f32[512,1024]{1,0:T(8,128)} %get-tuple-element.417), channel_id=1, source_target_pairs={{0,2},{1,3},{2,0},{3,1},{4,6},{5,7},{6,4},{7,5}} | collective-permute-start | bytes 6291464 | tf_op jit(solution)/shard_map/ppermute | solution.py:373
  832.3 96.5 %collective-permute-start.32 = (bf16[2048,256]{1,0:T(8,128)(2,1)}, bf16[2048,256]{1,0:T(8,128)(2,1)}, u32[]{:S(2)}, u32[]{:S(2)}) collective-permute-start(bf16[2048,256]{1,0:T(8,128)(2,1)} %pad_maximum_fusion.1), channel_id=1, source_target_pairs={{0,1},{1,0},{2,3},{3,2},{4,5},{5,4},{6,7},{7,6}} | collective-permute-start | bytes 3145736 | tf_op jit(solution)/shard_map/ppermute | solution.py:373
  850.3 108.4 %collective-permute-start.33 = (bf16[2048,256]{1,0:T(8,128)(2,1)}, bf16[2048,256]{1,0:T(8,128)(2,1)}, u32[]{:S(2)}, u32[]{:S(2)}) collective-permute-start(bf16[2048,256]{1,0:T(8,128)(2,1)} %get-tuple-element.360.refs_14_.refs_15_), channel_id=1, source_target_pairs={{0,1},{1,0},{2,3},{3,2},{4,5},{5,4},{6,7},{7,6}} | collective-permute-start | bytes 3145736 | tf_op jit(solution)/shard_map/ppermute | solution.py:373
  854.5 104.3 %collective-permute-start.34 = (bf16[2048,256]{1,0:T(8,128)(2,1)}, bf16[2048,256]{1,0:T(8,128)(2,1)}, u32[]{:S(2)}, u32[]{:S(2)}) collective-permute-start(bf16[2048,256]{1,0:T(8,128)(2,1)} %get-tuple-element.384.refs_14_.refs_15_), channel_id=1, source_target_pairs={{0,1},{1,0},{2,3},{3,2},{4,5},{5,4},{6,7},{7,6}} | collective-permute-start | bytes 3145736 | tf_op jit(solution)/shard_map/ppermute | solution.py:373
  1006.6 92.1 %collective-permute-start.58 = (f32[2048,1024]{1,0:T(8,128)}, f32[2048,1024]{1,0:T(8,128)}, u32[]{:S(2)}, u32[]{:S(2)}) collective-permute-start(f32[2048,1024]{1,0:T(8,128)} %assemble.6.refs_0_), channel_id=1, source_target_pairs={{0,1},{1,0},{2,3},{3,2},{4,5},{5,4},{6,7},{7,6}} | collective-permute-start | bytes 25165832 | tf_op jit(solution)/shard_map/ppermute | solution.py:373
  1008.6 90.5 %collective-permute-start.59 = (f32[2048,1024]{1,0:T(8,128)}, f32[2048,1024]{1,0:T(8,128)}, u32[]{:S(2)}, u32[]{:S(2)}) collective-permute-start(f32[2048,1024]{1,0:T(8,128)} %assemble.7.refs_2_), channel_id=1, source_target_pairs={{0,1},{1,0},{2,3},{3,2},{4,5},{5,4},{6,7},{7,6}} | collective-permute-start | bytes 25165832 | tf_op jit(solution)/shard_map/ppermute | solution.py:373
  1060.4 126.6 %collective-permute-start.44 = (f32[256,1024]{1,0:T(8,128)S(1)}, f32[256,1024]{1,0:T(8,128)}, u32[]{:S(2)}, u32[]{:S(2)}) collective-permute-start(f32[256,1024]{1,0:T(8,128)S(1)} %copy-done.18), channel_id=1, source_target_pairs={{0,2},{1,3},{2,0},{3,1},{4,6},{5,7},{6,4},{7,5}} | collective-permute-start | bytes 3145736 | tf_op jit(solution)/shard_map/ppermute | solution.py:373
  1092.3 95.1 %collective-permute-start.45 = (f32[256,1024]{1,0:T(8,128)}, f32[256,1024]{1,0:T(8,128)}, u32[]{:S(2)}, u32[]{:S(2)}) collective-permute-start(f32[256,1024]{1,0:T(8,128)} %get-tuple-element.554.refs_1_), channel_id=1, source_target_pairs={{0,4},{1,5},{2,6},{3,7},{4,0},{5,1},{6,2},{7,3}} | collective-permute-start | bytes 3145736 | tf_op jit(solution)/shard_map/ppermute | solution.py:373
  1095.8 91.8 %collective-permute-start.46 = (f32[256,1024]{1,0:T(8,128)}, f32[256,1024]{1,0:T(8,128)}, u32[]{:S(2)}, u32[]{:S(2)}) collective-permute-start(f32[256,1024]{1,0:T(8,128)} %collective-permute-done.42.refs_2_), channel_id=1, source_target_pairs={{0,2},{1,3},{2,0},{3,1},{4,6},{5,7},{6,4},{7,5}} | collective-permute-start | bytes 3145736 | tf_op jit(solution)/shard_map/ppermute | solution.py:373
  1180.8 95.3 %collective-permute-start.62 = (f32[256,1024]{1,0:T(8,128)S(1)}, f32[256,1024]{1,0:T(8,128)}, u32[]{:S(2)}, u32[]{:S(2)}) collective-permute-start(f32[256,1024]{1,0:T(8,128)S(1)} %copy-done.19), channel_id=1, source_target_pairs={{0,2},{1,3},{2,0},{3,1},{4,6},{5,7},{6,4},{7,5}} | collective-permute-start | bytes 3145736 | tf_op jit(solution)/shard_map/ppermute | solution.py:373
  1187.0 89.0 %collective-permute-start.63 = (f32[256,1024]{1,0:T(8,128)S(1)}, f32[256,1024]{1,0:T(8,128)S(1)}, u32[]{:S(2)}, u32[]{:S(2)}) collective-permute-start(f32[256,1024]{1,0:T(8,128)S(1)} %copy-done.20), channel_id=1, source_target_pairs={{0,4},{1,5},{2,6},{3,7},{4,0},{5,1},{6,2},{7,3}} | collective-permute-start | bytes 3145736 | tf_op jit(solution)/shard_map/ppermute | solution.py:373
  1271.5 203.9 %collective-permute-start.72 = (f32[2048,1024]{1,0:T(8,128)}, f32[2048,1024]{1,0:T(8,128)}, u32[]{:S(2)}, u32[]{:S(2)}) collective-permute-start(f32[2048,1024]{1,0:T(8,128)} %assemble.8.refs_0_), channel_id=1, source_target_pairs={{0,1},{1,0},{2,3},{3,2},{4,5},{5,4},{6,7},{7,6}} | collective-permute-start | bytes 25165832 | tf_op jit(solution)/shard_map/ppermute | solution.py:373
  1286.0 198.5 %collective-permute-start.73 = (f32[2048,1024]{1,0:T(8,128)}, f32[2048,1024]{1,0:T(8,128)}, u32[]{:S(2)}, u32[]{:S(2)}) collective-permute-start(f32[2048,1024]{1,0:T(8,128)} %assemble.9.refs_2_), channel_id=1, source_target_pairs={{0,1},{1,0},{2,3},{3,2},{4,5},{5,4},{6,7},{7,6}} | collective-permute-start | bytes 25165832 | tf_op jit(solution)/shard_map/ppermute | solution.py:373
  1335.6 186.6 %all-to-all-start.3 = ((bf16[8,128,2048]{2,1,0:T(8,128)(2,1)}), bf16[8,128,2048]{2,1,0:T(8,128)(2,1)}, u32[]{:S(2)}, u32[]{:S(2)}) async-start(bf16[8,128,2048]{2,1,0:T(8,128)(2,1)} %bitcast.92), calls=%async_computation.3 | async-start | bytes 8388608 | tf_op jit(solution)/shard_map/all_to_all | solution.py:388
  1360.2 89.7 %collective-permute-start.75 = (f32[256,1024]{1,0:T(8,128)}, f32[256,1024]{1,0:T(8,128)}, u32[]{:S(2)}, u32[]{:S(2)}) collective-permute-start(f32[256,1024]{1,0:T(8,128)} %get-tuple-element.595.refs_1_), channel_id=1, source_target_pairs={{0,2},{1,3},{2,0},{3,1},{4,6},{5,7},{6,4},{7,5}} | collective-permute-start | bytes 3145736 | tf_op jit(solution)/shard_map/ppermute | solution.py:373
  1537.3 101.0 %all-to-all-start.5 = ((bf16[8,2,128,2048]{3,2,1,0:T(8,128)(2,1)}), bf16[8,2,128,2048]{3,2,1,0:T(8,128)(2,1)}, u32[]{:S(2)}, u32[]{:S(2)}) async-start(bf16[8,2,128,2048]{3,2,1,0:T(8,128)(2,1)} %get-tuple-element.552), calls=%async_computation.5 | async-start | bytes 16777216 | tf_op jit(solution)/shard_map/all_to_all | solution.py:388
  (133 other events, 4571.1 us)

commit v10 on v9

--- a/solution.py
+++ b/solution.py
@@ -484,7 +484,6 @@
                 rest, = after_chain([part_sums[2]])
                 kept, last = weight_grads(order[4:], units, (cw, co), (rest, part_sums[3]))
                 chain = (last,)
-                o_p, g_p = (jnp.concatenate(after_chain([got[s][n] for s in range(2)]), axis=0) for n in range(2))
             else:
                 held = after_chain(u + gy)
                 qkv = project(held[:4], w_own, k, cw, b_own)
@@ -528,8 +527,12 @@
                         chain = last_add(k - 1)
             started.append(last)
             halves.append((kept, hop(send_a, 2), hop(send_b, 4)))
-            o_got.append(partner(o_p))
-            g_got.append(partner(g_p))
+            if k > 0:
+                o_got.append(partner(o_p))
+                g_got.append(partner(g_p))
+            if k == 3:
+                for n, into in enumerate((o_got, g_got)):
+                    into.insert(0, partner(jnp.concatenate(after_chain([pair[n] for pair in got]), axis=0)))
             bias.append(bk)
 
         rows_of = lambda arrays, s: jnp.concatenate([a[s * seq:(s + 1) * seq] for a in arrays], axis=1)

time: 1660 us -> 1650 us (level)
  no operation moved by 1% of the time
where the time goes in v10:
time: 1650 us; the launch traced here: 1640 us
  Pallas kernels  869 us (53%)
  waiting for transfers between devices  319 us (19%)
  matrix products  144 us (9%)
  starting transfers between devices  117 us (7%)
  blocking collectives  97.9 us (6%)
  local copies, waits for them, and re-layouts  55 us (3%)
  other arithmetic  32.5 us (2%)
    ppermute x86, waiting for transfers between devices, solution(): lax.ppermute(a, 'sp', [(d, d ^ bit) for d in range(n_dev)])  276 us
    pallas_call x17, Pallas kernels, project(): pl.pallas_call(functools.partial(project_kernel, len(units), steps, trans...  203 us
    pallas_call x8, Pallas kernels, weight_grads(): pl.pallas_call(kernel, grid_spec=pltpu.PrefetchScalarGridSpec(num_scalar_...  190 us
    pallas_call x14, Pallas kernels, attention(): pl.pallas_call(kernel, grid=(n_seq, n_heads), in_specs=in_specs, out_spec...  182 us
    dot_general x6, matrix products, dot(): lax.dot_general(a, b, (((ca,), (cb,)), ((), ())), preferred_element_type=...  144 us
    all_to_all x1, blocking collectives, exchange(): return lax.all_to_all(a, 'sp', 0, 0, tiled=True)  97.9 us
    ppermute x86, starting transfers between devices, solution(): lax.ppermute(a, 'sp', [(d, d ^ bit) for d in range(n_dev)])  94.1 us
    pallas_call x3, Pallas kernels, place(): pl.pallas_call(functools.partial(place_kernel, counts, dh), grid_spec=plt...  89.8 us
  transfers between devices with their start and end apart: 91, of which 17 were waited for; matrix products, arithmetic and copies ran while one was open for 13% of the time, Pallas kernels for 50%

profile of v10, /device:TPU:1, one launch (start us, length us, event | category | flops | bytes accessed | tf_op | source)
XLA Modules:
  0.0 1636.9 jit_solution(3368378345396521555)
XLA Ops:
  0.6 97.9 %all_to_all.30.x_ref = bf16[8,2,128,2048]{3,2,1,0:T(8,128)(2,1)} all-to-all(bf16[8,2,128,2048]{3,2,1,0:T(8,128)(2,1)} %bitcast.88), channel_id=1, replica_groups=mesh['sp'=8] {'sp'}, dimensions={0} | all-to-all | bytes 16777216 | tf_op jit(solution)/shard_map/all_to_all | solution.py:388
  126.1 33.6 %lay_out_weights.2.refs_1_.refs_4_ = bf16[2048,4608]{1,0:T(8,128)(2,1)} custom-call(s32[1]{0:T(128)} %bitcast.6.core_ref, bf16[2048,3,24,128]{3,2,1,0:T(8,128)(2,1)} %w_ref.1), custom_call_target="tpu_custom_call" | custom-call | flops 3774873600 | bytes 56623104 | tf_op jit(solution)/shard_map/lay_out_weights/pallas_call | solution.py:227
  290.9 33.6 %lay_out_weights.3 = bf16[2048,4608]{1,0:T(8,128)(2,1)} custom-call(s32[1]{0:T(128)S(6)} %sub.11.core_ref, bf16[2048,3,24,128]{3,2,1,0:T(8,128)(2,1)} %w_ref.1), custom_call_target="tpu_custom_call" | custom-call | flops 3774873600 | bytes 56623104 | tf_op jit(solution)/shard_map/lay_out_weights/pallas_call | solution.py:227
  349.9 20.3 %project.25.qkv_ref = bf16[4096,768]{1,0:T(8,128)(2,1)} custom-call(bf16[1024,2048]{1,0:T(8,128)(2,1)} %norm.2.refs_0_, bf16[1024,2048]{1,0:T(8,128)(2,1)} %norm.3.refs_0_.refs_1_, bf16[1024,2048]{1,0:T(8,128)(2,1)} %collective-permute-done.refs_0_.refs_1_.refs_2_, bf16[1024,2048]{1,0:T(8,128)(2,1)} %collective-permute-done.1.refs_0_.refs_1_.refs_3_, ...), custom_call_target="tpu_custom_call" | custom-call | flops 12884901888 | bytes 23068672 | tf_op jit(solution)/shard_map/project/pallas_call | solution.py:115
  413.0 29.1 %weight_grads.11 = (f32[512,1024]{1,0:T(8,128)}, f32[512,1024]{1,0:T(8,128)}, f32[512,1024]{1,0:T(8,128)}, f32[512,1024]{1,0:T(8,128)}) custom-call(s32[8]{0:T(128)} %stack.50.order_ref, bf16[1024,2048]{1,0:T(8,128)(2,1)} %norm.2.refs_0_, bf16[1024,2048]{1,0:T(8,128)(2,1)} %norm.3.refs_0_.refs_1_, ...), custom_call_target="tpu_custom_call" | custom-call | flops 17179869184 | bytes 67108864 | tf_op jit(solution)/shard_map/weight_grads/pallas_call | solution.py:153
  454.8 20.3 %project.27.qkv_ref = bf16[4096,768]{1,0:T(8,128)(2,1)} custom-call(bf16[1024,2048]{1,0:T(8,128)(2,1)} %norm.2.refs_0_, bf16[1024,2048]{1,0:T(8,128)(2,1)} %norm.3.refs_0_.refs_1_, bf16[1024,2048]{1,0:T(8,128)(2,1)} %collective-permute-done.refs_0_.refs_1_.refs_2_, bf16[1024,2048]{1,0:T(8,128)(2,1)} %collective-permute-done.1.refs_0_.refs_1_.refs_3_, ...), custom_call_target="tpu_custom_call" | custom-call | flops 12884901888 | bytes 23068672 | tf_op jit(solution)/shard_map/project/pallas_call | solution.py:115
  514.9 29.1 %weight_grads.12 = (f32[512,1024]{1,0:T(8,128)}, f32[512,1024]{1,0:T(8,128)}, f32[512,1024]{1,0:T(8,128)}, f32[512,1024]{1,0:T(8,128)}) custom-call(s32[8]{0:T(128)} %stack.50.order_ref, bf16[1024,2048]{1,0:T(8,128)(2,1)} %norm.2.refs_0_, bf16[1024,2048]{1,0:T(8,128)(2,1)} %norm.3.refs_0_.refs_1_, ...), custom_call_target="tpu_custom_call" | custom-call | flops 17179869184 | bytes 67108864 | tf_op jit(solution)/shard_map/weight_grads/pallas_call | solution.py:153
  552.6 21.1 %collective-permute-done.11.b2 = f32[256,1024]{1,0:T(8,128)} collective-permute-done((f32[256,1024]{1,0:T(8,128)}, f32[256,1024]{1,0:T(8,128)}, u32[]{:S(2)}, u32[]{:S(2)}) %collective-permute-start.11) | collective-permute-done | bytes 1048608 | tf_op jit(solution)/shard_map/ppermute | solution.py:373
  592.2 20.5 %project.29.qkv_ref = bf16[4096,768]{1,0:T(8,128)(2,1)} custom-call(bf16[1024,2048]{1,0:T(8,128)(2,1)} %norm.2.refs_0_, bf16[1024,2048]{1,0:T(8,128)(2,1)} %norm.3.refs_0_.refs_1_, bf16[1024,2048]{1,0:T(8,128)(2,1)} %collective-permute-done.refs_0_.refs_1_.refs_2_, bf16[1024,2048]{1,0:T(8,128)(2,1)} %collective-permute-done.1.refs_0_.refs_1_.refs_3_, ...), custom_call_target="tpu_custom_call" | custom-call | flops 12884901888 | bytes 23068672 | tf_op jit(solution)/shard_map/project/pallas_call | solution.py:115
  650.1 29.4 %weight_grads.13 = (f32[512,1024]{1,0:T(8,128)}, f32[512,1024]{1,0:T(8,128)}, f32[512,1024]{1,0:T(8,128)}, f32[512,1024]{1,0:T(8,128)}) custom-call(s32[8]{0:T(128)} %stack.50.order_ref, bf16[1024,2048]{1,0:T(8,128)(2,1)} %norm.2.refs_0_, bf16[1024,2048]{1,0:T(8,128)(2,1)} %norm.3.refs_0_.refs_1_, ...), custom_call_target="tpu_custom_call" | custom-call | flops 17179869184 | bytes 67108864 | tf_op jit(solution)/shard_map/weight_grads/pallas_call | solution.py:153
  713.6 20.3 %project.31.qkv_ref = bf16[4096,768]{1,0:T(8,128)(2,1)} custom-call(bf16[1024,2048]{1,0:T(8,128)(2,1)} %norm.2.refs_0_, bf16[1024,2048]{1,0:T(8,128)(2,1)} %norm.3.refs_0_.refs_1_, bf16[1024,2048]{1,0:T(8,128)(2,1)} %collective-permute-done.refs_0_.refs_1_.refs_2_, bf16[1024,2048]{1,0:T(8,128)(2,1)} %collective-permute-done.1.refs_0_.refs_1_.refs_3_, ...), custom_call_target="tpu_custom_call" | custom-call | flops 12884901888 | bytes 23068672 | tf_op jit(solution)/shard_map/project/pallas_call | solution.py:115
  794.3 29.4 %weight_grads.14 = (f32[512,1024]{1,0:T(8,128)}, f32[512,1024]{1,0:T(8,128)}, f32[512,1024]{1,0:T(8,128)}, f32[512,1024]{1,0:T(8,128)}) custom-call(s32[8]{0:T(128)} %stack.50.order_ref, bf16[1024,2048]{1,0:T(8,128)(2,1)} %norm.2.refs_0_, bf16[1024,2048]{1,0:T(8,128)(2,1)} %norm.3.refs_0_.refs_1_, ...), custom_call_target="tpu_custom_call" | custom-call | flops 17179869184 | bytes 67108864 | tf_op jit(solution)/shard_map/weight_grads/pallas_call | solution.py:153
  861.8 20.5 %project.33.qkv_ref = bf16[4096,768]{1,0:T(8,128)(2,1)} custom-call(bf16[1024,2048]{1,0:T(8,128)(2,1)} %norm.2.refs_0_, bf16[1024,2048]{1,0:T(8,128)(2,1)} %norm.3.refs_0_.refs_1_, bf16[1024,2048]{1,0:T(8,128)(2,1)} %collective-permute-done.refs_0_.refs_1_.refs_2_, bf16[1024,2048]{1,0:T(8,128)(2,1)} %collective-permute-done.1.refs_0_.refs_1_.refs_3_, ...), custom_call_target="tpu_custom_call" | custom-call | flops 12884901888 | bytes 23068672 | tf_op jit(solution)/shard_map/project/pallas_call | solution.py:115
  920.5 29.8 %weight_grads.15 = (f32[512,1024]{1,0:T(8,128)}, f32[512,1024]{1,0:T(8,128)}, f32[512,1024]{1,0:T(8,128)}, f32[512,1024]{1,0:T(8,128)}) custom-call(s32[8]{0:T(128)} %stack.50.order_ref, bf16[1024,2048]{1,0:T(8,128)(2,1)} %norm.2.refs_0_, bf16[1024,2048]{1,0:T(8,128)(2,1)} %norm.3.refs_0_.refs_1_, ...), custom_call_target="tpu_custom_call" | custom-call | flops 17179869184 | bytes 67108864 | tf_op jit(solution)/shard_map/weight_grads/pallas_call | solution.py:153
  1091.0 29.9 %place.3 = (f32[2048,3,24,128]{3,2,1,0:T(8,128)}, f32[24,128,2048]{2,1,0:T(8,128)}) custom-call(s32[1]{0:T(128)} %bitcast.6.core_ref, f32[2048,1024]{1,0:T(8,128)} %assemble.6.refs_0_, f32[2048,1024]{1,0:T(8,128)} %collective-permute-done.58.refs_1_, f32[2048,1024]{1,0:T(8,128)} %assemble.7.refs_2_, f32[2048,1024]{1,0:T(8,128)} %collective-permute-done.59.refs_3_), custom_call_target="tpu_custom_call" | custom-call | flops 8388608 | bytes 8388608 | tf_op jit(solution)/shard_map/place/pallas_call | solution.py:271
  1120.9 50.2 %fusion.7 = f32[2048,2048]{1,0:T(8,128)} fusion(bf16[2048,4608]{1,0:T(8,128)(2,1)} %get-tuple-element.542.refs_8_.refs_9_, bf16[2048,4608]{1,0:T(8,128)(2,1)} %lay_out_weights.2.refs_1_.refs_4_), kind=kOutput, calls=%fused_computation.65 | convolution fusion | flops 38654705664 | bytes 54525952 | tf_op jit(solution)/shard_map/dot_general | solution.py:20
  1180.4 50.8 %convolution_add_fusion.grad_ref = bf16[2048,2048]{1,0:T(8,128)(2,1)} fusion(f32[2048,2048]{1,0:T(8,128)} %fusion.7, bf16[2048,4608]{1,0:T(8,128)(2,1)} %copy-done.37, bf16[2048,4608]{1,0:T(8,128)(2,1)} %lay_out_weights.3), kind=kOutput, calls=%fused_computation | convolution fusion | flops 38663094272 | bytes 62914560 | tf_op jit(solution)/shard_map/dot_general | solution.py:20
  1283.9 43.0 %all-to-all-done.4.in_ref = bf16[8,128,2048]{2,1,0:T(8,128)(2,1)} async-done(((bf16[8,128,2048]{2,1,0:T(8,128)(2,1)}), bf16[8,128,2048]{2,1,0:T(8,128)(2,1)}, u32[]{:S(2)}, u32[]{:S(2)}) %all-to-all-start.4) | async-done | bytes 4194336 | tf_op jit(solution)/shard_map/all_to_all | solution.py:388
  1353.3 65.4 %collective-permute-done.68.refs_4_ = f32[256,1024]{1,0:T(8,128)S(1)} collective-permute-done((f32[256,1024]{1,0:T(8,128)S(1)}, f32[256,1024]{1,0:T(8,128)S(1)}, u32[]{:S(2)}, u32[]{:S(2)}) %collective-permute-start.68) | collective-permute-done | bytes 1048608 | tf_op jit(solution)/shard_map/ppermute | solution.py:373
  1420.2 20.9 %collective-permute-done.75.refs_3_ = f32[256,1024]{1,0:T(8,128)} collective-permute-done((f32[256,1024]{1,0:T(8,128)}, f32[256,1024]{1,0:T(8,128)}, u32[]{:S(2)}, u32[]{:S(2)}) %collective-permute-start.75) | collective-permute-done | bytes 1048608 | tf_op jit(solution)/shard_map/ppermute | solution.py:373
  1443.1 20.5 %collective-permute-done.70.refs_6_ = f32[256,1024]{1,0:T(8,128)S(1)} collective-permute-done((f32[256,1024]{1,0:T(8,128)}, f32[256,1024]{1,0:T(8,128)S(1)}, u32[]{:S(2)}, u32[]{:S(2)}) %collective-permute-start.70) | collective-permute-done | bytes 1048608 | tf_op jit(solution)/shard_map/ppermute | solution.py:373
  1478.8 29.9 %place.4 = (f32[2048,3,24,128]{3,2,1,0:T(8,128)}, f32[24,128,2048]{2,1,0:T(8,128)}) custom-call(s32[1]{0:T(128)} %bitcast.6.core_ref, f32[2048,1024]{1,0:T(8,128)} %assemble.8.refs_0_, f32[2048,1024]{1,0:T(8,128)} %collective-permute-done.72.refs_1_, f32[2048,1024]{1,0:T(8,128)} %assemble.9.refs_2_, ...), custom_call_target="tpu_custom_call", output_to_operand_aliasing={{0}: (5, {}), {1}: (6, {})} | custom-call | flops 8388608 | bytes 8388608 | tf_op jit(solution)/shard_map/place/pallas_call | solution.py:271
  1546.2 29.9 %place.5 = (f32[2048,3,24,128]{3,2,1,0:T(8,128)}, f32[24,128,2048]{2,1,0:T(8,128)}) custom-call(s32[1]{0:T(128)} %bitcast.6.core_ref, f32[2048,1024]{1,0:T(8,128)} %assemble.10.refs_0_, f32[2048,1024]{1,0:T(8,128)} %collective-permute-done.80.refs_1_, f32[2048,1024]{1,0:T(8,128)} %assemble.11.refs_2_, ...), custom_call_target="tpu_custom_call", output_to_operand_aliasing={{0}: (5, {}), {1}: (6, {})} | custom-call | flops 8388608 | bytes 8388608 | tf_op jit(solution)/shard_map/place/pallas_call | solution.py:271
  1576.1 50.1 %collective-permute-done.83 = f32[120,128]{1,0:T(8,128)S(1)} collective-permute-done((f32[120,128]{1,0:T(8,128)S(1)}, f32[120,128]{1,0:T(8,128)S(1)}, u32[]{:S(2)}, u32[]{:S(2)}) %collective-permute-start.83) | collective-permute-done | bytes 61472 | tf_op jit(solution)/shard_map/ppermute | solution.py:373
  (425 shorter events, 809.3 us)
Async XLA Ops:
  410.5 97.1 %collective-permute-start.18 = (f32[256,1024]{1,0:T(8,128)}, f32[256,1024]{1,0:T(8,128)}, u32[]{:S(2)}, u32[]{:S(2)}) collective-permute-start(f32[256,1024]{1,0:T(8,128)} %get-tuple-element.423.refs_0_), channel_id=1, source_target_pairs={{0,4},{1,5},{2,6},{3,7},{4,0},{5,1},{6,2},{7,3}} | collective-permute-start | bytes 3145736 | tf_op jit(solution)/shard_map/ppermute | solution.py:373
  411.9 96.9 %collective-permute-start.19 = (f32[256,1024]{1,0:T(8,128)}, f32[256,1024]{1,0:T(8,128)}, u32[]{:S(2)}, u32[]{:S(2)}) collective-permute-start(f32[256,1024]{1,0:T(8,128)} %get-tuple-element.424.refs_1_), channel_id=1, source_target_pairs={{0,2},{1,3},{2,0},{3,1},{4,6},{5,7},{6,4},{7,5}} | collective-permute-start | bytes 3145736 | tf_op jit(solution)/shard_map/ppermute | solution.py:373
  506.2 142.4 %collective-permute-start.20 = (f32[256,1024]{1,0:T(8,128)S(1)}, f32[256,1024]{1,0:T(8,128)}, u32[]{:S(2)}, u32[]{:S(2)}) collective-permute-start(f32[256,1024]{1,0:T(8,128)S(1)} %copy-done.25), channel_id=1, source_target_pairs={{0,2},{1,3},{2,0},{3,1},{4,6},{5,7},{6,4},{7,5}} | collective-permute-start | bytes 3145736 | tf_op jit(solution)/shard_map/ppermute | solution.py:373
  507.5 142.3 %collective-permute-start.21 = (f32[256,1024]{1,0:T(8,128)}, f32[256,1024]{1,0:T(8,128)}, u32[]{:S(2)}, u32[]{:S(2)}) collective-permute-start(f32[256,1024]{1,0:T(8,128)} %get-tuple-element.424.refs_1_), channel_id=1, source_target_pairs={{0,4},{1,5},{2,6},{3,7},{4,0},{5,1},{6,2},{7,3}} | collective-permute-start | bytes 3145736 | tf_op jit(solution)/shard_map/ppermute | solution.py:373
  508.8 141.2 %collective-permute-start.22 = (f32[256,1024]{1,0:T(8,128)}, f32[256,1024]{1,0:T(8,128)}, u32[]{:S(2)}, u32[]{:S(2)}) collective-permute-start(f32[256,1024]{1,0:T(8,128)} %collective-permute-done.18.refs_2_), channel_id=1, source_target_pairs={{0,2},{1,3},{2,0},{3,1},{4,6},{5,7},{6,4},{7,5}} | collective-permute-start | bytes 3145736 | tf_op jit(solution)/shard_map/ppermute | solution.py:373
  552.5 91.0 %collective-permute-start.12 = (f32[512,1024]{1,0:T(8,128)}, f32[512,1024]{1,0:T(8,128)S(1)}, u32[]{:S(2)}, u32[]{:S(2)}) collective-permute-start(f32[512,1024]{1,0:T(8,128)} %get-tuple-element.406), channel_id=1, source_target_pairs={{0,2},{1,3},{2,0},{3,1},{4,6},{5,7},{6,4},{7,5}} | collective-permute-start | bytes 6291464 | tf_op jit(solution)/shard_map/ppermute | solution.py:373
  679.6 112.0 %collective-permute-start.28 = (f32[256,1024]{1,0:T(8,128)}, f32[256,1024]{1,0:T(8,128)}, u32[]{:S(2)}, u32[]{:S(2)}) collective-permute-start(f32[256,1024]{1,0:T(8,128)} %get-tuple-element.462.refs_0_), channel_id=1, source_target_pairs={{0,2},{1,3},{2,0},{3,1},{4,6},{5,7},{6,4},{7,5}} | collective-permute-start | bytes 3145736 | tf_op jit(solution)/shard_map/ppermute | solution.py:373
  684.7 107.6 %collective-permute-start.29 = (f32[256,1024]{1,0:T(8,128)}, f32[256,1024]{1,0:T(8,128)}, u32[]{:S(2)}, u32[]{:S(2)}) collective-permute-start(f32[256,1024]{1,0:T(8,128)} %get-tuple-element.463.refs_1_), channel_id=1, source_target_pairs={{0,4},{1,5},{2,6},{3,7},{4,0},{5,1},{6,2},{7,3}} | collective-permute-start | bytes 3145736 | tf_op jit(solution)/shard_map/ppermute | solution.py:373
  684.9 101.9 %collective-permute-start.14 = (f32[512,1024]{1,0:T(8,128)}, f32[512,1024]{1,0:T(8,128)}, u32[]{:S(2)}, u32[]{:S(2)}) collective-permute-start(f32[512,1024]{1,0:T(8,128)} %get-tuple-element.417), channel_id=1, source_target_pairs={{0,2},{1,3},{2,0},{3,1},{4,6},{5,7},{6,4},{7,5}} | collective-permute-start | bytes 6291464 | tf_op jit(solution)/shard_map/ppermute | solution.py:373
  823.7 96.0 %collective-permute-start.33 = (bf16[2048,256]{1,0:T(8,128)(2,1)S(1)}, bf16[2048,256]{1,0:T(8,128)(2,1)}, u32[]{:S(2)}, u32[]{:S(2)}) collective-permute-start(bf16[2048,256]{1,0:T(8,128)(2,1)S(1)} %copy-done.11), channel_id=1, source_target_pairs={{0,1},{1,0},{2,3},{3,2},{4,5},{5,4},{6,7},{7,6}} | collective-permute-start | bytes 3145736 | tf_op jit(solution)/shard_map/ppermute | solution.py:373
  839.3 110.9 %collective-permute-start.34 = (bf16[2048,256]{1,0:T(8,128)(2,1)}, bf16[2048,256]{1,0:T(8,128)(2,1)}, u32[]{:S(2)}, u32[]{:S(2)}) collective-permute-start(bf16[2048,256]{1,0:T(8,128)(2,1)} %get-tuple-element.384.refs_14_.refs_15_), channel_id=1, source_target_pairs={{0,1},{1,0},{2,3},{3,2},{4,5},{5,4},{6,7},{7,6}} | collective-permute-start | bytes 3145736 | tf_op jit(solution)/shard_map/ppermute | solution.py:373
  846.4 104.0 %collective-permute-start.35 = (bf16[2048,256]{1,0:T(8,128)(2,1)}, bf16[2048,256]{1,0:T(8,128)(2,1)}, u32[]{:S(2)}, u32[]{:S(2)}) collective-permute-start(bf16[2048,256]{1,0:T(8,128)(2,1)} %get-tuple-element.414.refs_14_.refs_15_), channel_id=1, source_target_pairs={{0,1},{1,0},{2,3},{3,2},{4,5},{5,4},{6,7},{7,6}} | collective-permute-start | bytes 3145736 | tf_op jit(solution)/shard_map/ppermute | solution.py:373
  998.2 91.6 %collective-permute-start.58 = (f32[2048,1024]{1,0:T(8,128)}, f32[2048,1024]{1,0:T(8,128)}, u32[]{:S(2)}, u32[]{:S(2)}) collective-permute-start(f32[2048,1024]{1,0:T(8,128)} %assemble.6.refs_0_), channel_id=1, source_target_pairs={{0,1},{1,0},{2,3},{3,2},{4,5},{5,4},{6,7},{7,6}} | collective-permute-start | bytes 25165832 | tf_op jit(solution)/shard_map/ppermute | solution.py:373
  1000.1 90.1 %collective-permute-start.59 = (f32[2048,1024]{1,0:T(8,128)}, f32[2048,1024]{1,0:T(8,128)}, u32[]{:S(2)}, u32[]{:S(2)}) collective-permute-start(f32[2048,1024]{1,0:T(8,128)} %assemble.7.refs_2_), channel_id=1, source_target_pairs={{0,1},{1,0},{2,3},{3,2},{4,5},{5,4},{6,7},{7,6}} | collective-permute-start | bytes 25165832 | tf_op jit(solution)/shard_map/ppermute | solution.py:373
  1051.7 126.2 %collective-permute-start.44 = (f32[256,1024]{1,0:T(8,128)}, f32[256,1024]{1,0:T(8,128)}, u32[]{:S(2)}, u32[]{:S(2)}) collective-permute-start(f32[256,1024]{1,0:T(8,128)} %get-tuple-element.553.refs_0_), channel_id=1, source_target_pairs={{0,2},{1,3},{2,0},{3,1},{4,6},{5,7},{6,4},{7,5}} | collective-permute-start | bytes 3145736 | tf_op jit(solution)/shard_map/ppermute | solution.py:373
  1083.4 95.0 %collective-permute-start.45 = (f32[256,1024]{1,0:T(8,128)S(1)}, f32[256,1024]{1,0:T(8,128)}, u32[]{:S(2)}, u32[]{:S(2)}) collective-permute-start(f32[256,1024]{1,0:T(8,128)S(1)} %copy-done.18), channel_id=1, source_target_pairs={{0,4},{1,5},{2,6},{3,7},{4,0},{5,1},{6,2},{7,3}} | collective-permute-start | bytes 3145736 | tf_op jit(solution)/shard_map/ppermute | solution.py:373
  1086.7 92.4 %collective-permute-start.46 = (f32[256,1024]{1,0:T(8,128)}, f32[256,1024]{1,0:T(8,128)}, u32[]{:S(2)}, u32[]{:S(2)}) collective-permute-start(f32[256,1024]{1,0:T(8,128)} %collective-permute-done.42.refs_2_), channel_id=1, source_target_pairs={{0,2},{1,3},{2,0},{3,1},{4,6},{5,7},{6,4},{7,5}} | collective-permute-start | bytes 3145736 | tf_op jit(solution)/shard_map/ppermute | solution.py:373
  1172.4 95.2 %collective-permute-start.62 = (f32[256,1024]{1,0:T(8,128)S(1)}, f32[256,1024]{1,0:T(8,128)}, u32[]{:S(2)}, u32[]{:S(2)}) collective-permute-start(f32[256,1024]{1,0:T(8,128)S(1)} %copy-done.21), channel_id=1, source_target_pairs={{0,2},{1,3},{2,0},{3,1},{4,6},{5,7},{6,4},{7,5}} | collective-permute-start | bytes 3145736 | tf_op jit(solution)/shard_map/ppermute | solution.py:373
  1177.9 89.8 %collective-permute-start.63 = (f32[256,1024]{1,0:T(8,128)}, f32[256,1024]{1,0:T(8,128)}, u32[]{:S(2)}, u32[]{:S(2)}) collective-permute-start(f32[256,1024]{1,0:T(8,128)} %get-tuple-element.566.refs_1_), channel_id=1, source_target_pairs={{0,4},{1,5},{2,6},{3,7},{4,0},{5,1},{6,2},{7,3}} | collective-permute-start | bytes 3145736 | tf_op jit(solution)/shard_map/ppermute | solution.py:373
  1263.3 203.4 %collective-permute-start.72 = (f32[2048,1024]{1,0:T(8,128)}, f32[2048,1024]{1,0:T(8,128)}, u32[]{:S(2)}, u32[]{:S(2)}) collective-permute-start(f32[2048,1024]{1,0:T(8,128)} %assemble.8.refs_0_), channel_id=1, source_target_pairs={{0,1},{1,0},{2,3},{3,2},{4,5},{5,4},{6,7},{7,6}} | collective-permute-start | bytes 25165832 | tf_op jit(solution)/shard_map/ppermute | solution.py:373
  1277.4 198.4 %collective-permute-start.73 = (f32[2048,1024]{1,0:T(8,128)}, f32[2048,1024]{1,0:T(8,128)}, u32[]{:S(2)}, u32[]{:S(2)}) collective-permute-start(f32[2048,1024]{1,0:T(8,128)} %assemble.9.refs_2_), channel_id=1, source_target_pairs={{0,1},{1,0},{2,3},{3,2},{4,5},{5,4},{6,7},{7,6}} | collective-permute-start | bytes 25165832 | tf_op jit(solution)/shard_map/ppermute | solution.py:373
  1326.9 186.5 %all-to-all-start.3 = ((bf16[8,128,2048]{2,1,0:T(8,128)(2,1)}), bf16[8,128,2048]{2,1,0:T(8,128)(2,1)}, u32[]{:S(2)}, u32[]{:S(2)}) async-start(bf16[8,128,2048]{2,1,0:T(8,128)(2,1)} %bitcast.92), calls=%async_computation.3 | async-start | bytes 8388608 | tf_op jit(solution)/shard_map/all_to_all | solution.py:388
  1351.5 89.7 %collective-permute-start.75 = (f32[256,1024]{1,0:T(8,128)}, f32[256,1024]{1,0:T(8,128)}, u32[]{:S(2)}, u32[]{:S(2)}) collective-permute-start(f32[256,1024]{1,0:T(8,128)} %get-tuple-element.595.refs_1_), channel_id=1, source_target_pairs={{0,2},{1,3},{2,0},{3,1},{4,6},{5,7},{6,4},{7,5}} | collective-permute-start | bytes 3145736 | tf_op jit(solution)/shard_map/ppermute | solution.py:373
  1528.6 101.0 %all-to-all-start.5 = ((bf16[8,2,128,2048]{3,2,1,0:T(8,128)(2,1)}), bf16[8,2,128,2048]{3,2,1,0:T(8,128)(2,1)}, u32[]{:S(2)}, u32[]{:S(2)}) async-start(bf16[8,2,128,2048]{3,2,1,0:T(8,128)(2,1)} %get-tuple-element.552), calls=%async_computation.5 | async-start | bytes 16777216 | tf_op jit(solution)/shard_map/all_to_all | solution.py:388
  (132 other events, 4631.3 us)
